TPU v7x, 128 devices: a whole 4x4x4 slice. The times are simulated.
128 devices in a mesh: sub: 32 (over y, z, core), grp: 4 (over x).
Axes of the slice: x: 4, y: 4, z: 4, core: 2. Of those that a mesh axis runs over, the one named last changes fastest.
Arguments:
- rr_inverse: float32 [256, 512, 512], P(('sub', 'grp')), may hold values from -4 to 4, as said below
- corner_modes: float32 [256, 64, 512], P(('sub', 'grp')), may hold values from -0.5 to 0.5
- coarse_inverse: float32 [8192, 8192], P(('sub', 'grp')), may hold values from -1 to 1, as said below
- inertia: float32 [256, 512], P(('sub', 'grp')), may hold values from 0.5 to 2
- disp_now: float32 [8, 256, 512], P(None, ('sub', 'grp')), may hold values from -4 to 4
- vel_now: float32 [8, 256, 512], P(None, ('sub', 'grp')), may hold values from -4 to 4
- acc_now: float32 [8, 256, 512], P(None, ('sub', 'grp')), may hold values from -8 to 8
- load_next: float32 [8, 256, 512], P(None, ('sub', 'grp')), may hold values from -10 to 10
- basis_rows: float32 [131072, 256], P(('sub', 'grp')), may hold values from -0.015625 to 0.015625
- piece_owner: int32 [128], replicated, may hold values from 0 to 127, each once
Outputs:
- disp_new: float32 [8, 256, 512], P(None, ('sub', 'grp'))
- vel_new: float32 [8, 256, 512], P(None, ('sub', 'grp'))
- projection: float32 [256, 8], replicated
- r_factor: float32 [8, 8], replicated
- new_columns: float32 [8, 131072], P(None, ('sub', 'grp'))
Inputs may be any that keep to these rules, and one draw needn't show every extreme that they name: piece_owner is a permutation. `rr_inverse`: each of the 256 blocks is symmetric positive definite. `coarse_inverse`: symmetric positive definite.
All inputs are finite; a program needn't handle non-finite values.
Results may differ from a plain program's by a relative error of at most 0.00018.
Values sent between devices are 32-bit elements; how exact they have to be, the bound alone decides.
No kernel may reach another device: no remote copies, remote signals or barrier semaphores. Data moves between devices by JAX's collectives and lax.ppermute only.
A program may use at most 64 MiB of HBM per device.

v0:
```python
import math

import jax
import jax.numpy as jnp
from jax import lax
from jax.sharding import Mesh
from jax.sharding import PartitionSpec as P

NC = 32
ITERS = 2
NI = 128
SUB_GRP = ("sub_0", "sub_1", "sub_2", "grp")


highest = lax.Precision.HIGHEST
time_step = 0.5
newmark_beta = 0.25
newmark_gamma = 0.5


def copy_for_each(array, axis):
    copies = jnp.broadcast_to(array, (lax.axis_size(axis), *array.shape))
    return lax.all_to_all(copies, axis, split_axis=0, concat_axis=0, tiled=True)


def laid_out(tiles, dim):
    lengths = list(tiles.shape[1:])
    lengths[dim] *= tiles.shape[0]
    return jnp.moveaxis(tiles, 0, dim).reshape(lengths)


def gather_axes(array, axes, dim):
    far, near = axes
    initial = copy_for_each(array, far)
    tiles = jnp.swapaxes(copy_for_each(initial, near), 0, 1)
    return laid_out(tiles.reshape(-1, *array.shape), dim)


def shifted(array, axis, by):
    count = lax.axis_size(axis)
    return lax.ppermute(array, axis, [(i, (i + by) % count) for i in range(count)])


def of_everyone(array, axis):
    return copy_for_each(array, axis).sum(axis=0)


def by_axis(array, axes):
    far, near = axes
    nearer = of_everyone(array, near)
    return of_everyone(nearer, far)


def contract(segment, matrix_rows):
    return lax.dot_general(segment, matrix_rows, (((1,), (1,)), ((), ())), precision=highest)


def shards(
    rr_inverse,
    corner_modes,
    coarse_inverse,
    inertia,
    disp_now,
    vel_now,
    acc_now,
    load_next,
    basis_rows,
    piece_owner,
):
    case_count, sub_count, unknowns = disp_now.shape
    coarse_total = coarse_inverse.shape[1]
    row_count = sub_count * NC
    shifted_rows = jnp.roll(coarse_inverse, NC, axis=1)
    coarse_pairs = jnp.concatenate(
        [
            shifted_rows.reshape(row_count, coarse_total // NC, NC),
            coarse_inverse.reshape(row_count, coarse_total // NC, NC),
        ],
        axis=2,
    ).reshape(row_count, 2 * coarse_total)

    def apply_green(field):
        local_part = jnp.einsum("jab,cjb->cja", rr_inverse, field, precision=highest)
        corner_terms = jnp.einsum("jmb,cjb->cjm", corner_modes, field, precision=highest)
        flat_terms = corner_terms.reshape(case_count, sub_count * 2 * NC)
        owned_sums = contract(
            gather_axes(flat_terms, (("sub_0", "sub_1"), ("sub_2", "grp")), 1), coarse_pairs
        )
        previous = shifted(owned_sums[:, row_count - NC :], SUB_GRP, 1)
        owned_blocks = owned_sums.reshape(case_count, sub_count, NC)
        left_values = jnp.concatenate(
            [previous.reshape(case_count, 1, NC), owned_blocks[:, :-1]], axis=1
        )
        coarse_values = jnp.concatenate([left_values, owned_blocks], axis=2)
        return local_part + jnp.einsum(
            "jmb,cjm->cjb", corner_modes, coarse_values, precision=highest
        )

    def interface_jump(field):
        following = shifted(field[:, :1, :NI], SUB_GRP, -1)
        first_parts = jnp.concatenate([field[:, 1:, :NI], following], axis=1)
        return field[:, :, unknowns - NI :] - first_parts

    def squared_norm(values):
        return by_axis(
            jnp.sum(values * values, axis=(1, 2)), (("sub_0", "sub_1"), ("sub_2", "grp"))
        )

    right_side = load_next + inertia[None] * (
        disp_now + time_step * vel_now + (0.5 - newmark_beta) * time_step * time_step * acc_now
    )
    green_rhs = apply_green(right_side)
    residual = interface_jump(green_rhs)
    carried = green_rhs
    direction = residual
    norm_now = squared_norm(residual)
    for iteration in range(ITERS):
        earlier = shifted(direction[:, -1:], SUB_GRP, 1)
        left_parts = jnp.concatenate([earlier, direction[:, :-1]], axis=1)
        middle = jnp.zeros((case_count, sub_count, unknowns - 2 * NI), jnp.float32)
        image_field = apply_green(jnp.concatenate([-left_parts, middle, direction], axis=2))
        image = interface_jump(image_field)
        curvature = by_axis(
            jnp.sum(direction * image, axis=(1, 2)), (("sub_0", "sub_1"), ("sub_2", "grp"))
        )
        alpha = (norm_now / curvature)[:, None, None]
        carried = carried - alpha * image_field
        residual = residual - alpha * image
        if iteration + 1 < ITERS:
            norm_next = squared_norm(residual)
            direction = residual + (norm_next / norm_now)[:, None, None] * direction
            norm_now = norm_next
    accel_new = (
        (carried - disp_now) / (newmark_beta * time_step * time_step)
        - vel_now / (newmark_beta * time_step)
        - (0.5 / newmark_beta - 1.0) * acc_now
    )
    vel_new = vel_now + time_step * ((1.0 - newmark_gamma) * acc_now + newmark_gamma * accel_new)
    piece_total = lax.axis_size(SUB_GRP)
    piece_rows = unknowns // piece_total
    inverse = (
        jnp.zeros((piece_total,), jnp.int32)
        .at[piece_owner]
        .set(jnp.arange(piece_total, dtype=jnp.int32))
    )
    outgoing = carried.reshape(case_count, sub_count, piece_total, piece_rows)[:, :, inverse, :]
    outgoing = jnp.transpose(outgoing, (0, 2, 1, 3)).reshape(
        case_count, piece_total * sub_count * piece_rows
    )
    received = lax.all_to_all(outgoing, SUB_GRP, split_axis=1, concat_axis=1, tiled=True)
    projection_part = lax.dot_general(
        basis_rows, received, (((0,), (1,)), ((), ())), precision=highest
    )
    projection = by_axis(projection_part, (("sub_0", "sub_1"), ("sub_2", "grp")))
    remainder = received - lax.dot_general(
        projection, basis_rows, (((0,), (1,)), ((), ())), precision=highest
    )
    gram_local = lax.dot_general(remainder, remainder, (((1,), (1,)), ((), ())), precision=highest)
    lower = jnp.linalg.cholesky(by_axis(gram_local, (("sub_0", "sub_1"), ("sub_2", "grp"))))
    scale_rows = math.sqrt(received.shape[1] * piece_total)
    new_columns = jax.scipy.linalg.solve_triangular(lower, remainder, lower=True) * scale_rows
    r_factor = lower.T / scale_rows
    return (carried, vel_new, projection, r_factor, new_columns)


def solution(mesh):
    finer = Mesh(
        mesh.devices.reshape(4, 4, 2, mesh.shape["grp"]), ("sub_0", "sub_1", "sub_2", "grp")
    )
    placed = (
        P(SUB_GRP, None, None),
        P(SUB_GRP, None, None),
        P(SUB_GRP, None),
        P(SUB_GRP, None),
        P(None, SUB_GRP, None),
        P(None, SUB_GRP, None),
        P(None, SUB_GRP, None),
        P(None, SUB_GRP, None),
        P(SUB_GRP, None),
        P(),
    )
    return jax.shard_map(
        shards,
        mesh=finer,
        in_specs=placed,
        out_specs=(P(None, SUB_GRP, None), P(None, SUB_GRP, None), P(), P(), P(None, SUB_GRP)),
        check_vma=False,
    )
```

profile of v0, /device:TPU:0, one launch (start us, length us, event | category | flops | bytes accessed | tf_op | source)
XLA Modules:
  0.0 315.4 jit_solution(2492551397365498527)
XLA Ops:
  3.6 8.2 %all-to-all-start = ((f32[16,8,128]{2,1,0:T(8,128)}), f32[16,8,128]{2,1,0:T(8,128)S(1)}, u32[]{:S(2)}, u32[]{:S(2)}) async-start(f32[16,8,128]{2,1,0:T(8,128)} %broadcast_in_dim.66), calls=%async_computation | async-start | bytes 131072 | tf_op jit(solution)/shard_map/all_to_all | solution.py:23
  12.6 6.8 %all-to-all-done = f32[16,8,128]{2,1,0:T(8,128)S(1)} async-done(((f32[16,8,128]{2,1,0:T(8,128)}), f32[16,8,128]{2,1,0:T(8,128)S(1)}, u32[]{:S(2)}, u32[]{:S(2)}) %all-to-all-start) | async-done | bytes 65568 | tf_op jit(solution)/shard_map/all_to_all | solution.py:23
  20.3 4.3 %all-to-all-start.1 = ((f32[8,16,8,128]{3,2,1,0:T(8,128)}), f32[8,16,8,128]{3,2,1,0:T(8,128)S(1)}, u32[]{:S(2)}, u32[]{:S(2)}) async-start(f32[8,16,8,128]{3,2,1,0:T(8,128)} %broadcast_in_dim.67), calls=%async_computation.1 | async-start | bytes 1048576 | tf_op jit(solution)/shard_map/all_to_all | solution.py:23
  24.6 3.5 %pad_maximum_fusion.1 = f32[64,8192]{1,0:T(8,128)} fusion(f32[64,8160]{1,0:T(8,128)} %bitcast.91, f32[64,32]{1,0:T(8,128)S(1)} %slice.77), kind=kLoop, calls=%fused_computation.3 | loop fusion | flops 524288 | bytes 4194304 | tf_op jit(solution)/shard_map/jit(_roll_static)/concatenate | solution.py:73
  28.1 3.8 %copy.129 = f32[64,8192]{0,1:T(8,128)} copy(f32[64,8192]{1,0:T(8,128)} %param.12) | data formatting | bytes 4194304 | tf_op args[2]
  32.0 3.8 %copy.128 = f32[64,8192]{0,1:T(8,128)} copy(f32[64,8192]{1,0:T(8,128)} %pad_maximum_fusion.1) | data formatting | bytes 4194304 | tf_op jit(solution)/shard_map/jit(_roll_static)/concatenate | solution.py:73
  35.8 8.4 %pad_maximum_fusion = f32[64,256,64]{0,2,1:T(8,128)} fusion(f32[64,256,32]{0,2,1:T(8,128)} %bitcast.89, f32[64,256,32]{0,2,1:T(8,128)} %bitcast.90), kind=kLoop, calls=%fused_computation.2 | loop fusion | flops 1048576 | bytes 8388608 | tf_op jit(solution)/shard_map/concatenate | solution.py:74
  44.2 6.5 %fusion.50 = f32[8,64]{1,0:T(8,128)S(1)} fusion(f32[8,16384]{1,0:T(8,128)S(1)} %bitcast.96, f32[64,16384]{0,1:T(8,128)} %bitcast.86), kind=kOutput, calls=%fused_computation.90 | convolution fusion | flops 100663296 | bytes 4720640 | tf_op jit(solution)/shard_map/dot_general | solution.py:55
  50.7 2.0 collective-permute-start
  52.8 1.8 fusion.10
  54.7 4.5 %collective-permute-done = f32[8,32]{1,0:T(8,128)S(1)} collective-permute-done((f32[8,32]{1,0:T(8,128)S(1)}, f32[8,32]{1,0:T(8,128)S(1)}, u32[]{:S(2)}, u32[]{:S(2)}) %collective-permute-start) | collective-permute-done | bytes 1056 | tf_op jit(solution)/shard_map/ppermute | solution.py:41
  60.2 3.0 collective-permute-done.1
  63.2 8.4 %collective-permute-done.2 = f32[8,1,128]{2,0,1:T(8,128)S(1)} collective-permute-done((f32[8,1,128]{2,0,1:T(8,128)S(1)}, f32[8,1,128]{2,0,1:T(8,128)S(1)}, u32[]{:S(2)}, u32[]{:S(2)}) %collective-permute-start.2) | collective-permute-done | bytes 4128 | tf_op jit(solution)/shard_map/ppermute | solution.py:41
  72.1 10.2 %all_to_all.110 = f32[16,8,128]{2,1,0:T(8,128)S(1)} all-to-all(f32[16,8,128]{2,1,0:T(8,128)S(1)} %broadcast_in_dim.70), channel_id=1, replica_groups=mesh['sub_0'=4,'sub_1'=4,'sub_2'=2,'grp'=4] {'sub_0','sub_1'}, dimensions={0} | all-to-all | bytes 131072 | tf_op jit(solution)/shard_map/all_to_all | solution.py:23
  82.4 12.1 %all_to_all.111 = f32[8,16,8,128]{3,2,1,0:T(8,128)S(1)} all-to-all(f32[8,16,8,128]{3,2,1,0:T(8,128)S(1)} %broadcast_in_dim.71), channel_id=1, replica_groups=mesh['sub_0'=4,'sub_1'=4,'sub_2'=2,'grp'=4] {'sub_2','grp'}, dimensions={0} | all-to-all | bytes 1048576 | tf_op jit(solution)/shard_map/all_to_all | solution.py:23
  94.5 6.4 %fusion.51 = f32[8,64]{1,0:T(8,128)S(1)} fusion(f32[8,16384]{1,0:T(8,128)S(1)} %bitcast.97, f32[64,16384]{0,1:T(8,128)} %bitcast.87), kind=kOutput, calls=%fused_computation.91 | convolution fusion | flops 100663296 | bytes 4720640 | tf_op jit(solution)/shard_map/dot_general | solution.py:55
  102.1 1.8 fusion.5
  104.0 5.7 %collective-permute-done.3 = f32[8,32]{1,0:T(8,128)S(1)} collective-permute-done((f32[8,32]{1,0:T(8,128)S(1)}, f32[8,32]{1,0:T(8,128)S(1)}, u32[]{:S(2)}, u32[]{:S(2)}) %collective-permute-start.3) | collective-permute-done | bytes 1056 | tf_op jit(solution)/shard_map/ppermute | solution.py:41
  110.7 3.0 collective-permute-done.4
  113.8 7.6 %all_to_all.112 = f32[8,1,8]{2,1,0:T(1,128)S(1)} all-to-all(f32[8,1,8]{2,1,0:T(1,128)S(1)} %broadcast_in_dim.68), channel_id=1, replica_groups=mesh['sub_0'=4,'sub_1'=4,'sub_2'=2,'grp'=4] {'sub_2','grp'}, dimensions={0} | all-to-all | bytes 512 | tf_op jit(solution)/shard_map/all_to_all | solution.py:23
  122.0 3.3 %all-to-all-start.6 = ((f32[8,1,8]{2,1,0:T(1,128)}), f32[8,1,8]{2,1,0:T(1,128)S(1)}, u32[]{:S(2)}, u32[]{:S(2)}) async-start(f32[8,1,8]{2,1,0:T(1,128)} %broadcast_in_dim.72), calls=%async_computation.6 | async-start | bytes 8192 | tf_op jit(solution)/shard_map/all_to_all | solution.py:23
  125.4 5.1 %all-to-all-done.6 = f32[8,1,8]{2,1,0:T(1,128)S(1)} async-done(((f32[8,1,8]{2,1,0:T(1,128)}), f32[8,1,8]{2,1,0:T(1,128)S(1)}, u32[]{:S(2)}, u32[]{:S(2)}) %all-to-all-start.6) | async-done | bytes 288 | tf_op jit(solution)/shard_map/all_to_all | solution.py:23
  131.1 6.2 %all-to-all-start.3 = ((f32[16,1,8]{2,1,0:T(1,128)}), f32[16,1,8]{2,1,0:T(1,128)S(1)}, u32[]{:S(2)}, u32[]{:S(2)}) async-start(f32[16,1,8]{2,1,0:T(1,128)} %broadcast_in_dim.69), calls=%async_computation.3 | async-start | bytes 16384 | tf_op jit(solution)/shard_map/all_to_all | solution.py:23
  137.3 7.5 %all-to-all-done.3 = f32[16,1,8]{2,1,0:T(1,128)S(1)} async-done(((f32[16,1,8]{2,1,0:T(1,128)}), f32[16,1,8]{2,1,0:T(1,128)S(1)}, u32[]{:S(2)}, u32[]{:S(2)}) %all-to-all-start.3) | async-done | bytes 544 | tf_op jit(solution)/shard_map/all_to_all | solution.py:23
  145.3 3.5 %all-to-all-start.7 = ((f32[16,1,8]{2,1,0:T(1,128)}), f32[16,1,8]{2,1,0:T(1,128)S(1)}, u32[]{:S(2)}, u32[]{:S(2)}) async-start(f32[16,1,8]{2,1,0:T(1,128)} %broadcast_in_dim.73), calls=%async_computation.7 | async-start | bytes 16384 | tf_op jit(solution)/shard_map/all_to_all | solution.py:23
  148.9 7.4 %all-to-all-done.7 = f32[16,1,8]{2,1,0:T(1,128)S(1)} async-done(((f32[16,1,8]{2,1,0:T(1,128)}), f32[16,1,8]{2,1,0:T(1,128)S(1)}, u32[]{:S(2)}, u32[]{:S(2)}) %all-to-all-start.7) | async-done | bytes 544 | tf_op jit(solution)/shard_map/all_to_all | solution.py:23
  156.5 7.6 %all_to_all.113 = f32[8,1,8]{2,1,0:T(1,128)S(1)} all-to-all(f32[8,1,8]{2,1,0:T(1,128)S(1)} %broadcast_in_dim.74), channel_id=1, replica_groups=mesh['sub_0'=4,'sub_1'=4,'sub_2'=2,'grp'=4] {'sub_2','grp'}, dimensions={0} | all-to-all | bytes 512 | tf_op jit(solution)/shard_map/all_to_all | solution.py:23
  164.2 10.6 %all_to_all.114 = f32[16,1,8]{2,1,0:T(1,128)S(1)} all-to-all(f32[16,1,8]{2,1,0:T(1,128)S(1)} %broadcast_in_dim.75), channel_id=1, replica_groups=mesh['sub_0'=4,'sub_1'=4,'sub_2'=2,'grp'=4] {'sub_0','sub_1'}, dimensions={0} | all-to-all | bytes 1024 | tf_op jit(solution)/shard_map/all_to_all | solution.py:23
  175.5 7.9 %collective-permute-done.5 = f32[8,1,128]{2,0,1:T(8,128)S(1)} collective-permute-done((f32[8,1,128]{2,0,1:T(8,128)S(1)}, f32[8,1,128]{2,0,1:T(8,128)S(1)}, u32[]{:S(2)}, u32[]{:S(2)}) %collective-permute-start.5) | collective-permute-done | bytes 4128 | tf_op jit(solution)/shard_map/ppermute | solution.py:41
  183.8 10.2 %all_to_all.115 = f32[16,8,128]{2,1,0:T(8,128)S(1)} all-to-all(f32[16,8,128]{2,1,0:T(8,128)S(1)} %broadcast_in_dim.76), channel_id=1, replica_groups=mesh['sub_0'=4,'sub_1'=4,'sub_2'=2,'grp'=4] {'sub_0','sub_1'}, dimensions={0} | all-to-all | bytes 131072 | tf_op jit(solution)/shard_map/all_to_all | solution.py:23
  194.1 12.1 %all_to_all.116 = f32[8,16,8,128]{3,2,1,0:T(8,128)S(1)} all-to-all(f32[8,16,8,128]{3,2,1,0:T(8,128)S(1)} %broadcast_in_dim.77), channel_id=1, replica_groups=mesh['sub_0'=4,'sub_1'=4,'sub_2'=2,'grp'=4] {'sub_2','grp'}, dimensions={0} | all-to-all | bytes 1048576 | tf_op jit(solution)/shard_map/all_to_all | solution.py:23
  206.3 6.5 %fusion.52 = f32[8,64]{1,0:T(8,128)S(1)} fusion(f32[8,16384]{1,0:T(8,128)S(1)} %bitcast.95, f32[64,16384]{0,1:T(8,128)} %bitcast.88), kind=kOutput, calls=%fused_computation.92 | convolution fusion | flops 100663296 | bytes 4720640 | tf_op jit(solution)/shard_map/dot_general | solution.py:55
  213.7 1.8 fusion.6
  215.6 5.7 %collective-permute-done.6 = f32[8,32]{1,0:T(8,128)S(1)} collective-permute-done((f32[8,32]{1,0:T(8,128)S(1)}, f32[8,32]{1,0:T(8,128)S(1)}, u32[]{:S(2)}, u32[]{:S(2)}) %collective-permute-start.6) | collective-permute-done | bytes 1056 | tf_op jit(solution)/shard_map/ppermute | solution.py:41
  223.3 2.0 collective-permute-done.7
  226.0 3.3 %all-to-all-start.12 = ((f32[8,1,8]{2,1,0:T(1,128)}), f32[8,1,8]{2,1,0:T(1,128)S(1)}, u32[]{:S(2)}, u32[]{:S(2)}) async-start(f32[8,1,8]{2,1,0:T(1,128)} %broadcast_in_dim.78), calls=%async_computation.12 | async-start | bytes 8192 | tf_op jit(solution)/shard_map/all_to_all | solution.py:23
  229.3 5.1 %all-to-all-done.12 = f32[8,1,8]{2,1,0:T(1,128)S(1)} async-done(((f32[8,1,8]{2,1,0:T(1,128)}), f32[8,1,8]{2,1,0:T(1,128)S(1)}, u32[]{:S(2)}, u32[]{:S(2)}) %all-to-all-start.12) | async-done | bytes 288 | tf_op jit(solution)/shard_map/all_to_all | solution.py:23
  235.0 5.5 %all-to-all-start.13 = ((f32[16,1,8]{2,1,0:T(1,128)}), f32[16,1,8]{2,1,0:T(1,128)S(1)}, u32[]{:S(2)}, u32[]{:S(2)}) async-start(f32[16,1,8]{2,1,0:T(1,128)} %broadcast_in_dim.79), calls=%async_computation.13 | async-start | bytes 16384 | tf_op jit(solution)/shard_map/all_to_all | solution.py:23
  240.5 7.5 %all-to-all-done.13 = f32[16,1,8]{2,1,0:T(1,128)S(1)} async-done(((f32[16,1,8]{2,1,0:T(1,128)}), f32[16,1,8]{2,1,0:T(1,128)S(1)}, u32[]{:S(2)}, u32[]{:S(2)}) %all-to-all-start.13) | async-done | bytes 544 | tf_op jit(solution)/shard_map/all_to_all | solution.py:23
  249.3 17.4 %all_to_all.117 = f32[8,128,8]{0,2,1:T(8,128)S(1)} all-to-all(f32[8,128,8]{0,2,1:T(8,128)S(1)} %bitcast.93), channel_id=1, replica_groups=mesh['sub_0'=4,'sub_1'=4,'sub_2'=2,'grp'=4] {'sub_0','sub_1','sub_2','grp'}, dimensions={1} | all-to-all | bytes 65536 | tf_op jit(solution)/shard_map/all_to_all | solution.py:150
  266.7 2.2 convolution_bitcast_fusion
  268.9 8.1 %all_to_all.118 = f32[8,256,8]{1,2,0:T(8,128)S(1)} all-to-all(f32[8,256,8]{1,2,0:T(8,128)S(1)} %broadcast_in_dim.82), channel_id=1, replica_groups=mesh['sub_0'=4,'sub_1'=4,'sub_2'=2,'grp'=4] {'sub_2','grp'}, dimensions={0} | all-to-all | bytes 131072 | tf_op jit(solution)/shard_map/all_to_all | solution.py:23
  277.7 3.5 %all-to-all-start.16 = ((f32[16,256,8]{1,2,0:T(8,128)}), f32[16,256,8]{1,2,0:T(8,128)S(1)}, u32[]{:S(2)}, u32[]{:S(2)}) async-start(f32[16,256,8]{1,2,0:T(8,128)} %broadcast_in_dim.83), calls=%async_computation.16 | async-start | bytes 262144 | tf_op jit(solution)/shard_map/all_to_all | solution.py:23
  281.4 7.6 %all-to-all-done.16 = f32[16,256,8]{1,2,0:T(8,128)S(1)} async-done(((f32[16,256,8]{1,2,0:T(8,128)}), f32[16,256,8]{1,2,0:T(8,128)S(1)}, u32[]{:S(2)}, u32[]{:S(2)}) %all-to-all-start.16) | async-done | bytes 131104 | tf_op jit(solution)/shard_map/all_to_all | solution.py:23
  289.0 2.2 convolution_subtract_fusion
  291.4 7.8 %all_to_all.119 = f32[8,8,8]{2,1,0:T(8,128)S(1)} all-to-all(f32[8,8,8]{2,1,0:T(8,128)S(1)} %broadcast_in_dim.84), channel_id=1, replica_groups=mesh['sub_0'=4,'sub_1'=4,'sub_2'=2,'grp'=4] {'sub_2','grp'}, dimensions={0} | all-to-all | bytes 4096 | tf_op jit(solution)/shard_map/all_to_all | solution.py:23
  299.8 3.6 %all-to-all-start.18 = ((f32[16,8,8]{2,1,0:T(8,128)}), f32[16,8,8]{2,1,0:T(8,128)S(1)}, u32[]{:S(2)}, u32[]{:S(2)}) async-start(f32[16,8,8]{2,1,0:T(8,128)} %broadcast_in_dim.85), calls=%async_computation.18 | async-start | bytes 131072 | tf_op jit(solution)/shard_map/all_to_all | solution.py:23
  304.8 6.4 %all-to-all-done.18 = f32[16,8,8]{2,1,0:T(8,128)S(1)} async-done(((f32[16,8,8]{2,1,0:T(8,128)}), f32[16,8,8]{2,1,0:T(8,128)S(1)}, u32[]{:S(2)}, u32[]{:S(2)}) %all-to-all-start.18) | async-done | bytes 4128 | tf_op jit(solution)/shard_map/all_to_all | solution.py:23
  (119 shorter events, 25.0 us)
Async XLA Ops:
  0.6 52.2 %copy-start = (f32[2,512,512]{2,1,0:T(8,128)S(1)}, f32[2,512,512]{2,1,0:T(8,128)}, u32[]{:S(2)}) copy-start(f32[2,512,512]{2,1,0:T(8,128)} %param.10) | copy-start | bytes 6291460
  3.6 15.8 %all-to-all-start = ((f32[16,8,128]{2,1,0:T(8,128)}), f32[16,8,128]{2,1,0:T(8,128)S(1)}, u32[]{:S(2)}, u32[]{:S(2)}) async-start(f32[16,8,128]{2,1,0:T(8,128)} %broadcast_in_dim.66), calls=%async_computation | async-start | bytes 131072 | tf_op jit(solution)/shard_map/all_to_all | solution.py:23
  20.3 23.8 %all-to-all-start.1 = ((f32[8,16,8,128]{3,2,1,0:T(8,128)}), f32[8,16,8,128]{3,2,1,0:T(8,128)S(1)}, u32[]{:S(2)}, u32[]{:S(2)}) async-start(f32[8,16,8,128]{3,2,1,0:T(8,128)} %broadcast_in_dim.67), calls=%async_computation.1 | async-start | bytes 1048576 | tf_op jit(solution)/shard_map/all_to_all | solution.py:23
  44.2 15.1 %copy-start.1 = (f32[2,64,512]{2,1,0:T(8,128)S(1)}, f32[2,64,512]{2,1,0:T(8,128)}, u32[]{:S(2)}) copy-start(f32[2,64,512]{2,1,0:T(8,128)} %param.11) | copy-start | bytes 786436
  50.7 8.5 %collective-permute-start = (f32[8,32]{1,0:T(8,128)S(1)}, f32[8,32]{1,0:T(8,128)S(1)}, u32[]{:S(2)}, u32[]{:S(2)}) collective-permute-start(f32[8,32]{1,0:T(8,128)S(1)} %slice.79), channel_id=1, source_target_pairs={{0,1},{1,2},{2,3},{3,4},{4,5},{5,6},{6,7},{7,8},{8,9},{9,10},{10,1... | collective-permute-start | bytes 3080 | tf_op jit(solution)/shard_map/ppermute | solution.py:41
  59.5 3.7 %collective-permute-start.1 = (f32[8,1,128]{2,0,1:T(8,128)S(1)}, f32[8,1,128]{2,0,1:T(8,128)S(1)}, u32[]{:S(2)}, u32[]{:S(2)}) collective-permute-start(f32[8,1,128]{2,0,1:T(8,128)S(1)} %get-tuple-element.39), channel_id=1, source_target_pairs={{0,127},{1,0},{2,1},{3,2},{4,3},{5,4},{6,5},{7,6},{8,7},{9,8},{10,... | collective-permute-start | bytes 12296 | tf_op jit(solution)/shard_map/ppermute | solution.py:41
  63.2 8.5 %collective-permute-start.2 = (f32[8,1,128]{2,0,1:T(8,128)S(1)}, f32[8,1,128]{2,0,1:T(8,128)S(1)}, u32[]{:S(2)}, u32[]{:S(2)}) collective-permute-start(f32[8,1,128]{2,0,1:T(8,128)S(1)} %get-tuple-element.42), channel_id=1, source_target_pairs={{0,1},{1,2},{2,3},{3,4},{4,5},{5,6},{6,7},{7,8},{8,9},{9,10},{10,1... | collective-permute-start | bytes 12296 | tf_op jit(solution)/shard_map/ppermute | solution.py:41
  101.0 8.7 %collective-permute-start.3 = (f32[8,32]{1,0:T(8,128)S(1)}, f32[8,32]{1,0:T(8,128)S(1)}, u32[]{:S(2)}, u32[]{:S(2)}) collective-permute-start(f32[8,32]{1,0:T(8,128)S(1)} %slice.86), channel_id=1, source_target_pairs={{0,1},{1,2},{2,3},{3,4},{4,5},{5,6},{6,7},{7,8},{8,9},{9,10},{10,1... | collective-permute-start | bytes 3080 | tf_op jit(solution)/shard_map/ppermute | solution.py:41
  110.0 3.7 %collective-permute-start.4 = (f32[8,1,128]{2,0,1:T(8,128)S(1)}, f32[8,1,128]{2,0,1:T(8,128)S(1)}, u32[]{:S(2)}, u32[]{:S(2)}) collective-permute-start(f32[8,1,128]{2,0,1:T(8,128)S(1)} %get-tuple-element.37), channel_id=1, source_target_pairs={{0,127},{1,0},{2,1},{3,2},{4,3},{5,4},{6,5},{7,6},{8,7},{9,8},{10,... | collective-permute-start | bytes 12296 | tf_op jit(solution)/shard_map/ppermute | solution.py:41
  122.0 8.4 %all-to-all-start.6 = ((f32[8,1,8]{2,1,0:T(1,128)}), f32[8,1,8]{2,1,0:T(1,128)S(1)}, u32[]{:S(2)}, u32[]{:S(2)}) async-start(f32[8,1,8]{2,1,0:T(1,128)} %broadcast_in_dim.72), calls=%async_computation.6 | async-start | bytes 8192 | tf_op jit(solution)/shard_map/all_to_all | solution.py:23
  131.1 13.7 %all-to-all-start.3 = ((f32[16,1,8]{2,1,0:T(1,128)}), f32[16,1,8]{2,1,0:T(1,128)S(1)}, u32[]{:S(2)}, u32[]{:S(2)}) async-start(f32[16,1,8]{2,1,0:T(1,128)} %broadcast_in_dim.69), calls=%async_computation.3 | async-start | bytes 16384 | tf_op jit(solution)/shard_map/all_to_all | solution.py:23
  145.3 10.9 %all-to-all-start.7 = ((f32[16,1,8]{2,1,0:T(1,128)}), f32[16,1,8]{2,1,0:T(1,128)S(1)}, u32[]{:S(2)}, u32[]{:S(2)}) async-start(f32[16,1,8]{2,1,0:T(1,128)} %broadcast_in_dim.73), calls=%async_computation.7 | async-start | bytes 16384 | tf_op jit(solution)/shard_map/all_to_all | solution.py:23
  174.9 8.5 %collective-permute-start.5 = (f32[8,1,128]{2,0,1:T(8,128)S(1)}, f32[8,1,128]{2,0,1:T(8,128)S(1)}, u32[]{:S(2)}, u32[]{:S(2)}) collective-permute-start(f32[8,1,128]{2,0,1:T(8,128)S(1)} %get-tuple-element.40), channel_id=1, source_target_pairs={{0,1},{1,2},{2,3},{3,4},{4,5},{5,6},{6,7},{7,8},{8,9},{9,10},{10,1... | collective-permute-start | bytes 12296 | tf_op jit(solution)/shard_map/ppermute | solution.py:41
  206.2 16.1 %copy-start.6 = (s32[128]{0:T(128)S(1)}, s32[128]{0:T(128)}, u32[]{:S(2)}) copy-start(s32[128]{0:T(128)} %param.19) | copy-start | bytes 1540
  206.2 41.9 %copy-start.2 = (f32[8,2,512]{2,1,0:T(2,128)S(1)}, f32[8,2,512]{2,1,0:T(2,128)}, u32[]{:S(2)}) copy-start(f32[8,2,512]{2,1,0:T(2,128)} %param.16) | copy-start | bytes 98308
  206.2 41.8 %copy-start.3 = (f32[8,2,512]{2,1,0:T(2,128)S(1)}, f32[8,2,512]{2,1,0:T(2,128)}, u32[]{:S(2)}) copy-start(f32[8,2,512]{2,1,0:T(2,128)} %param.14) | copy-start | bytes 98308
  206.2 41.8 %copy-start.4 = (f32[8,2,512]{2,1,0:T(2,128)S(1)}, f32[8,2,512]{2,1,0:T(2,128)}, u32[]{:S(2)}) copy-start(f32[8,2,512]{2,1,0:T(2,128)} %param.15) | copy-start | bytes 98308
  212.8 8.5 %collective-permute-start.6 = (f32[8,32]{1,0:T(8,128)S(1)}, f32[8,32]{1,0:T(8,128)S(1)}, u32[]{:S(2)}, u32[]{:S(2)}) collective-permute-start(f32[8,32]{1,0:T(8,128)S(1)} %slice.93), channel_id=1, source_target_pairs={{0,1},{1,2},{2,3},{3,4},{4,5},{5,6},{6,7},{7,8},{8,9},{9,10},{10,1... | collective-permute-start | bytes 3080 | tf_op jit(solution)/shard_map/ppermute | solution.py:41
  221.6 3.7 %collective-permute-start.7 = (f32[8,1,128]{2,0,1:T(8,128)S(1)}, f32[8,1,128]{2,0,1:T(8,128)S(1)}, u32[]{:S(2)}, u32[]{:S(2)}) collective-permute-start(f32[8,1,128]{2,0,1:T(8,128)S(1)} %get-tuple-element.35), channel_id=1, source_target_pairs={{0,127},{1,0},{2,1},{3,2},{4,3},{5,4},{6,5},{7,6},{8,7},{9,8},{10,... | collective-permute-start | bytes 12296 | tf_op jit(solution)/shard_map/ppermute | solution.py:41
  226.0 8.4 %all-to-all-start.12 = ((f32[8,1,8]{2,1,0:T(1,128)}), f32[8,1,8]{2,1,0:T(1,128)S(1)}, u32[]{:S(2)}, u32[]{:S(2)}) async-start(f32[8,1,8]{2,1,0:T(1,128)} %broadcast_in_dim.78), calls=%async_computation.12 | async-start | bytes 8192 | tf_op jit(solution)/shard_map/all_to_all | solution.py:23
  235.0 13.0 %all-to-all-start.13 = ((f32[16,1,8]{2,1,0:T(1,128)}), f32[16,1,8]{2,1,0:T(1,128)S(1)}, u32[]{:S(2)}, u32[]{:S(2)}) async-start(f32[16,1,8]{2,1,0:T(1,128)} %broadcast_in_dim.79), calls=%async_computation.13 | async-start | bytes 16384 | tf_op jit(solution)/shard_map/all_to_all | solution.py:23
  277.7 11.3 %all-to-all-start.16 = ((f32[16,256,8]{1,2,0:T(8,128)}), f32[16,256,8]{1,2,0:T(8,128)S(1)}, u32[]{:S(2)}, u32[]{:S(2)}) async-start(f32[16,256,8]{1,2,0:T(8,128)} %broadcast_in_dim.83), calls=%async_computation.16 | async-start | bytes 262144 | tf_op jit(solution)/shard_map/all_to_all | solution.py:23
  289.0 26.4 %copy-start.5 = (f32[256,8]{0,1:T(8,128)}, f32[256,8]{0,1:T(8,128)S(1)}, u32[]{:S(2)}) copy-start(f32[256,8]{0,1:T(8,128)S(1)} %reduce_sum.157) | copy-start | bytes 24580
  299.8 11.3 %all-to-all-start.18 = ((f32[16,8,8]{2,1,0:T(8,128)}), f32[16,8,8]{2,1,0:T(8,128)S(1)}, u32[]{:S(2)}, u32[]{:S(2)}) async-start(f32[16,8,8]{2,1,0:T(8,128)} %broadcast_in_dim.85), calls=%async_computation.18 | async-start | bytes 131072 | tf_op jit(solution)/shard_map/all_to_all | solution.py:23
where the time goes:
time: 317 us; the launch traced here: 315 us
  blocking collectives  104 us (33%)
  waiting for transfers between devices  93.6 us (30%)
  starting transfers between devices  48 us (15%)
  matrix products  32.9 us (10%)
  local copies, waits for them, and re-layouts  19.6 us (6%)
  other arithmetic  16.5 us (5%)
    all_to_all x9, blocking collectives, copy_for_each(): return lax.all_to_all(copies, axis, split_axis=0, concat_axis=0, tiled=True)  86.4 us
    all_to_all x9, waiting for transfers between devices, copy_for_each(): return lax.all_to_all(copies, axis, split_axis=0, concat_axis=0, tiled=True)  53.4 us
    all_to_all x9, starting transfers between devices, copy_for_each(): return lax.all_to_all(copies, axis, split_axis=0, concat_axis=0, tiled=True)  41.3 us
    ppermute x8, waiting for transfers between devices, shifted(): lax.ppermute(array, axis, [(i, (i + by) % count) for i in range(count)])  40.2 us
    dot_general x3, matrix products, contract(): lax.dot_general(segment, matrix_rows, (((1,), (1,)), ((), ())), precision...  19.4 us
    all_to_all x1, blocking collectives, shards(): lax.all_to_all(outgoing, SUB_GRP, split_axis=1, concat_axis=1, tiled=True)  17.4 us
    concatenate x1, other arithmetic, shards(): jnp.concatenate([shifted_rows.reshape(row_count, coarse_total // NC, NC),...  8.36 us
    ppermute x8, starting transfers between devices, shifted(): lax.ppermute(array, axis, [(i, (i + by) % count) for i in range(count)])  6.71 us
  transfers between devices with their start and end apart: 17, of which 16 were waited for; matrix products, arithmetic and copies ran while one was open for 9% of the time, Pallas kernels for 0%

commit v1 on v0

v1 whole, which is shorter than its diff:
```python
import math

import jax
import jax.numpy as jnp
from jax import lax
from jax.sharding import Mesh
from jax.sharding import PartitionSpec as P

NC = 32
NI = 128
AXES = ("sub_0", "sub_1", "sub_2", "grp")
FAR, NEAR = ("sub_0", "sub_1"), ("sub_2", "grp")

highest = lax.Precision.HIGHEST
time_step = 0.5
newmark_beta = 0.25
newmark_gamma = 0.5


def exchange(pieces, axes=AXES):
    return lax.all_to_all(pieces, axes, split_axis=0, concat_axis=0, tiled=True)


def to_everyone(array, axes=AXES):
    return exchange(jnp.broadcast_to(array, (lax.axis_size(axes), *array.shape)), axes)


def shifted(array, by):
    count = lax.axis_size(AXES)
    return lax.ppermute(array, AXES, [(i, (i + by) % count) for i in range(count)])


def total(array):
    return to_everyone(to_everyone(array, NEAR).sum(axis=0), FAR).sum(axis=0)


def ein(spec, *operands):
    return jnp.einsum(spec, *operands, precision=highest)


def shards(
    rr_inverse,
    corner_modes,
    coarse_inverse,
    inertia,
    disp_now,
    vel_now,
    acc_now,
    load_next,
    basis_rows,
    piece_owner,
):
    case_count, sub_count, unknowns = disp_now.shape
    devices = lax.axis_size(AXES)
    coarse_total = coarse_inverse.shape[1]
    last = unknowns - NI

    right_modes = shifted(corner_modes, -1)
    left_edge_modes = shifted(corner_modes[1, :, last:], 1)

    def edges(field):
        return field[..., :NI], field[..., last:]

    def corner_blocks(y_first, y_last):
        d_a = -y_first[0]
        d_b = y_last[0] - y_first[1]
        d_c = y_last[1] - y_first[2]
        d_d = y_last[2]
        c0f, c0l = edges(corner_modes[0])
        c1f, c1l = edges(corner_modes[1])
        c2f, c2l = edges(right_modes[0])
        c3f, _ = edges(right_modes[1])
        mul = lambda d, m: ein("ci,mi->cm", d, m)
        h_l = mul(d_a, left_edge_modes)
        h_0 = mul(-d_a, c0f) + mul(d_b, c0l)
        h_1 = mul(-d_b, c1f) + mul(d_c, c1l)
        h_2 = mul(-d_c, c2f) + mul(d_d, c2l)
        h_3 = mul(-d_d, c3f)
        return jnp.concatenate(
            [
                h_l[:, :NC],
                h_l[:, NC:] + h_0[:, :NC],
                h_0[:, NC:] + h_1[:, :NC],
                h_1[:, NC:] + h_2[:, :NC],
                h_2[:, NC:] + h_3[:, :NC],
                h_3[:, NC:],
            ],
            axis=1,
        )

    def spread_owned(z):
        z_a, z_b = z[:, :NC], z[:, NC:]
        y_0 = ein("cm,mb->cb", z_a, corner_modes[0, NC:])
        y_1 = ein("cm,mb->cb", z, corner_modes[1])
        y_2 = ein("cm,mb->cb", z_b, right_modes[0, :NC])
        return y_0, y_1, y_2

    def blocks_of(y_0, y_1, y_2):
        return corner_blocks(
            [y_0[:, :NI], y_1[:, :NI], y_2[:, :NI]], [y_0[:, last:], y_1[:, last:], y_2[:, last:]]
        )

    coupling = blocks_of(*spread_owned(jnp.eye(2 * NC, dtype=jnp.float32)))

    def solve(blocks):
        got = to_everyone(blocks)
        width = 2 * NC
        assembled = (
            got[:, :, width : 2 * width]
            + jnp.roll(got[:, :, 2 * width :], 1, axis=0)
            + jnp.roll(got[:, :, :width], -1, axis=0)
        )
        full = jnp.transpose(assembled, (1, 0, 2)).reshape(case_count, coarse_total)
        owned = lax.dynamic_index_in_dim(assembled, lax.axis_index(AXES), 0, keepdims=False)
        return owned, lax.dot_general(
            full, coarse_inverse, (((1,), (1,)), ((), ())), precision=highest
        )

    def finish(local, z):
        y_0, y_1, y_2 = spread_owned(z)
        mine_0, mine_1 = local[:, 0] + y_0, local[:, 1] + y_1
        from_left = shifted(jnp.concatenate([mine_1[:, last:], z[:, NC:]], axis=1), 1)
        from_right = shifted(mine_0[:, :NI], -1)
        mine_0 = mine_0 + ein("cm,mb->cb", from_left[:, NI:], corner_modes[0, :NC])
        jump_a = from_left[:, :NI] - mine_0[:, :NI]
        jump_b = mine_0[:, last:] - mine_1[:, :NI]
        jump_c = mine_1[:, last:] - (from_right + y_2[:, :NI])
        return jnp.stack([mine_0, mine_1], axis=1), jump_a, jump_b, jump_c

    def local_apply(jump_a, jump_b, jump_c):
        first = jnp.stack([-jump_a, -jump_b], axis=1)
        final = jnp.stack([jump_b, jump_c], axis=1)
        out = ein("jab,cjb->cja", rr_inverse[:, :, :NI], first) + ein(
            "jab,cjb->cja", rr_inverse[:, :, last:], final
        )
        inner = jnp.sum(out[:, :, :NI] * first + out[:, :, last:] * final, axis=(1, 2))
        none = jnp.zeros((case_count, unknowns), jnp.float32)
        return out, inner, blocks_of(out[:, 0], out[:, 1], none)

    right_side = load_next + inertia[None] * (
        disp_now + time_step * vel_now + (0.5 - newmark_beta) * time_step * time_step * acc_now
    )
    terms = ein("jmb,cjb->cjm", corner_modes, right_side)
    blank = jnp.zeros((case_count, NC), jnp.float32)
    start_blocks = jnp.concatenate(
        [
            blank,
            terms[:, 0, :NC],
            terms[:, 0, NC:] + terms[:, 1, :NC],
            terms[:, 1, NC:],
            blank,
            blank,
        ],
        axis=1,
    )
    _, z_0 = solve(start_blocks)
    local_0 = ein("jab,cjb->cja", rr_inverse, right_side)
    none = jnp.zeros((case_count, unknowns), jnp.float32)
    local_blocks_0 = blocks_of(local_0[:, 0], local_0[:, 1], none)
    blocks_1 = local_blocks_0 + jnp.dot(z_0, coupling, precision=highest)
    coarse_1, z_1 = solve(blocks_1)
    green, b_a, b_b, b_c = finish(local_0, z_0)
    local_1, inner_1, local_blocks_1 = local_apply(b_a, b_b, b_c)
    blocks_2 = local_blocks_1 + jnp.dot(z_1, coupling, precision=highest)
    coarse_2, z_2 = solve(blocks_2)
    image_1, v_a, v_b, v_c = finish(local_1, z_1)
    local_2, inner_2, _ = local_apply(v_a, v_b, v_c)

    sums = jnp.stack(
        [
            jnp.sum(b_b * b_b + b_c * b_c, axis=1),
            inner_1 + jnp.sum(coarse_1 * z_1, axis=1),
            jnp.sum(v_b * v_b + v_c * v_c, axis=1),
            inner_2 + jnp.sum(coarse_2 * z_2, axis=1),
        ]
    )
    y_0, y_1, y_2 = spread_owned(z_2)
    part_2 = jnp.stack([local_2[:, 0] + y_0, local_2[:, 1] + y_1, y_2], axis=1)
    inverse = (
        jnp.zeros((devices,), jnp.int32)
        .at[piece_owner]
        .set(jnp.arange(devices, dtype=jnp.int32))
    )
    piece_rows = unknowns // devices
    sent = jnp.concatenate([green, image_1, part_2], axis=1)
    sent = sent.reshape(case_count, 7, devices, piece_rows)[:, :, inverse, :]
    sent = jnp.transpose(sent, (2, 0, 1, 3)).reshape(devices, case_count * 7 * piece_rows)
    sent = jnp.concatenate(
        [sent, jnp.broadcast_to(sums.reshape(1, -1), (devices, 4 * case_count))], axis=1
    )
    got = exchange(sent.reshape(devices, 2, 128)).reshape(devices, 256)
    sums = got[:, 7 * case_count * piece_rows :].sum(axis=0).reshape(4, case_count)
    bb, bf, ff, fff = sums
    alpha_0 = bb / bf
    norm_1 = bb - 2.0 * alpha_0 * bf + alpha_0 * alpha_0 * ff
    beta_0 = norm_1 / bb
    gain = 1.0 + beta_0
    curvature = gain * gain * bf - 2.0 * gain * alpha_0 * ff + alpha_0 * alpha_0 * fff
    alpha_1 = norm_1 / curvature
    kappa_1 = (alpha_0 + alpha_1 * gain)[:, None, None]
    kappa_2 = (alpha_1 * alpha_0)[:, None, None]

    got = got[:, : 7 * case_count * piece_rows].reshape(devices, case_count, 7, piece_rows)
    late = got[:, :, 4:6].at[:, :, 0].add(jnp.roll(got[:, :, 6], 1, axis=0))
    snapshots = got[:, :, 0:2] - kappa_1 * got[:, :, 2:4] + kappa_2 * late
    snapshots = jnp.transpose(snapshots, (1, 0, 2, 3)).reshape(case_count, -1)

    ghost = shifted(z_2[:, NC:], 1)
    image_2 = part_2[:, :2].at[:, 0].add(ein("cm,mb->cb", ghost, corner_modes[0, :NC]))
    disp_new = green - kappa_1 * image_1 + kappa_2 * image_2
    accel_new = (
        (disp_new - disp_now) / (newmark_beta * time_step * time_step)
        - vel_now / (newmark_beta * time_step)
        - (0.5 / newmark_beta - 1.0) * acc_now
    )
    vel_new = vel_now + time_step * ((1.0 - newmark_gamma) * acc_now + newmark_gamma * accel_new)

    projection = total(
        lax.dot_general(basis_rows, snapshots, (((0,), (1,)), ((), ())), precision=highest)
    )
    remainder = snapshots - lax.dot_general(
        projection, basis_rows, (((0,), (1,)), ((), ())), precision=highest
    )
    gram = lax.dot_general(remainder, remainder, (((1,), (1,)), ((), ())), precision=highest)
    lower = jnp.linalg.cholesky(to_everyone(gram).sum(axis=0))
    scale_rows = math.sqrt(snapshots.shape[1] * devices)
    new_columns = jax.scipy.linalg.solve_triangular(lower, remainder, lower=True) * scale_rows
    r_factor = lower.T / scale_rows
    return (disp_new, vel_new, projection, r_factor, new_columns)


def solution(mesh):
    finer = Mesh(
        mesh.devices.reshape(4, 4, 2, mesh.shape["grp"]), ("sub_0", "sub_1", "sub_2", "grp")
    )
    placed = (
        P(AXES, None, None),
        P(AXES, None, None),
        P(AXES, None),
        P(AXES, None),
        P(None, AXES, None),
        P(None, AXES, None),
        P(None, AXES, None),
        P(None, AXES, None),
        P(AXES, None),
        P(),
    )
    return jax.shard_map(
        shards,
        mesh=finer,
        in_specs=placed,
        out_specs=(P(None, AXES, None), P(None, AXES, None), P(), P(), P(None, AXES)),
        check_vma=False,
    )
```

time: 317 us -> 204 us (0.64)
  blocking collectives: 104 us -> 0 us
  waiting for transfers between devices: 93.6 us -> 60.4 us
  local copies, waits for them, and re-layouts: 19.6 us -> 39 us
  other arithmetic: 16.5 us -> 10 us
  starting transfers between devices: 48 us -> 53.6 us
  matrix products: 32.9 us -> 36.5 us
    all_to_all x10 -> x0, blocking collectives: 104 us -> none  [the longest x9 86.4 us: copy_for_each(): return lax.all_to_all(copies, axis, split_axis=0, concat_axis=0, tiled=True)]
    ppermute x8 -> x7, waiting for transfers between devices: 40.2 us -> 7.6 us  [shifted(): lax.ppermute(array, AXES, [(i, (i + by) % count) for i in range(count)])]
    concatenate x2 -> x3, other arithmetic: 11.9 us -> 0.11 us  [the longest x1 0.1 us: shards(): jnp.concatenate([sent, jnp.broadcast_to(sums.reshape(1, -1), (devices, 4...]
    ppermute x8 -> x7, starting transfers between devices: 6.71 us -> 14.9 us  [shifted(): lax.ppermute(array, AXES, [(i, (i + by) % count) for i in range(count)])]
    gather x1 -> x2, local copies, waits for them, and re-layouts: 0.95 us -> 6.76 us  [shards(): sent = sent.reshape(case_count, 7, devices, piece_rows)[:, :, inverse, :]]
    add x0 -> x6, local copies, waits for them, and re-layouts: none -> 3.75 us  [the longest x2 1.76 us: finish(): mine_0 = mine_0 + ein('cm,mb->cb', from_left[:, NI:], corner_modes[0, :NC])]
    dot_general x13 -> x49, matrix products: 29.7 us -> 33.3 us  [the longest x43 23.9 us: ein(): return jnp.einsum(spec, *operands, precision=highest)]
    dot_general x0 -> x2, local copies, waits for them, and re-layouts: none -> 3.21 us  [ein(): return jnp.einsum(spec, *operands, precision=highest)]
  transfers between devices with their start and end apart: 17 -> 14, of which waited for: 16 -> 9; matrix products, arithmetic and copies ran while one was open for 9% -> 24% of each run, Pallas kernels for 0% -> 0%
where the time goes in v1:
time: 204 us; the launch traced here: 201 us
  waiting for transfers between devices  60.4 us (30%)
  starting transfers between devices  53.6 us (26%)
  local copies, waits for them, and re-layouts  39 us (19%)
  matrix products  36.5 us (18%)
  other arithmetic  10 us (5%)
    all_to_all x7, waiting for transfers between devices, exchange(): return lax.all_to_all(pieces, axes, split_axis=0, concat_axis=0, tiled=True)  52.8 us
    all_to_all x7, starting transfers between devices, exchange(): return lax.all_to_all(pieces, axes, split_axis=0, concat_axis=0, tiled=True)  38.7 us
    dot_general x43, matrix products, ein(): return jnp.einsum(spec, *operands, precision=highest)  23.9 us
    ppermute x7, starting transfers between devices, shifted(): lax.ppermute(array, AXES, [(i, (i + by) % count) for i in range(count)])  14.9 us
    ppermute x7, waiting for transfers between devices, shifted(): lax.ppermute(array, AXES, [(i, (i + by) % count) for i in range(count)])  7.6 us
    unnamed x92, local copies, waits for them, and re-layouts  6.86 us
    dot_general x3, matrix products, solve(): lax.dot_general(full, coarse_inverse, (((1,), (1,)), ((), ())), precision...  6.77 us
    gather x2, local copies, waits for them, and re-layouts, shards(): sent = sent.reshape(case_count, 7, devices, piece_rows)[:, :, inverse, :]  6.76 us
  transfers between devices with their start and end apart: 14, of which 9 were waited for; matrix products, arithmetic and copies ran while one was open for 24% of the time, Pallas kernels for 0%

profile of v1, /device:TPU:0, one launch (start us, length us, event | category | flops | bytes accessed | tf_op | source)
XLA Modules:
  0.0 201.0 jit_solution(14592303359766357146)
XLA Ops:
  0.7 8.3 %collective-permute-start.2 = (f32[2,64,512]{2,1,0:T(8,128)}, f32[2,64,512]{2,1,0:T(8,128)}, u32[]{:S(2)}, u32[]{:S(2)}) collective-permute-start(f32[2,64,512]{2,1,0:T(8,128)} %param.15), channel_id=1, source_target_pairs={{0,127},{1,0},{2,1},{3,2},{4,3},{5,4},{6,5},{7,6},{8,7},{9,8},{10,... | collective-permute-start | bytes 786440 | tf_op jit(solution)/shard_map/ppermute | solution.py:30
  9.0 1.4 slice_bitcast_fusion.6
  11.8 1.3 convolution_bitcast_fusion.3
  13.3 1.1 broadcast_in_dim.40
  14.3 9.1 %all-to-all-start = ((f32[128,8,192]{2,1,0:T(8,128)}), f32[128,8,192]{2,1,0:T(8,128)S(1)}, u32[]{:S(2)}, u32[]{:S(2)}) async-start(f32[128,8,192]{2,1,0:T(8,128)} %broadcast_in_dim.40), calls=%async_computation | async-start | bytes 2097152 | tf_op jit(solution)/shard_map/all_to_all | solution.py:21
  23.7 3.5 %convolution_bitcast_fusion = f32[8,2,512]{2,0,1:T(8,128)S(1)} fusion(f32[2,512,512]{2,1,0:T(8,128)} %param.14, f32[8,2,512]{2,1,0:T(2,128)} %copy-done.14), kind=kOutput, calls=%fused_computation.7 | convolution fusion | flops 50331648 | bytes 2162688 | tf_op jit(solution)/shard_map/jab,cjb->cja/dot_general | solution.py:38
  29.9 1.5 fusion.114
  32.4 1.0 slice_bitcast_fusion
  33.5 1.1 fusion.48
  37.0 1.5 slice_bitcast_fusion.4
  38.6 3.7 %all-to-all-done = f32[128,8,192]{2,1,0:T(8,128)S(1)} async-done(((f32[128,8,192]{2,1,0:T(8,128)}), f32[128,8,192]{2,1,0:T(8,128)S(1)}, u32[]{:S(2)}, u32[]{:S(2)}) %all-to-all-start) | async-done | bytes 786464 | tf_op jit(solution)/shard_map/all_to_all | solution.py:21
  43.0 1.7 fusion.149
  45.1 3.4 %collective-permute-start.1 = (f32[8,128]{1,0:T(8,128)S(1)}, f32[8,128]{1,0:T(8,128)S(1)}, u32[]{:S(2)}, u32[]{:S(2)}) collective-permute-start(f32[8,128]{1,0:T(8,128)S(1)} %slice.646), channel_id=1, source_target_pairs={{0,127},{1,0},{2,1},{3,2},{4,3},{5,4},{6,5},{7,6},{8,7},{9,8},{10,... | collective-permute-start | bytes 12296 | tf_op jit(solution)/shard_map/ppermute | solution.py:30
  48.6 1.3 collective-permute-done.1
  50.8 6.3 %collective-permute-done = f32[8,160]{1,0:T(8,128)S(1)} collective-permute-done((f32[8,160]{1,0:T(8,128)S(1)}, f32[8,160]{1,0:T(8,128)S(1)}, u32[]{:S(2)}, u32[]{:S(2)}) %collective-permute-start) | collective-permute-done | bytes 5152 | tf_op jit(solution)/shard_map/ppermute | solution.py:30
  62.1 1.1 broadcast_in_dim.41
  63.2 4.6 %all-to-all-start.1 = ((f32[128,8,192]{2,1,0:T(8,128)}), f32[128,8,192]{2,1,0:T(8,128)S(1)}, u32[]{:S(2)}, u32[]{:S(2)}) async-start(f32[128,8,192]{2,1,0:T(8,128)} %broadcast_in_dim.41), calls=%async_computation.1 | async-start | bytes 2097152 | tf_op jit(solution)/shard_map/all_to_all | solution.py:21
  68.6 1.2 scatter_custom_fusion
  70.3 1.7 copy.161
  72.9 1.0 copy.164
  74.8 1.0 copy.163
  78.0 8.7 %all-to-all-done.1 = f32[128,8,192]{2,1,0:T(8,128)S(1)} async-done(((f32[128,8,192]{2,1,0:T(8,128)}), f32[128,8,192]{2,1,0:T(8,128)S(1)}, u32[]{:S(2)}, u32[]{:S(2)}) %all-to-all-start.1) | async-done | bytes 786464 | tf_op jit(solution)/shard_map/all_to_all | solution.py:21
  88.1 2.5 %fusion.104 = (f32[8]{0:T(128)S(1)}, f32[8,64]{1,0:T(8,128)S(1)}) fusion(f32[128,8,64]{2,1,0:T(8,128)} %copy-done.4, s32[]{:T(128)S(6)} %select_n.17, f32[8,8192]{1,0:T(8,128)S(1)} %reshape.177, f32[64,8192]{1,0:T(8,128)S(1)} %copy-done), kind=kOutput, calls=%fused_computation.204 | convolution fusion | flops 50332664 | bytes 2363428 | tf_op jit(solution)/shard_map/dot_general | solution.py:115
  91.3 1.3 collective-permute-start.5
  93.4 1.1 broadcast_in_dim.42
  94.5 8.3 %all-to-all-start.2 = ((f32[128,8,192]{2,1,0:T(8,128)}), f32[128,8,192]{2,1,0:T(8,128)S(1)}, u32[]{:S(2)}, u32[]{:S(2)}) async-start(f32[128,8,192]{2,1,0:T(8,128)} %broadcast_in_dim.42), calls=%async_computation.2 | async-start | bytes 2097152 | tf_op jit(solution)/shard_map/all_to_all | solution.py:21
  104.2 1.0 copy.166
  105.2 0.9 fusion.5
  107.2 1.0 copy.165
  109.4 1.3 add_reduce_fusion
  110.8 1.6 fusion.13
  112.3 1.6 fusion
  114.0 7.6 %all-to-all-done.2 = f32[128,8,192]{2,1,0:T(8,128)S(1)} async-done(((f32[128,8,192]{2,1,0:T(8,128)}), f32[128,8,192]{2,1,0:T(8,128)S(1)}, u32[]{:S(2)}, u32[]{:S(2)}) %all-to-all-start.2) | async-done | bytes 786464 | tf_op jit(solution)/shard_map/all_to_all | solution.py:21
  123.0 2.5 %fusion.103 = (f32[8]{0:T(128)S(1)}, f32[8,64]{1,0:T(8,128)S(1)}) fusion(f32[128,8,64]{2,1,0:T(8,128)} %copy-done.3, s32[]{:T(128)S(6)} %select_n.17, f32[8,8192]{1,0:T(8,128)S(1)} %reshape.178, f32[64,8192]{1,0:T(8,128)S(1)} %copy-done), kind=kOutput, calls=%fused_computation.202 | convolution fusion | flops 50332664 | bytes 2363428 | tf_op jit(solution)/shard_map/dot_general | solution.py:115
  126.9 1.7 copy.169
  128.6 4.7 %gather_fusion = f32[128,8,7,4]{1,3,2,0:T(4,128)} fusion(f32[8,7,128,4]{0,3,2,1:T(4,128)} %copy.169, s32[1024]{0:T(1024)} %pad_clamp_fusion), kind=kCustom, calls=%fused_computation | custom fusion | bytes 229888 | tf_op jit(solution)/shard_map/gather | solution.py:186
  133.3 2.1 %copy.170 = f32[128,8,7,4]{0,3,2,1:T(4,128)S(1)} copy(f32[128,8,7,4]{1,3,2,0:T(4,128)} %gather_fusion) | data formatting | bytes 229376 | tf_op jit(solution)/shard_map/gather | solution.py:186
  136.3 4.6 %all-to-all-start.3 = ((f32[128,2,128]{2,1,0:T(2,128)}), f32[128,2,128]{2,1,0:T(2,128)S(1)}, u32[]{:S(2)}, u32[]{:S(2)}) async-start(f32[128,2,128]{2,1,0:T(2,128)} %copy.171), calls=%async_computation.3 | async-start | bytes 262144 | tf_op jit(solution)/shard_map/all_to_all | solution.py:21
  141.0 1.1 collective-permute-start.6
  142.1 8.2 %all-to-all-done.3 = f32[128,2,128]{2,1,0:T(2,128)S(1)} async-done(((f32[128,2,128]{2,1,0:T(2,128)}), f32[128,2,128]{2,1,0:T(2,128)S(1)}, u32[]{:S(2)}, u32[]{:S(2)}) %all-to-all-start.3) | async-done | bytes 131104 | tf_op jit(solution)/shard_map/all_to_all | solution.py:21
  151.5 2.2 %convolution_bitcast_fusion.2 = f32[256,8]{0,1:T(8,128)S(1)} fusion(f32[8,1024]{0,1:T(8,128)S(1)} %bitcast.197, f32[1024,256]{1,0:T(8,128)} %param.22), kind=kOutput, calls=%fused_computation.25 | convolution fusion | flops 25165824 | bytes 1089536 | tf_op jit(solution)/shard_map/dot_general | solution.py:219
  154.3 3.5 %all-to-all-start.4 = ((f32[8,256,8]{1,2,0:T(8,128)}), f32[8,256,8]{1,2,0:T(8,128)S(1)}, u32[]{:S(2)}, u32[]{:S(2)}) async-start(f32[8,256,8]{1,2,0:T(8,128)} %broadcast_in_dim.47), calls=%async_computation.4 | async-start | bytes 131072 | tf_op jit(solution)/shard_map/all_to_all | solution.py:21
  157.8 5.3 %all-to-all-done.4 = f32[8,256,8]{1,2,0:T(8,128)S(1)} async-done(((f32[8,256,8]{1,2,0:T(8,128)}), f32[8,256,8]{1,2,0:T(8,128)S(1)}, u32[]{:S(2)}, u32[]{:S(2)}) %all-to-all-start.4) | async-done | bytes 65568 | tf_op jit(solution)/shard_map/all_to_all | solution.py:21
  163.7 3.6 %all-to-all-start.5 = ((f32[16,256,8]{1,2,0:T(8,128)}), f32[16,256,8]{1,2,0:T(8,128)S(1)}, u32[]{:S(2)}, u32[]{:S(2)}) async-start(f32[16,256,8]{1,2,0:T(8,128)} %broadcast_in_dim.48), calls=%async_computation.5 | async-start | bytes 262144 | tf_op jit(solution)/shard_map/all_to_all | solution.py:21
  167.6 7.5 %all-to-all-done.5 = f32[16,256,8]{1,2,0:T(8,128)S(1)} async-done(((f32[16,256,8]{1,2,0:T(8,128)}), f32[16,256,8]{1,2,0:T(8,128)S(1)}, u32[]{:S(2)}, u32[]{:S(2)}) %all-to-all-start.5) | async-done | bytes 131104 | tf_op jit(solution)/shard_map/all_to_all | solution.py:21
  175.2 2.2 %convolution_subtract_fusion = f32[8,1024]{1,0:T(8,128)S(1)} fusion(f32[8,1024]{1,0:T(8,128)S(1)} %copy.183, f32[256,8]{0,1:T(8,128)S(1)} %reduce_sum.98, f32[1024,256]{1,0:T(8,128)} %param.22), kind=kOutput, calls=%fused_computation.3 | convolution fusion | flops 25174016 | bytes 1122304 | tf_op jit(solution)/shard_map/dot_general | solution.py:221
  178.4 5.0 %all-to-all-start.6 = ((f32[128,8,8]{2,1,0:T(8,128)}), f32[128,8,8]{2,1,0:T(8,128)S(1)}, u32[]{:S(2)}, u32[]{:S(2)}) async-start(f32[128,8,8]{2,1,0:T(8,128)} %broadcast_in_dim.49), calls=%async_computation.6 | async-start | bytes 1048576 | tf_op jit(solution)/shard_map/all_to_all | solution.py:21
  184.8 11.8 %all-to-all-done.6 = f32[128,8,8]{2,1,0:T(8,128)S(1)} async-done(((f32[128,8,8]{2,1,0:T(8,128)}), f32[128,8,8]{2,1,0:T(8,128)S(1)}, u32[]{:S(2)}, u32[]{:S(2)}) %all-to-all-start.6) | async-done | bytes 32800 | tf_op jit(solution)/shard_map/all_to_all | solution.py:21
  (233 shorter events, 39.8 us)
Async XLA Ops:
  0.6 42.3 %copy-start = (f32[64,8192]{1,0:T(8,128)S(1)}, f32[64,8192]{1,0:T(8,128)}, u32[]{:S(2)}) copy-start(f32[64,8192]{1,0:T(8,128)} %param.16) | copy-start | bytes 6291460
  0.6 22.8 %copy-start.1 = (f32[2,64,512]{2,1,0:T(8,128)S(1)}, f32[2,64,512]{2,1,0:T(8,128)}, u32[]{:S(2)}) copy-start(f32[2,64,512]{2,1,0:T(8,128)} %param.15) | copy-start | bytes 786436
  0.7 31.7 %collective-permute-start.2 = (f32[2,64,512]{2,1,0:T(8,128)}, f32[2,64,512]{2,1,0:T(8,128)}, u32[]{:S(2)}, u32[]{:S(2)}) collective-permute-start(f32[2,64,512]{2,1,0:T(8,128)} %param.15), channel_id=1, source_target_pairs={{0,127},{1,0},{2,1},{3,2},{4,3},{5,4},{6,5},{7,6},{8,7},{9,8},{10,... | collective-permute-start | bytes 786440 | tf_op jit(solution)/shard_map/ppermute | solution.py:30
  10.4 19.5 %collective-permute-start.3 = (f32[64,128]{1,0:T(8,128)}, f32[64,128]{1,0:T(8,128)}, u32[]{:S(2)}, u32[]{:S(2)}) collective-permute-start(f32[64,128]{1,0:T(8,128)} %slice_bitcast_fusion.6), channel_id=1, source_target_pairs={{0,1},{1,2},{2,3},{3,4},{4,5},{5,6},{6,7},{7,8},{8,9},{9,10},{10,1... | collective-permute-start | bytes 98312 | tf_op jit(solution)/shard_map/ppermute | solution.py:30
  14.3 27.9 %all-to-all-start = ((f32[128,8,192]{2,1,0:T(8,128)}), f32[128,8,192]{2,1,0:T(8,128)S(1)}, u32[]{:S(2)}, u32[]{:S(2)}) async-start(f32[128,8,192]{2,1,0:T(8,128)} %broadcast_in_dim.40), calls=%async_computation | async-start | bytes 2097152 | tf_op jit(solution)/shard_map/all_to_all | solution.py:21
  23.7 11.3 %copy-start.6 = (f32[64,512]{1,0:T(8,128)}, f32[64,512]{1,0:T(8,128)S(1)}, u32[]{:S(2)}) copy-start(f32[64,512]{1,0:T(8,128)S(1)} %get-tuple-element.77) | copy-start | bytes 393220
  27.2 9.8 %copy-start.15 = (f32[8,2,512]{2,0,1:T(8,128)}, f32[8,2,512]{2,0,1:T(8,128)S(1)}, u32[]{:S(2)}) copy-start(f32[8,2,512]{2,0,1:T(8,128)S(1)} %convolution_bitcast_fusion) | copy-start | bytes 98308
  33.4 3.7 %copy-start.8 = (f32[64,512]{1,0:T(8,128)}, f32[64,512]{1,0:T(8,128)S(1)}, u32[]{:S(2)}) copy-start(f32[64,512]{1,0:T(8,128)S(1)} %get-tuple-element.76) | copy-start | bytes 393220
  33.5 3.5 %copy-start.29 = (f32[8,64]{1,0:T(8,128)}, f32[8,64]{1,0:T(8,128)S(1)}, u32[]{:S(2)}) copy-start(f32[8,64]{1,0:T(8,128)S(1)} %fusion.61) | copy-start | bytes 6148
  42.6 2.2 %copy-start.16 = (f32[8,2,512]{2,0,1:T(8,128)S(1)}, f32[8,2,512]{2,0,1:T(8,128)}, u32[]{:S(2)}) copy-start(f32[8,2,512]{2,0,1:T(8,128)} %copy-done.15) | copy-start | bytes 98308
  42.9 15.1 %copy-start.2 = (f32[2,512,512]{2,1,0:T(8,128)S(1)}, f32[2,512,512]{2,1,0:T(8,128)}, u32[]{:S(2)}) copy-start(f32[2,512,512]{2,1,0:T(8,128)} %param.14) | copy-start | bytes 6291460
  42.9 16.2 %copy-start.30 = (f32[8,64]{1,0:T(8,128)S(1)}, f32[8,64]{1,0:T(8,128)}, u32[]{:S(2)}) copy-start(f32[8,64]{1,0:T(8,128)} %copy-done.29) | copy-start | bytes 6148
  42.9 17.1 %copy-start.7 = (f32[64,512]{1,0:T(8,128)S(1)}, f32[64,512]{1,0:T(8,128)}, u32[]{:S(2)}) copy-start(f32[64,512]{1,0:T(8,128)} %copy-done.6) | copy-start | bytes 393220
  42.9 18.7 %copy-start.31 = (f32[8,64]{1,0:T(8,128)S(1)}, f32[8,64]{1,0:T(8,128)}, u32[]{:S(2)}) copy-start(f32[8,64]{1,0:T(8,128)} %convolution_add_fusion.21) | copy-start | bytes 6148
  42.9 18.7 %copy-start.32 = (f32[8,64]{1,0:T(8,128)S(1)}, f32[8,64]{1,0:T(8,128)}, u32[]{:S(2)}) copy-start(f32[8,64]{1,0:T(8,128)} %fusion.114) | copy-start | bytes 6148
  42.9 18.7 %copy-start.33 = (f32[8,64]{1,0:T(8,128)S(1)}, f32[8,64]{1,0:T(8,128)}, u32[]{:S(2)}) copy-start(f32[8,64]{1,0:T(8,128)} %fusion.58) | copy-start | bytes 6148
  43.0 18.7 %copy-start.34 = (f32[8,64]{1,0:T(8,128)S(1)}, f32[8,64]{1,0:T(8,128)}, u32[]{:S(2)}) copy-start(f32[8,64]{1,0:T(8,128)} %convolution_add_fusion.20) | copy-start | bytes 6148
  43.0 18.7 %copy-start.35 = (f32[8,64]{1,0:T(8,128)S(1)}, f32[8,64]{1,0:T(8,128)}, u32[]{:S(2)}) copy-start(f32[8,64]{1,0:T(8,128)} %convolution_add_fusion.19) | copy-start | bytes 6148
  43.0 18.9 %copy-start.10 = (f32[64,192]{0,1:T(8,128)S(1)}, f32[64,192]{0,1:T(8,128)}, u32[]{:S(2)}) copy-start(f32[64,192]{0,1:T(8,128)} %copy-done.9) | copy-start | bytes 147460
  45.1 4.7 %collective-permute-start.1 = (f32[8,128]{1,0:T(8,128)S(1)}, f32[8,128]{1,0:T(8,128)S(1)}, u32[]{:S(2)}, u32[]{:S(2)}) collective-permute-start(f32[8,128]{1,0:T(8,128)S(1)} %slice.646), channel_id=1, source_target_pairs={{0,127},{1,0},{2,1},{3,2},{4,3},{5,4},{6,5},{7,6},{8,7},{9,8},{10,... | collective-permute-start | bytes 12296 | tf_op jit(solution)/shard_map/ppermute | solution.py:30
  48.6 8.5 %collective-permute-start = (f32[8,160]{1,0:T(8,128)S(1)}, f32[8,160]{1,0:T(8,128)S(1)}, u32[]{:S(2)}, u32[]{:S(2)}) collective-permute-start(f32[8,160]{1,0:T(8,128)S(1)} %pad_maximum_fusion.2), channel_id=1, source_target_pairs={{0,1},{1,2},{2,3},{3,4},{4,5},{5,6},{6,7},{7,8},{8,9},{9,10},{10,1... | collective-permute-start | bytes 15368 | tf_op jit(solution)/shard_map/ppermute | solution.py:30
  50.8 12.4 %copy-start.23 = (f32[8,128]{1,0:T(8,128)}, f32[8,128]{1,0:T(8,128)S(1)}, u32[]{:S(2)}) copy-start(f32[8,128]{1,0:T(8,128)S(1)} %fusion.6) | copy-start | bytes 12292
  58.0 5.3 %copy-start.24 = (f32[8,1,128]{2,0,1:T(8,128)}, f32[8,1,128]{2,0,1:T(8,128)S(1)}, u32[]{:S(2)}) copy-start(f32[8,1,128]{2,0,1:T(8,128)S(1)} %get-tuple-element.80) | copy-start | bytes 12292
  59.1 4.2 %copy-start.12 = (f32[8,2,512]{2,0,1:T(8,128)}, f32[8,2,512]{2,0,1:T(8,128)S(1)}, u32[]{:S(2)}) copy-start(f32[8,2,512]{2,0,1:T(8,128)S(1)} %fusion.1) | copy-start | bytes 98308
  61.9 12.0 %copy-start.18 = (f32[8,512]{1,0:T(8,128)S(1)}, f32[8,512]{1,0:T(8,128)}, u32[]{:S(2)}) copy-start(f32[8,512]{1,0:T(8,128)} %copy-done.17) | copy-start | bytes 49156
  63.2 13.9 %copy-start.26 = (f32[8,1,128]{2,0,1:T(8,128)S(1)}, f32[8,1,128]{2,0,1:T(8,128)}, u32[]{:S(2)}) copy-start(f32[8,1,128]{2,0,1:T(8,128)} %copy-done.25) | copy-start | bytes 12292
  63.2 13.9 %copy-start.28 = (f32[8,1,128]{2,0,1:T(8,128)S(1)}, f32[8,1,128]{2,0,1:T(8,128)}, u32[]{:S(2)}) copy-start(f32[8,1,128]{2,0,1:T(8,128)} %copy-done.27) | copy-start | bytes 12292
  63.2 23.5 %all-to-all-start.1 = ((f32[128,8,192]{2,1,0:T(8,128)}), f32[128,8,192]{2,1,0:T(8,128)S(1)}, u32[]{:S(2)}, u32[]{:S(2)}) async-start(f32[128,8,192]{2,1,0:T(8,128)} %broadcast_in_dim.41), calls=%async_computation.1 | async-start | bytes 2097152 | tf_op jit(solution)/shard_map/all_to_all | solution.py:21
  87.8 2.9 %copy-start.13 = (f32[8,2,512]{2,0,1:T(8,128)S(1)}, f32[8,2,512]{2,0,1:T(8,128)}, u32[]{:S(2)}) copy-start(f32[8,2,512]{2,0,1:T(8,128)} %copy-done.12) | copy-start | bytes 98308
  87.8 3.2 %copy-start.11 = (f32[64,192]{0,1:T(8,128)S(1)}, f32[64,192]{0,1:T(8,128)}, u32[]{:S(2)}) copy-start(f32[64,192]{0,1:T(8,128)} %copy-done.9) | copy-start | bytes 147460
  91.3 13.9 %collective-permute-start.5 = (f32[8,128]{1,0:T(8,128)S(1)}, f32[8,128]{1,0:T(8,128)S(1)}, u32[]{:S(2)}, u32[]{:S(2)}) collective-permute-start(f32[8,128]{1,0:T(8,128)S(1)} %slice.693), channel_id=1, source_target_pairs={{0,127},{1,0},{2,1},{3,2},{4,3},{5,4},{6,5},{7,6},{8,7},{9,8},{10,... | collective-permute-start | bytes 12296 | tf_op jit(solution)/shard_map/ppermute | solution.py:30
  92.6 13.5 %collective-permute-start.4 = (f32[8,160]{1,0:T(8,128)S(1)}, f32[8,160]{1,0:T(8,128)S(1)}, u32[]{:S(2)}, u32[]{:S(2)}) collective-permute-start(f32[8,160]{1,0:T(8,128)S(1)} %pad_maximum_fusion.5), channel_id=1, source_target_pairs={{0,1},{1,2},{2,3},{3,4},{4,5},{5,6},{6,7},{7,8},{8,9},{9,10},{10,1... | collective-permute-start | bytes 15368 | tf_op jit(solution)/shard_map/ppermute | solution.py:30
  94.5 27.1 %all-to-all-start.2 = ((f32[128,8,192]{2,1,0:T(8,128)}), f32[128,8,192]{2,1,0:T(8,128)S(1)}, u32[]{:S(2)}, u32[]{:S(2)}) async-start(f32[128,8,192]{2,1,0:T(8,128)} %broadcast_in_dim.42), calls=%async_computation.2 | async-start | bytes 2097152 | tf_op jit(solution)/shard_map/all_to_all | solution.py:21
  106.2 2.7 %copy-start.37 = (f32[8,160]{1,0:T(8,128)}, f32[8,160]{1,0:T(8,128)S(1)}, u32[]{:S(2)}) copy-start(f32[8,160]{1,0:T(8,128)S(1)} %collective-permute-done.4) | copy-start | bytes 15364
  122.7 3.2 %copy-start.38 = (f32[8]{0:T(128)S(1)}, f32[8]{0:T(128)}, u32[]{:S(2)}) copy-start(f32[8]{0:T(128)} %get-tuple-element.79) | copy-start | bytes 100
  122.7 3.2 %copy-start.39 = (f32[8]{0:T(128)S(1)}, f32[8]{0:T(128)}, u32[]{:S(2)}) copy-start(f32[8]{0:T(128)} %get-tuple-element.82) | copy-start | bytes 100
  122.7 3.2 %copy-start.40 = (f32[1,8]{1,0:T(1,128)S(1)}, f32[1,8]{1,0:T(1,128)}, u32[]{:S(2)}) copy-start(f32[1,8]{1,0:T(1,128)} %add_bitcast_fusion.1) | copy-start | bytes 100
  122.8 3.7 %copy-start.19 = (f32[8,7,128,4]{2,0,3,1:T(8,128)S(1)}, f32[8,7,128,4]{2,0,3,1:T(8,128)}, u32[]{:S(2)}) copy-start(f32[8,7,128,4]{2,0,3,1:T(8,128)} %constant_dynamic-update-slice_fusion.8) | copy-start | bytes 344068
  123.0 3.5 %copy-start.5 = (f32[512,32]{1,0:T(8,128)S(1)}, f32[512,32]{1,0:T(8,128)}, u32[]{:S(2)}) copy-start(f32[512,32]{1,0:T(8,128)} %copy.161) | copy-start | bytes 196612
  136.3 14.0 %all-to-all-start.3 = ((f32[128,2,128]{2,1,0:T(2,128)}), f32[128,2,128]{2,1,0:T(2,128)S(1)}, u32[]{:S(2)}, u32[]{:S(2)}) async-start(f32[128,2,128]{2,1,0:T(2,128)} %copy.171), calls=%async_computation.3 | async-start | bytes 262144 | tf_op jit(solution)/shard_map/all_to_all | solution.py:21
  141.0 26.3 %collective-permute-start.6 = (f32[8,32]{1,0:T(8,128)S(1)}, f32[8,32]{1,0:T(8,128)S(1)}, u32[]{:S(2)}, u32[]{:S(2)}) collective-permute-start(f32[8,32]{1,0:T(8,128)S(1)} %slice.610), channel_id=1, source_target_pairs={{0,1},{1,2},{2,3},{3,4},{4,5},{5,6},{6,7},{7,8},{8,9},{9,10},{10,1... | collective-permute-start | bytes 3080 | tf_op jit(solution)/shard_map/ppermute | solution.py:30
  154.3 29.1 %copy-start.20 = (f32[8,2,512]{2,1,0:T(2,128)S(1)}, f32[8,2,512]{2,1,0:T(2,128)}, u32[]{:S(2)}) copy-start(f32[8,2,512]{2,1,0:T(2,128)} %param.20) | copy-start | bytes 98308
  154.3 29.1 %copy-start.21 = (f32[8,2,512]{2,1,0:T(2,128)S(1)}, f32[8,2,512]{2,1,0:T(2,128)}, u32[]{:S(2)}) copy-start(f32[8,2,512]{2,1,0:T(2,128)} %param.18) | copy-start | bytes 98308
  154.3 29.1 %copy-start.22 = (f32[8,2,512]{2,1,0:T(2,128)S(1)}, f32[8,2,512]{2,1,0:T(2,128)}, u32[]{:S(2)}) copy-start(f32[8,2,512]{2,1,0:T(2,128)} %param.19) | copy-start | bytes 98308
  154.3 8.8 %all-to-all-start.4 = ((f32[8,256,8]{1,2,0:T(8,128)}), f32[8,256,8]{1,2,0:T(8,128)S(1)}, u32[]{:S(2)}, u32[]{:S(2)}) async-start(f32[8,256,8]{1,2,0:T(8,128)} %broadcast_in_dim.47), calls=%async_computation.4 | async-start | bytes 131072 | tf_op jit(solution)/shard_map/all_to_all | solution.py:21
  163.7 11.4 %all-to-all-start.5 = ((f32[16,256,8]{1,2,0:T(8,128)}), f32[16,256,8]{1,2,0:T(8,128)S(1)}, u32[]{:S(2)}, u32[]{:S(2)}) async-start(f32[16,256,8]{1,2,0:T(8,128)} %broadcast_in_dim.48), calls=%async_computation.5 | async-start | bytes 262144 | tf_op jit(solution)/shard_map/all_to_all | solution.py:21
  175.1 25.8 %copy-start.36 = (f32[256,8]{0,1:T(8,128)}, f32[256,8]{0,1:T(8,128)S(1)}, u32[]{:S(2)}) copy-start(f32[256,8]{0,1:T(8,128)S(1)} %reduce_sum.98) | copy-start | bytes 24580
  178.4 18.2 %all-to-all-start.6 = ((f32[128,8,8]{2,1,0:T(8,128)}), f32[128,8,8]{2,1,0:T(8,128)S(1)}, u32[]{:S(2)}, u32[]{:S(2)}) async-start(f32[128,8,8]{2,1,0:T(8,128)} %broadcast_in_dim.49), calls=%async_computation.6 | async-start | bytes 1048576 | tf_op jit(solution)/shard_map/all_to_all | solution.py:21
  (7 other events, 6.2 us)

commit v2 on v0

v2 whole, which is shorter than its diff:
```python
import functools
import math

import jax
import jax.numpy as jnp
from jax import lax
from jax.experimental import pallas as pl
from jax.experimental.pallas import tpu as pltpu
from jax.sharding import Mesh
from jax.sharding import PartitionSpec as P

NC = 32
NI = 128
LANES = 128
HALF = 64
AXES = ("sub_0", "sub_1", "sub_2", "grp")
FAR, NEAR = ("sub_0", "sub_1"), ("sub_2", "grp")

highest = lax.Precision.HIGHEST
time_step = 0.5
newmark_beta = 0.25
newmark_gamma = 0.5
f32, bf16 = jnp.float32, jnp.bfloat16
NT = (((1,), (1,)), ((), ()))
NN = (((1,), (0,)), ((), ()))
VMEM = pl.BlockSpec(memory_space=pltpu.VMEM)
SMEM = pl.BlockSpec(memory_space=pltpu.SMEM)


def exchange(pieces, axes=AXES):
    return lax.all_to_all(pieces, axes, split_axis=0, concat_axis=0, tiled=True)


def to_everyone(array, axes=AXES):
    return exchange(jnp.broadcast_to(array, (lax.axis_size(axes), *array.shape)), axes)


def shifted(array, by):
    count = lax.axis_size(AXES)
    return lax.ppermute(array, AXES, [(i, (i + by) % count) for i in range(count)])


def ein(spec, *operands):
    return jnp.einsum(spec, *operands, precision=highest)


def dot(a, b, dims):
    return lax.dot_general(a, b, dims, precision=highest, preferred_element_type=f32)


def fast(a, b, dims):
    return lax.dot_general(a, b, dims, preferred_element_type=f32)


def call(body, outs, ins, scratch=(), flops=0):
    return pl.pallas_call(
        body,
        out_shape=[jax.ShapeDtypeStruct(shape, f32 if len(rest) == 0 else rest[0]) for shape, *rest in outs],
        in_specs=ins,
        out_specs=[VMEM] * len(outs),
        scratch_shapes=list(scratch),
        cost_estimate=pl.CostEstimate(flops=flops, bytes_accessed=1 << 20, transcendentals=0),
    )


def two_parts(x):
    high = x.astype(bf16)
    return high, (x - high.astype(f32)).astype(bf16)


def three_parts(x):
    high = x.astype(bf16)
    rest = x - high.astype(f32)
    middle = rest.astype(bf16)
    return high, middle, (rest - middle.astype(f32)).astype(bf16)


def split_body(matrix_ref, parts_ref):
    rows = matrix_ref.shape[0]
    high, low = two_parts(matrix_ref[...])
    parts_ref[:rows] = high
    parts_ref[rows:] = low


def coarse_product(assembled_ref, parts_ref):
    cases = assembled_ref.shape[0]
    high, low = two_parts(assembled_ref[...])
    both = fast(jnp.concatenate([high, low], axis=0), parts_ref[...], NT)
    both = both[:cases] + both[cases:]
    return both[:, :HALF] + both[:, HALF:]


def assemble_packed(got_ref, assembled_ref):
    tiles = assembled_ref.shape[1] // LANES
    lane = lax.broadcasted_iota(jnp.int32, (4, LANES), 1)
    lower = lane < HALF
    for m in range(tiles):
        even, odd = 8 * m, 8 * m + 4
        following = 8 * ((m + 1) % tiles) + 2
        previous = 8 * ((m - 1) % tiles) + 6
        extra_even, extra_odd = got_ref[following], got_ref[previous]
        top = got_ref[even] + got_ref[odd] + jnp.where(lower, extra_odd, extra_even)
        turned = pltpu.roll(jnp.where(lower, extra_even, extra_odd), HALF, 1)
        bottom = got_ref[even + 1] + got_ref[odd + 1] + turned
        assembled_ref[0:4, m * LANES : (m + 1) * LANES] = top
        assembled_ref[4:8, m * LANES : (m + 1) * LANES] = bottom


def assemble_first(got_ref, assembled_ref):
    tiles = assembled_ref.shape[1] // LANES
    lane = lax.broadcasted_iota(jnp.int32, (8, LANES), 1)
    for m in range(tiles):
        following = (2 * m + 2) % (2 * tiles)
        own = got_ref[2 * m + 1] + jnp.where(lane < HALF, got_ref[2 * m], 0.0)
        assembled_ref[:, m * LANES : (m + 1) * LANES] = own + jnp.where(
            lane >= LANES - NC, got_ref[following], 0.0
        )


def owned_terms(device_ref, assembled_ref, z):
    device = device_ref[0]
    tile = assembled_ref[:, pl.ds(pl.multiple_of((device // 2) * LANES, LANES), LANES)]
    even = lax.rem(device, 2) == 0
    return jnp.where(even, tile[:, :HALF], tile[:, HALF:]) * z


def send_blocks(z, coupling_ref, local_ref, riding, pieces_ref):
    blocks = local_ref[...] + dot(z, coupling_ref[...], NN)
    main, extra = blocks[:, :LANES], blocks[:, LANES:]
    turned = pltpu.roll(extra, HALF, 1)
    packed = extra[0:4] + turned[4:8]
    for d in range(pieces_ref.shape[0] // 4):
        pieces_ref[4 * d] = main[0:4]
        pieces_ref[4 * d + 1] = main[4:8]
        pieces_ref[4 * d + 2] = packed
        pieces_ref[4 * d + 3] = riding(d)


def first_body(got_ref, parts_ref, coupling_ref, local_ref, square_ref, pieces_ref, z_ref, assembled_ref):
    assemble_first(got_ref, assembled_ref)
    z = coarse_product(assembled_ref, parts_ref)
    z_ref[...] = z
    send_blocks(z, coupling_ref, local_ref, lambda d: square_ref[d], pieces_ref)


def second_body(device_ref, got_ref, parts_ref, coupling_ref, local_ref, pieces_ref, z_ref, terms_ref, assembled_ref):
    assemble_packed(got_ref, assembled_ref)
    z = coarse_product(assembled_ref, parts_ref)
    z_ref[...] = z
    terms_ref[...] = owned_terms(device_ref, assembled_ref, z)
    square = got_ref[3]
    for d in range(1, got_ref.shape[0] // 4):
        square = square + got_ref[4 * d + 3]
    send_blocks(z, coupling_ref, local_ref, lambda d: square, pieces_ref)


def choose_rows(select_ref, rows):
    high, middle, low = three_parts(rows)
    select = select_ref[...]
    return fast(select, high, NT) + fast(select, middle, NT) + fast(select, low, NT)


def by_offset(field):
    lane = lax.broadcasted_iota(jnp.int32, field.shape, 1)
    return [jnp.where(lane % 4 == o, field, 0.0) for o in range(4)]


def early_body(select_ref, green_ref, image_ref, chosen_ref):
    rows = []
    for ref in (green_ref, image_ref):
        for s in range(2):
            rows += by_offset(ref[s])
    chosen_ref[...] = choose_rows(select_ref, jnp.concatenate(rows, axis=0))


def third_body(
    device_ref, got_ref, parts_ref, local_ref, modes_a_ref, modes_b_ref, modes_c_ref, select_ref, sums_ref, early_ref,
    sent_ref, z_ref, assembled_ref,
):
    assemble_packed(got_ref, assembled_ref)
    z = coarse_product(assembled_ref, parts_ref)
    z_ref[...] = z
    y_0 = local_ref[0] + dot(z[:, :NC], modes_a_ref[...], NN)
    y_1 = local_ref[1] + dot(z, modes_b_ref[...], NN)
    y_2 = dot(z[:, NC:], modes_c_ref[...], NN)
    rows = by_offset(y_0) + by_offset(y_1) + by_offset(y_2)
    rows.append(jnp.zeros((32, y_0.shape[1]), f32))
    late = choose_rows(select_ref, jnp.concatenate(rows, axis=0))
    curvature = jnp.sum(owned_terms(device_ref, assembled_ref, z), axis=1, keepdims=True)
    lane = lax.broadcasted_iota(jnp.int32, (8, LANES), 1)
    case = lax.broadcasted_iota(jnp.int32, (8, LANES), 0)
    placed = jnp.where(lane == 120 + case, curvature, 0.0)
    for k in range(4):
        placed = placed + jnp.where(lane == 96 + 8 * k + case, sums_ref[:, k : k + 1], 0.0)
    late = late + jnp.sum(placed, axis=0, keepdims=True)
    sent_ref[:, 0, :] = early_ref[...]
    sent_ref[:, 1, :] = late


def project_body(got_ref, basis_ref, part_ref, rows_ref, gains_ref):
    early, late = got_ref[:, 0, :], got_ref[:, 1, :]
    sums = jnp.broadcast_to(jnp.sum(late, axis=0, keepdims=True), (8, LANES))
    lane = lax.broadcasted_iota(jnp.int32, (8, LANES), 1)
    bb, bf, ff, fff = (pltpu.roll(sums, 32 - 8 * k, 1) for k in range(4))
    good = lane < 8
    bb, bf = jnp.where(good, bb, 1.0), jnp.where(good, bf, 1.0)
    ff, fff = jnp.where(good, ff, 2.0), jnp.where(good, fff, 8.0)
    alpha_0 = bb / bf
    norm_1 = bb - 2.0 * alpha_0 * bf + alpha_0 * alpha_0 * ff
    gain = 1.0 + norm_1 / bb
    curvature = gain * gain * bf - 2.0 * gain * alpha_0 * ff + alpha_0 * alpha_0 * fff
    alpha_1 = norm_1 / curvature
    kappas = []
    for kappa in (alpha_0 + alpha_1 * gain, alpha_1 * alpha_0):
        kappa = jnp.where(good, kappa, 0.0)
        for shift in (8, 16, 32, 64):
            kappa = kappa + pltpu.roll(kappa, shift, 1)
        kappas.append(kappa)
    gains_ref[0], gains_ref[1] = kappas[0], kappas[1]
    kappa_1, kappa_2 = kappas[0][:1], kappas[1][:1]
    wide = lax.broadcasted_iota(jnp.int32, late.shape, 1)
    extra = pltpu.roll(pltpu.roll(late, HALF, 1), 1, 0)
    last = late + jnp.where(wide < NC, extra, 0.0)
    rows = early - kappa_1 * pltpu.roll(early, HALF, 1) + kappa_2 * last
    turned = jnp.transpose(rows)
    snapshots = jnp.concatenate([turned[8 * j : 8 * j + 8] for j in range(8)], axis=1)
    rows_ref[...] = snapshots
    high, low = two_parts(snapshots)
    both = jnp.concatenate([high, low], axis=0)
    count = snapshots.shape[1]
    product = fast(both, basis_ref[:count], NN) + fast(both, basis_ref[count:], NN)
    part_ref[:, : basis_ref.shape[1]] = product[:8] + product[8:]
    part_ref[:, basis_ref.shape[1] :] = dot(
        snapshots, jnp.concatenate([snapshots, jnp.zeros((LANES - 8, count), f32)], axis=0), NT
    )


def finish_body(got_ref, square_ref, basis_ref, rows_ref, columns_ref, projection_ref, factor_ref, *, scale):
    count = got_ref.shape[0]
    reduced = got_ref[0]
    for i in range(1, count):
        reduced = reduced + got_ref[i]
    rank = reduced.shape[1] - LANES
    coefficients = reduced[:, :rank]
    projection_ref[...] = coefficients
    low_rows, high_rows = coefficients[:, :LANES], coefficients[:, LANES:]
    squares = [square_ref[:, i, :] for i in range(4)]
    image = jnp.concatenate(
        [
            dot(low_rows, squares[0], NN) + dot(high_rows, squares[2], NN),
            dot(low_rows, squares[1], NN) + dot(high_rows, squares[3], NN),
        ],
        axis=1,
    )
    gap = image - 2.0 * coefficients
    gram = reduced[:, rank : rank + 8]
    blank = jnp.zeros((LANES - 8, rank), f32)
    gram = reduced[:, rank:] + dot(coefficients, jnp.concatenate([gap, blank], axis=0), NT)
    row = lax.broadcasted_iota(jnp.int32, (8, LANES), 0)
    lane = lax.broadcasted_iota(jnp.int32, (8, LANES), 1)
    gram = jnp.where(lane < 8, gram, 0.0)
    work = gram + jnp.where(lane == row + 8, 1.0, 0.0)
    upper = jnp.zeros((8, LANES), f32)
    for j in range(8):
        pivot = jnp.sum(jnp.where((row == j) & (lane == j), work, 0.0), axis=(0, 1), keepdims=True)
        line = jnp.sum(jnp.where(row == j, work, 0.0), axis=0, keepdims=True) / jnp.sqrt(pivot)
        upper = jnp.where(row == j, line, upper)
        column = jnp.sum(jnp.where(lane == j, work, 0.0), axis=1, keepdims=True) / jnp.sqrt(pivot)
        work = jnp.where(row > j, work - column * line, work)
    factor_ref[...] = jnp.where((lane >= row) & (lane < 8), upper, 0.0) * (1.0 / scale)
    inverse = pltpu.roll(upper, LANES - 8, 1)
    inverse = jnp.where((lane <= row) & (lane < 8), inverse, 0.0)[:, :8]
    high, low = two_parts(coefficients)
    total = rows_ref.shape[1]
    both = jnp.concatenate([high, low], axis=0)
    product = fast(both, basis_ref[:total], NT) + fast(both, basis_ref[total:], NT)
    remainder = rows_ref[...] - (product[:8] + product[8:])
    columns = dot(inverse, remainder, NN) * scale
    for t in range(8):
        index = 16 * t + lane // 8
        out = jnp.zeros((8, LANES), f32)
        for j in range(8):
            picked = jnp.take_along_axis(columns[:, j * LANES : (j + 1) * LANES], index, axis=1)
            out = jnp.where(lane % 8 == j, picked, out)
        columns_ref[:, t * LANES : (t + 1) * LANES] = out


def shards(
    rr_inverse,
    corner_modes,
    coarse_inverse,
    inertia,
    disp_now,
    vel_now,
    acc_now,
    load_next,
    basis_rows,
    piece_owner,
):
    case_count, sub_count, unknowns = disp_now.shape
    devices = lax.axis_size(AXES)
    coarse_total = coarse_inverse.shape[1]
    rank = basis_rows.shape[1]
    last = unknowns - NI
    me = lax.axis_index(AXES)
    even = me % 2 == 0
    device = me.reshape(1).astype(jnp.int32)

    right_modes = shifted(corner_modes, -1)
    left_edge = shifted(corner_modes[1, :, last:], 1)

    right_side = load_next + inertia[None] * (
        disp_now + time_step * vel_now + (0.5 - newmark_beta) * time_step * time_step * acc_now
    )
    terms = ein("jmb,cjb->jcm", corner_modes, right_side)
    low, middle, high = terms[0, :, :NC], terms[0, :, NC:] + terms[1, :, :NC], terms[1, :, NC:]
    gap = jnp.zeros((case_count, NC), f32)
    start = jnp.where(
        even,
        jnp.concatenate([middle, high, gap, low], axis=1),
        jnp.concatenate([gap, low, middle, high], axis=1),
    )
    got_1 = to_everyone(start)

    (coarse_parts,) = call(split_body, [((4 * NC, coarse_total), bf16)], [VMEM], flops=1 << 22)(coarse_inverse)
    basis_sorted = basis_rows.reshape(devices, -1, rank).swapaxes(0, 1).reshape(-1, rank)
    (basis_parts,) = call(split_body, [((2 * basis_sorted.shape[0], rank), bf16)], [VMEM], flops=1 << 22)(basis_sorted)
    square = lax.dot_general(basis_rows, basis_rows, (((0,), (0,)), ((), ())), precision=highest)
    square = jnp.stack(
        [square[:LANES, :LANES], square[:LANES, LANES:], square[LANES:, :LANES], square[LANES:, LANES:]], axis=1
    )
    owner = jnp.broadcast_to(piece_owner[:, None], (devices, unknowns // devices)).reshape(1, unknowns)
    select = (owner == lax.broadcasted_iota(jnp.int32, (devices, unknowns), 0)).astype(bf16)

    zero = jnp.zeros((NC, NI), f32)
    first, final = corner_modes[:, :, :NI], corner_modes[:, :, last:]
    right_first, right_final = right_modes[:, :, :NI], right_modes[:, :, last:]
    rows = [
        [left_edge[:NC], zero, zero, zero],
        [left_edge[NC:] - first[0, :NC], final[0, :NC], zero, zero],
        [-first[0, NC:], final[0, NC:] - first[1, :NC], final[1, :NC], zero],
        [zero, -first[1, NC:], final[1, NC:] - right_first[0, :NC], right_final[0, :NC]],
        [zero, zero, -right_first[0, NC:], right_final[0, NC:] - right_first[1, :NC]],
        [zero, zero, zero, -right_first[1, NC:]],
    ]
    rows = jnp.concatenate([jnp.concatenate(parts, axis=1) for parts in rows], axis=0)
    blank = jnp.zeros((HALF, 4 * NI), f32)
    to_blocks = jnp.where(
        even,
        jnp.concatenate([rows[HALF:], blank, rows[:HALF]], axis=0),
        jnp.concatenate([rows, blank], axis=0),
    )

    def blocks_of(d_a, d_b, d_c, d_d):
        return dot(jnp.concatenate([d_a, d_b, d_c, d_d], axis=1), to_blocks, NT)

    def local_blocks(field):
        return blocks_of(
            -field[0, :, :NI], field[0, :, last:] - field[1, :, :NI], field[1, :, last:], jnp.zeros((case_count, NI), f32)
        )

    unit_0 = jnp.concatenate([corner_modes[0, NC:], jnp.zeros((NC, unknowns), f32)], axis=0)
    unit_1 = corner_modes[1]
    unit_2 = jnp.concatenate([jnp.zeros((NC, unknowns), f32), right_modes[0, :NC]], axis=0)
    coupling = blocks_of(
        -unit_0[:, :NI], unit_0[:, last:] - unit_1[:, :NI], unit_1[:, last:] - unit_2[:, :NI], unit_2[:, last:]
    )

    def finish(local, z):
        z_a, z_b = z[:, :NC], z[:, NC:]
        mine_0 = local[0] + dot(z_a, corner_modes[0, NC:], NN)
        mine_1 = local[1] + dot(z, corner_modes[1], NN)
        from_left = shifted(jnp.concatenate([mine_1[:, last:], z_b], axis=1), 1)
        from_right = shifted(mine_0[:, :NI], -1)
        mine_0 = mine_0 + dot(from_left[:, NI:], corner_modes[0, :NC], NN)
        jump_a = from_left[:, :NI] - mine_0[:, :NI]
        jump_b = mine_0[:, last:] - mine_1[:, :NI]
        jump_c = mine_1[:, last:] - (from_right + dot(z_b, right_modes[0, :NC, :NI], NN))
        return jnp.stack([mine_0, mine_1]), jump_a, jump_b, jump_c

    def local_apply(jump_a, jump_b, jump_c):
        first = jnp.stack([-jump_a, -jump_b])
        final = jnp.stack([jump_b, jump_c])
        out = ein("jcb,jab->jca", first, rr_inverse[:, :, :NI]) + ein("jcb,jab->jca", final, rr_inverse[:, :, last:])
        inner = jnp.sum(out[:, :, :NI] * first + out[:, :, last:] * final, axis=(0, 2))
        return out, inner

    local_0 = ein("cjb,jab->jca", right_side, rr_inverse)
    assembled = [pltpu.VMEM((case_count, coarse_total), f32)]
    piece_shape = ((4 * devices, 4, LANES),)
    z_shape = ((case_count, 2 * NC),)
    pieces, z_0 = call(first_body, [piece_shape, z_shape], [VMEM] * 5, assembled, flops=1 << 24)(
        got_1, coarse_parts, coupling, local_blocks(local_0), square
    )
    got_2 = exchange(pieces)
    green, b_a, b_b, b_c = finish(local_0, z_0)
    local_1, inner_1 = local_apply(b_a, b_b, b_c)
    pieces, z_1, terms_1 = call(second_body, [piece_shape, z_shape, z_shape], [SMEM] + [VMEM] * 4, assembled, flops=1 << 24)(
        device, got_2, coarse_parts, coupling, local_blocks(local_1)
    )
    got_3 = exchange(pieces)
    image_1, v_a, v_b, v_c = finish(local_1, z_1)
    local_2, inner_2 = local_apply(v_a, v_b, v_c)
    sums = jnp.stack(
        [
            jnp.sum(b_b * b_b + b_c * b_c, axis=1),
            inner_1 + jnp.sum(terms_1, axis=1),
            jnp.sum(v_b * v_b + v_c * v_c, axis=1),
            inner_2,
        ],
        axis=1,
    )
    (early,) = call(early_body, [((devices, LANES),)], [VMEM] * 3, flops=1 << 24)(select, green, image_1)
    sent, z_2 = call(third_body, [((devices, 2, LANES),), z_shape], [SMEM] + [VMEM] * 9, assembled, flops=1 << 24)(
        device, got_3, coarse_parts, local_2, corner_modes[0, NC:], corner_modes[1], right_modes[0, :NC], select, sums, early
    )
    got_4 = exchange(sent)
    ghost = shifted(z_2[:, NC:], 1)
    part, snapshots, gains = call(
        project_body,
        [((case_count, rank + LANES),), ((case_count, basis_rows.shape[0]),), ((2, case_count, LANES),)],
        [VMEM] * 2,
        flops=1 << 24,
    )(got_4, basis_parts)
    near = to_everyone(part, NEAR).sum(axis=0)
    got_5 = to_everyone(near, FAR)
    squares = got_3.reshape(devices, 4, 4, LANES)[:, 3]
    scale = math.sqrt(basis_rows.shape[0] * devices)
    new_columns, projection, factor = call(
        functools.partial(finish_body, scale=scale),
        [((case_count, basis_rows.shape[0]),), ((case_count, rank),), ((case_count, LANES),)],
        [VMEM] * 4,
        flops=1 << 24,
    )(got_5, squares, basis_parts, snapshots)

    kappa_1, kappa_2 = gains[0, 0, :case_count, None], gains[1, 0, :case_count, None]
    image_2 = jnp.stack(
        [
            local_2[0] + dot(z_2[:, :NC], corner_modes[0, NC:], NN) + dot(ghost, corner_modes[0, :NC], NN),
            local_2[1] + dot(z_2, corner_modes[1], NN),
        ]
    )
    disp_new = green - kappa_1 * image_1 + kappa_2 * image_2
    disp_new = jnp.swapaxes(disp_new, 0, 1)
    accel_new = (
        (disp_new - disp_now) / (newmark_beta * time_step * time_step)
        - vel_now / (newmark_beta * time_step)
        - (0.5 / newmark_beta - 1.0) * acc_now
    )
    vel_new = vel_now + time_step * ((1.0 - newmark_gamma) * acc_now + newmark_gamma * accel_new)
    return (disp_new, vel_new, projection.T, factor[:, :case_count], new_columns)


def solution(mesh):
    finer = Mesh(
        mesh.devices.reshape(4, 4, 2, mesh.shape["grp"]), ("sub_0", "sub_1", "sub_2", "grp")
    )
    placed = (
        P(AXES, None, None),
        P(AXES, None, None),
        P(AXES, None),
        P(AXES, None),
        P(None, AXES, None),
        P(None, AXES, None),
        P(None, AXES, None),
        P(None, AXES, None),
        P(AXES, None),
        P(),
    )
    return jax.shard_map(
        shards,
        mesh=finer,
        in_specs=placed,
        out_specs=(P(None, AXES, None), P(None, AXES, None), P(), P(), P(None, AXES)),
        check_vma=False,
    )
```

time: 317 us -> 183 us (0.58)
  blocking collectives: 104 us -> 0 us
  waiting for transfers between devices: 93.6 us -> 45.3 us
  Pallas kernels: 0 us -> 26.2 us
  matrix products: 32.9 us -> 19.6 us
  starting transfers between devices: 48 us -> 59.1 us
  other arithmetic: 16.5 us -> 11.4 us
    all_to_all x10 -> x0, blocking collectives: 104 us -> none  [the longest x9 86.4 us: copy_for_each(): return lax.all_to_all(copies, axis, split_axis=0, concat_axis=0, tiled=True)]
    ppermute x8 -> x7, waiting for transfers between devices: 40.2 us -> 6.74 us  [shifted(): lax.ppermute(array, AXES, [(i, (i + by) % count) for i in range(count)])]
    pallas_call x0 -> x8, Pallas kernels: none -> 26.2 us  [the longest x1 4.25 us: shards(): call(third_body, [((devices, 2, LANES),), z_shape], [SMEM] + [VMEM] * 9,...]
    ppermute x8 -> x7, starting transfers between devices: 6.71 us -> 23.5 us  [shifted(): lax.ppermute(array, AXES, [(i, (i + by) % count) for i in range(count)])]
    all_to_all x9 -> x6, waiting for transfers between devices: 53.4 us -> 38.5 us  [exchange(): return lax.all_to_all(pieces, axes, split_axis=0, concat_axis=0, tiled=True)]
    dot_general x15 -> x21, matrix products: 32.1 us -> 19.6 us  [the longest x14 11.1 us: dot(): lax.dot_general(a, b, dims, precision=highest, preferred_element_type=f32)]
    concatenate x2 -> x3, other arithmetic: 11.9 us -> 0.02 us  [the longest x2 0.01 us: finish(): from_left = shifted(jnp.concatenate([mine_1[:, last:], z_b], axis=1), 1)]
    all_to_all x9 -> x6, starting transfers between devices: 41.3 us -> 35.6 us  [exchange(): return lax.all_to_all(pieces, axes, split_axis=0, concat_axis=0, tiled=True)]
  transfers between devices with their start and end apart: 17 -> 13, of which waited for: 16 -> 5; matrix products, arithmetic and copies ran while one was open for 9% -> 21% of each run, Pallas kernels for 0% -> 4%
where the time goes in v2:
time: 183 us; the launch traced here: 181 us
  starting transfers between devices  59.1 us (32%)
  waiting for transfers between devices  45.3 us (25%)
  Pallas kernels  26.2 us (14%)
  matrix products  19.6 us (11%)
  local copies, waits for them, and re-layouts  18.9 us (10%)
  other arithmetic  11.4 us (6%)
    all_to_all x6, waiting for transfers between devices, exchange(): return lax.all_to_all(pieces, axes, split_axis=0, concat_axis=0, tiled=True)  38.5 us
    all_to_all x6, starting transfers between devices, exchange(): return lax.all_to_all(pieces, axes, split_axis=0, concat_axis=0, tiled=True)  35.6 us
    ppermute x7, starting transfers between devices, shifted(): lax.ppermute(array, AXES, [(i, (i + by) % count) for i in range(count)])  23.5 us
    dot_general x14, matrix products, dot(): lax.dot_general(a, b, dims, precision=highest, preferred_element_type=f32)  11.1 us
    ppermute x7, waiting for transfers between devices, shifted(): lax.ppermute(array, AXES, [(i, (i + by) % count) for i in range(count)])  6.74 us
    dot_general x6, matrix products, ein(): return jnp.einsum(spec, *operands, precision=highest)  6.66 us
    pallas_call x1, Pallas kernels, shards(): call(third_body, [((devices, 2, LANES),), z_shape], [SMEM] + [VMEM] * 9,...  4.25 us
    pallas_call x1, Pallas kernels, shards(): call(functools.partial(finish_body, scale=scale), [((case_count, basis_ro...  4.02 us
  transfers between devices with their start and end apart: 13, of which 5 were waited for; matrix products, arithmetic and copies ran while one was open for 21% of the time, Pallas kernels for 4%

profile of v2, /device:TPU:0, one launch (start us, length us, event | category | flops | bytes accessed | tf_op | source)
XLA Modules:
  0.0 181.5 jit_solution(6204476312938157464)
XLA Ops:
  0.7 8.3 %collective-permute-start = (f32[2,64,512]{2,1,0:T(8,128)}, f32[2,64,512]{2,1,0:T(8,128)}, u32[]{:S(2)}, u32[]{:S(2)}) collective-permute-start(f32[2,64,512]{2,1,0:T(8,128)} %param.11), channel_id=1, source_target_pairs={{0,127},{1,0},{2,1},{3,2},{4,3},{5,4},{6,5},{7,6},{8,7},{9,8},{10,... | collective-permute-start | bytes 786440 | tf_op jit(solution)/shard_map/ppermute | solution.py:40
  9.0 1.4 slice_bitcast_fusion.4
  10.4 0.8 multiply_add_fusion
  11.2 1.3 fusion.42
  12.7 0.9 broadcast_in_dim.26
  13.5 9.6 %all-to-all-start = ((f32[128,8,128]{2,1,0:T(8,128)}), f32[128,8,128]{2,1,0:T(8,128)}, u32[]{:S(2)}, u32[]{:S(2)}) async-start(f32[128,8,128]{2,1,0:T(8,128)} %broadcast_in_dim.26), calls=%async_computation | async-start | bytes 1048576 | tf_op jit(solution)/shard_map/all_to_all | solution.py:31
  24.5 3.2 %fusion.44 = f32[2,8,512]{2,1,0:T(8,128)} fusion(f32[2,512,512]{2,1,0:T(8,128)S(1)} %copy-done.1, f32[8,2,512]{2,1,0:T(2,128)} %copy-done.10), kind=kOutput, calls=%fused_computation.85 | convolution fusion | flops 50331648 | bytes 2162688 | tf_op jit(solution)/shard_map/cjb,jab->jca/dot_general | solution.py:44
  27.8 1.8 %fusion.96 = f32[256,256]{1,0:T(8,128)S(1)} fusion(f32[1024,256]{1,0:T(8,128)S(1)} %copy-done), kind=kOutput, calls=%fused_computation.186 | convolution fusion | flops 805306368 | bytes 1310720 | tf_op jit(solution)/shard_map/dot_general | solution.py:328
  31.0 1.5 eq.16
  32.6 1.4 fusion.10.select_ref
  33.9 1.3 fusion.78
  35.3 1.9 %pad_maximum_fusion.square_ref = f32[128,4,128]{2,1,0:T(4,128)} fusion(f32[128,1,128]{2,1,0:T(1,128)} %bitcast.156, f32[128,1,128]{2,1,0:T(1,128)} %bitcast.157, f32[128,1,128]{2,1,0:T(1,128)} %bitcast.158, f32[128,1,128]{2,1,0:T(1,128)} %bitcast.155), kind=kLoop, calls=%fused_computation.24 | loop fusion | flops 196608 | bytes 524288 | tf_op jit(solution)/shard_map/stack | solution.py:329
  37.2 1.3 copy.51
  38.5 3.3 %shard_map.137.parts_ref = bf16[128,8192]{1,0:T(8,128)(2,1)} custom-call(f32[64,8192]{1,0:T(8,128)} %matrix_ref.1), custom_call_target="tpu_custom_call" | custom-call | flops 4194304 | bytes 1048576 | tf_op jit(solution)/shard_map/pallas_call | solution.py:325
  41.7 2.4 %shard_map.142.basis_ref = bf16[2048,256]{1,0:T(8,128)(2,1)} custom-call(f32[1024,256]{1,0:T(8,128)} %bitcast.154), custom_call_target="tpu_custom_call" | custom-call | flops 4194304 | bytes 1048576 | tf_op jit(solution)/shard_map/pallas_call | solution.py:327
  46.1 0.8 slice_bitcast_fusion.2.modes_c_ref
  47.0 1.1 fusion.49.local_ref
  48.1 1.2 fusion.11.coupling_ref
  49.4 3.8 %shard_map.138 = (f32[512,4,128]{2,1,0:T(4,128)}, f32[8,64]{1,0:T(8,128)}) custom-call(f32[128,8,128]{2,1,0:T(8,128)} %all-to-all-done.got_ref, bf16[128,8192]{1,0:T(8,128)(2,1)} %shard_map.137.parts_ref, f32[64,256]{1,0:T(8,128)} %fusion.11.coupling_ref, f32[8,256]{1,0:T(8,128)} %fusion.49.local_ref, f32[128,4,128]{2,1,0:T(4,128)} %pad_maximum_fusion.square_ref), custom_call_target="tpu_custom_call" | custom-call | flops 16777216 | bytes 1048576 | tf_op jit(solution)/shard_map/pallas_call | solution.py:392
  53.2 0.9 convolution_add_fusion.9
  54.9 0.8 convolution_add_fusion.10
  55.7 7.0 %collective-permute-start.3 = (f32[8,128]{1,0:T(8,128)S(1)}, f32[8,128]{1,0:T(8,128)S(1)}, u32[]{:S(2)}, u32[]{:S(2)}) collective-permute-start(f32[8,128]{1,0:T(8,128)S(1)} %slice.386), channel_id=1, source_target_pairs={{0,127},{1,0},{2,1},{3,2},{4,3},{5,4},{6,5},{7,6},{8,7},{9,8},{10,... | collective-permute-start | bytes 12296 | tf_op jit(solution)/shard_map/ppermute | solution.py:40
  62.8 9.8 %all-to-all-start.1 = ((f32[512,4,128]{2,1,0:T(4,128)}), f32[512,4,128]{2,1,0:T(4,128)}, u32[]{:S(2)}, u32[]{:S(2)}) async-start(f32[512,4,128]{2,1,0:T(4,128)} %get-tuple-element.19), calls=%async_computation.1 | async-start | bytes 2097152 | tf_op jit(solution)/shard_map/all_to_all | solution.py:31
  72.6 0.9 fusion.3
  75.8 1.1 fusion.56.local_ref
  76.9 13.9 %all-to-all-done.1.got_ref = f32[512,4,128]{2,1,0:T(4,128)} async-done(((f32[512,4,128]{2,1,0:T(4,128)}), f32[512,4,128]{2,1,0:T(4,128)}, u32[]{:S(2)}, u32[]{:S(2)}) %all-to-all-start.1) | async-done | bytes 1048608 | tf_op jit(solution)/shard_map/all_to_all | solution.py:31
  90.8 3.9 %shard_map.139 = (f32[512,4,128]{2,1,0:T(4,128)}, f32[8,64]{1,0:T(8,128)}, f32[8,64]{1,0:T(8,128)}) custom-call(s32[1]{0:T(128)} %bitcast.31.device_ref, f32[512,4,128]{2,1,0:T(4,128)} %all-to-all-done.1.got_ref, bf16[128,8192]{1,0:T(8,128)(2,1)} %shard_map.137.parts_ref, f32[64,256]{1,0:T(8,128)} %fusion.11.coupling_ref, f32[8,256]{1,0:T(8,128)} %fusion.56.local_ref), custom_call_target="tpu_custom_call" | custom-call | flops 16777216 | bytes 1048576 | tf_op jit(solution)/shard_map/pallas_call | solution.py:398
  94.7 0.9 convolution_add_fusion.7
  96.4 0.8 convolution_add_fusion.6
  98.7 6.7 %collective-permute-start.5 = (f32[8,128]{1,0:T(8,128)S(1)}, f32[8,128]{1,0:T(8,128)S(1)}, u32[]{:S(2)}, u32[]{:S(2)}) collective-permute-start(f32[8,128]{1,0:T(8,128)S(1)} %slice.399), channel_id=1, source_target_pairs={{0,127},{1,0},{2,1},{3,2},{4,3},{5,4},{6,5},{7,6},{8,7},{9,8},{10,... | collective-permute-start | bytes 12296 | tf_op jit(solution)/shard_map/ppermute | solution.py:40
  105.5 4.6 %all-to-all-start.2 = ((f32[512,4,128]{2,1,0:T(4,128)}), f32[512,4,128]{2,1,0:T(4,128)S(1)}, u32[]{:S(2)}, u32[]{:S(2)}) async-start(f32[512,4,128]{2,1,0:T(4,128)} %get-tuple-element.20), calls=%async_computation.2 | async-start | bytes 2097152 | tf_op jit(solution)/shard_map/all_to_all | solution.py:31
  110.2 0.9 fusion.2
  113.4 1.8 %shard_map.140.early_ref = f32[128,128]{1,0:T(8,128)} custom-call(bf16[128,512]{1,0:T(8,128)(2,1)} %fusion.10.select_ref, f32[2,8,512]{2,1,0:T(8,128)} %pad_maximum_fusion.5.green_ref, f32[2,8,512]{2,1,0:T(8,128)} %pad_maximum_fusion.6.image_ref), custom_call_target="tpu_custom_call" | custom-call | flops 16777216 | bytes 1048576 | tf_op jit(solution)/shard_map/pallas_call | solution.py:413
  115.9 13.1 %all-to-all-done.2.got_ref = f32[512,4,128]{2,1,0:T(4,128)S(1)} async-done(((f32[512,4,128]{2,1,0:T(4,128)}), f32[512,4,128]{2,1,0:T(4,128)S(1)}, u32[]{:S(2)}, u32[]{:S(2)}) %all-to-all-start.2) | async-done | bytes 1048608 | tf_op jit(solution)/shard_map/all_to_all | solution.py:31
  128.9 1.0 copy-done.3
  129.9 4.3 %shard_map.141 = (f32[128,2,128]{2,1,0:T(2,128)}, f32[8,64]{1,0:T(8,128)}) custom-call(s32[1]{0:T(128)} %bitcast.31.device_ref, f32[512,4,128]{2,1,0:T(4,128)} %copy-done.3, bf16[128,8192]{1,0:T(8,128)(2,1)} %shard_map.137.parts_ref, f32[2,8,512]{2,1,0:T(8,128)} %copy-done.9, f32[32,512]{1,0:T(8,128)} %slice_bitcast_fusion.3.modes_a_ref, ...), custom_call_target="tpu_custom_call" | custom-call | flops 16777216 | bytes 1048576 | tf_op jit(solution)/shard_map/pallas_call | solution.py:414
  134.2 0.9 convolution_add_fusion.4
  135.9 4.6 %all-to-all-start.3 = ((f32[128,2,128]{2,1,0:T(2,128)}), f32[128,2,128]{2,1,0:T(2,128)S(1)}, u32[]{:S(2)}, u32[]{:S(2)}) async-start(f32[128,2,128]{2,1,0:T(2,128)} %get-tuple-element.23), calls=%async_computation.3 | async-start | bytes 262144 | tf_op jit(solution)/shard_map/all_to_all | solution.py:31
  140.5 1.7 slice_bitcast_fusion.square_ref
  143.0 0.9 fusion
  143.9 6.7 %collective-permute-done.6 = f32[8,32]{1,0:T(8,128)S(1)} collective-permute-done((f32[8,32]{1,0:T(8,128)S(1)}, f32[8,32]{1,0:T(8,128)S(1)}, u32[]{:S(2)}, u32[]{:S(2)}) %collective-permute-start.6) | collective-permute-done | bytes 1056 | tf_op jit(solution)/shard_map/ppermute | solution.py:40
  151.4 2.7 %shard_map.143 = (f32[8,384]{1,0:T(8,128)}, f32[8,1024]{1,0:T(8,128)}, f32[2,8,128]{2,1,0:T(8,128)}) custom-call(f32[128,2,128]{2,1,0:T(2,128)} %copy-done.8, bf16[2048,256]{1,0:T(8,128)(2,1)} %shard_map.142.basis_ref), custom_call_target="tpu_custom_call" | custom-call | flops 16777216 | bytes 1048576 | tf_op jit(solution)/shard_map/pallas_call | solution.py:419
  154.1 1.3 broadcast_in_dim.30
  155.5 3.4 %all-to-all-start.4 = ((f32[8,8,384]{2,1,0:T(8,128)}), f32[8,8,384]{2,1,0:T(8,128)S(1)}, u32[]{:S(2)}, u32[]{:S(2)}) async-start(f32[8,8,384]{2,1,0:T(8,128)} %broadcast_in_dim.30), calls=%async_computation.4 | async-start | bytes 196608 | tf_op jit(solution)/shard_map/all_to_all | solution.py:31
  159.6 4.6 %all-to-all-done.4 = f32[8,8,384]{2,1,0:T(8,128)S(1)} async-done(((f32[8,8,384]{2,1,0:T(8,128)}), f32[8,8,384]{2,1,0:T(8,128)S(1)}, u32[]{:S(2)}, u32[]{:S(2)}) %all-to-all-start.4) | async-done | bytes 98336 | tf_op jit(solution)/shard_map/all_to_all | solution.py:31
  164.9 3.5 %all-to-all-start.5 = ((f32[16,8,384]{2,1,0:T(8,128)}), f32[16,8,384]{2,1,0:T(8,128)S(1)}, u32[]{:S(2)}, u32[]{:S(2)}) async-start(f32[16,8,384]{2,1,0:T(8,128)} %broadcast_in_dim.31), calls=%async_computation.5 | async-start | bytes 393216 | tf_op jit(solution)/shard_map/all_to_all | solution.py:31
  169.8 6.9 %all-to-all-done.5.got_ref = f32[16,8,384]{2,1,0:T(8,128)S(1)} async-done(((f32[16,8,384]{2,1,0:T(8,128)}), f32[16,8,384]{2,1,0:T(8,128)S(1)}, u32[]{:S(2)}, u32[]{:S(2)}) %all-to-all-start.5) | async-done | bytes 196640 | tf_op jit(solution)/shard_map/all_to_all | solution.py:31
  177.4 4.0 %shard_map.144 = (f32[8,1024]{1,0:T(8,128)}, f32[8,256]{1,0:T(8,128)}, f32[8,128]{1,0:T(8,128)}) custom-call(f32[16,8,384]{2,1,0:T(8,128)} %copy-done.5, f32[128,4,128]{2,1,0:T(4,128)} %slice_bitcast_fusion.square_ref, bf16[2048,256]{1,0:T(8,128)(2,1)} %shard_map.142.basis_ref, f32[8,1024]{1,0:T(8,128)} %get-tuple-element.27.rows_ref), custom_call_target="tpu_custom_call" | custom-call | flops 16777216 | bytes 1048576 | tf_op jit(solution)/shard_map/pallas_call | solution.py:429
  (122 shorter events, 19.0 us)
Async XLA Ops:
  0.6 22.6 %copy-start.2 = (f32[2,64,512]{2,1,0:T(8,128)S(1)}, f32[2,64,512]{2,1,0:T(8,128)}, u32[]{:S(2)}) copy-start(f32[2,64,512]{2,1,0:T(8,128)} %param.11) | copy-start | bytes 786436
  0.6 23.9 %copy-start.1 = (f32[2,512,512]{2,1,0:T(8,128)S(1)}, f32[2,512,512]{2,1,0:T(8,128)}, u32[]{:S(2)}) copy-start(f32[2,512,512]{2,1,0:T(8,128)} %param.10) | copy-start | bytes 6291460
  0.7 43.5 %collective-permute-start = (f32[2,64,512]{2,1,0:T(8,128)}, f32[2,64,512]{2,1,0:T(8,128)}, u32[]{:S(2)}, u32[]{:S(2)}) collective-permute-start(f32[2,64,512]{2,1,0:T(8,128)} %param.11), channel_id=1, source_target_pairs={{0,127},{1,0},{2,1},{3,2},{4,3},{5,4},{6,5},{7,6},{8,7},{9,8},{10,... | collective-permute-start | bytes 786440 | tf_op jit(solution)/shard_map/ppermute | solution.py:40
  10.4 33.8 %collective-permute-start.1 = (f32[64,128]{1,0:T(8,128)}, f32[64,128]{1,0:T(8,128)}, u32[]{:S(2)}, u32[]{:S(2)}) collective-permute-start(f32[64,128]{1,0:T(8,128)} %slice_bitcast_fusion.4), channel_id=1, source_target_pairs={{0,1},{1,2},{2,3},{3,4},{4,5},{5,6},{6,7},{7,8},{8,9},{9,10},{10,1... | collective-permute-start | bytes 98312 | tf_op jit(solution)/shard_map/ppermute | solution.py:40
  11.2 1.4 copy-start.10
  12.7 15.1 %copy-start = (f32[1024,256]{1,0:T(8,128)S(1)}, f32[1024,256]{1,0:T(8,128)}, u32[]{:S(2)}) copy-start(f32[1024,256]{1,0:T(8,128)} %param.18) | copy-start | bytes 3145732
  13.5 35.8 %all-to-all-start = ((f32[128,8,128]{2,1,0:T(8,128)}), f32[128,8,128]{2,1,0:T(8,128)}, u32[]{:S(2)}, u32[]{:S(2)}) async-start(f32[128,8,128]{2,1,0:T(8,128)} %broadcast_in_dim.26), calls=%async_computation | async-start | bytes 1048576 | tf_op jit(solution)/shard_map/all_to_all | solution.py:31
  23.8 23.1 %copy-start.4 = (f32[64,512]{1,0:T(8,128)}, f32[64,512]{1,0:T(8,128)S(1)}, u32[]{:S(2)}) copy-start(f32[64,512]{1,0:T(8,128)S(1)} %slice_bitcast_fusion.1.modes_b_ref) | copy-start | bytes 393220
  24.5 5.8 %copy-start.24 = (s32[128]{0:T(128)S(1)}, s32[128]{0:T(128)}, u32[]{:S(2)}) copy-start(s32[128]{0:T(128)} %param.19) | copy-start | bytes 1540
  41.7 3.3 %copy-start.16 = (f32[32,128]{1,0:T(8,128)S(1)}, f32[32,128]{1,0:T(8,128)}, u32[]{:S(2)}) copy-start(f32[32,128]{1,0:T(8,128)} %get-tuple-element.56) | copy-start | bytes 49156
  41.7 3.3 %copy-start.17 = (f32[32,128]{1,0:T(8,128)S(1)}, f32[32,128]{1,0:T(8,128)}, u32[]{:S(2)}) copy-start(f32[32,128]{1,0:T(8,128)} %get-tuple-element.57) | copy-start | bytes 49156
  41.7 3.3 %copy-start.18 = (f32[32,128]{1,0:T(8,128)S(1)}, f32[32,128]{1,0:T(8,128)}, u32[]{:S(2)}) copy-start(f32[32,128]{1,0:T(8,128)} %get-tuple-element.58) | copy-start | bytes 49156
  41.7 4.1 %copy-start.15 = (f32[32,128]{1,0:T(8,128)S(1)}, f32[32,128]{1,0:T(8,128)}, u32[]{:S(2)}) copy-start(f32[32,128]{1,0:T(8,128)} %get-tuple-element.55) | copy-start | bytes 49156
  44.1 2.8 %copy-start.6 = (f32[32,512]{1,0:T(8,128)S(1)}, f32[32,512]{1,0:T(8,128)}, u32[]{:S(2)}) copy-start(f32[32,512]{1,0:T(8,128)} %slice_bitcast_fusion.3.modes_a_ref) | copy-start | bytes 196612
  44.1 2.9 %copy-start.21 = (f32[8,128]{1,0:T(8,128)S(1)}, f32[8,128]{1,0:T(8,128)}, u32[]{:S(2)}) copy-start(f32[8,128]{1,0:T(8,128)} %get-tuple-element.82) | copy-start | bytes 12292
  44.1 2.9 %copy-start.22 = (f32[8,128]{1,0:T(8,128)S(1)}, f32[8,128]{1,0:T(8,128)}, u32[]{:S(2)}) copy-start(f32[8,128]{1,0:T(8,128)} %get-tuple-element.83) | copy-start | bytes 12292
  44.1 2.9 %copy-start.23 = (f32[8,128]{1,0:T(8,128)S(1)}, f32[8,128]{1,0:T(8,128)}, u32[]{:S(2)}) copy-start(f32[8,128]{1,0:T(8,128)} %get-tuple-element.84) | copy-start | bytes 12292
  47.0 6.2 %copy-start.7 = (f32[32,512]{1,0:T(8,128)}, f32[32,512]{1,0:T(8,128)S(1)}, u32[]{:S(2)}) copy-start(f32[32,512]{1,0:T(8,128)S(1)} %slice_bitcast_fusion.2.modes_c_ref) | copy-start | bytes 196612
  47.0 6.2 %copy-start.11 = (f32[2,8,512]{2,1,0:T(8,128)S(1)}, f32[2,8,512]{2,1,0:T(8,128)}, u32[]{:S(2)}) copy-start(f32[2,8,512]{2,1,0:T(8,128)} %fusion.44) | copy-start | bytes 98308
  53.2 19.4 %copy-start.20 = (f32[8,64]{1,0:T(8,128)S(1)}, f32[8,64]{1,0:T(8,128)}, u32[]{:S(2)}) copy-start(f32[8,64]{1,0:T(8,128)} %get-tuple-element.18) | copy-start | bytes 6148
  55.7 16.9 %collective-permute-start.3 = (f32[8,128]{1,0:T(8,128)S(1)}, f32[8,128]{1,0:T(8,128)S(1)}, u32[]{:S(2)}, u32[]{:S(2)}) collective-permute-start(f32[8,128]{1,0:T(8,128)S(1)} %slice.386), channel_id=1, source_target_pairs={{0,127},{1,0},{2,1},{3,2},{4,3},{5,4},{6,5},{7,6},{8,7},{9,8},{10,... | collective-permute-start | bytes 12296 | tf_op jit(solution)/shard_map/ppermute | solution.py:40
  62.8 10.8 %collective-permute-start.2 = (f32[8,160]{1,0:T(8,128)S(1)}, f32[8,160]{1,0:T(8,128)S(1)}, u32[]{:S(2)}, u32[]{:S(2)}) collective-permute-start(f32[8,160]{1,0:T(8,128)S(1)} %pad_maximum_fusion.7), channel_id=1, source_target_pairs={{0,1},{1,2},{2,3},{3,4},{4,5},{5,6},{6,7},{7,8},{8,9},{9,10},{10,1... | collective-permute-start | bytes 15368 | tf_op jit(solution)/shard_map/ppermute | solution.py:40
  62.8 28.0 %all-to-all-start.1 = ((f32[512,4,128]{2,1,0:T(4,128)}), f32[512,4,128]{2,1,0:T(4,128)}, u32[]{:S(2)}, u32[]{:S(2)}) async-start(f32[512,4,128]{2,1,0:T(4,128)} %get-tuple-element.19), calls=%async_computation.1 | async-start | bytes 2097152 | tf_op jit(solution)/shard_map/all_to_all | solution.py:31
  94.7 15.4 %copy-start.19 = (f32[8,64]{1,0:T(8,128)S(1)}, f32[8,64]{1,0:T(8,128)}, u32[]{:S(2)}) copy-start(f32[8,64]{1,0:T(8,128)} %get-tuple-element.21) | copy-start | bytes 6148
  97.3 13.8 %collective-permute-start.4 = (f32[8,160]{1,0:T(8,128)S(1)}, f32[8,160]{1,0:T(8,128)S(1)}, u32[]{:S(2)}, u32[]{:S(2)}) collective-permute-start(f32[8,160]{1,0:T(8,128)S(1)} %pad_maximum_fusion.10), channel_id=1, source_target_pairs={{0,1},{1,2},{2,3},{3,4},{4,5},{5,6},{6,7},{7,8},{8,9},{9,10},{10,1... | collective-permute-start | bytes 15368 | tf_op jit(solution)/shard_map/ppermute | solution.py:40
  98.7 11.4 %collective-permute-start.5 = (f32[8,128]{1,0:T(8,128)S(1)}, f32[8,128]{1,0:T(8,128)S(1)}, u32[]{:S(2)}, u32[]{:S(2)}) collective-permute-start(f32[8,128]{1,0:T(8,128)S(1)} %slice.399), channel_id=1, source_target_pairs={{0,127},{1,0},{2,1},{3,2},{4,3},{5,4},{6,5},{7,6},{8,7},{9,8},{10,... | collective-permute-start | bytes 12296 | tf_op jit(solution)/shard_map/ppermute | solution.py:40
  105.5 23.4 %all-to-all-start.2 = ((f32[512,4,128]{2,1,0:T(4,128)}), f32[512,4,128]{2,1,0:T(4,128)S(1)}, u32[]{:S(2)}, u32[]{:S(2)}) async-start(f32[512,4,128]{2,1,0:T(4,128)} %get-tuple-element.20), calls=%async_computation.2 | async-start | bytes 2097152 | tf_op jit(solution)/shard_map/all_to_all | solution.py:31
  112.4 16.5 %copy-start.9 = (f32[2,8,512]{2,1,0:T(8,128)}, f32[2,8,512]{2,1,0:T(8,128)S(1)}, u32[]{:S(2)}) copy-start(f32[2,8,512]{2,1,0:T(8,128)S(1)} %convolution_add_fusion.local_ref) | copy-start | bytes 98308
  128.9 1.0 copy-start.3
  134.2 34.2 %copy-start.12 = (f32[8,2,512]{2,1,0:T(2,128)S(1)}, f32[8,2,512]{2,1,0:T(2,128)}, u32[]{:S(2)}) copy-start(f32[8,2,512]{2,1,0:T(2,128)} %param.16) | copy-start | bytes 98308
  134.2 34.2 %copy-start.13 = (f32[8,2,512]{2,1,0:T(2,128)S(1)}, f32[8,2,512]{2,1,0:T(2,128)}, u32[]{:S(2)}) copy-start(f32[8,2,512]{2,1,0:T(2,128)} %param.14) | copy-start | bytes 98308
  134.2 34.2 %copy-start.14 = (f32[8,2,512]{2,1,0:T(2,128)S(1)}, f32[8,2,512]{2,1,0:T(2,128)}, u32[]{:S(2)}) copy-start(f32[8,2,512]{2,1,0:T(2,128)} %param.15) | copy-start | bytes 98308
  135.9 14.9 %all-to-all-start.3 = ((f32[128,2,128]{2,1,0:T(2,128)}), f32[128,2,128]{2,1,0:T(2,128)S(1)}, u32[]{:S(2)}, u32[]{:S(2)}) async-start(f32[128,2,128]{2,1,0:T(2,128)} %get-tuple-element.23), calls=%async_computation.3 | async-start | bytes 262144 | tf_op jit(solution)/shard_map/all_to_all | solution.py:31
  142.1 8.5 %collective-permute-start.6 = (f32[8,32]{1,0:T(8,128)S(1)}, f32[8,32]{1,0:T(8,128)S(1)}, u32[]{:S(2)}, u32[]{:S(2)}) collective-permute-start(f32[8,32]{1,0:T(8,128)S(1)} %slice.351), channel_id=1, source_target_pairs={{0,1},{1,2},{2,3},{3,4},{4,5},{5,6},{6,7},{7,8},{8,9},{9,10},{10,1... | collective-permute-start | bytes 3080 | tf_op jit(solution)/shard_map/ppermute | solution.py:40
  150.8 0.7 copy-start.8
  155.5 8.7 %all-to-all-start.4 = ((f32[8,8,384]{2,1,0:T(8,128)}), f32[8,8,384]{2,1,0:T(8,128)S(1)}, u32[]{:S(2)}, u32[]{:S(2)}) async-start(f32[8,8,384]{2,1,0:T(8,128)} %broadcast_in_dim.30), calls=%async_computation.4 | async-start | bytes 196608 | tf_op jit(solution)/shard_map/all_to_all | solution.py:31
  164.9 11.9 %all-to-all-start.5 = ((f32[16,8,384]{2,1,0:T(8,128)}), f32[16,8,384]{2,1,0:T(8,128)S(1)}, u32[]{:S(2)}, u32[]{:S(2)}) async-start(f32[16,8,384]{2,1,0:T(8,128)} %broadcast_in_dim.31), calls=%async_computation.5 | async-start | bytes 393216 | tf_op jit(solution)/shard_map/all_to_all | solution.py:31
  176.8 0.7 copy-start.5

commit v3 on v2

--- a/solution.py
+++ b/solution.py
@@ -59,6 +59,7 @@
         in_specs=ins,
         out_specs=[VMEM] * len(outs),
         scratch_shapes=list(scratch),
+        compiler_params=pltpu.CompilerParams(vmem_limit_bytes=16 << 20),
         cost_estimate=pl.CostEstimate(flops=flops, bytes_accessed=1 << 20, transcendentals=0),
     )
 
@@ -90,14 +91,14 @@
     return both[:, :HALF] + both[:, HALF:]
 
 
-def assemble_packed(got_ref, assembled_ref):
+def assemble_packed(got_ref, assembled_ref, slots):
     tiles = assembled_ref.shape[1] // LANES
     lane = lax.broadcasted_iota(jnp.int32, (4, LANES), 1)
     lower = lane < HALF
     for m in range(tiles):
-        even, odd = 8 * m, 8 * m + 4
-        following = 8 * ((m + 1) % tiles) + 2
-        previous = 8 * ((m - 1) % tiles) + 6
+        even, odd = 2 * slots * m, 2 * slots * m + slots
+        following = 2 * slots * ((m + 1) % tiles) + 2
+        previous = 2 * slots * ((m - 1) % tiles) + slots + 2
         extra_even, extra_odd = got_ref[following], got_ref[previous]
         top = got_ref[even] + got_ref[odd] + jnp.where(lower, extra_odd, extra_even)
         turned = pltpu.roll(jnp.where(lower, extra_even, extra_odd), HALF, 1)
@@ -124,34 +125,34 @@
     return jnp.where(even, tile[:, :HALF], tile[:, HALF:]) * z
 
 
-def send_blocks(z, coupling_ref, local_ref, riding, pieces_ref):
+def send_blocks(z, coupling_ref, local_ref, pieces_ref, slots, riding_ref=None):
     blocks = local_ref[...] + dot(z, coupling_ref[...], NN)
     main, extra = blocks[:, :LANES], blocks[:, LANES:]
     turned = pltpu.roll(extra, HALF, 1)
     packed = extra[0:4] + turned[4:8]
-    for d in range(pieces_ref.shape[0] // 4):
-        pieces_ref[4 * d] = main[0:4]
-        pieces_ref[4 * d + 1] = main[4:8]
-        pieces_ref[4 * d + 2] = packed
-        pieces_ref[4 * d + 3] = riding(d)
-
-
-def first_body(got_ref, parts_ref, coupling_ref, local_ref, square_ref, pieces_ref, z_ref, assembled_ref):
+    for d in range(pieces_ref.shape[0] // slots):
+        pieces_ref[slots * d] = main[0:4]
+        pieces_ref[slots * d + 1] = main[4:8]
+        pieces_ref[slots * d + 2] = packed
+        if riding_ref is not None:
+            pieces_ref[slots * d + 3] = riding_ref[d]
+
+
+def first_body(got_ref, parts_ref, coupling_ref, local_ref, pieces_ref, z_ref, assembled_ref):
     assemble_first(got_ref, assembled_ref)
     z = coarse_product(assembled_ref, parts_ref)
     z_ref[...] = z
-    send_blocks(z, coupling_ref, local_ref, lambda d: square_ref[d], pieces_ref)
-
-
-def second_body(device_ref, got_ref, parts_ref, coupling_ref, local_ref, pieces_ref, z_ref, terms_ref, assembled_ref):
-    assemble_packed(got_ref, assembled_ref)
+    send_blocks(z, coupling_ref, local_ref, pieces_ref, 3)
+
+
+def second_body(
+    device_ref, got_ref, parts_ref, coupling_ref, local_ref, square_ref, pieces_ref, z_ref, terms_ref, assembled_ref
+):
+    assemble_packed(got_ref, assembled_ref, 3)
     z = coarse_product(assembled_ref, parts_ref)
     z_ref[...] = z
     terms_ref[...] = owned_terms(device_ref, assembled_ref, z)
-    square = got_ref[3]
-    for d in range(1, got_ref.shape[0] // 4):
-        square = square + got_ref[4 * d + 3]
-    send_blocks(z, coupling_ref, local_ref, lambda d: square, pieces_ref)
+    send_blocks(z, coupling_ref, local_ref, pieces_ref, 4, square_ref)
 
 
 def choose_rows(select_ref, rows):
@@ -177,9 +178,12 @@
     device_ref, got_ref, parts_ref, local_ref, modes_a_ref, modes_b_ref, modes_c_ref, select_ref, sums_ref, early_ref,
     sent_ref, z_ref, assembled_ref,
 ):
-    assemble_packed(got_ref, assembled_ref)
+    assemble_packed(got_ref, assembled_ref, 4)
     z = coarse_product(assembled_ref, parts_ref)
     z_ref[...] = z
+    square = got_ref[3]
+    for d in range(1, got_ref.shape[0] // 4):
+        square = square + got_ref[4 * d + 3]
     y_0 = local_ref[0] + dot(z[:, :NC], modes_a_ref[...], NN)
     y_1 = local_ref[1] + dot(z, modes_b_ref[...], NN)
     y_2 = dot(z[:, NC:], modes_c_ref[...], NN)
@@ -193,12 +197,14 @@
     for k in range(4):
         placed = placed + jnp.where(lane == 96 + 8 * k + case, sums_ref[:, k : k + 1], 0.0)
     late = late + jnp.sum(placed, axis=0, keepdims=True)
-    sent_ref[:, 0, :] = early_ref[...]
-    sent_ref[:, 1, :] = late
+    sent_ref[:, 0, 0, :] = early_ref[...]
+    sent_ref[:, 0, 1, :] = late
+    sent_ref[:, 1] = jnp.broadcast_to(square[None, 0:2], (late.shape[0], 2, LANES))
+    sent_ref[:, 2] = jnp.broadcast_to(square[None, 2:4], (late.shape[0], 2, LANES))
 
 
 def project_body(got_ref, basis_ref, part_ref, rows_ref, gains_ref):
-    early, late = got_ref[:, 0, :], got_ref[:, 1, :]
+    early, late = got_ref[:, 0, 0, :], got_ref[:, 0, 1, :]
     sums = jnp.broadcast_to(jnp.sum(late, axis=0, keepdims=True), (8, LANES))
     lane = lax.broadcasted_iota(jnp.int32, (8, LANES), 1)
     bb, bf, ff, fff = (pltpu.roll(sums, 32 - 8 * k, 1) for k in range(4))
@@ -229,10 +235,10 @@
     both = jnp.concatenate([high, low], axis=0)
     count = snapshots.shape[1]
     product = fast(both, basis_ref[:count], NN) + fast(both, basis_ref[count:], NN)
-    part_ref[:, : basis_ref.shape[1]] = product[:8] + product[8:]
-    part_ref[:, basis_ref.shape[1] :] = dot(
-        snapshots, jnp.concatenate([snapshots, jnp.zeros((LANES - 8, count), f32)], axis=0), NT
-    )
+    gram = dot(snapshots, jnp.concatenate([snapshots, jnp.zeros((LANES - 8, count), f32)], axis=0), NT)
+    part = jnp.concatenate([product[:8] + product[8:], gram], axis=1)
+    for d in range(part_ref.shape[0]):
+        part_ref[d] = part
 
 
 def finish_body(got_ref, square_ref, basis_ref, rows_ref, columns_ref, projection_ref, factor_ref, *, scale):
@@ -244,7 +250,7 @@
     coefficients = reduced[:, :rank]
     projection_ref[...] = coefficients
     low_rows, high_rows = coefficients[:, :LANES], coefficients[:, LANES:]
-    squares = [square_ref[:, i, :] for i in range(4)]
+    squares = [square_ref[:, 1 + i // 2, i % 2, :] for i in range(4)]
     image = jnp.concatenate(
         [
             dot(low_rows, squares[0], NN) + dot(high_rows, squares[2], NN),
@@ -253,7 +259,6 @@
         axis=1,
     )
     gap = image - 2.0 * coefficients
-    gram = reduced[:, rank : rank + 8]
     blank = jnp.zeros((LANES - 8, rank), f32)
     gram = reduced[:, rank:] + dot(coefficients, jnp.concatenate([gap, blank], axis=0), NT)
     row = lax.broadcasted_iota(jnp.int32, (8, LANES), 0)
@@ -297,7 +302,7 @@
     basis_rows,
     piece_owner,
 ):
-    case_count, sub_count, unknowns = disp_now.shape
+    case_count, _, unknowns = disp_now.shape
     devices = lax.axis_size(AXES)
     coarse_total = coarse_inverse.shape[1]
     rank = basis_rows.shape[1]
@@ -306,9 +311,6 @@
     even = me % 2 == 0
     device = me.reshape(1).astype(jnp.int32)
 
-    right_modes = shifted(corner_modes, -1)
-    left_edge = shifted(corner_modes[1, :, last:], 1)
-
     right_side = load_next + inertia[None] * (
         disp_now + time_step * vel_now + (0.5 - newmark_beta) * time_step * time_step * acc_now
     )
@@ -321,17 +323,10 @@
         jnp.concatenate([gap, low, middle, high], axis=1),
     )
     got_1 = to_everyone(start)
+    right_modes = shifted(corner_modes, -1)
+    left_edge = shifted(corner_modes[1, :, last:], 1)
 
     (coarse_parts,) = call(split_body, [((4 * NC, coarse_total), bf16)], [VMEM], flops=1 << 22)(coarse_inverse)
-    basis_sorted = basis_rows.reshape(devices, -1, rank).swapaxes(0, 1).reshape(-1, rank)
-    (basis_parts,) = call(split_body, [((2 * basis_sorted.shape[0], rank), bf16)], [VMEM], flops=1 << 22)(basis_sorted)
-    square = lax.dot_general(basis_rows, basis_rows, (((0,), (0,)), ((), ())), precision=highest)
-    square = jnp.stack(
-        [square[:LANES, :LANES], square[:LANES, LANES:], square[LANES:, :LANES], square[LANES:, LANES:]], axis=1
-    )
-    owner = jnp.broadcast_to(piece_owner[:, None], (devices, unknowns // devices)).reshape(1, unknowns)
-    select = (owner == lax.broadcasted_iota(jnp.int32, (devices, unknowns), 0)).astype(bf16)
-
     zero = jnp.zeros((NC, NI), f32)
     first, final = corner_modes[:, :, :NI], corner_modes[:, :, last:]
     right_first, right_final = right_modes[:, :, :NI], right_modes[:, :, last:]
@@ -387,17 +382,26 @@
 
     local_0 = ein("cjb,jab->jca", right_side, rr_inverse)
     assembled = [pltpu.VMEM((case_count, coarse_total), f32)]
-    piece_shape = ((4 * devices, 4, LANES),)
     z_shape = ((case_count, 2 * NC),)
-    pieces, z_0 = call(first_body, [piece_shape, z_shape], [VMEM] * 5, assembled, flops=1 << 24)(
-        got_1, coarse_parts, coupling, local_blocks(local_0), square
+    pieces, z_0 = call(first_body, [((3 * devices, 4, LANES),), z_shape], [VMEM] * 4, assembled, flops=1 << 24)(
+        got_1, coarse_parts, coupling, local_blocks(local_0)
     )
     got_2 = exchange(pieces)
     green, b_a, b_b, b_c = finish(local_0, z_0)
+    b_b, basis_rows, piece_owner = lax.optimization_barrier((b_b, basis_rows, piece_owner))
+    basis_sorted = basis_rows.reshape(devices, -1, rank).swapaxes(0, 1).reshape(-1, rank)
+    (basis_parts,) = call(split_body, [((2 * basis_sorted.shape[0], rank), bf16)], [VMEM], flops=1 << 22)(basis_sorted)
+    square = lax.dot_general(basis_rows, basis_rows, (((0,), (0,)), ((), ())), precision=highest)
+    square = jnp.stack(
+        [square[:LANES, :LANES], square[:LANES, LANES:], square[LANES:, :LANES], square[LANES:, LANES:]], axis=1
+    )
+    owner = jnp.broadcast_to(piece_owner[:, None], (devices, unknowns // devices)).reshape(1, unknowns)
+    select = (owner == lax.broadcasted_iota(jnp.int32, (devices, unknowns), 0)).astype(bf16)
+
     local_1, inner_1 = local_apply(b_a, b_b, b_c)
-    pieces, z_1, terms_1 = call(second_body, [piece_shape, z_shape, z_shape], [SMEM] + [VMEM] * 4, assembled, flops=1 << 24)(
-        device, got_2, coarse_parts, coupling, local_blocks(local_1)
-    )
+    pieces, z_1, terms_1 = call(
+        second_body, [((4 * devices, 4, LANES),), z_shape, z_shape], [SMEM] + [VMEM] * 5, assembled, flops=1 << 24
+    )(device, got_2, coarse_parts, coupling, local_blocks(local_1), square)
     got_3 = exchange(pieces)
     image_1, v_a, v_b, v_c = finish(local_1, z_1)
     local_2, inner_2 = local_apply(v_a, v_b, v_c)
@@ -411,27 +415,30 @@
         axis=1,
     )
     (early,) = call(early_body, [((devices, LANES),)], [VMEM] * 3, flops=1 << 24)(select, green, image_1)
-    sent, z_2 = call(third_body, [((devices, 2, LANES),), z_shape], [SMEM] + [VMEM] * 9, assembled, flops=1 << 24)(
+    sent, z_2 = call(third_body, [((devices, 3, 2, LANES),), z_shape], [SMEM] + [VMEM] * 9, assembled, flops=1 << 24)(
         device, got_3, coarse_parts, local_2, corner_modes[0, NC:], corner_modes[1], right_modes[0, :NC], select, sums, early
     )
     got_4 = exchange(sent)
     ghost = shifted(z_2[:, NC:], 1)
     part, snapshots, gains = call(
         project_body,
-        [((case_count, rank + LANES),), ((case_count, basis_rows.shape[0]),), ((2, case_count, LANES),)],
+        [
+            ((lax.axis_size(NEAR), case_count, rank + LANES),),
+            ((case_count, basis_rows.shape[0]),),
+            ((2, case_count, LANES),),
+        ],
         [VMEM] * 2,
         flops=1 << 24,
     )(got_4, basis_parts)
-    near = to_everyone(part, NEAR).sum(axis=0)
+    near = exchange(part, NEAR).sum(axis=0)
     got_5 = to_everyone(near, FAR)
-    squares = got_3.reshape(devices, 4, 4, LANES)[:, 3]
     scale = math.sqrt(basis_rows.shape[0] * devices)
     new_columns, projection, factor = call(
         functools.partial(finish_body, scale=scale),
         [((case_count, basis_rows.shape[0]),), ((case_count, rank),), ((case_count, LANES),)],
         [VMEM] * 4,
         flops=1 << 24,
-    )(got_5, squares, basis_parts, snapshots)
+    )(got_5, got_4, basis_parts, snapshots)
 
     kappa_1, kappa_2 = gains[0, 0, :case_count, None], gains[1, 0, :case_count, None]
     image_2 = jnp.stack(
@@ -467,6 +474,7 @@
         P(AXES, None),
         P(),
     )
+
     return jax.shard_map(
         shards,
         mesh=finer,

time: 183 us -> 154 us (0.84)
  Pallas kernels: 26.2 us -> 12 us
  waiting for transfers between devices: 45.3 us -> 37 us
  starting transfers between devices: 59.1 us -> 54.5 us
  other arithmetic: 11.4 us -> 8.36 us
    all_to_all x6, waiting for transfers between devices: 38.5 us -> 29.3 us  [exchange(): return lax.all_to_all(pieces, axes, split_axis=0, concat_axis=0, tiled=True)]
    pallas_call x4, Pallas kernels: 14.7 us -> 8.63 us  [the longest x1 2.97 us: shards(): call(third_body, [((devices, 3, 2, LANES),), z_shape], [SMEM] + [VMEM] *...]
    unnamed x55 -> x85, local copies, waits for them, and re-layouts: 3.72 us -> 9.45 us
    ppermute x7, starting transfers between devices: 23.5 us -> 18.6 us  [shifted(): lax.ppermute(array, AXES, [(i, (i + by) % count) for i in range(count)])]
    another operation x3, local copies, waits for them, and re-layouts: 0.25 us -> 3.27 us  [shards(): jnp.stack([jnp.sum(b_b * b_b + b_c * b_c, axis=1), inner_1 + jnp.sum(term...]
    pallas_call x1, Pallas kernels: 3.26 us -> 0.33 us  [shards(): call(split_body, [((4 * NC, coarse_total), bf16)], [VMEM], flops=1 << 22)]
    dot_general x14, matrix products: 11.1 us -> 8.24 us  [dot(): lax.dot_general(a, b, dims, precision=highest, preferred_element_type=f32)]
    pallas_call x1, Pallas kernels: 2.39 us -> 0.14 us  [shards(): call(split_body, [((2 * basis_sorted.shape[0], rank), bf16)], [VMEM], flo...]
  transfers between devices with their start and end apart: 13 -> 13, of which waited for: 5 -> 6; matrix products, arithmetic and copies ran while one was open for 21% -> 24% of each run, Pallas kernels for 4% -> 0%
where the time goes in v3:
time: 154 us; the launch traced here: 152 us
  starting transfers between devices  54.5 us (35%)
  waiting for transfers between devices  37 us (24%)
  local copies, waits for them, and re-layouts  20 us (13%)
  matrix products  19 us (12%)
  Pallas kernels  12 us (8%)
  other arithmetic  8.36 us (5%)
    all_to_all x6, starting transfers between devices, exchange(): return lax.all_to_all(pieces, axes, split_axis=0, concat_axis=0, tiled=True)  35.9 us
    all_to_all x6, waiting for transfers between devices, exchange(): return lax.all_to_all(pieces, axes, split_axis=0, concat_axis=0, tiled=True)  29.3 us
    ppermute x7, starting transfers between devices, shifted(): lax.ppermute(array, AXES, [(i, (i + by) % count) for i in range(count)])  18.6 us
    unnamed x85, local copies, waits for them, and re-layouts  9.45 us
    dot_general x14, matrix products, dot(): lax.dot_general(a, b, dims, precision=highest, preferred_element_type=f32)  8.24 us
    ppermute x7, waiting for transfers between devices, shifted(): lax.ppermute(array, AXES, [(i, (i + by) % count) for i in range(count)])  7.7 us
    dot_general x6, matrix products, ein(): return jnp.einsum(spec, *operands, precision=highest)  7.26 us
    dot_general x1, matrix products, shards(): lax.dot_general(basis_rows, basis_rows, (((0,), (0,)), ((), ())), precisi...  3.49 us
  transfers between devices with their start and end apart: 13, of which 6 were waited for; matrix products, arithmetic and copies ran while one was open for 24% of the time, Pallas kernels for 0%

profile of v3, /device:TPU:0, one launch (start us, length us, event | category | flops | bytes accessed | tf_op | source)
XLA Modules:
  0.0 152.2 jit_solution(12885654215261498692)
XLA Ops:
  0.7 8.3 %collective-permute-start = (f32[2,64,512]{2,1,0:T(8,128)}, f32[2,64,512]{2,1,0:T(8,128)S(1)}, u32[]{:S(2)}, u32[]{:S(2)}) collective-permute-start(f32[2,64,512]{2,1,0:T(8,128)} %param.11), channel_id=1, source_target_pairs={{0,127},{1,0},{2,1},{3,2},{4,3},{5,4},{6,5},{7,6},{8,7},{9,8},{10,... | collective-permute-start | bytes 786440 | tf_op jit(solution)/shard_map/ppermute | solution.py:40
  9.0 0.8 slice_bitcast_fusion.3
  9.8 0.8 multiply_add_fusion
  10.6 1.3 fusion.42
  12.0 0.9 broadcast_in_dim.23
  12.9 9.1 %all-to-all-start = ((f32[128,8,128]{2,1,0:T(8,128)}), f32[128,8,128]{2,1,0:T(8,128)S(1)}, u32[]{:S(2)}, u32[]{:S(2)}) async-start(f32[128,8,128]{2,1,0:T(8,128)} %broadcast_in_dim.23), calls=%async_computation | async-start | bytes 1048576 | tf_op jit(solution)/shard_map/all_to_all | solution.py:31
  22.1 1.8 %fusion.44 = f32[2,8,512]{2,1,0:T(8,128)S(1)} fusion(f32[2,512,512]{2,1,0:T(8,128)S(1)} %copy-done.16, f32[8,2,512]{2,1,0:T(2,128)S(1)} %multiply_add_fusion), kind=kOutput, calls=%fused_computation.84 | convolution fusion | flops 50331648 | bytes 2162688 | tf_op jit(solution)/shard_map/cjb,jab->jca/dot_general | solution.py:44
  24.0 1.6 %copy-done = f32[64,8192]{1,0:T(8,128)S(1)} copy-done((f32[64,8192]{1,0:T(8,128)S(1)}, f32[64,8192]{1,0:T(8,128)}, u32[]{:S(2)}) %copy-start) | copy-done | bytes 2097176
  27.7 7.5 %all-to-all-done.got_ref = f32[128,8,128]{2,1,0:T(8,128)S(1)} async-done(((f32[128,8,128]{2,1,0:T(8,128)}), f32[128,8,128]{2,1,0:T(8,128)S(1)}, u32[]{:S(2)}, u32[]{:S(2)}) %all-to-all-start) | async-done | bytes 524320 | tf_op jit(solution)/shard_map/all_to_all | solution.py:31
  35.2 1.9 %shard_map.138 = (f32[384,4,128]{2,1,0:T(4,128)}, f32[8,64]{1,0:T(8,128)S(1)}) custom-call(f32[128,8,128]{2,1,0:T(8,128)S(1)} %all-to-all-done.got_ref, bf16[128,8192]{1,0:T(8,128)(2,1)S(1)} %shard_map.137.parts_ref, f32[64,256]{1,0:T(8,128)S(1)} %fusion.11.coupling_ref, f32[8,256]{1,0:T(8,128)S(1)} %fusion.49.local_ref), custom_call_target="tpu_custom_call" | custom-call | flops 16777216 | bytes 1048576 | tf_op jit(solution)/shard_map/pallas_call | solution.py:386
  37.5 1.4 collective-permute-start.3
  39.6 9.1 %all-to-all-start.1 = ((f32[384,4,128]{2,1,0:T(4,128)}), f32[384,4,128]{2,1,0:T(4,128)}, u32[]{:S(2)}, u32[]{:S(2)}) async-start(f32[384,4,128]{2,1,0:T(4,128)} %get-tuple-element.22), calls=%async_computation.1 | async-start | bytes 1572864 | tf_op jit(solution)/shard_map/all_to_all | solution.py:31
  49.1 3.5 %fusion.95 = f32[256,256]{1,0:T(8,128)S(1)} fusion(f32[1024,256]{1,0:T(8,128)} %param.18), kind=kOutput, calls=%fused_computation.184 | convolution fusion | flops 805306368 | bytes 1310720 | tf_op jit(solution)/shard_map/dot_general | solution.py:394
  54.3 1.7 %copy.35 = f32[128,8,256]{2,0,1:T(8,128)S(1)} copy(f32[128,8,256]{2,1,0:T(8,128)} %bitcast.147) | data formatting | bytes 2097152 | tf_op jit(solution)/shard_map/reshape | solution.py:392
  59.4 4.8 %all-to-all-done.1.got_ref = f32[384,4,128]{2,1,0:T(4,128)} async-done(((f32[384,4,128]{2,1,0:T(4,128)}), f32[384,4,128]{2,1,0:T(4,128)}, u32[]{:S(2)}, u32[]{:S(2)}) %all-to-all-start.1) | async-done | bytes 786464 | tf_op jit(solution)/shard_map/all_to_all | solution.py:31
  64.2 0.8 copy-done.9
  65.0 2.3 %shard_map.139 = (f32[512,4,128]{2,1,0:T(4,128)S(1)}, f32[8,64]{1,0:T(8,128)S(1)}, f32[8,64]{1,0:T(8,128)S(1)}) custom-call(s32[1]{0:T(128)} %bitcast.27.device_ref, f32[384,4,128]{2,1,0:T(4,128)} %all-to-all-done.1.got_ref, bf16[128,8192]{1,0:T(8,128)(2,1)S(1)} %shard_map.137.parts_ref, f32[64,256]{1,0:T(8,128)S(1)} %copy-done.9, ...), custom_call_target="tpu_custom_call" | custom-call | flops 16777216 | bytes 1048576 | tf_op jit(solution)/shard_map/pallas_call | solution.py:402
  67.3 1.0 copy-done.1
  68.6 0.8 convolution_add_fusion.6
  71.4 6.6 %collective-permute-start.5 = (f32[8,128]{1,0:T(8,128)S(1)}, f32[8,128]{1,0:T(8,128)}, u32[]{:S(2)}, u32[]{:S(2)}) collective-permute-start(f32[8,128]{1,0:T(8,128)S(1)} %slice.395), channel_id=1, source_target_pairs={{0,127},{1,0},{2,1},{3,2},{4,3},{5,4},{6,5},{7,6},{8,7},{9,8},{10,... | collective-permute-start | bytes 12296 | tf_op jit(solution)/shard_map/ppermute | solution.py:40
  78.0 1.2 add_bitcast_fusion
  79.2 1.3 copy.32
  80.5 5.8 %all-to-all-start.2 = ((f32[512,4,128]{2,1,0:T(4,128)}), f32[512,4,128]{2,1,0:T(4,128)}, u32[]{:S(2)}, u32[]{:S(2)}) async-start(f32[512,4,128]{2,1,0:T(4,128)} %copy-done.1), calls=%async_computation.2 | async-start | bytes 2097152 | tf_op jit(solution)/shard_map/all_to_all | solution.py:31
  86.3 0.9 fusion.2
  87.3 1.0 convolution_add_fusion.5
  88.3 1.3 add_reduce_fusion
  89.6 1.6 %fusion.6 = f32[2,8,512]{2,1,0:T(8,128)S(1)} fusion(f32[2,512,512]{2,1,0:T(8,128)} %param.10, f32[1,8,128]{2,1,0:T(8,128)S(1)} %get-tuple-element.76, f32[1,8,128]{2,1,0:T(8,128)S(1)} %get-tuple-element.84), kind=kOutput, calls=%fused_computation.19 | convolution fusion | flops 12584960 | bytes 565248 | tf_op jit(solution)/shard_map/jcb,jab->jca/dot_general | solution.py:44
  91.2 1.6 %convolution_add_fusion.local_ref = f32[2,8,512]{2,1,0:T(8,128)S(1)} fusion(f32[2,8,512]{2,1,0:T(8,128)S(1)} %fusion.6, f32[2,512,512]{2,1,0:T(8,128)} %param.10, f32[1,8,128]{2,1,0:T(8,128)S(1)} %bitcast.164, f32[1,8,128]{2,1,0:T(8,128)S(1)} %get-tuple-element.75), kind=kOutput, calls=%fused_computation | convolution fusion | flops 12593152 | bytes 598016 | tf_op jit(solution)/shard_map/jcb,jab->jca/dot_general | solution.py:44
  94.0 1.3 copy.34
  95.3 1.3 copy.33
  97.3 0.8 copy-done.15
  99.0 0.8 pad_maximum_fusion.17.sums_ref
  99.8 4.9 %all-to-all-done.2.got_ref = f32[512,4,128]{2,1,0:T(4,128)} async-done(((f32[512,4,128]{2,1,0:T(4,128)}), f32[512,4,128]{2,1,0:T(4,128)}, u32[]{:S(2)}, u32[]{:S(2)}) %all-to-all-start.2) | async-done | bytes 1048608 | tf_op jit(solution)/shard_map/all_to_all | solution.py:31
  105.5 0.8 copy-done.14
  106.3 3.0 %shard_map.141 = (f32[128,3,2,128]{3,2,1,0:T(2,128)S(1)}, f32[8,64]{1,0:T(8,128)S(1)}) custom-call(s32[1]{0:T(128)} %bitcast.27.device_ref, f32[512,4,128]{2,1,0:T(4,128)} %all-to-all-done.2.got_ref, bf16[128,8192]{1,0:T(8,128)(2,1)S(1)} %shard_map.137.parts_ref, f32[2,8,512]{2,1,0:T(8,128)S(1)} %copy-done.11, f32[32,512]{1,0:T(8,128)S(1)} %copy-done.5, ...), custom_call_target="tpu_custom_call" | custom-call | flops 16777216 | bytes 1048576 | tf_op jit(solution)/shard_map/pallas_call | solution.py:418
  109.3 0.8 copy-done.12
  110.1 4.8 %all-to-all-start.3 = ((f32[128,3,2,128]{3,2,1,0:T(2,128)}), f32[128,3,2,128]{3,2,1,0:T(2,128)S(1)}, u32[]{:S(2)}, u32[]{:S(2)}) async-start(f32[128,3,2,128]{3,2,1,0:T(2,128)} %copy-done.12), calls=%async_computation.3 | async-start | bytes 786432 | tf_op jit(solution)/shard_map/all_to_all | solution.py:31
  115.0 1.0 collective-permute-start.6
  115.9 1.0 convolution_add_fusion.4
  116.9 1.1 fusion
  118.0 7.7 %collective-permute-done.6 = f32[8,32]{1,0:T(8,128)S(1)} collective-permute-done((f32[8,32]{1,0:T(8,128)S(1)}, f32[8,32]{1,0:T(8,128)S(1)}, u32[]{:S(2)}, u32[]{:S(2)}) %collective-permute-start.6) | collective-permute-done | bytes 1056 | tf_op jit(solution)/shard_map/ppermute | solution.py:40
  125.7 1.0 fusion.1
  126.7 1.4 shard_map.143
  128.2 3.4 %all-to-all-start.4 = ((f32[8,8,384]{2,1,0:T(8,128)}), f32[8,8,384]{2,1,0:T(8,128)S(1)}, u32[]{:S(2)}, u32[]{:S(2)}) async-start(f32[8,8,384]{2,1,0:T(8,128)} %get-tuple-element.32), calls=%async_computation.4 | async-start | bytes 196608 | tf_op jit(solution)/shard_map/all_to_all | solution.py:31
  131.5 5.3 %all-to-all-done.4 = f32[8,8,384]{2,1,0:T(8,128)S(1)} async-done(((f32[8,8,384]{2,1,0:T(8,128)}), f32[8,8,384]{2,1,0:T(8,128)S(1)}, u32[]{:S(2)}, u32[]{:S(2)}) %all-to-all-start.4) | async-done | bytes 98336 | tf_op jit(solution)/shard_map/all_to_all | solution.py:31
  137.6 3.8 %all-to-all-start.5 = ((f32[16,8,384]{2,1,0:T(8,128)}), f32[16,8,384]{2,1,0:T(8,128)S(1)}, u32[]{:S(2)}, u32[]{:S(2)}) async-start(f32[16,8,384]{2,1,0:T(8,128)} %broadcast_in_dim.27), calls=%async_computation.5 | async-start | bytes 393216 | tf_op jit(solution)/shard_map/all_to_all | solution.py:31
  142.8 6.8 %all-to-all-done.5.got_ref = f32[16,8,384]{2,1,0:T(8,128)S(1)} async-done(((f32[16,8,384]{2,1,0:T(8,128)}), f32[16,8,384]{2,1,0:T(8,128)S(1)}, u32[]{:S(2)}, u32[]{:S(2)}) %all-to-all-start.5) | async-done | bytes 196640 | tf_op jit(solution)/shard_map/all_to_all | solution.py:31
  149.6 2.6 %shard_map.144 = (f32[8,1024]{1,0:T(8,128)}, f32[8,256]{1,0:T(8,128)}, f32[8,128]{1,0:T(8,128)}) custom-call(f32[16,8,384]{2,1,0:T(8,128)S(1)} %all-to-all-done.5.got_ref, f32[128,3,2,128]{3,2,1,0:T(2,128)S(1)} %all-to-all-done.3.got_ref.square_ref, bf16[2048,256]{1,0:T(8,128)(2,1)S(1)} %shard_map.142.basis_ref, f32[8,1024]{1,0:T(8,128)S(1)} %get-tuple-element.33.rows_ref), custom_call_target="tpu_custom_call" | custom-call | flops 16777216 | bytes 1048576 | tf_op jit(solution)/shard_map/pallas_call | solution.py:436
  (151 shorter events, 16.7 us)
Async XLA Ops:
  0.6 21.4 %copy-start.20 = (f32[2,64,512]{2,1,0:T(8,128)S(1)}, f32[2,64,512]{2,1,0:T(8,128)}, u32[]{:S(2)}) copy-start(f32[2,64,512]{2,1,0:T(8,128)} %param.11) | copy-start | bytes 786436
  0.6 21.4 %copy-start.16 = (f32[2,512,512]{2,1,0:T(8,128)S(1)}, f32[2,512,512]{2,1,0:T(8,128)}, u32[]{:S(2)}) copy-start(f32[2,512,512]{2,1,0:T(8,128)} %param.10) | copy-start | bytes 6291460
  0.7 25.3 %collective-permute-start = (f32[2,64,512]{2,1,0:T(8,128)}, f32[2,64,512]{2,1,0:T(8,128)S(1)}, u32[]{:S(2)}, u32[]{:S(2)}) collective-permute-start(f32[2,64,512]{2,1,0:T(8,128)} %param.11), channel_id=1, source_target_pairs={{0,127},{1,0},{2,1},{3,2},{4,3},{5,4},{6,5},{7,6},{8,7},{9,8},{10,... | collective-permute-start | bytes 786440 | tf_op jit(solution)/shard_map/ppermute | solution.py:40
  9.8 16.1 %collective-permute-start.1 = (f32[64,128]{1,0:T(8,128)S(1)}, f32[64,128]{1,0:T(8,128)S(1)}, u32[]{:S(2)}, u32[]{:S(2)}) collective-permute-start(f32[64,128]{1,0:T(8,128)S(1)} %slice_bitcast_fusion.3), channel_id=1, source_target_pairs={{0,1},{1,2},{2,3},{3,4},{4,5},{5,6},{6,7},{7,8},{8,9},{9,10},{10,1... | collective-permute-start | bytes 98312 | tf_op jit(solution)/shard_map/ppermute | solution.py:40
  12.9 22.3 %all-to-all-start = ((f32[128,8,128]{2,1,0:T(8,128)}), f32[128,8,128]{2,1,0:T(8,128)S(1)}, u32[]{:S(2)}, u32[]{:S(2)}) async-start(f32[128,8,128]{2,1,0:T(8,128)} %broadcast_in_dim.23), calls=%async_computation | async-start | bytes 1048576 | tf_op jit(solution)/shard_map/all_to_all | solution.py:31
  22.0 4.2 %copy-start.2 = (f32[64,512]{1,0:T(8,128)}, f32[64,512]{1,0:T(8,128)S(1)}, u32[]{:S(2)}) copy-start(f32[64,512]{1,0:T(8,128)S(1)} %slice_bitcast_fusion.modes_b_ref) | copy-start | bytes 393220
  22.1 4.2 %copy-start.4 = (f32[32,512]{1,0:T(8,128)}, f32[32,512]{1,0:T(8,128)S(1)}, u32[]{:S(2)}) copy-start(f32[32,512]{1,0:T(8,128)S(1)} %slice_bitcast_fusion.2.modes_a_ref) | copy-start | bytes 196612
  24.0 1.6 %copy-start = (f32[64,8192]{1,0:T(8,128)S(1)}, f32[64,8192]{1,0:T(8,128)}, u32[]{:S(2)}) copy-start(f32[64,8192]{1,0:T(8,128)} %matrix_ref.1) | copy-start | bytes 6291460
  25.9 22.8 %copy-start.35 = (f32[2,64,512]{2,1,0:T(8,128)}, f32[2,64,512]{2,1,0:T(8,128)S(1)}, u32[]{:S(2)}) copy-start(f32[2,64,512]{2,1,0:T(8,128)S(1)} %collective-permute-done) | copy-start | bytes 786436
  26.2 0.8 copy-start.18
  26.3 0.8 copy-start.6
  27.7 12.0 %copy-start.8 = (f32[64,256]{1,0:T(8,128)}, f32[64,256]{1,0:T(8,128)S(1)}, u32[]{:S(2)}) copy-start(f32[64,256]{1,0:T(8,128)S(1)} %fusion.11.coupling_ref) | copy-start | bytes 196612
  37.3 19.4 %copy-start.27 = (f32[8,512]{1,0:T(8,128)}, f32[8,512]{1,0:T(8,128)S(1)}, u32[]{:S(2)}) copy-start(f32[8,512]{1,0:T(8,128)S(1)} %convolution_add_fusion.9) | copy-start | bytes 49156
  37.5 11.2 %collective-permute-start.3 = (f32[8,128]{1,0:T(8,128)S(1)}, f32[8,128]{1,0:T(8,128)S(1)}, u32[]{:S(2)}, u32[]{:S(2)}) collective-permute-start(f32[8,128]{1,0:T(8,128)S(1)} %slice.378), channel_id=1, source_target_pairs={{0,127},{1,0},{2,1},{3,2},{4,3},{5,4},{6,5},{7,6},{8,7},{9,8},{10,... | collective-permute-start | bytes 12296 | tf_op jit(solution)/shard_map/ppermute | solution.py:40
  39.0 10.0 %collective-permute-start.2 = (f32[8,160]{1,0:T(8,128)S(1)}, f32[8,160]{1,0:T(8,128)S(1)}, u32[]{:S(2)}, u32[]{:S(2)}) collective-permute-start(f32[8,160]{1,0:T(8,128)S(1)} %pad_maximum_fusion.7), channel_id=1, source_target_pairs={{0,1},{1,2},{2,3},{3,4},{4,5},{5,6},{6,7},{7,8},{8,9},{9,10},{10,1... | collective-permute-start | bytes 15368 | tf_op jit(solution)/shard_map/ppermute | solution.py:40
  39.6 13.7 %copy-start.39 = (s32[128]{0:T(128)S(1)}, s32[128]{0:T(128)}, u32[]{:S(2)}) copy-start(s32[128]{0:T(128)} %param.19) | copy-start | bytes 1540
  39.6 24.5 %all-to-all-start.1 = ((f32[384,4,128]{2,1,0:T(4,128)}), f32[384,4,128]{2,1,0:T(4,128)}, u32[]{:S(2)}, u32[]{:S(2)}) async-start(f32[384,4,128]{2,1,0:T(4,128)} %get-tuple-element.22), calls=%async_computation.1 | async-start | bytes 1572864 | tf_op jit(solution)/shard_map/all_to_all | solution.py:31
  49.1 7.6 %copy-start.31 = (f32[8,512]{1,0:T(8,128)}, f32[8,512]{1,0:T(8,128)S(1)}, u32[]{:S(2)}) copy-start(f32[8,512]{1,0:T(8,128)S(1)} %convolution_add_fusion.8) | copy-start | bytes 49156
  54.3 1.9 %copy-start.17 = (f32[2,512,512]{2,1,0:T(8,128)S(1)}, f32[2,512,512]{2,1,0:T(8,128)}, u32[]{:S(2)}) copy-start(f32[2,512,512]{2,1,0:T(8,128)} %param.10) | copy-start | bytes 6291460
  56.0 1.9 %copy-start.24 = (f32[128,128]{1,0:T(8,128)S(1)}, f32[128,128]{1,0:T(8,128)}, u32[]{:S(2)}) copy-start(f32[128,128]{1,0:T(8,128)} %get-tuple-element.50) | copy-start | bytes 196612
  56.0 1.9 %copy-start.25 = (f32[128,128]{1,0:T(8,128)S(1)}, f32[128,128]{1,0:T(8,128)}, u32[]{:S(2)}) copy-start(f32[128,128]{1,0:T(8,128)} %get-tuple-element.51) | copy-start | bytes 196612
  56.0 1.9 %copy-start.26 = (f32[128,128]{1,0:T(8,128)S(1)}, f32[128,128]{1,0:T(8,128)}, u32[]{:S(2)}) copy-start(f32[128,128]{1,0:T(8,128)} %get-tuple-element.52) | copy-start | bytes 196612
  56.0 2.8 %copy-start.19 = (f32[256,512]{1,0:T(8,128)S(1)}, f32[256,512]{1,0:T(8,128)}, u32[]{:S(2)}) copy-start(f32[256,512]{1,0:T(8,128)} %copy-done.18) | copy-start | bytes 1572868
  57.9 0.9 copy-start.22
  64.2 0.8 copy-start.9
  65.0 3.3 %copy-start.21 = (f32[2,64,512]{2,1,0:T(8,128)S(1)}, f32[2,64,512]{2,1,0:T(8,128)}, u32[]{:S(2)}) copy-start(f32[2,64,512]{2,1,0:T(8,128)} %param.11) | copy-start | bytes 786436
  65.0 3.3 %copy-start.23 = (f32[2,8,512]{2,1,0:T(8,128)S(1)}, f32[2,8,512]{2,1,0:T(8,128)}, u32[]{:S(2)}) copy-start(f32[2,8,512]{2,1,0:T(8,128)} %copy-done.22) | copy-start | bytes 98308
  67.3 1.0 copy-start.1
  68.3 36.4 %copy-start.3 = (f32[64,512]{1,0:T(8,128)S(1)}, f32[64,512]{1,0:T(8,128)}, u32[]{:S(2)}) copy-start(f32[64,512]{1,0:T(8,128)} %copy-done.2) | copy-start | bytes 393220
  68.3 36.4 %copy-start.5 = (f32[32,512]{1,0:T(8,128)S(1)}, f32[32,512]{1,0:T(8,128)}, u32[]{:S(2)}) copy-start(f32[32,512]{1,0:T(8,128)} %copy-done.4) | copy-start | bytes 196612
  68.3 36.4 %copy-start.7 = (f32[32,512]{1,0:T(8,128)S(1)}, f32[32,512]{1,0:T(8,128)}, u32[]{:S(2)}) copy-start(f32[32,512]{1,0:T(8,128)} %copy-done.6) | copy-start | bytes 196612
  68.5 0.8 copy-start.29
  69.4 17.8 %collective-permute-start.4 = (f32[8,160]{1,0:T(8,128)S(1)}, f32[8,160]{1,0:T(8,128)}, u32[]{:S(2)}, u32[]{:S(2)}) collective-permute-start(f32[8,160]{1,0:T(8,128)S(1)} %pad_maximum_fusion.10), channel_id=1, source_target_pairs={{0,1},{1,2},{2,3},{3,4},{4,5},{5,6},{6,7},{7,8},{8,9},{9,10},{10,1... | collective-permute-start | bytes 15368 | tf_op jit(solution)/shard_map/ppermute | solution.py:40
  71.4 14.9 %collective-permute-start.5 = (f32[8,128]{1,0:T(8,128)S(1)}, f32[8,128]{1,0:T(8,128)}, u32[]{:S(2)}, u32[]{:S(2)}) collective-permute-start(f32[8,128]{1,0:T(8,128)S(1)} %slice.395), channel_id=1, source_target_pairs={{0,127},{1,0},{2,1},{3,2},{4,3},{5,4},{6,5},{7,6},{8,7},{9,8},{10,... | collective-permute-start | bytes 12296 | tf_op jit(solution)/shard_map/ppermute | solution.py:40
  80.5 24.1 %all-to-all-start.2 = ((f32[512,4,128]{2,1,0:T(4,128)}), f32[512,4,128]{2,1,0:T(4,128)}, u32[]{:S(2)}, u32[]{:S(2)}) async-start(f32[512,4,128]{2,1,0:T(4,128)} %copy-done.1), calls=%async_computation.2 | async-start | bytes 2097152 | tf_op jit(solution)/shard_map/all_to_all | solution.py:31
  88.3 9.1 %copy-start.33 = (f32[8,512]{1,0:T(8,128)}, f32[8,512]{1,0:T(8,128)S(1)}, u32[]{:S(2)}) copy-start(f32[8,512]{1,0:T(8,128)S(1)} %convolution_add_fusion.5) | copy-start | bytes 49156
  105.5 0.8 copy-start.14
  110.0 31.3 %copy-start.28 = (f32[8,512]{1,0:T(8,128)S(1)}, f32[8,512]{1,0:T(8,128)}, u32[]{:S(2)}) copy-start(f32[8,512]{1,0:T(8,128)} %copy-done.27) | copy-start | bytes 49156
  110.0 31.3 %copy-start.30 = (f32[8,512]{1,0:T(8,128)S(1)}, f32[8,512]{1,0:T(8,128)}, u32[]{:S(2)}) copy-start(f32[8,512]{1,0:T(8,128)} %copy-done.29) | copy-start | bytes 49156
  110.0 31.3 %copy-start.32 = (f32[8,512]{1,0:T(8,128)S(1)}, f32[8,512]{1,0:T(8,128)}, u32[]{:S(2)}) copy-start(f32[8,512]{1,0:T(8,128)} %copy-done.31) | copy-start | bytes 49156
  110.0 31.3 %copy-start.34 = (f32[8,512]{1,0:T(8,128)S(1)}, f32[8,512]{1,0:T(8,128)}, u32[]{:S(2)}) copy-start(f32[8,512]{1,0:T(8,128)} %copy-done.33) | copy-start | bytes 49156
  110.1 31.3 %copy-start.36 = (f32[8,2,512]{2,1,0:T(2,128)S(1)}, f32[8,2,512]{2,1,0:T(2,128)}, u32[]{:S(2)}) copy-start(f32[8,2,512]{2,1,0:T(2,128)} %param.16) | copy-start | bytes 98308
  110.1 31.3 %copy-start.37 = (f32[8,2,512]{2,1,0:T(2,128)S(1)}, f32[8,2,512]{2,1,0:T(2,128)}, u32[]{:S(2)}) copy-start(f32[8,2,512]{2,1,0:T(2,128)} %param.14) | copy-start | bytes 98308
  110.1 31.3 %copy-start.38 = (f32[8,2,512]{2,1,0:T(2,128)S(1)}, f32[8,2,512]{2,1,0:T(2,128)}, u32[]{:S(2)}) copy-start(f32[8,2,512]{2,1,0:T(2,128)} %param.15) | copy-start | bytes 98308
  110.1 16.6 %all-to-all-start.3 = ((f32[128,3,2,128]{3,2,1,0:T(2,128)}), f32[128,3,2,128]{3,2,1,0:T(2,128)S(1)}, u32[]{:S(2)}, u32[]{:S(2)}) async-start(f32[128,3,2,128]{3,2,1,0:T(2,128)} %copy-done.12), calls=%async_computation.3 | async-start | bytes 786432 | tf_op jit(solution)/shard_map/all_to_all | solution.py:31
  115.0 10.8 %collective-permute-start.6 = (f32[8,32]{1,0:T(8,128)S(1)}, f32[8,32]{1,0:T(8,128)S(1)}, u32[]{:S(2)}, u32[]{:S(2)}) collective-permute-start(f32[8,32]{1,0:T(8,128)S(1)} %slice.348), channel_id=1, source_target_pairs={{0,1},{1,2},{2,3},{3,4},{4,5},{5,6},{6,7},{7,8},{8,9},{9,10},{10,1... | collective-permute-start | bytes 3080 | tf_op jit(solution)/shard_map/ppermute | solution.py:40
  128.2 8.7 %all-to-all-start.4 = ((f32[8,8,384]{2,1,0:T(8,128)}), f32[8,8,384]{2,1,0:T(8,128)S(1)}, u32[]{:S(2)}, u32[]{:S(2)}) async-start(f32[8,8,384]{2,1,0:T(8,128)} %get-tuple-element.32), calls=%async_computation.4 | async-start | bytes 196608 | tf_op jit(solution)/shard_map/all_to_all | solution.py:31
  137.6 12.0 %all-to-all-start.5 = ((f32[16,8,384]{2,1,0:T(8,128)}), f32[16,8,384]{2,1,0:T(8,128)S(1)}, u32[]{:S(2)}, u32[]{:S(2)}) async-start(f32[16,8,384]{2,1,0:T(8,128)} %broadcast_in_dim.27), calls=%async_computation.5 | async-start | bytes 393216 | tf_op jit(solution)/shard_map/all_to_all | solution.py:31
  (5 other events, 3.5 us)

commit v4 on v3

--- a/solution.py
+++ b/solution.py
@@ -40,10 +40,6 @@
     return lax.ppermute(array, AXES, [(i, (i + by) % count) for i in range(count)])
 
 
-def ein(spec, *operands):
-    return jnp.einsum(spec, *operands, precision=highest)
-
-
 def dot(a, b, dims):
     return lax.dot_general(a, b, dims, precision=highest, preferred_element_type=f32)
 
@@ -76,11 +72,152 @@
     return high, middle, (rest - middle.astype(f32)).astype(bf16)
 
 
-def split_body(matrix_ref, parts_ref):
+def start_body(device_ref, load_ref, inertia_ref, disp_ref, vel_ref, acc_ref, modes_ref, start_ref, right_ref):
+    blank = jnp.zeros((NC, modes_ref.shape[2]), f32)
+    fields = []
+    for s in range(2):
+        moved = disp_ref[:, s, :] + time_step * vel_ref[:, s, :]
+        moved = moved + (0.5 - newmark_beta) * time_step * time_step * acc_ref[:, s, :]
+        fields.append(load_ref[:, s, :] + inertia_ref[s : s + 1] * moved)
+        right_ref[s] = fields[s]
+    part_0 = jnp.concatenate([modes_ref[0, NC:], blank, blank, modes_ref[0, :NC]], axis=0)
+    part_1 = jnp.concatenate([modes_ref[1, :NC], modes_ref[1, NC:], blank, blank], axis=0)
+    blocks = dot(fields[0], part_0, NT) + dot(fields[1], part_1, NT)
+    even = lax.rem(device_ref[0], 2) == 0
+    blocks = jnp.where(even, blocks, pltpu.roll(blocks, HALF, 1))
+    for d in range(start_ref.shape[0]):
+        start_ref[d] = blocks
+
+
+def pre_body(matrix_ref, right_ref, rr_ref, parts_ref, local_ref):
     rows = matrix_ref.shape[0]
     high, low = two_parts(matrix_ref[...])
     parts_ref[:rows] = high
     parts_ref[rows:] = low
+    for s in range(2):
+        local_ref[s] = dot(right_ref[s], rr_ref[s], NN)
+
+
+def couple_body(device_ref, modes_ref, right_ref, left_ref, local_ref, blocks_ref, coupling_ref, to_blocks_ref):
+    last = modes_ref.shape[2] - NI
+    even = jnp.where(lax.rem(device_ref[0], 2) == 0, 1, 0)
+    first, final = [modes_ref[s, :, :NI] for s in range(2)], [modes_ref[s, :, last:] for s in range(2)]
+    right_first, right_final = [right_ref[s, :, :NI] for s in range(2)], right_ref[0, :, last:]
+    left = left_ref[...]
+    rows = [
+        {0: left[:NC]},
+        {0: left[NC:] - first[0][:NC], 1: final[0][:NC]},
+        {0: -first[0][NC:], 1: final[0][NC:] - first[1][:NC], 2: final[1][:NC]},
+        {1: -first[1][NC:], 2: final[1][NC:] - right_first[0][:NC], 3: right_final[:NC]},
+        {2: -right_first[0][NC:], 3: right_final[NC:] - right_first[1][:NC]},
+        {3: -right_first[1][NC:]},
+    ]
+    to_blocks_ref[...] = jnp.zeros(to_blocks_ref.shape, f32)
+    for i, parts in enumerate(rows):
+        at = pl.multiple_of(lax.rem(i * NC + 192 * even, 256), NC)
+        for k, values in parts.items():
+            to_blocks_ref[pl.ds(at, NC), k * NI : (k + 1) * NI] = values
+    blank = jnp.zeros((NC, modes_ref.shape[2]), f32)
+    unit_0 = jnp.concatenate([modes_ref[0, NC:], blank], axis=0)
+    unit_1 = modes_ref[1]
+    unit_2 = jnp.concatenate([blank, right_ref[0, :NC]], axis=0)
+    jumps = jnp.concatenate(
+        [-unit_0[:, :NI], unit_0[:, last:] - unit_1[:, :NI], unit_1[:, last:] - unit_2[:, :NI], unit_2[:, last:]], axis=1
+    )
+    coupling_ref[...] = dot(jumps, to_blocks_ref[...], NT)
+    blocks_ref[...] = own_blocks(local_ref[0], local_ref[1], to_blocks_ref)
+
+
+def own_blocks(field_0, field_1, to_blocks_ref):
+    last = field_0.shape[1] - NI
+    jumps = [-field_0[:, :NI], field_0[:, last:] - field_1[:, :NI], field_1[:, last:]]
+    return dot(jnp.concatenate(jumps, axis=1), to_blocks_ref[:, : 3 * NI], NT)
+
+
+def edge_body(local_ref, z_ref, modes_ref, mine_ref, to_right_ref, to_left_ref):
+    last = local_ref.shape[2] - NI
+    z = z_ref[...]
+    mine_0 = local_ref[0] + dot(z[:, :NC], modes_ref[0, NC:], NN)
+    mine_1 = local_ref[1] + dot(z, modes_ref[1], NN)
+    mine_ref[0], mine_ref[1] = mine_0, mine_1
+    to_left_ref[...] = mine_0[:, :NI]
+    to_right_ref[:, :NI] = mine_1[:, last:]
+    to_right_ref[:, NI:] = jnp.concatenate([z, z], axis=1)
+
+
+def join_body(
+    mine_ref, from_left_ref, from_right_ref, z_ref, modes_ref, right_ref, rr_ref, to_blocks_ref,
+    field_ref, local_ref, blocks_ref, sums_ref,
+):
+    last = mine_ref.shape[2] - NI
+    mine_1 = mine_ref[1]
+    ghost = from_left_ref[:, NI : NI + 2 * NC]
+    mine_0 = mine_ref[0] + dot(ghost[:, NC:], modes_ref[0, :NC], NN)
+    field_ref[0], field_ref[1] = mine_0, mine_1
+    jump_a = from_left_ref[:, :NI] - mine_0[:, :NI]
+    jump_b = mine_0[:, last:] - mine_1[:, :NI]
+    jump_c = mine_1[:, last:] - (from_right_ref[...] + dot(z_ref[:, NC:], right_ref[0, :NC, :NI], NN))
+    inner = jnp.zeros((mine_1.shape[0], 1), f32)
+    outs = []
+    for s, (first, final) in enumerate([(-jump_a, jump_b), (-jump_b, jump_c)]):
+        out = dot(first, rr_ref[s, :NI], NN) + dot(final, rr_ref[s, last:], NN)
+        local_ref[s] = out
+        inner = inner + jnp.sum(out[:, :NI] * first + out[:, last:] * final, axis=1, keepdims=True)
+        outs.append(out)
+    blocks_ref[...] = own_blocks(outs[0], outs[1], to_blocks_ref)
+    square = jnp.sum(jump_b * jump_b + jump_c * jump_c, axis=1, keepdims=True)
+    lane = lax.broadcasted_iota(jnp.int32, sums_ref.shape, 1)
+    sums_ref[...] = jnp.where(lane == 0, square, 0.0) + jnp.where(lane == 1, inner, 0.0)
+
+
+def prep_body(basis_ref, owner_ref, after_ref, parts_ref, square_ref, select_ref):
+    devices, width, rank = basis_ref.shape
+    total = devices * width
+    square = jnp.zeros((rank, rank), f32)
+    for j in range(width):
+        rows = basis_ref[:, j, :]
+        high, low = two_parts(rows)
+        parts_ref[j * devices : (j + 1) * devices] = high
+        parts_ref[total + j * devices : total + (j + 1) * devices] = low
+        turned_high, turned_low = two_parts(jnp.transpose(rows))
+        square = square + fast(turned_high, high, NN) + (fast(turned_high, low, NN) + fast(turned_low, high, NN))
+    for i in range(4):
+        r, h = i // 2, i % 2
+        square_ref[:, i, :] = square[r * LANES : (r + 1) * LANES, h * LANES : (h + 1) * LANES]
+    unknowns = select_ref.shape[1]
+    rows = lax.broadcasted_iota(jnp.int32, (devices, unknowns), 0)
+    columns = lax.broadcasted_iota(jnp.int32, (devices, unknowns), 1)
+    each = unknowns // devices
+    repeat = jnp.where(columns // each == rows, 1.0, 0.0).astype(bf16)
+    owner = jnp.broadcast_to(owner_ref[...].astype(f32), (8, devices)).astype(bf16)
+    owner = fast(owner, repeat, NN)[:1]
+    select_ref[...] = jnp.where(owner == rows.astype(f32), 1.0, 0.0).astype(bf16)
+
+
+def out_body(
+    green_ref, image_ref, local_ref, z_ref, ghost_ref, modes_ref, gains_ref, disp_ref, vel_ref, acc_ref,
+    disp_out_ref, vel_out_ref,
+):
+    kappa_1, kappa_2 = gains_ref[0], gains_ref[1]
+    case = lax.broadcasted_iota(jnp.int32, kappa_1.shape, 0)
+    lane = lax.broadcasted_iota(jnp.int32, kappa_1.shape, 1)
+    kappa_1 = jnp.sum(jnp.where(case == lane, kappa_1, 0.0), axis=1, keepdims=True)
+    kappa_2 = jnp.sum(jnp.where(case == lane, kappa_2, 0.0), axis=1, keepdims=True)
+    z = z_ref[...]
+    late = [
+        local_ref[0] + dot(z[:, :NC], modes_ref[0, NC:], NN) + dot(ghost_ref[:, NC:], modes_ref[0, :NC], NN),
+        local_ref[1] + dot(z, modes_ref[1], NN),
+    ]
+    for s in range(2):
+        disp = green_ref[s] - kappa_1 * image_ref[s] + kappa_2 * late[s]
+        vel, acc = vel_ref[:, s, :], acc_ref[:, s, :]
+        accel = (
+            (disp - disp_ref[:, s, :]) * (1.0 / (newmark_beta * time_step * time_step))
+            - vel * (1.0 / (newmark_beta * time_step))
+            - (0.5 / newmark_beta - 1.0) * acc
+        )
+        disp_out_ref[:, s, :] = disp
+        vel_out_ref[:, s, :] = vel + time_step * ((1.0 - newmark_gamma) * acc + newmark_gamma * accel)
 
 
 def coarse_product(assembled_ref, parts_ref):
@@ -175,7 +312,8 @@
 
 
 def third_body(
-    device_ref, got_ref, parts_ref, local_ref, modes_a_ref, modes_b_ref, modes_c_ref, select_ref, sums_ref, early_ref,
+    device_ref, got_ref, parts_ref, local_ref, modes_ref, right_ref, select_ref, sums_2_ref, sums_3_ref, terms_ref,
+    early_ref,
     sent_ref, z_ref, assembled_ref,
 ):
     assemble_packed(got_ref, assembled_ref, 4)
@@ -184,18 +322,24 @@
     square = got_ref[3]
     for d in range(1, got_ref.shape[0] // 4):
         square = square + got_ref[4 * d + 3]
-    y_0 = local_ref[0] + dot(z[:, :NC], modes_a_ref[...], NN)
-    y_1 = local_ref[1] + dot(z, modes_b_ref[...], NN)
-    y_2 = dot(z[:, NC:], modes_c_ref[...], NN)
+    y_0 = local_ref[0] + dot(z[:, :NC], modes_ref[0, NC:], NN)
+    y_1 = local_ref[1] + dot(z, modes_ref[1], NN)
+    y_2 = dot(z[:, NC:], right_ref[0, :NC], NN)
     rows = by_offset(y_0) + by_offset(y_1) + by_offset(y_2)
     rows.append(jnp.zeros((32, y_0.shape[1]), f32))
     late = choose_rows(select_ref, jnp.concatenate(rows, axis=0))
     curvature = jnp.sum(owned_terms(device_ref, assembled_ref, z), axis=1, keepdims=True)
     lane = lax.broadcasted_iota(jnp.int32, (8, LANES), 1)
     case = lax.broadcasted_iota(jnp.int32, (8, LANES), 0)
-    placed = jnp.where(lane == 120 + case, curvature, 0.0)
+    parts = [
+        sums_2_ref[:, 0:1],
+        sums_2_ref[:, 1:2] + jnp.sum(terms_ref[...], axis=1, keepdims=True),
+        sums_3_ref[:, 0:1],
+        sums_3_ref[:, 1:2] + curvature,
+    ]
+    placed = jnp.zeros((8, LANES), f32)
     for k in range(4):
-        placed = placed + jnp.where(lane == 96 + 8 * k + case, sums_ref[:, k : k + 1], 0.0)
+        placed = placed + jnp.where(lane == 96 + 8 * k + case, parts[k], 0.0)
     late = late + jnp.sum(placed, axis=0, keepdims=True)
     sent_ref[:, 0, 0, :] = early_ref[...]
     sent_ref[:, 0, 1, :] = late
@@ -307,119 +451,57 @@
     coarse_total = coarse_inverse.shape[1]
     rank = basis_rows.shape[1]
     last = unknowns - NI
-    me = lax.axis_index(AXES)
-    even = me % 2 == 0
-    device = me.reshape(1).astype(jnp.int32)
-
-    right_side = load_next + inertia[None] * (
-        disp_now + time_step * vel_now + (0.5 - newmark_beta) * time_step * time_step * acc_now
-    )
-    terms = ein("jmb,cjb->jcm", corner_modes, right_side)
-    low, middle, high = terms[0, :, :NC], terms[0, :, NC:] + terms[1, :, :NC], terms[1, :, NC:]
-    gap = jnp.zeros((case_count, NC), f32)
-    start = jnp.where(
-        even,
-        jnp.concatenate([middle, high, gap, low], axis=1),
-        jnp.concatenate([gap, low, middle, high], axis=1),
-    )
-    got_1 = to_everyone(start)
+    device = lax.axis_index(AXES).reshape(1).astype(jnp.int32)
+    pair = ((2, case_count, unknowns),)
+    z_shape = ((case_count, 2 * NC),)
+    blocks_shape = ((case_count, 2 * LANES),)
+    assembled = [pltpu.VMEM((case_count, coarse_total), f32)]
+
+    start, right_side = call(start_body, [((devices, case_count, LANES),), pair], [SMEM] + [VMEM] * 6)(
+        device, load_next, inertia, disp_now, vel_now, acc_now, corner_modes
+    )
+    got_1 = exchange(start)
     right_modes = shifted(corner_modes, -1)
     left_edge = shifted(corner_modes[1, :, last:], 1)
-
-    (coarse_parts,) = call(split_body, [((4 * NC, coarse_total), bf16)], [VMEM], flops=1 << 22)(coarse_inverse)
-    zero = jnp.zeros((NC, NI), f32)
-    first, final = corner_modes[:, :, :NI], corner_modes[:, :, last:]
-    right_first, right_final = right_modes[:, :, :NI], right_modes[:, :, last:]
-    rows = [
-        [left_edge[:NC], zero, zero, zero],
-        [left_edge[NC:] - first[0, :NC], final[0, :NC], zero, zero],
-        [-first[0, NC:], final[0, NC:] - first[1, :NC], final[1, :NC], zero],
-        [zero, -first[1, NC:], final[1, NC:] - right_first[0, :NC], right_final[0, :NC]],
-        [zero, zero, -right_first[0, NC:], right_final[0, NC:] - right_first[1, :NC]],
-        [zero, zero, zero, -right_first[1, NC:]],
-    ]
-    rows = jnp.concatenate([jnp.concatenate(parts, axis=1) for parts in rows], axis=0)
-    blank = jnp.zeros((HALF, 4 * NI), f32)
-    to_blocks = jnp.where(
-        even,
-        jnp.concatenate([rows[HALF:], blank, rows[:HALF]], axis=0),
-        jnp.concatenate([rows, blank], axis=0),
-    )
-
-    def blocks_of(d_a, d_b, d_c, d_d):
-        return dot(jnp.concatenate([d_a, d_b, d_c, d_d], axis=1), to_blocks, NT)
-
-    def local_blocks(field):
-        return blocks_of(
-            -field[0, :, :NI], field[0, :, last:] - field[1, :, :NI], field[1, :, last:], jnp.zeros((case_count, NI), f32)
+    coarse_parts, local_0 = call(pre_body, [((4 * NC, coarse_total), bf16), pair], [VMEM] * 3, flops=1 << 26)(
+        coarse_inverse, right_side, rr_inverse
+    )
+    blocks_0, coupling, to_blocks = call(
+        couple_body, [blocks_shape, ((2 * NC, 2 * LANES),), ((2 * LANES, 4 * NI),)], [SMEM] + [VMEM] * 4, flops=1 << 26
+    )(device, corner_modes, right_modes, left_edge, local_0)
+
+    def finish(local, z):
+        mine, to_right, to_left = call(
+            edge_body, [pair, ((case_count, 2 * NI),), ((case_count, NI),)], [VMEM] * 3, flops=1 << 20
+        )(local, z, corner_modes)
+        from_left = shifted(to_right, 1)
+        from_right = shifted(to_left, -1)
+        return call(join_body, [pair, pair, blocks_shape, ((case_count, LANES),)], [VMEM] * 8, flops=1 << 26)(
+            mine, from_left, from_right, z, corner_modes, right_modes, rr_inverse, to_blocks
         )
 
-    unit_0 = jnp.concatenate([corner_modes[0, NC:], jnp.zeros((NC, unknowns), f32)], axis=0)
-    unit_1 = corner_modes[1]
-    unit_2 = jnp.concatenate([jnp.zeros((NC, unknowns), f32), right_modes[0, :NC]], axis=0)
-    coupling = blocks_of(
-        -unit_0[:, :NI], unit_0[:, last:] - unit_1[:, :NI], unit_1[:, last:] - unit_2[:, :NI], unit_2[:, last:]
-    )
-
-    def finish(local, z):
-        z_a, z_b = z[:, :NC], z[:, NC:]
-        mine_0 = local[0] + dot(z_a, corner_modes[0, NC:], NN)
-        mine_1 = local[1] + dot(z, corner_modes[1], NN)
-        from_left = shifted(jnp.concatenate([mine_1[:, last:], z_b], axis=1), 1)
-        from_right = shifted(mine_0[:, :NI], -1)
-        mine_0 = mine_0 + dot(from_left[:, NI:], corner_modes[0, :NC], NN)
-        jump_a = from_left[:, :NI] - mine_0[:, :NI]
-        jump_b = mine_0[:, last:] - mine_1[:, :NI]
-        jump_c = mine_1[:, last:] - (from_right + dot(z_b, right_modes[0, :NC, :NI], NN))
-        return jnp.stack([mine_0, mine_1]), jump_a, jump_b, jump_c
-
-    def local_apply(jump_a, jump_b, jump_c):
-        first = jnp.stack([-jump_a, -jump_b])
-        final = jnp.stack([jump_b, jump_c])
-        out = ein("jcb,jab->jca", first, rr_inverse[:, :, :NI]) + ein("jcb,jab->jca", final, rr_inverse[:, :, last:])
-        inner = jnp.sum(out[:, :, :NI] * first + out[:, :, last:] * final, axis=(0, 2))
-        return out, inner
-
-    local_0 = ein("cjb,jab->jca", right_side, rr_inverse)
-    assembled = [pltpu.VMEM((case_count, coarse_total), f32)]
-    z_shape = ((case_count, 2 * NC),)
     pieces, z_0 = call(first_body, [((3 * devices, 4, LANES),), z_shape], [VMEM] * 4, assembled, flops=1 << 24)(
-        got_1, coarse_parts, coupling, local_blocks(local_0)
+        got_1, coarse_parts, coupling, blocks_0
     )
     got_2 = exchange(pieces)
-    green, b_a, b_b, b_c = finish(local_0, z_0)
-    b_b, basis_rows, piece_owner = lax.optimization_barrier((b_b, basis_rows, piece_owner))
-    basis_sorted = basis_rows.reshape(devices, -1, rank).swapaxes(0, 1).reshape(-1, rank)
-    (basis_parts,) = call(split_body, [((2 * basis_sorted.shape[0], rank), bf16)], [VMEM], flops=1 << 22)(basis_sorted)
-    square = lax.dot_general(basis_rows, basis_rows, (((0,), (0,)), ((), ())), precision=highest)
-    square = jnp.stack(
-        [square[:LANES, :LANES], square[:LANES, LANES:], square[LANES:, :LANES], square[LANES:, LANES:]], axis=1
-    )
-    owner = jnp.broadcast_to(piece_owner[:, None], (devices, unknowns // devices)).reshape(1, unknowns)
-    select = (owner == lax.broadcasted_iota(jnp.int32, (devices, unknowns), 0)).astype(bf16)
-
-    local_1, inner_1 = local_apply(b_a, b_b, b_c)
+    basis_parts, square, select = call(
+        prep_body,
+        [((2 * basis_rows.shape[0], rank), bf16), ((devices, 4, LANES),), ((devices, unknowns), bf16)],
+        [VMEM, VMEM, VMEM],
+        flops=1 << 26,
+    )(basis_rows.reshape(devices, -1, rank), piece_owner.reshape(1, devices), z_0)
+    green, local_1, blocks_1, sums_2 = finish(local_0, z_0)
     pieces, z_1, terms_1 = call(
         second_body, [((4 * devices, 4, LANES),), z_shape, z_shape], [SMEM] + [VMEM] * 5, assembled, flops=1 << 24
-    )(device, got_2, coarse_parts, coupling, local_blocks(local_1), square)
+    )(device, got_2, coarse_parts, coupling, blocks_1, square)
     got_3 = exchange(pieces)
-    image_1, v_a, v_b, v_c = finish(local_1, z_1)
-    local_2, inner_2 = local_apply(v_a, v_b, v_c)
-    sums = jnp.stack(
-        [
-            jnp.sum(b_b * b_b + b_c * b_c, axis=1),
-            inner_1 + jnp.sum(terms_1, axis=1),
-            jnp.sum(v_b * v_b + v_c * v_c, axis=1),
-            inner_2,
-        ],
-        axis=1,
-    )
+    image_1, local_2, _, sums_3 = finish(local_1, z_1)
     (early,) = call(early_body, [((devices, LANES),)], [VMEM] * 3, flops=1 << 24)(select, green, image_1)
-    sent, z_2 = call(third_body, [((devices, 3, 2, LANES),), z_shape], [SMEM] + [VMEM] * 9, assembled, flops=1 << 24)(
-        device, got_3, coarse_parts, local_2, corner_modes[0, NC:], corner_modes[1], right_modes[0, :NC], select, sums, early
+    sent, z_2 = call(third_body, [((devices, 3, 2, LANES),), z_shape], [SMEM] + [VMEM] * 10, assembled, flops=1 << 24)(
+        device, got_3, coarse_parts, local_2, corner_modes, right_modes, select, sums_2, sums_3, terms_1, early
     )
     got_4 = exchange(sent)
-    ghost = shifted(z_2[:, NC:], 1)
+    ghost = shifted(z_2, 1)
     part, snapshots, gains = call(
         project_body,
         [
@@ -430,8 +512,12 @@
         [VMEM] * 2,
         flops=1 << 24,
     )(got_4, basis_parts)
-    near = exchange(part, NEAR).sum(axis=0)
+    near = exchange(part, NEAR)
+    near = near.sum(axis=0)
     got_5 = to_everyone(near, FAR)
+    disp_new, vel_new = call(
+        out_body, [(disp_now.shape,), (disp_now.shape,)], [VMEM] * 10, flops=1 << 22
+    )(green, image_1, local_2, z_2, ghost, corner_modes, gains, disp_now, vel_now, acc_now)
     scale = math.sqrt(basis_rows.shape[0] * devices)
     new_columns, projection, factor = call(
         functools.partial(finish_body, scale=scale),
@@ -439,22 +525,6 @@
         [VMEM] * 4,
         flops=1 << 24,
     )(got_5, got_4, basis_parts, snapshots)
-
-    kappa_1, kappa_2 = gains[0, 0, :case_count, None], gains[1, 0, :case_count, None]
-    image_2 = jnp.stack(
-        [
-            local_2[0] + dot(z_2[:, :NC], corner_modes[0, NC:], NN) + dot(ghost, corner_modes[0, :NC], NN),
-            local_2[1] + dot(z_2, corner_modes[1], NN),
-        ]
-    )
-    disp_new = green - kappa_1 * image_1 + kappa_2 * image_2
-    disp_new = jnp.swapaxes(disp_new, 0, 1)
-    accel_new = (
-        (disp_new - disp_now) / (newmark_beta * time_step * time_step)
-        - vel_now / (newmark_beta * time_step)
-        - (0.5 / newmark_beta - 1.0) * acc_now
-    )
-    vel_new = vel_now + time_step * ((1.0 - newmark_gamma) * acc_now + newmark_gamma * accel_new)
     return (disp_new, vel_new, projection.T, factor[:, :case_count], new_columns)
 
 

time: 154 us -> 146 us (0.948)
  blocking collectives: 0 us -> 24.7 us
  matrix products: 19 us -> 0 us
  waiting for transfers between devices: 37 us -> 21.7 us
  local copies, waits for them, and re-layouts: 20 us -> 29.9 us
  other arithmetic: 8.36 us -> 0.01 us
  Pallas kernels: 12 us -> 19.4 us
  starting transfers between devices: 54.5 us -> 47.8 us
    all_to_all x6 -> x4, waiting for transfers between devices: 29.3 us -> 0.01 us  [exchange(): return lax.all_to_all(pieces, axes, split_axis=0, concat_axis=0, tiled=True)]
    all_to_all x0 -> x2, blocking collectives: none -> 24.7 us  [exchange(): return lax.all_to_all(pieces, axes, split_axis=0, concat_axis=0, tiled=True)]
    dot_general x21 -> x0, matrix products: 19 us -> none  [the longest x14 8.24 us: dot(): lax.dot_general(a, b, dims, precision=highest, preferred_element_type=f32)]
    unnamed x85 -> x88, local copies, waits for them, and re-layouts: 9.45 us -> 28.4 us
    ppermute x7, waiting for transfers between devices: 7.7 us -> 21.7 us  [shifted(): lax.ppermute(array, AXES, [(i, (i + by) % count) for i in range(count)])]
    pallas_call x2 -> x9, Pallas kernels: 0.47 us -> 11.9 us  [the longest x1 4.02 us: shards(): call(prep_body, [((2 * basis_rows.shape[0], rank), bf16), ((devices, 4, L...]
    all_to_all x6 -> x4, starting transfers between devices: 35.9 us -> 25.3 us  [exchange(): return lax.all_to_all(pieces, axes, split_axis=0, concat_axis=0, tiled=True)]
    ppermute x7, starting transfers between devices: 18.6 us -> 22.5 us  [shifted(): lax.ppermute(array, AXES, [(i, (i + by) % count) for i in range(count)])]
  transfers between devices with their start and end apart: 13 -> 11, of which waited for: 6 -> 5; matrix products, arithmetic and copies ran while one was open for 24% -> 1% of each run, Pallas kernels for 0% -> 8%
where the time goes in v4:
time: 146 us; the launch traced here: 144 us
  starting transfers between devices  47.8 us (33%)
  local copies, waits for them, and re-layouts  29.9 us (20%)
  blocking collectives  24.7 us (17%)
  waiting for transfers between devices  21.7 us (15%)
  Pallas kernels  19.4 us (13%)
    unnamed x88, local copies, waits for them, and re-layouts  28.4 us
    all_to_all x4, starting transfers between devices, exchange(): return lax.all_to_all(pieces, axes, split_axis=0, concat_axis=0, tiled=True)  25.3 us
    all_to_all x2, blocking collectives, exchange(): return lax.all_to_all(pieces, axes, split_axis=0, concat_axis=0, tiled=True)  24.7 us
    ppermute x7, starting transfers between devices, shifted(): lax.ppermute(array, AXES, [(i, (i + by) % count) for i in range(count)])  22.5 us
    ppermute x7, waiting for transfers between devices, shifted(): lax.ppermute(array, AXES, [(i, (i + by) % count) for i in range(count)])  21.7 us
    pallas_call x1, Pallas kernels, shards(): call(prep_body, [((2 * basis_rows.shape[0], rank), bf16), ((devices, 4, L...  4.02 us
  transfers between devices with their start and end apart: 11, of which 5 were waited for; matrix products, arithmetic and copies ran while one was open for 1% of the time, Pallas kernels for 8%

profile of v4, /device:TPU:0, one launch (start us, length us, event | category | flops | bytes accessed | tf_op | source)
XLA Modules:
  0.0 144.2 jit_solution(15984231343351307258)
XLA Ops:
  0.7 0.9 copy-done.5
  1.6 0.8 copy-done.26
  2.4 0.8 copy-done.28
  5.3 1.3 shard_map.137
  6.7 11.2 %all-to-all-start = ((f32[128,8,128]{2,1,0:T(8,128)}), f32[128,8,128]{2,1,0:T(8,128)S(1)}, u32[]{:S(2)}, u32[]{:S(2)}) async-start(f32[128,8,128]{2,1,0:T(8,128)} %get-tuple-element.45), calls=%async_computation | async-start | bytes 1048576 | tf_op jit(solution)/shard_map/all_to_all | solution.py:31
  17.8 7.1 %collective-permute-start = (f32[2,64,512]{2,1,0:T(8,128)}, f32[2,64,512]{2,1,0:T(8,128)S(1)}, u32[]{:S(2)}, u32[]{:S(2)}) collective-permute-start(f32[2,64,512]{2,1,0:T(8,128)} %modes_ref.15), channel_id=1, source_target_pairs={{0,127},{1,0},{2,1},{3,2},{4,3},{5,4},{6,5},{7,6},{8,7},{9,8},{10,... | collective-permute-start | bytes 786440 | tf_op jit(solution)/shard_map/ppermute | solution.py:40
  24.9 0.8 slice_bitcast_fusion
  25.7 1.6 %copy-done = f32[2,512,512]{2,1,0:T(8,128)S(1)} copy-done((f32[2,512,512]{2,1,0:T(8,128)S(1)}, f32[2,512,512]{2,1,0:T(8,128)}, u32[]{:S(2)}) %copy-start) | copy-done | bytes 2097176
  27.3 1.6 %copy-done.15 = f32[64,8192]{1,0:T(8,128)S(1)} copy-done((f32[64,8192]{1,0:T(8,128)S(1)}, f32[64,8192]{1,0:T(8,128)}, u32[]{:S(2)}) %copy-start.15) | copy-done | bytes 2097176
  28.9 1.6 %shard_map.138 = (bf16[128,8192]{1,0:T(8,128)(2,1)S(1)}, f32[2,8,512]{2,1,0:T(8,128)S(1)}) custom-call(f32[64,8192]{1,0:T(8,128)S(1)} %copy-done.15, f32[2,8,512]{2,1,0:T(8,128)S(1)} %get-tuple-element.43.right_ref, f32[2,512,512]{2,1,0:T(8,128)S(1)} %copy-done), custom_call_target="tpu_custom_call" | custom-call | flops 67108864 | bytes 1048576 | tf_op jit(solution)/shard_map/pallas_call | solution.py:466
  30.5 4.0 %collective-permute-done.1.left_ref = f32[64,128]{1,0:T(8,128)S(1)} collective-permute-done((f32[64,128]{1,0:T(8,128)S(1)}, f32[64,128]{1,0:T(8,128)S(1)}, u32[]{:S(2)}, u32[]{:S(2)}) %collective-permute-start.1) | collective-permute-done | bytes 32800 | tf_op jit(solution)/shard_map/ppermute | solution.py:40
  34.5 0.9 shard_map.139
  35.4 0.8 copy-done.12
  36.3 1.0 shard_map.140
  37.3 1.3 copy-done.2
  38.6 0.9 copy-done.18
  39.5 5.8 %all-to-all-start.1 = ((f32[384,4,128]{2,1,0:T(4,128)}), f32[384,4,128]{2,1,0:T(4,128)S(1)}, u32[]{:S(2)}, u32[]{:S(2)}) async-start(f32[384,4,128]{2,1,0:T(4,128)} %copy-done.18), calls=%async_computation.1 | async-start | bytes 1572864 | tf_op jit(solution)/shard_map/all_to_all | solution.py:31
  45.5 1.0 collective-permute-start.2
  46.5 6.3 %collective-permute-start.3 = (f32[8,128]{1,0:T(8,128)S(1)}, f32[8,128]{1,0:T(8,128)S(1)}, u32[]{:S(2)}, u32[]{:S(2)}) collective-permute-start(f32[8,128]{1,0:T(8,128)S(1)} %get-tuple-element.52), channel_id=1, source_target_pairs={{0,127},{1,0},{2,1},{3,2},{4,3},{5,4},{6,5},{7,6},{8,7},{9,8},{10,... | collective-permute-start | bytes 12296 | tf_op jit(solution)/shard_map/ppermute | solution.py:40
  52.9 1.2 copy-done.16
  54.1 4.0 %shard_map.143 = (bf16[2048,256]{1,0:T(8,128)(2,1)S(1)}, f32[128,4,128]{2,1,0:T(4,128)S(1)}, bf16[128,512]{1,0:T(8,128)(2,1)S(1)}) custom-call(f32[128,8,256]{2,1,0:T(8,128)S(1)} %bitcast.7, s32[1,128]{1,0:T(1,128)S(1)} %bitcast.8, f32[8,64]{1,0:T(8,128)S(1)} %get-tuple-element.49.z_ref.after_ref), custom_call_target="tpu_custom_call" | custom-call | flops 67108864 | bytes 1048576 | tf_op jit(solution)/shard_map/pallas_call | solution.py:487
  58.1 1.0 copy-done.10
  60.3 1.0 copy-done.13
  61.4 1.1 shard_map.142
  63.7 1.6 %copy-done.3 = bf16[128,8192]{1,0:T(8,128)(2,1)S(1)} copy-done((bf16[128,8192]{1,0:T(8,128)(2,1)S(1)}, bf16[128,8192]{1,0:T(8,128)(2,1)}, u32[]{:S(2)}) %copy-start.3) | copy-done | bytes 2097176
  65.3 0.9 copy-done.20
  66.2 0.8 copy-done.22
  67.1 1.1 shard_map.144
  68.2 1.0 copy-done.17
  69.7 4.8 %all-to-all-start.2 = ((f32[512,4,128]{2,1,0:T(4,128)}), f32[512,4,128]{2,1,0:T(4,128)S(1)}, u32[]{:S(2)}, u32[]{:S(2)}) async-start(f32[512,4,128]{2,1,0:T(4,128)} %copy-done.17), calls=%async_computation.2 | async-start | bytes 2097152 | tf_op jit(solution)/shard_map/all_to_all | solution.py:31
  75.5 1.0 collective-permute-start.4
  76.5 6.2 %collective-permute-start.5 = (f32[8,128]{1,0:T(8,128)S(1)}, f32[8,128]{1,0:T(8,128)S(1)}, u32[]{:S(2)}, u32[]{:S(2)}) collective-permute-start(f32[8,128]{1,0:T(8,128)S(1)} %get-tuple-element.62), channel_id=1, source_target_pairs={{0,127},{1,0},{2,1},{3,2},{4,3},{5,4},{6,5},{7,6},{8,7},{9,8},{10,... | collective-permute-start | bytes 12296 | tf_op jit(solution)/shard_map/ppermute | solution.py:40
  82.7 4.4 %collective-permute-done.5.from_right_ref = f32[8,128]{1,0:T(8,128)S(1)} collective-permute-done((f32[8,128]{1,0:T(8,128)S(1)}, f32[8,128]{1,0:T(8,128)S(1)}, u32[]{:S(2)}, u32[]{:S(2)}) %collective-permute-start.5) | collective-permute-done | bytes 4128 | tf_op jit(solution)/shard_map/ppermute | solution.py:40
  87.1 5.1 %collective-permute-done.4.from_left_ref = f32[8,256]{1,0:T(8,128)S(1)} collective-permute-done((f32[8,256]{1,0:T(8,128)S(1)}, f32[8,256]{1,0:T(8,128)S(1)}, u32[]{:S(2)}, u32[]{:S(2)}) %collective-permute-start.4) | collective-permute-done | bytes 8224 | tf_op jit(solution)/shard_map/ppermute | solution.py:40
  92.2 0.9 copy-done.8
  93.2 1.0 copy-done.14
  94.2 1.7 %shard_map.146 = (f32[2,8,512]{2,1,0:T(8,128)S(1)}, f32[2,8,512]{2,1,0:T(8,128)S(1)}, f32[8,256]{1,0:T(8,128)}, f32[8,128]{1,0:T(8,128)S(1)}) custom-call(f32[2,8,512]{2,1,0:T(8,128)S(1)} %get-tuple-element.60.mine_ref, f32[8,256]{1,0:T(8,128)S(1)} %collective-permute-done.4.from_left_ref, f32[8,128]{1,0:T(8,128)S(1)} %collective-permute-done.5.from_right_ref, ...), custom_call_target="tpu_custom_call" | custom-call | flops 67108864 | bytes 1048576 | tf_op jit(solution)/shard_map/pallas_call | solution.py:479
  97.4 1.6 %copy-done.4 = bf16[128,8192]{1,0:T(8,128)(2,1)S(1)} copy-done((bf16[128,8192]{1,0:T(8,128)(2,1)S(1)}, bf16[128,8192]{1,0:T(8,128)(2,1)}, u32[]{:S(2)}) %copy-start.4) | copy-done | bytes 2097176
  99.0 0.9 copy-done.9
  100.7 1.6 %shard_map.148 = (f32[128,3,2,128]{3,2,1,0:T(2,128)S(1)}, f32[8,64]{1,0:T(8,128)S(1)}) custom-call(s32[1]{0:T(128)} %bitcast.device_ref, f32[512,4,128]{2,1,0:T(4,128)S(1)} %all-to-all-done.2.got_ref, bf16[128,8192]{1,0:T(8,128)(2,1)S(1)} %copy-done.4, f32[2,8,512]{2,1,0:T(8,128)S(1)} %copy-done.24, f32[2,64,512]{2,1,0:T(8,128)S(1)} %copy-done.6, ...), custom_call_target="tpu_custom_call" | custom-call | flops 16777216 | bytes 1048576 | tf_op jit(solution)/shard_map/pallas_call | solution.py:500
  102.4 16.5 %all_to_all.30.got_ref.square_ref = f32[128,3,2,128]{3,2,1,0:T(2,128)S(1)} all-to-all(f32[128,3,2,128]{3,2,1,0:T(2,128)S(1)} %get-tuple-element.71), channel_id=1, replica_groups=mesh['sub_0'=4,'sub_1'=4,'sub_2'=2,'grp'=4] {'sub_0','sub_1','sub_2','grp'}, dimensions={0} | all-to-all | bytes 786432 | tf_op jit(solution)/shard_map/all_to_all | solution.py:31
  118.9 0.8 shard_map.149
  119.7 8.2 %all_to_all.31 = f32[8,8,384]{2,1,0:T(8,128)S(1)} all-to-all(f32[8,8,384]{2,1,0:T(8,128)S(1)} %get-tuple-element.76), channel_id=1, replica_groups=mesh['sub_0'=4,'sub_1'=4,'sub_2'=2,'grp'=4] {'sub_2','grp'}, dimensions={0} | all-to-all | bytes 196608 | tf_op jit(solution)/shard_map/all_to_all | solution.py:31
  128.6 3.5 %all-to-all-start.5 = ((f32[16,8,384]{2,1,0:T(8,128)}), f32[16,8,384]{2,1,0:T(8,128)S(1)}, u32[]{:S(2)}, u32[]{:S(2)}) async-start(f32[16,8,384]{2,1,0:T(8,128)} %broadcast_in_dim.3), calls=%async_computation.5 | async-start | bytes 393216 | tf_op jit(solution)/shard_map/all_to_all | solution.py:31
  132.1 0.9 collective-permute-start.6
  133.0 7.6 %collective-permute-done.6.ghost_ref = f32[8,64]{1,0:T(8,128)S(1)} collective-permute-done((f32[8,64]{1,0:T(8,128)S(1)}, f32[8,64]{1,0:T(8,128)S(1)}, u32[]{:S(2)}, u32[]{:S(2)}) %collective-permute-start.6) | collective-permute-done | bytes 2080 | tf_op jit(solution)/shard_map/ppermute | solution.py:40
  140.7 0.9 shard_map.150
  141.6 2.6 %shard_map.151 = (f32[8,1024]{1,0:T(8,128)}, f32[8,256]{1,0:T(8,128)}, f32[8,128]{1,0:T(8,128)}) custom-call(f32[16,8,384]{2,1,0:T(8,128)S(1)} %all-to-all-done.5.got_ref, f32[128,3,2,128]{3,2,1,0:T(2,128)S(1)} %all_to_all.30.got_ref.square_ref, bf16[2048,256]{1,0:T(8,128)(2,1)S(1)} %copy-done.11, f32[8,1024]{1,0:T(8,128)S(1)} %get-tuple-element.77.rows_ref), custom_call_target="tpu_custom_call" | custom-call | flops 16777216 | bytes 1048576 | tf_op jit(solution)/shard_map/pallas_call | solution.py:522
  (82 shorter events, 9.5 us)
Async XLA Ops:
  0.6 1.0 copy-start.5
  1.6 0.8 copy-start.26
  2.4 0.8 copy-start.28
  3.1 0.8 copy-start.30
  3.9 0.8 copy-start.37
  6.7 29.6 %all-to-all-start = ((f32[128,8,128]{2,1,0:T(8,128)}), f32[128,8,128]{2,1,0:T(8,128)S(1)}, u32[]{:S(2)}, u32[]{:S(2)}) async-start(f32[128,8,128]{2,1,0:T(8,128)} %get-tuple-element.45), calls=%async_computation | async-start | bytes 1048576 | tf_op jit(solution)/shard_map/all_to_all | solution.py:31
  17.8 16.7 %collective-permute-start = (f32[2,64,512]{2,1,0:T(8,128)}, f32[2,64,512]{2,1,0:T(8,128)S(1)}, u32[]{:S(2)}, u32[]{:S(2)}) collective-permute-start(f32[2,64,512]{2,1,0:T(8,128)} %modes_ref.15), channel_id=1, source_target_pairs={{0,127},{1,0},{2,1},{3,2},{4,3},{5,4},{6,5},{7,6},{8,7},{9,8},{10,... | collective-permute-start | bytes 786440 | tf_op jit(solution)/shard_map/ppermute | solution.py:40
  25.7 8.8 %collective-permute-start.1 = (f32[64,128]{1,0:T(8,128)S(1)}, f32[64,128]{1,0:T(8,128)S(1)}, u32[]{:S(2)}, u32[]{:S(2)}) collective-permute-start(f32[64,128]{1,0:T(8,128)S(1)} %slice_bitcast_fusion), channel_id=1, source_target_pairs={{0,1},{1,2},{2,3},{3,4},{4,5},{5,6},{6,7},{7,8},{8,9},{9,10},{10,1... | collective-permute-start | bytes 98312 | tf_op jit(solution)/shard_map/ppermute | solution.py:40
  25.7 1.6 %copy-start = (f32[2,512,512]{2,1,0:T(8,128)S(1)}, f32[2,512,512]{2,1,0:T(8,128)}, u32[]{:S(2)}) copy-start(f32[2,512,512]{2,1,0:T(8,128)} %rr_ref.5) | copy-start | bytes 6291460
  27.3 1.6 %copy-start.15 = (f32[64,8192]{1,0:T(8,128)S(1)}, f32[64,8192]{1,0:T(8,128)}, u32[]{:S(2)}) copy-start(f32[64,8192]{1,0:T(8,128)} %matrix_ref.1) | copy-start | bytes 6291460
  28.9 5.6 %copy-start.6 = (f32[2,64,512]{2,1,0:T(8,128)S(1)}, f32[2,64,512]{2,1,0:T(8,128)}, u32[]{:S(2)}) copy-start(f32[2,64,512]{2,1,0:T(8,128)} %modes_ref.15) | copy-start | bytes 786436
  34.5 25.8 %copy-start.7 = (f32[2,64,512]{2,1,0:T(8,128)}, f32[2,64,512]{2,1,0:T(8,128)S(1)}, u32[]{:S(2)}) copy-start(f32[2,64,512]{2,1,0:T(8,128)S(1)} %collective-permute-done.right_ref) | copy-start | bytes 786436
  35.4 0.8 copy-start.12
  36.3 3.3 %copy-start.21 = (f32[64,256]{1,0:T(8,128)}, f32[64,256]{1,0:T(8,128)S(1)}, u32[]{:S(2)}) copy-start(f32[64,256]{1,0:T(8,128)S(1)} %get-tuple-element.47.coupling_ref) | copy-start | bytes 196612
  36.3 16.6 %copy-start.43 = (s32[128]{0:T(128)S(1)}, s32[128]{0:T(128)}, u32[]{:S(2)}) copy-start(s32[128]{0:T(128)} %param.19) | copy-start | bytes 1540
  37.3 1.3 copy-start.2
  38.6 0.9 copy-start.18
  39.5 20.8 %copy-start.1 = (f32[2,512,512]{2,1,0:T(8,128)S(1)}, f32[2,512,512]{2,1,0:T(8,128)}, u32[]{:S(2)}) copy-start(f32[2,512,512]{2,1,0:T(8,128)} %rr_ref.5) | copy-start | bytes 6291460
  39.5 24.2 %all-to-all-start.1 = ((f32[384,4,128]{2,1,0:T(4,128)}), f32[384,4,128]{2,1,0:T(4,128)S(1)}, u32[]{:S(2)}, u32[]{:S(2)}) async-start(f32[384,4,128]{2,1,0:T(4,128)} %copy-done.18), calls=%async_computation.1 | async-start | bytes 1572864 | tf_op jit(solution)/shard_map/all_to_all | solution.py:31
  45.5 14.8 %collective-permute-start.2 = (f32[8,256]{1,0:T(8,128)S(1)}, f32[8,256]{1,0:T(8,128)S(1)}, u32[]{:S(2)}, u32[]{:S(2)}) collective-permute-start(f32[8,256]{1,0:T(8,128)S(1)} %get-tuple-element.51), channel_id=1, source_target_pairs={{0,1},{1,2},{2,3},{3,4},{4,5},{5,6},{6,7},{7,8},{8,9},{9,10},{10,1... | collective-permute-start | bytes 24584 | tf_op jit(solution)/shard_map/ppermute | solution.py:40
  46.5 13.3 %collective-permute-start.3 = (f32[8,128]{1,0:T(8,128)S(1)}, f32[8,128]{1,0:T(8,128)S(1)}, u32[]{:S(2)}, u32[]{:S(2)}) collective-permute-start(f32[8,128]{1,0:T(8,128)S(1)} %get-tuple-element.52), channel_id=1, source_target_pairs={{0,127},{1,0},{2,1},{3,2},{4,3},{5,4},{6,5},{7,6},{8,7},{9,8},{10,... | collective-permute-start | bytes 12296 | tf_op jit(solution)/shard_map/ppermute | solution.py:40
  52.8 1.2 copy-start.16
  58.1 1.0 copy-start.10
  60.3 1.0 copy-start.13
  63.7 1.6 %copy-start.3 = (bf16[128,8192]{1,0:T(8,128)(2,1)S(1)}, bf16[128,8192]{1,0:T(8,128)(2,1)}, u32[]{:S(2)}) copy-start(bf16[128,8192]{1,0:T(8,128)(2,1)} %copy-done.2) | copy-start | bytes 6291460
  65.3 0.9 copy-start.20
  66.2 0.8 copy-start.22
  68.2 1.0 copy-start.17
  69.7 27.7 %copy-start.42 = (f32[8,64]{1,0:T(8,128)S(1)}, f32[8,64]{1,0:T(8,128)}, u32[]{:S(2)}) copy-start(f32[8,64]{1,0:T(8,128)} %copy-done.41) | copy-start | bytes 6148
  69.7 27.7 %all-to-all-start.2 = ((f32[512,4,128]{2,1,0:T(4,128)}), f32[512,4,128]{2,1,0:T(4,128)S(1)}, u32[]{:S(2)}, u32[]{:S(2)}) async-start(f32[512,4,128]{2,1,0:T(4,128)} %copy-done.17), calls=%async_computation.2 | async-start | bytes 2097152 | tf_op jit(solution)/shard_map/all_to_all | solution.py:31
  74.5 22.0 %copy-start.33 = (f32[2,8,512]{2,1,0:T(8,128)S(1)}, f32[2,8,512]{2,1,0:T(8,128)}, u32[]{:S(2)}) copy-start(f32[2,8,512]{2,1,0:T(8,128)} %copy-done.32) | copy-start | bytes 98308
  74.5 0.8 copy-start.39
  75.5 16.7 %collective-permute-start.4 = (f32[8,256]{1,0:T(8,128)S(1)}, f32[8,256]{1,0:T(8,128)S(1)}, u32[]{:S(2)}, u32[]{:S(2)}) collective-permute-start(f32[8,256]{1,0:T(8,128)S(1)} %get-tuple-element.61), channel_id=1, source_target_pairs={{0,1},{1,2},{2,3},{3,4},{4,5},{5,6},{6,7},{7,8},{8,9},{9,10},{10,1... | collective-permute-start | bytes 24584 | tf_op jit(solution)/shard_map/ppermute | solution.py:40
  76.5 10.6 %collective-permute-start.5 = (f32[8,128]{1,0:T(8,128)S(1)}, f32[8,128]{1,0:T(8,128)S(1)}, u32[]{:S(2)}, u32[]{:S(2)}) collective-permute-start(f32[8,128]{1,0:T(8,128)S(1)} %get-tuple-element.62), channel_id=1, source_target_pairs={{0,127},{1,0},{2,1},{3,2},{4,3},{5,4},{6,5},{7,6},{8,7},{9,8},{10,... | collective-permute-start | bytes 12296 | tf_op jit(solution)/shard_map/ppermute | solution.py:40
  92.2 1.0 copy-start.8
  93.2 1.0 copy-start.14
  97.4 1.6 %copy-start.4 = (bf16[128,8192]{1,0:T(8,128)(2,1)S(1)}, bf16[128,8192]{1,0:T(8,128)(2,1)}, u32[]{:S(2)}) copy-start(bf16[128,8192]{1,0:T(8,128)(2,1)} %copy-done.2) | copy-start | bytes 6291460
  99.0 0.9 copy-start.9
  100.0 0.8 copy-start.24
  100.7 18.2 %copy-start.11 = (bf16[2048,256]{1,0:T(8,128)(2,1)S(1)}, bf16[2048,256]{1,0:T(8,128)(2,1)}, u32[]{:S(2)}) copy-start(bf16[2048,256]{1,0:T(8,128)(2,1)} %copy-done.10) | copy-start | bytes 3145732
  102.4 38.3 %copy-start.25 = (f32[2,8,512]{2,1,0:T(8,128)S(1)}, f32[2,8,512]{2,1,0:T(8,128)}, u32[]{:S(2)}) copy-start(f32[2,8,512]{2,1,0:T(8,128)} %copy-done.23) | copy-start | bytes 98308
  102.4 38.3 %copy-start.27 = (f32[8,2,512]{2,1,0:T(2,128)S(1)}, f32[8,2,512]{2,1,0:T(2,128)}, u32[]{:S(2)}) copy-start(f32[8,2,512]{2,1,0:T(2,128)} %disp_ref.3) | copy-start | bytes 98308
  102.4 38.3 %copy-start.29 = (f32[8,2,512]{2,1,0:T(2,128)S(1)}, f32[8,2,512]{2,1,0:T(2,128)}, u32[]{:S(2)}) copy-start(f32[8,2,512]{2,1,0:T(2,128)} %vel_ref.3) | copy-start | bytes 98308
  102.4 38.3 %copy-start.31 = (f32[8,2,512]{2,1,0:T(2,128)S(1)}, f32[8,2,512]{2,1,0:T(2,128)}, u32[]{:S(2)}) copy-start(f32[8,2,512]{2,1,0:T(2,128)} %acc_ref.3) | copy-start | bytes 98308
  102.4 38.3 %copy-start.34 = (f32[2,8,512]{2,1,0:T(8,128)S(1)}, f32[2,8,512]{2,1,0:T(8,128)}, u32[]{:S(2)}) copy-start(f32[2,8,512]{2,1,0:T(8,128)} %copy-done.32) | copy-start | bytes 98308
  102.4 38.3 %copy-start.36 = (f32[2,8,512]{2,1,0:T(8,128)S(1)}, f32[2,8,512]{2,1,0:T(8,128)}, u32[]{:S(2)}) copy-start(f32[2,8,512]{2,1,0:T(8,128)} %copy-done.35) | copy-start | bytes 98308
  128.6 13.0 %all-to-all-start.5 = ((f32[16,8,384]{2,1,0:T(8,128)}), f32[16,8,384]{2,1,0:T(8,128)S(1)}, u32[]{:S(2)}, u32[]{:S(2)}) async-start(f32[16,8,384]{2,1,0:T(8,128)} %broadcast_in_dim.3), calls=%async_computation.5 | async-start | bytes 393216 | tf_op jit(solution)/shard_map/all_to_all | solution.py:31
  132.1 8.5 %collective-permute-start.6 = (f32[8,64]{1,0:T(8,128)S(1)}, f32[8,64]{1,0:T(8,128)S(1)}, u32[]{:S(2)}, u32[]{:S(2)}) collective-permute-start(f32[8,64]{1,0:T(8,128)S(1)} %get-tuple-element.70.z_ref), channel_id=1, source_target_pairs={{0,1},{1,2},{2,3},{3,4},{4,5},{5,6},{6,7},{7,8},{8,9},{9,10},{10,1... | collective-permute-start | bytes 6152 | tf_op jit(solution)/shard_map/ppermute | solution.py:40
  (7 other events, 4.5 us)

commit v5 on v4

--- a/solution.py
+++ b/solution.py
@@ -48,14 +48,14 @@
     return lax.dot_general(a, b, dims, preferred_element_type=f32)
 
 
-def call(body, outs, ins, scratch=(), flops=0):
+def call(body, outs, ins, scratch=(), flops=0, room=0):
     return pl.pallas_call(
         body,
         out_shape=[jax.ShapeDtypeStruct(shape, f32 if len(rest) == 0 else rest[0]) for shape, *rest in outs],
         in_specs=ins,
         out_specs=[VMEM] * len(outs),
         scratch_shapes=list(scratch),
-        compiler_params=pltpu.CompilerParams(vmem_limit_bytes=16 << 20),
+        compiler_params=pltpu.CompilerParams(vmem_limit_bytes=(60 * 1024 - room) << 10),
         cost_estimate=pl.CostEstimate(flops=flops, bytes_accessed=1 << 20, transcendentals=0),
     )
 
@@ -194,20 +194,22 @@
     select_ref[...] = jnp.where(owner == rows.astype(f32), 1.0, 0.0).astype(bf16)
 
 
+def late_body(local_ref, z_ref, modes_ref, late_ref, to_right_ref):
+    z = z_ref[...]
+    late_ref[0] = local_ref[0] + dot(z[:, :NC], modes_ref[0, NC:], NN)
+    late_ref[1] = local_ref[1] + dot(z, modes_ref[1], NN)
+    to_right_ref[...] = jnp.concatenate([z, z], axis=1)
+
+
 def out_body(
-    green_ref, image_ref, local_ref, z_ref, ghost_ref, modes_ref, gains_ref, disp_ref, vel_ref, acc_ref,
-    disp_out_ref, vel_out_ref,
+    green_ref, image_ref, late_ref, ghost_ref, modes_ref, gains_ref, disp_ref, vel_ref, acc_ref, disp_out_ref, vel_out_ref
 ):
     kappa_1, kappa_2 = gains_ref[0], gains_ref[1]
     case = lax.broadcasted_iota(jnp.int32, kappa_1.shape, 0)
     lane = lax.broadcasted_iota(jnp.int32, kappa_1.shape, 1)
     kappa_1 = jnp.sum(jnp.where(case == lane, kappa_1, 0.0), axis=1, keepdims=True)
     kappa_2 = jnp.sum(jnp.where(case == lane, kappa_2, 0.0), axis=1, keepdims=True)
-    z = z_ref[...]
-    late = [
-        local_ref[0] + dot(z[:, :NC], modes_ref[0, NC:], NN) + dot(ghost_ref[:, NC:], modes_ref[0, :NC], NN),
-        local_ref[1] + dot(z, modes_ref[1], NN),
-    ]
+    late = [late_ref[0] + dot(ghost_ref[:, NC : 2 * NC], modes_ref[0, :NC], NN), late_ref[1]]
     for s in range(2):
         disp = green_ref[s] - kappa_1 * image_ref[s] + kappa_2 * late[s]
         vel, acc = vel_ref[:, s, :], acc_ref[:, s, :]
@@ -467,20 +469,20 @@
         coarse_inverse, right_side, rr_inverse
     )
     blocks_0, coupling, to_blocks = call(
-        couple_body, [blocks_shape, ((2 * NC, 2 * LANES),), ((2 * LANES, 4 * NI),)], [SMEM] + [VMEM] * 4, flops=1 << 26
+        couple_body, [blocks_shape, ((2 * NC, 2 * LANES),), ((2 * LANES, 4 * NI),)], [SMEM] + [VMEM] * 4, flops=1 << 26, room=296
     )(device, corner_modes, right_modes, left_edge, local_0)
 
     def finish(local, z):
         mine, to_right, to_left = call(
-            edge_body, [pair, ((case_count, 2 * NI),), ((case_count, NI),)], [VMEM] * 3, flops=1 << 20
+            edge_body, [pair, ((case_count, 2 * NI),), ((case_count, NI),)], [VMEM] * 3, flops=1 << 20, room=16
         )(local, z, corner_modes)
         from_left = shifted(to_right, 1)
         from_right = shifted(to_left, -1)
-        return call(join_body, [pair, pair, blocks_shape, ((case_count, LANES),)], [VMEM] * 8, flops=1 << 26)(
+        return call(join_body, [pair, pair, blocks_shape, ((case_count, LANES),)], [VMEM] * 8, flops=1 << 26, room=16)(
             mine, from_left, from_right, z, corner_modes, right_modes, rr_inverse, to_blocks
         )
 
-    pieces, z_0 = call(first_body, [((3 * devices, 4, LANES),), z_shape], [VMEM] * 4, assembled, flops=1 << 24)(
+    pieces, z_0 = call(first_body, [((3 * devices, 4, LANES),), z_shape], [VMEM] * 4, assembled, flops=1 << 24, room=516)(
         got_1, coarse_parts, coupling, blocks_0
     )
     got_2 = exchange(pieces)
@@ -492,16 +494,19 @@
     )(basis_rows.reshape(devices, -1, rank), piece_owner.reshape(1, devices), z_0)
     green, local_1, blocks_1, sums_2 = finish(local_0, z_0)
     pieces, z_1, terms_1 = call(
-        second_body, [((4 * devices, 4, LANES),), z_shape, z_shape], [SMEM] + [VMEM] * 5, assembled, flops=1 << 24
+        second_body, [((4 * devices, 4, LANES),), z_shape, z_shape], [SMEM] + [VMEM] * 5, assembled, flops=1 << 24, room=772
     )(device, got_2, coarse_parts, coupling, blocks_1, square)
     got_3 = exchange(pieces)
     image_1, local_2, _, sums_3 = finish(local_1, z_1)
     (early,) = call(early_body, [((devices, LANES),)], [VMEM] * 3, flops=1 << 24)(select, green, image_1)
-    sent, z_2 = call(third_body, [((devices, 3, 2, LANES),), z_shape], [SMEM] + [VMEM] * 10, assembled, flops=1 << 24)(
+    sent, z_2 = call(third_body, [((devices, 3, 2, LANES),), z_shape], [SMEM] + [VMEM] * 10, assembled, flops=1 << 24, room=1028)(
         device, got_3, coarse_parts, local_2, corner_modes, right_modes, select, sums_2, sums_3, terms_1, early
     )
     got_4 = exchange(sent)
-    ghost = shifted(z_2, 1)
+    late, to_right = call(late_body, [pair, ((case_count, LANES),)], [VMEM] * 3, flops=1 << 20)(
+        local_2, z_2, corner_modes
+    )
+    ghost = shifted(to_right, 1)
     part, snapshots, gains = call(
         project_body,
         [
@@ -511,19 +516,21 @@
         ],
         [VMEM] * 2,
         flops=1 << 24,
+        room=388,
     )(got_4, basis_parts)
     near = exchange(part, NEAR)
     near = near.sum(axis=0)
     got_5 = to_everyone(near, FAR)
     disp_new, vel_new = call(
-        out_body, [(disp_now.shape,), (disp_now.shape,)], [VMEM] * 10, flops=1 << 22
-    )(green, image_1, local_2, z_2, ghost, corner_modes, gains, disp_now, vel_now, acc_now)
+        out_body, [(disp_now.shape,), (disp_now.shape,)], [VMEM] * 9, flops=1 << 22, room=8
+    )(green, image_1, late, ghost, corner_modes, gains, disp_now, vel_now, acc_now)
     scale = math.sqrt(basis_rows.shape[0] * devices)
     new_columns, projection, factor = call(
         functools.partial(finish_body, scale=scale),
         [((case_count, basis_rows.shape[0]),), ((case_count, rank),), ((case_count, LANES),)],
         [VMEM] * 4,
         flops=1 << 24,
+        room=196,
     )(got_5, got_4, basis_parts, snapshots)
     return (disp_new, vel_new, projection.T, factor[:, :case_count], new_columns)
 

time: 146 us -> 154 us (1.055)
  Pallas kernels: 19.4 us -> 51.6 us
  local copies, waits for them, and re-layouts: 29.9 us -> 7.32 us
    unnamed x88 -> x22, local copies, waits for them, and re-layouts: 28.4 us -> 5.85 us
    pallas_call x2, Pallas kernels: 2.74 us -> 7.15 us  [finish(): call(join_body, [pair, pair, blocks_shape, ((case_count, LANES),)], [VMEM...]
    pallas_call x1, Pallas kernels: 1.61 us -> 5.11 us  [shards(): call(pre_body, [((4 * NC, coarse_total), bf16), pair], [VMEM] * 3, flops=...]
    pallas_call x2, Pallas kernels: 0.41 us -> 3.64 us  [finish(): call(edge_body, [pair, ((case_count, 2 * NI),), ((case_count, NI),)], [VM...]
    pallas_call x1, Pallas kernels: 1.64 us -> 4.51 us  [shards(): call(third_body, [((devices, 3, 2, LANES),), z_shape], [SMEM] + [VMEM] *...]
    pallas_call x1, Pallas kernels: 1.07 us -> 3.91 us  [shards(): call(second_body, [((4 * devices, 4, LANES),), z_shape, z_shape], [SMEM]...]
    pallas_call x1 -> x2, Pallas kernels: 0.91 us -> 3.73 us  [the longest x1 1.92 us: shards(): call(out_body, [(disp_now.shape,), (disp_now.shape,)], [VMEM] * 9, flops=...]
    pallas_call x1, Pallas kernels: 1.02 us -> 3.59 us  [shards(): call(first_body, [((3 * devices, 4, LANES),), z_shape], [VMEM] * 4, assem...]
  transfers between devices with their start and end apart: 11 -> 11, of which waited for: 5 -> 4; matrix products, arithmetic and copies ran while one was open for 1% -> 1% of each run, Pallas kernels for 8% -> 20%
where the time goes in v5:
time: 154 us
  Pallas kernels  51.6 us (34%)
  starting transfers between devices  47.7 us (31%)
  blocking collectives  26 us (17%)
  waiting for transfers between devices  20.2 us (13%)
  local copies, waits for them, and re-layouts  7.32 us (5%)
    all_to_all x2, blocking collectives, exchange(): return lax.all_to_all(pieces, axes, split_axis=0, concat_axis=0, tiled=True)  26 us
    all_to_all x4, starting transfers between devices, exchange(): return lax.all_to_all(pieces, axes, split_axis=0, concat_axis=0, tiled=True)  25.5 us
    ppermute x7, starting transfers between devices, shifted(): lax.ppermute(array, AXES, [(i, (i + by) % count) for i in range(count)])  22.3 us
    ppermute x7, waiting for transfers between devices, shifted(): lax.ppermute(array, AXES, [(i, (i + by) % count) for i in range(count)])  20.2 us
    pallas_call x2, Pallas kernels, finish(): call(join_body, [pair, pair, blocks_shape, ((case_count, LANES),)], [VMEM...  7.15 us
    pallas_call x1, Pallas kernels, shards(): call(prep_body, [((2 * basis_rows.shape[0], rank), bf16), ((devices, 4, L...  6.08 us
    unnamed x22, local copies, waits for them, and re-layouts  5.85 us
    pallas_call x1, Pallas kernels, shards(): call(pre_body, [((4 * NC, coarse_total), bf16), pair], [VMEM] * 3, flops=...  5.11 us
  transfers between devices with their start and end apart: 11, of which 4 were waited for; matrix products, arithmetic and copies ran while one was open for 1% of the time, Pallas kernels for 20%

profile of v5, /device:TPU:0, one launch (start us, length us, event | category | flops | bytes accessed | tf_op | source)
XLA Modules:
  0.0 153.6 jit_solution(11646817293035387552)
XLA Ops:
  0.6 2.4 %shard_map.137 = (f32[128,8,128]{2,1,0:T(8,128)}, f32[2,8,512]{2,1,0:T(8,128)}) custom-call(s32[1]{0:T(128)} %bitcast.device_ref, f32[8,2,512]{2,1,0:T(2,128)} %load_ref.1, f32[2,512]{1,0:T(2,128)} %inertia_ref.1, f32[8,2,512]{2,1,0:T(2,128)} %disp_ref.3, f32[8,2,512]{2,1,0:T(2,128)} %vel_ref.3, f32[8,2,512]{2,1,0:T(2,128)} %acc_ref.3, f32[2,64,512]{2,1,0:T(8,128)} %modes_ref.17), custom_call_target="tpu_custom_call" | custom-call | bytes 1048576 | tf_op jit(solution)/shard_map/pallas_call | solution.py:462
  3.0 11.2 %all-to-all-start = ((f32[128,8,128]{2,1,0:T(8,128)}), f32[128,8,128]{2,1,0:T(8,128)S(1)}, u32[]{:S(2)}, u32[]{:S(2)}) async-start(f32[128,8,128]{2,1,0:T(8,128)} %get-tuple-element.47), calls=%async_computation | async-start | bytes 1048576 | tf_op jit(solution)/shard_map/all_to_all | solution.py:31
  14.2 7.1 %collective-permute-start = (f32[2,64,512]{2,1,0:T(8,128)}, f32[2,64,512]{2,1,0:T(8,128)S(1)}, u32[]{:S(2)}, u32[]{:S(2)}) collective-permute-start(f32[2,64,512]{2,1,0:T(8,128)} %modes_ref.17), channel_id=1, source_target_pairs={{0,127},{1,0},{2,1},{3,2},{4,3},{5,4},{6,5},{7,6},{8,7},{9,8},{10,... | collective-permute-start | bytes 786440 | tf_op jit(solution)/shard_map/ppermute | solution.py:40
  21.3 0.8 slice_bitcast_fusion
  22.1 0.0 collective-permute-start.1
  22.1 5.1 %shard_map.138 = (bf16[128,8192]{1,0:T(8,128)(2,1)}, f32[2,8,512]{2,1,0:T(8,128)}) custom-call(f32[64,8192]{1,0:T(8,128)} %matrix_ref.1, f32[2,8,512]{2,1,0:T(8,128)} %get-tuple-element.45.right_ref, f32[2,512,512]{2,1,0:T(8,128)} %rr_ref.5), custom_call_target="tpu_custom_call" | custom-call | flops 67108864 | bytes 1048576 | tf_op jit(solution)/shard_map/pallas_call | solution.py:468
  27.2 3.7 %collective-permute-done.1.left_ref = f32[64,128]{1,0:T(8,128)S(1)} collective-permute-done((f32[64,128]{1,0:T(8,128)S(1)}, f32[64,128]{1,0:T(8,128)S(1)}, u32[]{:S(2)}, u32[]{:S(2)}) %collective-permute-start.1) | collective-permute-done | bytes 32800 | tf_op jit(solution)/shard_map/ppermute | solution.py:40
  30.9 0.0 collective-permute-done.right_ref
  30.9 0.6 copy-done.5
  31.5 0.1 copy-done.1
  31.6 2.8 %shard_map.139 = (f32[8,256]{1,0:T(8,128)}, f32[64,256]{1,0:T(8,128)}, f32[256,512]{1,0:T(8,128)}) custom-call(s32[1]{0:T(128)} %bitcast.device_ref, f32[2,64,512]{2,1,0:T(8,128)} %modes_ref.17, f32[2,64,512]{2,1,0:T(8,128)} %copy-done.1, f32[64,128]{1,0:T(8,128)} %copy-done.5, f32[2,8,512]{2,1,0:T(8,128)} %get-tuple-element.46.local_ref), custom_call_target="tpu_custom_call" | custom-call | flops 67108864 | bytes 1048576 | tf_op jit(solution)/shard_map/pallas_call | solution.py:471
  34.4 0.0 all-to-all-done.got_ref
  34.4 0.8 copy-done.3
  35.2 3.6 %shard_map.140 = (f32[384,4,128]{2,1,0:T(4,128)}, f32[8,64]{1,0:T(8,128)}) custom-call(f32[128,8,128]{2,1,0:T(8,128)} %copy-done.3, bf16[128,8192]{1,0:T(8,128)(2,1)} %get-tuple-element.48.parts_ref, f32[64,256]{1,0:T(8,128)} %get-tuple-element.49.coupling_ref, f32[8,256]{1,0:T(8,128)} %get-tuple-element.50.local_ref), custom_call_target="tpu_custom_call" | custom-call | flops 16777216 | bytes 1048576 | tf_op jit(solution)/shard_map/pallas_call | solution.py:485
  38.8 5.8 %all-to-all-start.1 = ((f32[384,4,128]{2,1,0:T(4,128)}), f32[384,4,128]{2,1,0:T(4,128)S(1)}, u32[]{:S(2)}, u32[]{:S(2)}) async-start(f32[384,4,128]{2,1,0:T(4,128)} %get-tuple-element.58), calls=%async_computation.1 | async-start | bytes 1572864 | tf_op jit(solution)/shard_map/all_to_all | solution.py:31
  44.6 1.8 %shard_map.141 = (f32[2,8,512]{2,1,0:T(8,128)}, f32[8,256]{1,0:T(8,128)}, f32[8,128]{1,0:T(8,128)}) custom-call(f32[2,8,512]{2,1,0:T(8,128)} %get-tuple-element.46.local_ref, f32[8,64]{1,0:T(8,128)} %get-tuple-element.51.z_ref.after_ref, f32[2,64,512]{2,1,0:T(8,128)} %modes_ref.17), custom_call_target="tpu_custom_call" | custom-call | flops 1048576 | bytes 1048576 | tf_op jit(solution)/shard_map/pallas_call | solution.py:476
  46.4 1.0 collective-permute-start.2
  47.4 6.2 %collective-permute-start.3 = (f32[8,128]{1,0:T(8,128)}, f32[8,128]{1,0:T(8,128)S(1)}, u32[]{:S(2)}, u32[]{:S(2)}) collective-permute-start(f32[8,128]{1,0:T(8,128)} %get-tuple-element.54), channel_id=1, source_target_pairs={{0,127},{1,0},{2,1},{3,2},{4,3},{5,4},{6,5},{7,6},{8,7},{9,8},{10,... | collective-permute-start | bytes 12296 | tf_op jit(solution)/shard_map/ppermute | solution.py:40
  53.6 6.1 %shard_map.143 = (bf16[2048,256]{1,0:T(8,128)(2,1)}, f32[128,4,128]{2,1,0:T(4,128)}, bf16[128,512]{1,0:T(8,128)(2,1)}) custom-call(f32[128,8,256]{2,1,0:T(8,128)} %bitcast.7, s32[1,128]{1,0:T(1,128)} %bitcast.8, f32[8,64]{1,0:T(8,128)} %get-tuple-element.51.z_ref.after_ref), custom_call_target="tpu_custom_call" | custom-call | flops 67108864 | bytes 1048576 | tf_op jit(solution)/shard_map/pallas_call | solution.py:489
  59.7 0.0 copy-start.6
  59.7 0.6 copy-done.8
  60.3 0.0 copy-done.6
  60.3 3.6 %shard_map.142 = (f32[2,8,512]{2,1,0:T(8,128)}, f32[2,8,512]{2,1,0:T(8,128)}, f32[8,256]{1,0:T(8,128)}, f32[8,128]{1,0:T(8,128)}) custom-call(f32[2,8,512]{2,1,0:T(8,128)} %get-tuple-element.52.mine_ref, f32[8,256]{1,0:T(8,128)} %copy-done.6, f32[8,128]{1,0:T(8,128)} %copy-done.8, f32[8,64]{1,0:T(8,128)} %get-tuple-element.51.z_ref.after_ref, ...), custom_call_target="tpu_custom_call" | custom-call | flops 67108864 | bytes 1048576 | tf_op jit(solution)/shard_map/pallas_call | solution.py:481
  63.9 0.9 copy-done.2
  64.8 3.9 %shard_map.144 = (f32[512,4,128]{2,1,0:T(4,128)}, f32[8,64]{1,0:T(8,128)}, f32[8,64]{1,0:T(8,128)}) custom-call(s32[1]{0:T(128)} %bitcast.device_ref, f32[384,4,128]{2,1,0:T(4,128)} %copy-done.2, bf16[128,8192]{1,0:T(8,128)(2,1)} %get-tuple-element.48.parts_ref, f32[64,256]{1,0:T(8,128)} %get-tuple-element.49.coupling_ref, ...), custom_call_target="tpu_custom_call" | custom-call | flops 16777216 | bytes 1048576 | tf_op jit(solution)/shard_map/pallas_call | solution.py:496
  68.7 4.7 %all-to-all-start.2 = ((f32[512,4,128]{2,1,0:T(4,128)}), f32[512,4,128]{2,1,0:T(4,128)S(1)}, u32[]{:S(2)}, u32[]{:S(2)}) async-start(f32[512,4,128]{2,1,0:T(4,128)} %get-tuple-element.67), calls=%async_computation.2 | async-start | bytes 2097152 | tf_op jit(solution)/shard_map/all_to_all | solution.py:31
  73.4 1.8 %shard_map.145 = (f32[2,8,512]{2,1,0:T(8,128)}, f32[8,256]{1,0:T(8,128)}, f32[8,128]{1,0:T(8,128)}) custom-call(f32[2,8,512]{2,1,0:T(8,128)} %get-tuple-element.57.local_ref, f32[8,64]{1,0:T(8,128)} %get-tuple-element.61.z_ref, f32[2,64,512]{2,1,0:T(8,128)} %modes_ref.17), custom_call_target="tpu_custom_call" | custom-call | flops 1048576 | bytes 1048576 | tf_op jit(solution)/shard_map/pallas_call | solution.py:476
  75.2 1.0 collective-permute-start.4
  76.2 6.2 %collective-permute-start.5 = (f32[8,128]{1,0:T(8,128)}, f32[8,128]{1,0:T(8,128)S(1)}, u32[]{:S(2)}, u32[]{:S(2)}) collective-permute-start(f32[8,128]{1,0:T(8,128)} %get-tuple-element.64), channel_id=1, source_target_pairs={{0,127},{1,0},{2,1},{3,2},{4,3},{5,4},{6,5},{7,6},{8,7},{9,8},{10,... | collective-permute-start | bytes 12296 | tf_op jit(solution)/shard_map/ppermute | solution.py:40
  82.4 3.6 %collective-permute-done.5.from_right_ref = f32[8,128]{1,0:T(8,128)S(1)} collective-permute-done((f32[8,128]{1,0:T(8,128)}, f32[8,128]{1,0:T(8,128)S(1)}, u32[]{:S(2)}, u32[]{:S(2)}) %collective-permute-start.5) | collective-permute-done | bytes 4128 | tf_op jit(solution)/shard_map/ppermute | solution.py:40
  86.0 5.1 %collective-permute-done.4.from_left_ref = f32[8,256]{1,0:T(8,128)S(1)} collective-permute-done((f32[8,256]{1,0:T(8,128)}, f32[8,256]{1,0:T(8,128)S(1)}, u32[]{:S(2)}, u32[]{:S(2)}) %collective-permute-start.4) | collective-permute-done | bytes 8224 | tf_op jit(solution)/shard_map/ppermute | solution.py:40
  91.1 0.6 copy-done.7
  91.7 3.6 %shard_map.146 = (f32[2,8,512]{2,1,0:T(8,128)}, f32[2,8,512]{2,1,0:T(8,128)}, f32[8,256]{1,0:T(8,128)}, f32[8,128]{1,0:T(8,128)}) custom-call(f32[2,8,512]{2,1,0:T(8,128)} %get-tuple-element.62.mine_ref, f32[8,256]{1,0:T(8,128)} %copy-done.7, f32[8,128]{1,0:T(8,128)} %copy-done.9, f32[8,64]{1,0:T(8,128)} %get-tuple-element.61.z_ref, ...), custom_call_target="tpu_custom_call" | custom-call | flops 67108864 | bytes 1048576 | tf_op jit(solution)/shard_map/pallas_call | solution.py:481
  95.2 1.8 %shard_map.147.early_ref = f32[128,128]{1,0:T(8,128)} custom-call(bf16[128,512]{1,0:T(8,128)(2,1)} %get-tuple-element.68.select_ref, f32[2,8,512]{2,1,0:T(8,128)} %get-tuple-element.56.green_ref, f32[2,8,512]{2,1,0:T(8,128)} %get-tuple-element.65.image_ref), custom_call_target="tpu_custom_call" | custom-call | flops 16777216 | bytes 1048576 | tf_op jit(solution)/shard_map/pallas_call | solution.py:501
  97.1 1.0 copy-done
  98.1 4.5 %shard_map.148 = (f32[128,3,2,128]{3,2,1,0:T(2,128)}, f32[8,64]{1,0:T(8,128)}) custom-call(s32[1]{0:T(128)} %bitcast.device_ref, f32[512,4,128]{2,1,0:T(4,128)} %copy-done, bf16[128,8192]{1,0:T(8,128)(2,1)} %get-tuple-element.48.parts_ref, f32[2,8,512]{2,1,0:T(8,128)} %get-tuple-element.66.local_ref, f32[2,64,512]{2,1,0:T(8,128)} %modes_ref.17, ...), custom_call_target="tpu_custom_call" | custom-call | flops 16777216 | bytes 1048576 | tf_op jit(solution)/shard_map/pallas_call | solution.py:502
  102.6 17.3 %all_to_all.30.got_ref.square_ref = f32[128,3,2,128]{3,2,1,0:T(2,128)} all-to-all(f32[128,3,2,128]{3,2,1,0:T(2,128)} %get-tuple-element.75), channel_id=1, replica_groups=mesh['sub_0'=4,'sub_1'=4,'sub_2'=2,'grp'=4] {'sub_0','sub_1','sub_2','grp'}, dimensions={0} | all-to-all | bytes 786432 | tf_op jit(solution)/shard_map/all_to_all | solution.py:31
  119.9 2.8 %shard_map.150 = (f32[8,8,384]{2,1,0:T(8,128)}, f32[8,1024]{1,0:T(8,128)}, f32[2,8,128]{2,1,0:T(8,128)}) custom-call(f32[128,3,2,128]{3,2,1,0:T(2,128)} %all_to_all.30.got_ref.square_ref, bf16[2048,256]{1,0:T(8,128)(2,1)} %get-tuple-element.76.basis_ref), custom_call_target="tpu_custom_call" | custom-call | flops 16777216 | bytes 1048576 | tf_op jit(solution)/shard_map/pallas_call | solution.py:510
  122.7 8.7 %all_to_all.31 = f32[8,8,384]{2,1,0:T(8,128)S(1)} all-to-all(f32[8,8,384]{2,1,0:T(8,128)} %get-tuple-element.80), channel_id=1, replica_groups=mesh['sub_0'=4,'sub_1'=4,'sub_2'=2,'grp'=4] {'sub_2','grp'}, dimensions={0} | all-to-all | bytes 196608 | tf_op jit(solution)/shard_map/all_to_all | solution.py:31
  131.3 0.7 broadcast_in_dim.3
  132.0 3.8 %all-to-all-start.5 = ((f32[16,8,384]{2,1,0:T(8,128)}), f32[16,8,384]{2,1,0:T(8,128)S(1)}, u32[]{:S(2)}, u32[]{:S(2)}) async-start(f32[16,8,384]{2,1,0:T(8,128)} %broadcast_in_dim.3), calls=%async_computation.5 | async-start | bytes 393216 | tf_op jit(solution)/shard_map/all_to_all | solution.py:31
  135.8 1.8 %shard_map.149 = (f32[2,8,512]{2,1,0:T(8,128)}, f32[8,128]{1,0:T(8,128)}) custom-call(f32[2,8,512]{2,1,0:T(8,128)} %get-tuple-element.66.local_ref, f32[8,64]{1,0:T(8,128)} %get-tuple-element.72.z_ref, f32[2,64,512]{2,1,0:T(8,128)} %modes_ref.17), custom_call_target="tpu_custom_call" | custom-call | flops 1048576 | bytes 1048576 | tf_op jit(solution)/shard_map/pallas_call | solution.py:506
  137.6 0.8 collective-permute-start.6
  138.5 7.8 %collective-permute-done.6.ghost_ref = f32[8,128]{1,0:T(8,128)S(1)} collective-permute-done((f32[8,128]{1,0:T(8,128)}, f32[8,128]{1,0:T(8,128)S(1)}, u32[]{:S(2)}, u32[]{:S(2)}) %collective-permute-start.6) | collective-permute-done | bytes 4128 | tf_op jit(solution)/shard_map/ppermute | solution.py:40
  146.3 0.6 copy-done.10
  146.9 1.9 %shard_map.151 = (f32[8,2,512]{2,1,0:T(2,128)}, f32[8,2,512]{2,1,0:T(2,128)}) custom-call(f32[2,8,512]{2,1,0:T(8,128)} %get-tuple-element.56.green_ref, f32[2,8,512]{2,1,0:T(8,128)} %get-tuple-element.65.image_ref, f32[2,8,512]{2,1,0:T(8,128)} %get-tuple-element.73.late_ref, f32[8,128]{1,0:T(8,128)} %copy-done.10, f32[2,64,512]{2,1,0:T(8,128)} %modes_ref.17, ...), custom_call_target="tpu_custom_call" | custom-call | flops 4194304 | bytes 1048576 | tf_op jit(solution)/shard_map/pallas_call | solution.py:524
  148.8 0.7 copy-done.4
  149.5 4.1 %shard_map.152 = (f32[8,1024]{1,0:T(8,128)}, f32[8,256]{1,0:T(8,128)}, f32[8,128]{1,0:T(8,128)}) custom-call(f32[16,8,384]{2,1,0:T(8,128)} %copy-done.4, f32[128,3,2,128]{3,2,1,0:T(2,128)} %all_to_all.30.got_ref.square_ref, bf16[2048,256]{1,0:T(8,128)(2,1)} %get-tuple-element.76.basis_ref, f32[8,1024]{1,0:T(8,128)} %get-tuple-element.81.rows_ref), custom_call_target="tpu_custom_call" | custom-call | flops 16777216 | bytes 1048576 | tf_op jit(solution)/shard_map/pallas_call | solution.py:528
  (17 shorter events, 0.0 us)
Async XLA Ops:
  3.0 31.3 %all-to-all-start = ((f32[128,8,128]{2,1,0:T(8,128)}), f32[128,8,128]{2,1,0:T(8,128)S(1)}, u32[]{:S(2)}, u32[]{:S(2)}) async-start(f32[128,8,128]{2,1,0:T(8,128)} %get-tuple-element.47), calls=%async_computation | async-start | bytes 1048576 | tf_op jit(solution)/shard_map/all_to_all | solution.py:31
  14.2 16.7 %collective-permute-start = (f32[2,64,512]{2,1,0:T(8,128)}, f32[2,64,512]{2,1,0:T(8,128)S(1)}, u32[]{:S(2)}, u32[]{:S(2)}) collective-permute-start(f32[2,64,512]{2,1,0:T(8,128)} %modes_ref.17), channel_id=1, source_target_pairs={{0,127},{1,0},{2,1},{3,2},{4,3},{5,4},{6,5},{7,6},{8,7},{9,8},{10,... | collective-permute-start | bytes 786440 | tf_op jit(solution)/shard_map/ppermute | solution.py:40
  22.1 8.8 %collective-permute-start.1 = (f32[64,128]{1,0:T(8,128)S(1)}, f32[64,128]{1,0:T(8,128)S(1)}, u32[]{:S(2)}, u32[]{:S(2)}) collective-permute-start(f32[64,128]{1,0:T(8,128)S(1)} %slice_bitcast_fusion), channel_id=1, source_target_pairs={{0,1},{1,2},{2,3},{3,4},{4,5},{5,6},{6,7},{7,8},{8,9},{9,10},{10,1... | collective-permute-start | bytes 98312 | tf_op jit(solution)/shard_map/ppermute | solution.py:40
  30.9 0.6 copy-start.5
  30.9 0.7 copy-start.1
  34.4 0.8 copy-start.3
  38.8 25.1 %all-to-all-start.1 = ((f32[384,4,128]{2,1,0:T(4,128)}), f32[384,4,128]{2,1,0:T(4,128)S(1)}, u32[]{:S(2)}, u32[]{:S(2)}) async-start(f32[384,4,128]{2,1,0:T(4,128)} %get-tuple-element.58), calls=%async_computation.1 | async-start | bytes 1572864 | tf_op jit(solution)/shard_map/all_to_all | solution.py:31
  46.4 13.3 %collective-permute-start.2 = (f32[8,256]{1,0:T(8,128)}, f32[8,256]{1,0:T(8,128)S(1)}, u32[]{:S(2)}, u32[]{:S(2)}) collective-permute-start(f32[8,256]{1,0:T(8,128)} %get-tuple-element.53), channel_id=1, source_target_pairs={{0,1},{1,2},{2,3},{3,4},{4,5},{5,6},{6,7},{7,8},{8,9},{9,10},{10,1... | collective-permute-start | bytes 24584 | tf_op jit(solution)/shard_map/ppermute | solution.py:40
  47.4 12.3 %collective-permute-start.3 = (f32[8,128]{1,0:T(8,128)}, f32[8,128]{1,0:T(8,128)S(1)}, u32[]{:S(2)}, u32[]{:S(2)}) collective-permute-start(f32[8,128]{1,0:T(8,128)} %get-tuple-element.54), channel_id=1, source_target_pairs={{0,127},{1,0},{2,1},{3,2},{4,3},{5,4},{6,5},{7,6},{8,7},{9,8},{10,... | collective-permute-start | bytes 12296 | tf_op jit(solution)/shard_map/ppermute | solution.py:40
  59.7 0.6 copy-start.8
  59.7 0.6 copy-start.6
  63.8 0.9 copy-start.2
  68.7 28.4 %all-to-all-start.2 = ((f32[512,4,128]{2,1,0:T(4,128)}), f32[512,4,128]{2,1,0:T(4,128)S(1)}, u32[]{:S(2)}, u32[]{:S(2)}) async-start(f32[512,4,128]{2,1,0:T(4,128)} %get-tuple-element.67), calls=%async_computation.2 | async-start | bytes 2097152 | tf_op jit(solution)/shard_map/all_to_all | solution.py:31
  75.2 15.9 %collective-permute-start.4 = (f32[8,256]{1,0:T(8,128)}, f32[8,256]{1,0:T(8,128)S(1)}, u32[]{:S(2)}, u32[]{:S(2)}) collective-permute-start(f32[8,256]{1,0:T(8,128)} %get-tuple-element.63), channel_id=1, source_target_pairs={{0,1},{1,2},{2,3},{3,4},{4,5},{5,6},{6,7},{7,8},{8,9},{9,10},{10,1... | collective-permute-start | bytes 24584 | tf_op jit(solution)/shard_map/ppermute | solution.py:40
  76.2 9.8 %collective-permute-start.5 = (f32[8,128]{1,0:T(8,128)}, f32[8,128]{1,0:T(8,128)S(1)}, u32[]{:S(2)}, u32[]{:S(2)}) collective-permute-start(f32[8,128]{1,0:T(8,128)} %get-tuple-element.64), channel_id=1, source_target_pairs={{0,127},{1,0},{2,1},{3,2},{4,3},{5,4},{6,5},{7,6},{8,7},{9,8},{10,... | collective-permute-start | bytes 12296 | tf_op jit(solution)/shard_map/ppermute | solution.py:40
  86.0 5.1 %copy-start.9 = (f32[8,128]{1,0:T(8,128)}, f32[8,128]{1,0:T(8,128)S(1)}, u32[]{:S(2)}) copy-start(f32[8,128]{1,0:T(8,128)S(1)} %collective-permute-done.5.from_right_ref) | copy-start | bytes 12292
  91.1 0.6 copy-start.7
  97.1 1.0 copy-start
  132.0 16.8 %all-to-all-start.5 = ((f32[16,8,384]{2,1,0:T(8,128)}), f32[16,8,384]{2,1,0:T(8,128)S(1)}, u32[]{:S(2)}, u32[]{:S(2)}) async-start(f32[16,8,384]{2,1,0:T(8,128)} %broadcast_in_dim.3), calls=%async_computation.5 | async-start | bytes 393216 | tf_op jit(solution)/shard_map/all_to_all | solution.py:31
  137.6 8.7 %collective-permute-start.6 = (f32[8,128]{1,0:T(8,128)}, f32[8,128]{1,0:T(8,128)S(1)}, u32[]{:S(2)}, u32[]{:S(2)}) collective-permute-start(f32[8,128]{1,0:T(8,128)} %get-tuple-element.74), channel_id=1, source_target_pairs={{0,1},{1,2},{2,3},{3,4},{4,5},{5,6},{6,7},{7,8},{8,9},{9,10},{10,1... | collective-permute-start | bytes 12296 | tf_op jit(solution)/shard_map/ppermute | solution.py:40
  146.3 0.6 copy-start.10
  148.8 0.7 copy-start.4

commit v6 on v4

--- a/solution.py
+++ b/solution.py
@@ -48,14 +48,14 @@
     return lax.dot_general(a, b, dims, preferred_element_type=f32)
 
 
-def call(body, outs, ins, scratch=(), flops=0):
+def call(body, outs, ins, scratch=(), flops=0, grant=16000):
     return pl.pallas_call(
         body,
         out_shape=[jax.ShapeDtypeStruct(shape, f32 if len(rest) == 0 else rest[0]) for shape, *rest in outs],
         in_specs=ins,
         out_specs=[VMEM] * len(outs),
         scratch_shapes=list(scratch),
-        compiler_params=pltpu.CompilerParams(vmem_limit_bytes=16 << 20),
+        compiler_params=pltpu.CompilerParams(vmem_limit_bytes=grant << 10),
         cost_estimate=pl.CostEstimate(flops=flops, bytes_accessed=1 << 20, transcendentals=0),
     )
 
@@ -194,22 +194,23 @@
     select_ref[...] = jnp.where(owner == rows.astype(f32), 1.0, 0.0).astype(bf16)
 
 
+def late_body(local_ref, z_ref, ghost_ref, modes_ref, late_ref):
+    z = z_ref[...]
+    ghost = ghost_ref[...][:, NC:]
+    late_ref[0] = local_ref[0] + dot(z[:, :NC], modes_ref[0, NC:], NN) + dot(ghost, modes_ref[0, :NC], NN)
+    late_ref[1] = local_ref[1] + dot(z, modes_ref[1], NN)
+
+
 def out_body(
-    green_ref, image_ref, local_ref, z_ref, ghost_ref, modes_ref, gains_ref, disp_ref, vel_ref, acc_ref,
-    disp_out_ref, vel_out_ref,
+    green_ref, image_ref, late_ref, gains_ref, disp_ref, vel_ref, acc_ref, disp_out_ref, vel_out_ref
 ):
     kappa_1, kappa_2 = gains_ref[0], gains_ref[1]
     case = lax.broadcasted_iota(jnp.int32, kappa_1.shape, 0)
     lane = lax.broadcasted_iota(jnp.int32, kappa_1.shape, 1)
     kappa_1 = jnp.sum(jnp.where(case == lane, kappa_1, 0.0), axis=1, keepdims=True)
     kappa_2 = jnp.sum(jnp.where(case == lane, kappa_2, 0.0), axis=1, keepdims=True)
-    z = z_ref[...]
-    late = [
-        local_ref[0] + dot(z[:, :NC], modes_ref[0, NC:], NN) + dot(ghost_ref[:, NC:], modes_ref[0, :NC], NN),
-        local_ref[1] + dot(z, modes_ref[1], NN),
-    ]
     for s in range(2):
-        disp = green_ref[s] - kappa_1 * image_ref[s] + kappa_2 * late[s]
+        disp = green_ref[s] - kappa_1 * image_ref[s] + kappa_2 * late_ref[s]
         vel, acc = vel_ref[:, s, :], acc_ref[:, s, :]
         accel = (
             (disp - disp_ref[:, s, :]) * (1.0 / (newmark_beta * time_step * time_step))
@@ -303,17 +304,15 @@
     return [jnp.where(lane % 4 == o, field, 0.0) for o in range(4)]
 
 
-def early_body(select_ref, green_ref, image_ref, chosen_ref):
-    rows = []
-    for ref in (green_ref, image_ref):
-        for s in range(2):
-            rows += by_offset(ref[s])
+def early_body(select_ref, green_ref, chosen_ref):
+    rows = by_offset(green_ref[0]) + by_offset(green_ref[1])
+    rows.append(jnp.zeros((HALF, green_ref.shape[2]), f32))
     chosen_ref[...] = choose_rows(select_ref, jnp.concatenate(rows, axis=0))
 
 
 def third_body(
     device_ref, got_ref, parts_ref, local_ref, modes_ref, right_ref, select_ref, sums_2_ref, sums_3_ref, terms_ref,
-    early_ref,
+    image_ref, early_ref,
     sent_ref, z_ref, assembled_ref,
 ):
     assemble_packed(got_ref, assembled_ref, 4)
@@ -341,7 +340,8 @@
     for k in range(4):
         placed = placed + jnp.where(lane == 96 + 8 * k + case, parts[k], 0.0)
     late = late + jnp.sum(placed, axis=0, keepdims=True)
-    sent_ref[:, 0, 0, :] = early_ref[...]
+    rows = [jnp.zeros((HALF, y_0.shape[1]), f32)] + by_offset(image_ref[0]) + by_offset(image_ref[1])
+    sent_ref[:, 0, 0, :] = early_ref[...] + choose_rows(select_ref, jnp.concatenate(rows, axis=0))
     sent_ref[:, 0, 1, :] = late
     sent_ref[:, 1] = jnp.broadcast_to(square[None, 0:2], (late.shape[0], 2, LANES))
     sent_ref[:, 2] = jnp.broadcast_to(square[None, 2:4], (late.shape[0], 2, LANES))
@@ -457,12 +457,12 @@
     blocks_shape = ((case_count, 2 * LANES),)
     assembled = [pltpu.VMEM((case_count, coarse_total), f32)]
 
-    start, right_side = call(start_body, [((devices, case_count, LANES),), pair], [SMEM] + [VMEM] * 6)(
+    start, right_side = call(start_body, [((devices, case_count, LANES),), pair], [SMEM] + [VMEM] * 6, grant=60 * 1024)(
         device, load_next, inertia, disp_now, vel_now, acc_now, corner_modes
     )
     got_1 = exchange(start)
+    left_edge = shifted(corner_modes[1, :, last:], 1)
     right_modes = shifted(corner_modes, -1)
-    left_edge = shifted(corner_modes[1, :, last:], 1)
     coarse_parts, local_0 = call(pre_body, [((4 * NC, coarse_total), bf16), pair], [VMEM] * 3, flops=1 << 26)(
         coarse_inverse, right_side, rr_inverse
     )
@@ -476,7 +476,7 @@
         )(local, z, corner_modes)
         from_left = shifted(to_right, 1)
         from_right = shifted(to_left, -1)
-        return call(join_body, [pair, pair, blocks_shape, ((case_count, LANES),)], [VMEM] * 8, flops=1 << 26)(
+        return call(join_body, [pair, pair, blocks_shape, ((case_count, LANES),)], [VMEM] * 8, flops=1 << 26, grant=60 * 1024)(
             mine, from_left, from_right, z, corner_modes, right_modes, rr_inverse, to_blocks
         )
 
@@ -489,19 +489,21 @@
         [((2 * basis_rows.shape[0], rank), bf16), ((devices, 4, LANES),), ((devices, unknowns), bf16)],
         [VMEM, VMEM, VMEM],
         flops=1 << 26,
+        grant=60 * 1024,
     )(basis_rows.reshape(devices, -1, rank), piece_owner.reshape(1, devices), z_0)
     green, local_1, blocks_1, sums_2 = finish(local_0, z_0)
     pieces, z_1, terms_1 = call(
-        second_body, [((4 * devices, 4, LANES),), z_shape, z_shape], [SMEM] + [VMEM] * 5, assembled, flops=1 << 24
+        second_body, [((4 * devices, 4, LANES),), z_shape, z_shape], [SMEM] + [VMEM] * 5, assembled, flops=1 << 24, grant=60 * 1024
     )(device, got_2, coarse_parts, coupling, blocks_1, square)
     got_3 = exchange(pieces)
     image_1, local_2, _, sums_3 = finish(local_1, z_1)
-    (early,) = call(early_body, [((devices, LANES),)], [VMEM] * 3, flops=1 << 24)(select, green, image_1)
-    sent, z_2 = call(third_body, [((devices, 3, 2, LANES),), z_shape], [SMEM] + [VMEM] * 10, assembled, flops=1 << 24)(
-        device, got_3, coarse_parts, local_2, corner_modes, right_modes, select, sums_2, sums_3, terms_1, early
+    (early,) = call(early_body, [((devices, LANES),)], [VMEM] * 2, flops=1 << 24)(select, green)
+    sent, z_2 = call(third_body, [((devices, 3, 2, LANES),), z_shape], [SMEM] + [VMEM] * 11, assembled, flops=1 << 24, grant=60 * 1024)(
+        device, got_3, coarse_parts, local_2, corner_modes, right_modes, select, sums_2, sums_3, terms_1, image_1, early
     )
     got_4 = exchange(sent)
     ghost = shifted(z_2, 1)
+    (late,) = call(late_body, [pair], [VMEM] * 4, flops=1 << 20)(local_2, z_2, ghost, corner_modes)
     part, snapshots, gains = call(
         project_body,
         [
@@ -516,8 +518,8 @@
     near = near.sum(axis=0)
     got_5 = to_everyone(near, FAR)
     disp_new, vel_new = call(
-        out_body, [(disp_now.shape,), (disp_now.shape,)], [VMEM] * 10, flops=1 << 22
-    )(green, image_1, local_2, z_2, ghost, corner_modes, gains, disp_now, vel_now, acc_now)
+        out_body, [(disp_now.shape,), (disp_now.shape,)], [VMEM] * 7, flops=1 << 22
+    )(green, image_1, late, gains, disp_now, vel_now, acc_now)
     scale = math.sqrt(basis_rows.shape[0] * devices)
     new_columns, projection, factor = call(
         functools.partial(finish_body, scale=scale),

time: 146 us -> 139 us (0.952)
  local copies, waits for them, and re-layouts: 29.9 us -> 11.2 us
  Pallas kernels: 19.4 us -> 33 us
  waiting for transfers between devices: 21.7 us -> 20.1 us
    unnamed x88 -> x62, local copies, waits for them, and re-layouts: 28.4 us -> 9.73 us
    pallas_call x2, Pallas kernels: 2.74 us -> 7.14 us  [finish(): call(join_body, [pair, pair, blocks_shape, ((case_count, LANES),)], [VMEM...]
    pallas_call x1, Pallas kernels: 1.64 us -> 4.86 us  [shards(): call(third_body, [((devices, 3, 2, LANES),), z_shape], [SMEM] + [VMEM] *...]
    pallas_call x1, Pallas kernels: 1.07 us -> 3.95 us  [shards(): call(second_body, [((4 * devices, 4, LANES),), z_shape, z_shape], [SMEM]...]
    pallas_call x1, Pallas kernels: 4.02 us -> 6.09 us  [shards(): call(prep_body, [((2 * basis_rows.shape[0], rank), bf16), ((devices, 4, L...]
    ppermute x7, waiting for transfers between devices: 21.7 us -> 20 us  [shifted(): lax.ppermute(array, AXES, [(i, (i + by) % count) for i in range(count)])]
  transfers between devices with their start and end apart: 11 -> 11, of which waited for: 5 -> 5; matrix products, arithmetic and copies ran while one was open for 1% -> 1% of each run, Pallas kernels for 8% -> 13%
where the time goes in v6:
time: 139 us; the launch traced here: 138 us
  starting transfers between devices  48.2 us (35%)
  Pallas kernels  33 us (24%)
  blocking collectives  25 us (18%)
  waiting for transfers between devices  20.1 us (14%)
  local copies, waits for them, and re-layouts  11.2 us (8%)
    all_to_all x4, starting transfers between devices, exchange(): return lax.all_to_all(pieces, axes, split_axis=0, concat_axis=0, tiled=True)  25.9 us
    all_to_all x2, blocking collectives, exchange(): return lax.all_to_all(pieces, axes, split_axis=0, concat_axis=0, tiled=True)  25 us
    ppermute x7, starting transfers between devices, shifted(): lax.ppermute(array, AXES, [(i, (i + by) % count) for i in range(count)])  22.4 us
    ppermute x7, waiting for transfers between devices, shifted(): lax.ppermute(array, AXES, [(i, (i + by) % count) for i in range(count)])  20 us
    unnamed x62, local copies, waits for them, and re-layouts  9.73 us
    pallas_call x2, Pallas kernels, finish(): call(join_body, [pair, pair, blocks_shape, ((case_count, LANES),)], [VMEM...  7.14 us
    pallas_call x1, Pallas kernels, shards(): call(prep_body, [((2 * basis_rows.shape[0], rank), bf16), ((devices, 4, L...  6.09 us
    pallas_call x1, Pallas kernels, shards(): call(third_body, [((devices, 3, 2, LANES),), z_shape], [SMEM] + [VMEM] *...  4.86 us
  transfers between devices with their start and end apart: 11, of which 5 were waited for; matrix products, arithmetic and copies ran while one was open for 1% of the time, Pallas kernels for 13%

profile of v6, /device:TPU:0, one launch (start us, length us, event | category | flops | bytes accessed | tf_op | source)
XLA Modules:
  0.0 138.4 jit_solution(7893195858796648438)
XLA Ops:
  0.6 2.4 %shard_map.137 = (f32[128,8,128]{2,1,0:T(8,128)}, f32[2,8,512]{2,1,0:T(8,128)}) custom-call(s32[1]{0:T(128)} %bitcast.device_ref, f32[8,2,512]{2,1,0:T(2,128)} %load_ref.1, f32[2,512]{1,0:T(2,128)} %inertia_ref.1, f32[8,2,512]{2,1,0:T(2,128)} %disp_ref.3, f32[8,2,512]{2,1,0:T(2,128)} %vel_ref.3, f32[8,2,512]{2,1,0:T(2,128)} %acc_ref.3, f32[2,64,512]{2,1,0:T(8,128)} %modes_ref.15), custom_call_target="tpu_custom_call" | custom-call | bytes 1048576 | tf_op jit(solution)/shard_map/pallas_call | solution.py:460
  3.0 11.2 %all-to-all-start = ((f32[128,8,128]{2,1,0:T(8,128)}), f32[128,8,128]{2,1,0:T(8,128)S(1)}, u32[]{:S(2)}, u32[]{:S(2)}) async-start(f32[128,8,128]{2,1,0:T(8,128)} %get-tuple-element.45), calls=%async_computation | async-start | bytes 1048576 | tf_op jit(solution)/shard_map/all_to_all | solution.py:31
  14.2 7.1 %collective-permute-start = (f32[2,64,512]{2,1,0:T(8,128)}, f32[2,64,512]{2,1,0:T(8,128)S(1)}, u32[]{:S(2)}, u32[]{:S(2)}) collective-permute-start(f32[2,64,512]{2,1,0:T(8,128)} %modes_ref.15), channel_id=1, source_target_pairs={{0,127},{1,0},{2,1},{3,2},{4,3},{5,4},{6,5},{7,6},{8,7},{9,8},{10,... | collective-permute-start | bytes 786440 | tf_op jit(solution)/shard_map/ppermute | solution.py:40
  21.3 0.8 slice_bitcast_fusion
  22.1 1.6 %copy-done = f32[2,512,512]{2,1,0:T(8,128)S(1)} copy-done((f32[2,512,512]{2,1,0:T(8,128)S(1)}, f32[2,512,512]{2,1,0:T(8,128)}, u32[]{:S(2)}) %copy-start) | copy-done | bytes 2097176
  23.7 1.6 %copy-done.8 = f32[64,8192]{1,0:T(8,128)S(1)} copy-done((f32[64,8192]{1,0:T(8,128)S(1)}, f32[64,8192]{1,0:T(8,128)}, u32[]{:S(2)}) %copy-start.8) | copy-done | bytes 2097176
  25.3 0.8 copy-done.22
  26.1 1.6 %shard_map.138 = (bf16[128,8192]{1,0:T(8,128)(2,1)S(1)}, f32[2,8,512]{2,1,0:T(8,128)S(1)}) custom-call(f32[64,8192]{1,0:T(8,128)S(1)} %copy-done.8, f32[2,8,512]{2,1,0:T(8,128)S(1)} %copy-done.22, f32[2,512,512]{2,1,0:T(8,128)S(1)} %copy-done), custom_call_target="tpu_custom_call" | custom-call | flops 67108864 | bytes 1048576 | tf_op jit(solution)/shard_map/pallas_call | solution.py:466
  27.7 3.2 %collective-permute-done.1.left_ref = f32[64,128]{1,0:T(8,128)S(1)} collective-permute-done((f32[64,128]{1,0:T(8,128)S(1)}, f32[64,128]{1,0:T(8,128)S(1)}, u32[]{:S(2)}, u32[]{:S(2)}) %collective-permute-start.1) | collective-permute-done | bytes 32800 | tf_op jit(solution)/shard_map/ppermute | solution.py:40
  30.9 0.9 shard_map.139
  31.8 0.8 copy-done.7
  32.6 1.0 shard_map.140
  33.6 0.9 copy-done.9
  34.5 6.4 %all-to-all-start.1 = ((f32[384,4,128]{2,1,0:T(4,128)}), f32[384,4,128]{2,1,0:T(4,128)}, u32[]{:S(2)}, u32[]{:S(2)}) async-start(f32[384,4,128]{2,1,0:T(4,128)} %copy-done.9), calls=%async_computation.1 | async-start | bytes 1572864 | tf_op jit(solution)/shard_map/all_to_all | solution.py:31
  40.9 0.2 shard_map.141
  41.1 0.6 copy-done.20
  41.8 0.9 collective-permute-start.2
  42.7 6.3 %collective-permute-start.3 = (f32[8,128]{1,0:T(8,128)S(1)}, f32[8,128]{1,0:T(8,128)S(1)}, u32[]{:S(2)}, u32[]{:S(2)}) collective-permute-start(f32[8,128]{1,0:T(8,128)S(1)} %get-tuple-element.52), channel_id=1, source_target_pairs={{0,127},{1,0},{2,1},{3,2},{4,3},{5,4},{6,5},{7,6},{8,7},{9,8},{10,... | collective-permute-start | bytes 12296 | tf_op jit(solution)/shard_map/ppermute | solution.py:40
  48.9 6.1 %shard_map.143 = (bf16[2048,256]{1,0:T(8,128)(2,1)}, f32[128,4,128]{2,1,0:T(4,128)}, bf16[128,512]{1,0:T(8,128)(2,1)}) custom-call(f32[128,8,256]{2,1,0:T(8,128)} %bitcast.7, s32[1,128]{1,0:T(1,128)} %bitcast.8, f32[8,64]{1,0:T(8,128)} %copy-done.19), custom_call_target="tpu_custom_call" | custom-call | flops 67108864 | bytes 1048576 | tf_op jit(solution)/shard_map/pallas_call | solution.py:487
  55.0 0.4 collective-permute-done.2.from_left_ref
  55.5 0.2 copy-done.29
  55.6 0.4 copy-done.27
  56.1 3.6 %shard_map.142 = (f32[2,8,512]{2,1,0:T(8,128)}, f32[2,8,512]{2,1,0:T(8,128)}, f32[8,256]{1,0:T(8,128)}, f32[8,128]{1,0:T(8,128)}) custom-call(f32[2,8,512]{2,1,0:T(8,128)} %copy-done.20, f32[8,256]{1,0:T(8,128)} %copy-done.27, f32[8,128]{1,0:T(8,128)} %copy-done.29, f32[8,64]{1,0:T(8,128)} %copy-done.19, f32[2,64,512]{2,1,0:T(8,128)} %modes_ref.15, ...), custom_call_target="tpu_custom_call" | custom-call | flops 67108864 | bytes 1048576 | tf_op jit(solution)/shard_map/pallas_call | solution.py:479
  59.7 3.9 %shard_map.144 = (f32[512,4,128]{2,1,0:T(4,128)}, f32[8,64]{1,0:T(8,128)}, f32[8,64]{1,0:T(8,128)}) custom-call(s32[1]{0:T(128)} %bitcast.device_ref, f32[384,4,128]{2,1,0:T(4,128)} %all-to-all-done.1.got_ref, bf16[128,8192]{1,0:T(8,128)(2,1)} %copy-done.1, f32[64,256]{1,0:T(8,128)} %copy-done.12, f32[8,256]{1,0:T(8,128)} %get-tuple-element.57.local_ref, ...), custom_call_target="tpu_custom_call" | custom-call | flops 16777216 | bytes 1048576 | tf_op jit(solution)/shard_map/pallas_call | solution.py:495
  63.6 4.8 %all-to-all-start.2 = ((f32[512,4,128]{2,1,0:T(4,128)}), f32[512,4,128]{2,1,0:T(4,128)S(1)}, u32[]{:S(2)}, u32[]{:S(2)}) async-start(f32[512,4,128]{2,1,0:T(4,128)} %get-tuple-element.65), calls=%async_computation.2 | async-start | bytes 2097152 | tf_op jit(solution)/shard_map/all_to_all | solution.py:31
  68.4 0.2 shard_map.145
  68.7 0.6 copy-done.21
  69.3 1.0 collective-permute-start.4
  70.2 6.2 %collective-permute-start.5 = (f32[8,128]{1,0:T(8,128)S(1)}, f32[8,128]{1,0:T(8,128)S(1)}, u32[]{:S(2)}, u32[]{:S(2)}) collective-permute-start(f32[8,128]{1,0:T(8,128)S(1)} %get-tuple-element.62), channel_id=1, source_target_pairs={{0,127},{1,0},{2,1},{3,2},{4,3},{5,4},{6,5},{7,6},{8,7},{9,8},{10,... | collective-permute-start | bytes 12296 | tf_op jit(solution)/shard_map/ppermute | solution.py:40
  76.5 0.2 shard_map.147.early_ref
  76.7 0.6 copy-done.11
  77.3 3.7 %collective-permute-done.5.from_right_ref = f32[8,128]{1,0:T(8,128)S(1)} collective-permute-done((f32[8,128]{1,0:T(8,128)S(1)}, f32[8,128]{1,0:T(8,128)S(1)}, u32[]{:S(2)}, u32[]{:S(2)}) %collective-permute-start.5) | collective-permute-done | bytes 4128 | tf_op jit(solution)/shard_map/ppermute | solution.py:40
  81.0 5.1 %collective-permute-done.4.from_left_ref = f32[8,256]{1,0:T(8,128)S(1)} collective-permute-done((f32[8,256]{1,0:T(8,128)S(1)}, f32[8,256]{1,0:T(8,128)S(1)}, u32[]{:S(2)}, u32[]{:S(2)}) %collective-permute-start.4) | collective-permute-done | bytes 8224 | tf_op jit(solution)/shard_map/ppermute | solution.py:40
  86.1 0.6 copy-done.28
  86.7 3.6 %shard_map.146 = (f32[2,8,512]{2,1,0:T(8,128)}, f32[2,8,512]{2,1,0:T(8,128)}, f32[8,256]{1,0:T(8,128)}, f32[8,128]{1,0:T(8,128)}) custom-call(f32[2,8,512]{2,1,0:T(8,128)} %copy-done.21, f32[8,256]{1,0:T(8,128)} %copy-done.28, f32[8,128]{1,0:T(8,128)} %copy-done.30, f32[8,64]{1,0:T(8,128)} %get-tuple-element.59.z_ref, f32[2,64,512]{2,1,0:T(8,128)} %modes_ref.15, ...), custom_call_target="tpu_custom_call" | custom-call | flops 67108864 | bytes 1048576 | tf_op jit(solution)/shard_map/pallas_call | solution.py:479
  90.3 1.0 copy-done.26
  91.3 4.9 %shard_map.148 = (f32[128,3,2,128]{3,2,1,0:T(2,128)}, f32[8,64]{1,0:T(8,128)}) custom-call(s32[1]{0:T(128)} %bitcast.device_ref, f32[512,4,128]{2,1,0:T(4,128)} %copy-done.26, bf16[128,8192]{1,0:T(8,128)(2,1)} %copy-done.1, f32[2,8,512]{2,1,0:T(8,128)} %get-tuple-element.64.local_ref, f32[2,64,512]{2,1,0:T(8,128)} %modes_ref.15, f32[2,64,512]{2,1,0:T(8,128)} %copy-done.5, ...), custom_call_target="tpu_custom_call" | custom-call | flops 16777216 | bytes 1048576 | tf_op jit(solution)/shard_map/pallas_call | solution.py:501
  96.2 16.8 %all_to_all.30.got_ref.square_ref = f32[128,3,2,128]{3,2,1,0:T(2,128)S(1)} all-to-all(f32[128,3,2,128]{3,2,1,0:T(2,128)} %get-tuple-element.71), channel_id=1, replica_groups=mesh['sub_0'=4,'sub_1'=4,'sub_2'=2,'grp'=4] {'sub_0','sub_1','sub_2','grp'}, dimensions={0} | all-to-all | bytes 786432 | tf_op jit(solution)/shard_map/all_to_all | solution.py:31
  113.0 0.8 shard_map.150
  113.7 8.2 %all_to_all.31 = f32[8,8,384]{2,1,0:T(8,128)S(1)} all-to-all(f32[8,8,384]{2,1,0:T(8,128)S(1)} %get-tuple-element.76), channel_id=1, replica_groups=mesh['sub_0'=4,'sub_1'=4,'sub_2'=2,'grp'=4] {'sub_2','grp'}, dimensions={0} | all-to-all | bytes 196608 | tf_op jit(solution)/shard_map/all_to_all | solution.py:31
  121.9 0.7 broadcast_in_dim.3
  122.6 3.5 %all-to-all-start.5 = ((f32[16,8,384]{2,1,0:T(8,128)}), f32[16,8,384]{2,1,0:T(8,128)S(1)}, u32[]{:S(2)}, u32[]{:S(2)}) async-start(f32[16,8,384]{2,1,0:T(8,128)} %broadcast_in_dim.3), calls=%async_computation.5 | async-start | bytes 393216 | tf_op jit(solution)/shard_map/all_to_all | solution.py:31
  126.2 0.9 collective-permute-start.6
  127.1 7.6 %collective-permute-done.6.ghost_ref = f32[8,64]{1,0:T(8,128)S(1)} collective-permute-done((f32[8,64]{1,0:T(8,128)S(1)}, f32[8,64]{1,0:T(8,128)S(1)}, u32[]{:S(2)}, u32[]{:S(2)}) %collective-permute-start.6) | collective-permute-done | bytes 2080 | tf_op jit(solution)/shard_map/ppermute | solution.py:40
  134.7 0.3 shard_map.149.late_ref
  135.0 0.0 copy-done.16
  135.0 0.7 shard_map.151
  135.8 2.6 %shard_map.152 = (f32[8,1024]{1,0:T(8,128)}, f32[8,256]{1,0:T(8,128)}, f32[8,128]{1,0:T(8,128)}) custom-call(f32[16,8,384]{2,1,0:T(8,128)S(1)} %all-to-all-done.5.got_ref, f32[128,3,2,128]{3,2,1,0:T(2,128)S(1)} %all_to_all.30.got_ref.square_ref, bf16[2048,256]{1,0:T(8,128)(2,1)S(1)} %copy-done.6, f32[8,1024]{1,0:T(8,128)S(1)} %get-tuple-element.77.rows_ref), custom_call_target="tpu_custom_call" | custom-call | flops 16777216 | bytes 1048576 | tf_op jit(solution)/shard_map/pallas_call | solution.py:524
  (57 shorter events, 0.1 us)
Async XLA Ops:
  3.0 29.6 %all-to-all-start = ((f32[128,8,128]{2,1,0:T(8,128)}), f32[128,8,128]{2,1,0:T(8,128)S(1)}, u32[]{:S(2)}, u32[]{:S(2)}) async-start(f32[128,8,128]{2,1,0:T(8,128)} %get-tuple-element.45), calls=%async_computation | async-start | bytes 1048576 | tf_op jit(solution)/shard_map/all_to_all | solution.py:31
  14.2 16.7 %collective-permute-start = (f32[2,64,512]{2,1,0:T(8,128)}, f32[2,64,512]{2,1,0:T(8,128)S(1)}, u32[]{:S(2)}, u32[]{:S(2)}) collective-permute-start(f32[2,64,512]{2,1,0:T(8,128)} %modes_ref.15), channel_id=1, source_target_pairs={{0,127},{1,0},{2,1},{3,2},{4,3},{5,4},{6,5},{7,6},{8,7},{9,8},{10,... | collective-permute-start | bytes 786440 | tf_op jit(solution)/shard_map/ppermute | solution.py:40
  22.1 8.8 %collective-permute-start.1 = (f32[64,128]{1,0:T(8,128)S(1)}, f32[64,128]{1,0:T(8,128)S(1)}, u32[]{:S(2)}, u32[]{:S(2)}) collective-permute-start(f32[64,128]{1,0:T(8,128)S(1)} %slice_bitcast_fusion), channel_id=1, source_target_pairs={{0,1},{1,2},{2,3},{3,4},{4,5},{5,6},{6,7},{7,8},{8,9},{9,10},{10,1... | collective-permute-start | bytes 98312 | tf_op jit(solution)/shard_map/ppermute | solution.py:40
  22.1 1.6 %copy-start = (f32[2,512,512]{2,1,0:T(8,128)S(1)}, f32[2,512,512]{2,1,0:T(8,128)}, u32[]{:S(2)}) copy-start(f32[2,512,512]{2,1,0:T(8,128)} %rr_ref.5) | copy-start | bytes 6291460
  23.7 1.6 %copy-start.8 = (f32[64,8192]{1,0:T(8,128)S(1)}, f32[64,8192]{1,0:T(8,128)}, u32[]{:S(2)}) copy-start(f32[64,8192]{1,0:T(8,128)} %matrix_ref.1) | copy-start | bytes 6291460
  25.3 0.8 copy-start.22
  26.1 4.8 %copy-start.2 = (f32[2,64,512]{2,1,0:T(8,128)S(1)}, f32[2,64,512]{2,1,0:T(8,128)}, u32[]{:S(2)}) copy-start(f32[2,64,512]{2,1,0:T(8,128)} %modes_ref.15) | copy-start | bytes 786436
  27.7 6.9 %copy-start.1 = (bf16[128,8192]{1,0:T(8,128)(2,1)}, bf16[128,8192]{1,0:T(8,128)(2,1)S(1)}, u32[]{:S(2)}) copy-start(bf16[128,8192]{1,0:T(8,128)(2,1)S(1)} %get-tuple-element.46.parts_ref) | copy-start | bytes 6291460
  30.9 3.6 %copy-start.5 = (f32[2,64,512]{2,1,0:T(8,128)}, f32[2,64,512]{2,1,0:T(8,128)S(1)}, u32[]{:S(2)}) copy-start(f32[2,64,512]{2,1,0:T(8,128)S(1)} %collective-permute-done.right_ref) | copy-start | bytes 786436
  31.8 0.8 copy-start.7
  32.6 1.9 %copy-start.12 = (f32[64,256]{1,0:T(8,128)}, f32[64,256]{1,0:T(8,128)S(1)}, u32[]{:S(2)}) copy-start(f32[64,256]{1,0:T(8,128)S(1)} %get-tuple-element.47.coupling_ref) | copy-start | bytes 196612
  33.6 0.9 copy-start.9
  34.5 14.4 %copy-start.19 = (f32[8,64]{1,0:T(8,128)}, f32[8,64]{1,0:T(8,128)S(1)}, u32[]{:S(2)}) copy-start(f32[8,64]{1,0:T(8,128)S(1)} %get-tuple-element.49.z_ref.after_ref) | copy-start | bytes 6148
  34.5 25.1 %all-to-all-start.1 = ((f32[384,4,128]{2,1,0:T(4,128)}), f32[384,4,128]{2,1,0:T(4,128)}, u32[]{:S(2)}, u32[]{:S(2)}) async-start(f32[384,4,128]{2,1,0:T(4,128)} %copy-done.9), calls=%async_computation.1 | async-start | bytes 1572864 | tf_op jit(solution)/shard_map/all_to_all | solution.py:31
  41.1 0.6 copy-start.20
  41.8 13.7 %collective-permute-start.2 = (f32[8,256]{1,0:T(8,128)S(1)}, f32[8,256]{1,0:T(8,128)S(1)}, u32[]{:S(2)}, u32[]{:S(2)}) collective-permute-start(f32[8,256]{1,0:T(8,128)S(1)} %get-tuple-element.51), channel_id=1, source_target_pairs={{0,1},{1,2},{2,3},{3,4},{4,5},{5,6},{6,7},{7,8},{8,9},{9,10},{10,1... | collective-permute-start | bytes 24584 | tf_op jit(solution)/shard_map/ppermute | solution.py:40
  42.7 12.4 %collective-permute-start.3 = (f32[8,128]{1,0:T(8,128)S(1)}, f32[8,128]{1,0:T(8,128)S(1)}, u32[]{:S(2)}, u32[]{:S(2)}) collective-permute-start(f32[8,128]{1,0:T(8,128)S(1)} %get-tuple-element.52), channel_id=1, source_target_pairs={{0,127},{1,0},{2,1},{3,2},{4,3},{5,4},{6,5},{7,6},{8,7},{9,8},{10,... | collective-permute-start | bytes 12296 | tf_op jit(solution)/shard_map/ppermute | solution.py:40
  55.0 0.6 copy-start.29
  55.5 0.6 copy-start.27
  59.6 8.8 %copy-start.3 = (f32[2,64,512]{2,1,0:T(8,128)S(1)}, f32[2,64,512]{2,1,0:T(8,128)}, u32[]{:S(2)}) copy-start(f32[2,64,512]{2,1,0:T(8,128)} %modes_ref.15) | copy-start | bytes 786436
  59.6 8.8 %copy-start.23 = (f32[2,8,512]{2,1,0:T(8,128)S(1)}, f32[2,8,512]{2,1,0:T(8,128)}, u32[]{:S(2)}) copy-start(f32[2,8,512]{2,1,0:T(8,128)} %get-tuple-element.55.local_ref) | copy-start | bytes 98308
  59.6 16.8 %copy-start.10 = (bf16[128,512]{1,0:T(8,128)(2,1)S(1)}, bf16[128,512]{1,0:T(8,128)(2,1)}, u32[]{:S(2)}) copy-start(bf16[128,512]{1,0:T(8,128)(2,1)} %get-tuple-element.66.select_ref) | copy-start | bytes 393220
  59.7 16.8 %copy-start.18 = (f32[2,8,512]{2,1,0:T(8,128)S(1)}, f32[2,8,512]{2,1,0:T(8,128)}, u32[]{:S(2)}) copy-start(f32[2,8,512]{2,1,0:T(8,128)} %get-tuple-element.54.green_ref) | copy-start | bytes 98308
  63.6 4.8 %copy-start.24 = (f32[8,64]{1,0:T(8,128)S(1)}, f32[8,64]{1,0:T(8,128)}, u32[]{:S(2)}) copy-start(f32[8,64]{1,0:T(8,128)} %get-tuple-element.59.z_ref) | copy-start | bytes 6148
  63.6 26.7 %all-to-all-start.2 = ((f32[512,4,128]{2,1,0:T(4,128)}), f32[512,4,128]{2,1,0:T(4,128)S(1)}, u32[]{:S(2)}, u32[]{:S(2)}) async-start(f32[512,4,128]{2,1,0:T(4,128)} %get-tuple-element.65), calls=%async_computation.2 | async-start | bytes 2097152 | tf_op jit(solution)/shard_map/all_to_all | solution.py:31
  68.6 0.6 copy-start.21
  69.3 16.8 %collective-permute-start.4 = (f32[8,256]{1,0:T(8,128)S(1)}, f32[8,256]{1,0:T(8,128)S(1)}, u32[]{:S(2)}, u32[]{:S(2)}) collective-permute-start(f32[8,256]{1,0:T(8,128)S(1)} %get-tuple-element.61), channel_id=1, source_target_pairs={{0,1},{1,2},{2,3},{3,4},{4,5},{5,6},{6,7},{7,8},{8,9},{9,10},{10,1... | collective-permute-start | bytes 24584 | tf_op jit(solution)/shard_map/ppermute | solution.py:40
  70.2 10.8 %collective-permute-start.5 = (f32[8,128]{1,0:T(8,128)S(1)}, f32[8,128]{1,0:T(8,128)S(1)}, u32[]{:S(2)}, u32[]{:S(2)}) collective-permute-start(f32[8,128]{1,0:T(8,128)S(1)} %get-tuple-element.62), channel_id=1, source_target_pairs={{0,127},{1,0},{2,1},{3,2},{4,3},{5,4},{6,5},{7,6},{8,7},{9,8},{10,... | collective-permute-start | bytes 12296 | tf_op jit(solution)/shard_map/ppermute | solution.py:40
  76.7 0.6 copy-start.11
  81.0 5.1 %copy-start.30 = (f32[8,128]{1,0:T(8,128)}, f32[8,128]{1,0:T(8,128)S(1)}, u32[]{:S(2)}) copy-start(f32[8,128]{1,0:T(8,128)S(1)} %collective-permute-done.5.from_right_ref) | copy-start | bytes 12292
  86.1 0.6 copy-start.28
  90.3 1.0 copy-start.26
  91.3 21.7 %copy-start.6 = (bf16[2048,256]{1,0:T(8,128)(2,1)S(1)}, bf16[2048,256]{1,0:T(8,128)(2,1)}, u32[]{:S(2)}) copy-start(bf16[2048,256]{1,0:T(8,128)(2,1)} %get-tuple-element.72.basis_ref) | copy-start | bytes 3145732
  96.1 30.1 %copy-start.25 = (f32[8,64]{1,0:T(8,128)S(1)}, f32[8,64]{1,0:T(8,128)}, u32[]{:S(2)}) copy-start(f32[8,64]{1,0:T(8,128)} %get-tuple-element.70.z_ref) | copy-start | bytes 6148
  96.1 38.6 %copy-start.4 = (f32[2,64,512]{2,1,0:T(8,128)S(1)}, f32[2,64,512]{2,1,0:T(8,128)}, u32[]{:S(2)}) copy-start(f32[2,64,512]{2,1,0:T(8,128)} %modes_ref.15) | copy-start | bytes 786436
  96.1 38.6 %copy-start.14 = (f32[2,8,512]{2,1,0:T(8,128)S(1)}, f32[2,8,512]{2,1,0:T(8,128)}, u32[]{:S(2)}) copy-start(f32[2,8,512]{2,1,0:T(8,128)} %get-tuple-element.64.local_ref) | copy-start | bytes 98308
  96.1 38.9 %copy-start.13 = (f32[2,8,512]{2,1,0:T(8,128)S(1)}, f32[2,8,512]{2,1,0:T(8,128)}, u32[]{:S(2)}) copy-start(f32[2,8,512]{2,1,0:T(8,128)} %get-tuple-element.63.image_ref) | copy-start | bytes 98308
  96.1 38.8 %copy-start.15 = (f32[8,2,512]{2,1,0:T(2,128)S(1)}, f32[8,2,512]{2,1,0:T(2,128)}, u32[]{:S(2)}) copy-start(f32[8,2,512]{2,1,0:T(2,128)} %disp_ref.3) | copy-start | bytes 98308
  96.2 38.8 %copy-start.16 = (f32[8,2,512]{2,1,0:T(2,128)S(1)}, f32[8,2,512]{2,1,0:T(2,128)}, u32[]{:S(2)}) copy-start(f32[8,2,512]{2,1,0:T(2,128)} %vel_ref.3) | copy-start | bytes 98308
  96.2 38.8 %copy-start.17 = (f32[8,2,512]{2,1,0:T(2,128)S(1)}, f32[8,2,512]{2,1,0:T(2,128)}, u32[]{:S(2)}) copy-start(f32[8,2,512]{2,1,0:T(2,128)} %acc_ref.3) | copy-start | bytes 98308
  122.6 13.1 %all-to-all-start.5 = ((f32[16,8,384]{2,1,0:T(8,128)}), f32[16,8,384]{2,1,0:T(8,128)S(1)}, u32[]{:S(2)}, u32[]{:S(2)}) async-start(f32[16,8,384]{2,1,0:T(8,128)} %broadcast_in_dim.3), calls=%async_computation.5 | async-start | bytes 393216 | tf_op jit(solution)/shard_map/all_to_all | solution.py:31
  126.2 8.5 %collective-permute-start.6 = (f32[8,64]{1,0:T(8,128)S(1)}, f32[8,64]{1,0:T(8,128)S(1)}, u32[]{:S(2)}, u32[]{:S(2)}) collective-permute-start(f32[8,64]{1,0:T(8,128)S(1)} %copy-done.25), channel_id=1, source_target_pairs={{0,1},{1,2},{2,3},{3,4},{4,5},{5,6},{6,7},{7,8},{8,9},{9,10},{10,1... | collective-permute-start | bytes 6152 | tf_op jit(solution)/shard_map/ppermute | solution.py:40

commit v7 on v6

--- a/solution.py
+++ b/solution.py
@@ -38,6 +38,12 @@
 def shifted(array, by):
     count = lax.axis_size(AXES)
     return lax.ppermute(array, AXES, [(i, (i + by) % count) for i in range(count)])
+
+
+def swapped(array, offset):
+    count = lax.axis_size(AXES)
+    pairs = [(i % count, (i + 1) % count) for i in range(offset, count + offset, 2)]
+    return lax.ppermute(array, AXES, pairs + [(b, a) for a, b in pairs])
 
 
 def dot(a, b, dims):
@@ -98,12 +104,17 @@
         local_ref[s] = dot(right_ref[s], rr_ref[s], NN)
 
 
-def couple_body(device_ref, modes_ref, right_ref, left_ref, local_ref, blocks_ref, coupling_ref, to_blocks_ref):
+def couple_body(
+    device_ref, modes_ref, swap_a_ref, swap_b_ref, local_ref, blocks_ref, coupling_ref, to_blocks_ref, right_ref
+):
     last = modes_ref.shape[2] - NI
-    even = jnp.where(lax.rem(device_ref[0], 2) == 0, 1, 0)
+    first_right = lax.rem(device_ref[0], 2) == 0
+    for s in range(2):
+        right_ref[s] = jnp.where(first_right, swap_a_ref[s], swap_b_ref[s])
+    left = jnp.where(first_right, swap_b_ref[1, :, last:], swap_a_ref[1, :, last:])
+    even = jnp.where(first_right, 1, 0)
     first, final = [modes_ref[s, :, :NI] for s in range(2)], [modes_ref[s, :, last:] for s in range(2)]
     right_first, right_final = [right_ref[s, :, :NI] for s in range(2)], right_ref[0, :, last:]
-    left = left_ref[...]
     rows = [
         {0: left[:NC]},
         {0: left[NC:] - first[0][:NC], 1: final[0][:NC]},
@@ -134,29 +145,34 @@
     return dot(jnp.concatenate(jumps, axis=1), to_blocks_ref[:, : 3 * NI], NT)
 
 
-def edge_body(local_ref, z_ref, modes_ref, mine_ref, to_right_ref, to_left_ref):
+def edge_body(device_ref, local_ref, z_ref, modes_ref, mine_ref, swap_a_ref, swap_b_ref):
     last = local_ref.shape[2] - NI
     z = z_ref[...]
     mine_0 = local_ref[0] + dot(z[:, :NC], modes_ref[0, NC:], NN)
     mine_1 = local_ref[1] + dot(z, modes_ref[1], NN)
     mine_ref[0], mine_ref[1] = mine_0, mine_1
-    to_left_ref[...] = mine_0[:, :NI]
-    to_right_ref[:, :NI] = mine_1[:, last:]
-    to_right_ref[:, NI:] = jnp.concatenate([z, z], axis=1)
+    first_right = lax.rem(device_ref[0], 2) == 0
+    to_left = jnp.concatenate([mine_0[:, :NI], jnp.zeros_like(mine_0[:, :NI])], axis=1)
+    to_right = jnp.concatenate([mine_1[:, last:], jnp.concatenate([z, z], axis=1)], axis=1)
+    swap_a_ref[...] = jnp.where(first_right, to_right, to_left)
+    swap_b_ref[...] = jnp.where(first_right, to_left, to_right)
 
 
 def join_body(
-    mine_ref, from_left_ref, from_right_ref, z_ref, modes_ref, right_ref, rr_ref, to_blocks_ref,
+    device_ref, mine_ref, swap_a_ref, swap_b_ref, z_ref, modes_ref, right_ref, rr_ref, to_blocks_ref,
     field_ref, local_ref, blocks_ref, sums_ref,
 ):
     last = mine_ref.shape[2] - NI
     mine_1 = mine_ref[1]
-    ghost = from_left_ref[:, NI : NI + 2 * NC]
+    first_right = lax.rem(device_ref[0], 2) == 0
+    from_left = jnp.where(first_right, swap_b_ref[...], swap_a_ref[...])
+    from_right = jnp.where(first_right, swap_a_ref[...], swap_b_ref[...])[:, :NI]
+    ghost = from_left[:, NI : NI + 2 * NC]
     mine_0 = mine_ref[0] + dot(ghost[:, NC:], modes_ref[0, :NC], NN)
     field_ref[0], field_ref[1] = mine_0, mine_1
-    jump_a = from_left_ref[:, :NI] - mine_0[:, :NI]
+    jump_a = from_left[:, :NI] - mine_0[:, :NI]
     jump_b = mine_0[:, last:] - mine_1[:, :NI]
-    jump_c = mine_1[:, last:] - (from_right_ref[...] + dot(z_ref[:, NC:], right_ref[0, :NC, :NI], NN))
+    jump_c = mine_1[:, last:] - (from_right + dot(z_ref[:, NC:], right_ref[0, :NC, :NI], NN))
     inner = jnp.zeros((mine_1.shape[0], 1), f32)
     outs = []
     for s, (first, final) in enumerate([(-jump_a, jump_b), (-jump_b, jump_c)]):
@@ -450,7 +466,6 @@
     devices = lax.axis_size(AXES)
     coarse_total = coarse_inverse.shape[1]
     rank = basis_rows.shape[1]
-    last = unknowns - NI
     device = lax.axis_index(AXES).reshape(1).astype(jnp.int32)
     pair = ((2, case_count, unknowns),)
     z_shape = ((case_count, 2 * NC),)
@@ -461,23 +476,24 @@
         device, load_next, inertia, disp_now, vel_now, acc_now, corner_modes
     )
     got_1 = exchange(start)
-    left_edge = shifted(corner_modes[1, :, last:], 1)
-    right_modes = shifted(corner_modes, -1)
+    swap_a = swapped(corner_modes, 0)
+    swap_b = swapped(corner_modes, 1)
     coarse_parts, local_0 = call(pre_body, [((4 * NC, coarse_total), bf16), pair], [VMEM] * 3, flops=1 << 26)(
         coarse_inverse, right_side, rr_inverse
     )
-    blocks_0, coupling, to_blocks = call(
-        couple_body, [blocks_shape, ((2 * NC, 2 * LANES),), ((2 * LANES, 4 * NI),)], [SMEM] + [VMEM] * 4, flops=1 << 26
-    )(device, corner_modes, right_modes, left_edge, local_0)
+    blocks_0, coupling, to_blocks, right_modes = call(
+        couple_body, [blocks_shape, ((2 * NC, 2 * LANES),), ((2 * LANES, 4 * NI),), (corner_modes.shape,)],
+        [SMEM] + [VMEM] * 4, flops=1 << 26,
+    )(device, corner_modes, swap_a, swap_b, local_0)
 
     def finish(local, z):
-        mine, to_right, to_left = call(
-            edge_body, [pair, ((case_count, 2 * NI),), ((case_count, NI),)], [VMEM] * 3, flops=1 << 20
-        )(local, z, corner_modes)
-        from_left = shifted(to_right, 1)
-        from_right = shifted(to_left, -1)
-        return call(join_body, [pair, pair, blocks_shape, ((case_count, LANES),)], [VMEM] * 8, flops=1 << 26, grant=60 * 1024)(
-            mine, from_left, from_right, z, corner_modes, right_modes, rr_inverse, to_blocks
+        mine, to_a, to_b = call(edge_body, [pair, blocks_shape, blocks_shape], [SMEM] + [VMEM] * 3, flops=1 << 20)(
+            device, local, z, corner_modes
+        )
+        from_a = swapped(to_a, 0)
+        from_b = swapped(to_b, 1)
+        return call(join_body, [pair, pair, blocks_shape, ((case_count, LANES),)], [SMEM] + [VMEM] * 8, flops=1 << 26, grant=60 * 1024)(
+            device, mine, from_a, from_b, z, corner_modes, right_modes, rr_inverse, to_blocks
         )
 
     pieces, z_0 = call(first_body, [((3 * devices, 4, LANES),), z_shape], [VMEM] * 4, assembled, flops=1 << 24)(

time: 139 us -> 141 us (1.014)
  waiting for transfers between devices: 20.1 us -> 21.8 us
    ppermute x0 -> x6, starting transfers between devices: none -> 22.2 us  [swapped(): return lax.ppermute(array, AXES, pairs + [(b, a) for a, b in pairs])]
    ppermute x7 -> x1, starting transfers between devices: 22.4 us -> 0.9 us  [shifted(): lax.ppermute(array, AXES, [(i, (i + by) % count) for i in range(count)])]
    ppermute x0 -> x6, waiting for transfers between devices: none -> 14.1 us  [swapped(): return lax.ppermute(array, AXES, pairs + [(b, a) for a, b in pairs])]
    ppermute x7 -> x1, waiting for transfers between devices: 20 us -> 7.64 us  [shifted(): lax.ppermute(array, AXES, [(i, (i + by) % count) for i in range(count)])]
  transfers between devices with their start and end apart: 11 -> 11, of which waited for: 5 -> 5; matrix products, arithmetic and copies ran while one was open for 1% -> 0% of each run, Pallas kernels for 13% -> 12%
where the time goes in v7:
time: 141 us; the launch traced here: 140 us
  starting transfers between devices  48.5 us (34%)
  Pallas kernels  33.1 us (23%)
  blocking collectives  25 us (18%)
  waiting for transfers between devices  21.8 us (15%)
  local copies, waits for them, and re-layouts  11.1 us (8%)
    all_to_all x4, starting transfers between devices, exchange(): return lax.all_to_all(pieces, axes, split_axis=0, concat_axis=0, tiled=True)  25.3 us
    all_to_all x2, blocking collectives, exchange(): return lax.all_to_all(pieces, axes, split_axis=0, concat_axis=0, tiled=True)  25 us
    ppermute x6, starting transfers between devices, swapped(): return lax.ppermute(array, AXES, pairs + [(b, a) for a, b in pairs])  22.2 us
    ppermute x6, waiting for transfers between devices, swapped(): return lax.ppermute(array, AXES, pairs + [(b, a) for a, b in pairs])  14.1 us
    unnamed x62, local copies, waits for them, and re-layouts  10.4 us
    ppermute x1, waiting for transfers between devices, shifted(): lax.ppermute(array, AXES, [(i, (i + by) % count) for i in range(count)])  7.64 us
    pallas_call x2, Pallas kernels, finish(): call(join_body, [pair, pair, blocks_shape, ((case_count, LANES),)], [SMEM...  7.17 us
    pallas_call x1, Pallas kernels, shards(): call(prep_body, [((2 * basis_rows.shape[0], rank), bf16), ((devices, 4, L...  6.09 us
  transfers between devices with their start and end apart: 11, of which 5 were waited for; matrix products, arithmetic and copies ran while one was open for 0% of the time, Pallas kernels for 12%

profile of v7, /device:TPU:0, one launch (start us, length us, event | category | flops | bytes accessed | tf_op | source)
XLA Modules:
  0.0 140.3 jit_solution(2393206236871230409)
XLA Ops:
  0.6 2.4 %shard_map.137 = (f32[128,8,128]{2,1,0:T(8,128)}, f32[2,8,512]{2,1,0:T(8,128)}) custom-call(s32[1]{0:T(128)} %bitcast.device_ref, f32[8,2,512]{2,1,0:T(2,128)} %load_ref.1, f32[2,512]{1,0:T(2,128)} %inertia_ref.1, f32[8,2,512]{2,1,0:T(2,128)} %disp_ref.3, f32[8,2,512]{2,1,0:T(2,128)} %vel_ref.3, f32[8,2,512]{2,1,0:T(2,128)} %acc_ref.3, f32[2,64,512]{2,1,0:T(8,128)} %modes_ref.15), custom_call_target="tpu_custom_call" | custom-call | bytes 1048576 | tf_op jit(solution)/shard_map/pallas_call | solution.py:475
  3.0 11.2 %all-to-all-start = ((f32[128,8,128]{2,1,0:T(8,128)}), f32[128,8,128]{2,1,0:T(8,128)S(1)}, u32[]{:S(2)}, u32[]{:S(2)}) async-start(f32[128,8,128]{2,1,0:T(8,128)} %get-tuple-element.46), calls=%async_computation | async-start | bytes 1048576 | tf_op jit(solution)/shard_map/all_to_all | solution.py:31
  14.2 7.1 %collective-permute-start.1 = (f32[2,64,512]{2,1,0:T(8,128)}, f32[2,64,512]{2,1,0:T(8,128)S(1)}, u32[]{:S(2)}, u32[]{:S(2)}) collective-permute-start(f32[2,64,512]{2,1,0:T(8,128)} %modes_ref.15), channel_id=1, source_target_pairs={{1,2},{3,4},{5,6},{7,8},{9,10},{11,12},{13,14},{15,16},{17,18},{19... | collective-permute-start | bytes 786440 | tf_op jit(solution)/shard_map/ppermute | solution.py:46
  21.3 1.6 %copy-done.1 = f32[2,512,512]{2,1,0:T(8,128)S(1)} copy-done((f32[2,512,512]{2,1,0:T(8,128)S(1)}, f32[2,512,512]{2,1,0:T(8,128)}, u32[]{:S(2)}) %copy-start.1) | copy-done | bytes 2097176
  22.9 1.6 %copy-done.7 = f32[64,8192]{1,0:T(8,128)S(1)} copy-done((f32[64,8192]{1,0:T(8,128)S(1)}, f32[64,8192]{1,0:T(8,128)}, u32[]{:S(2)}) %copy-start.7) | copy-done | bytes 2097176
  24.5 0.8 copy-done.22
  25.3 1.6 %shard_map.138 = (bf16[128,8192]{1,0:T(8,128)(2,1)S(1)}, f32[2,8,512]{2,1,0:T(8,128)S(1)}) custom-call(f32[64,8192]{1,0:T(8,128)S(1)} %copy-done.7, f32[2,8,512]{2,1,0:T(8,128)S(1)} %copy-done.22, f32[2,512,512]{2,1,0:T(8,128)S(1)} %copy-done.1), custom_call_target="tpu_custom_call" | custom-call | flops 67108864 | bytes 1048576 | tf_op jit(solution)/shard_map/pallas_call | solution.py:481
  26.9 5.7 %collective-permute-done.1.swap_b_ref = f32[2,64,512]{2,1,0:T(8,128)S(1)} collective-permute-done((f32[2,64,512]{2,1,0:T(8,128)}, f32[2,64,512]{2,1,0:T(8,128)S(1)}, u32[]{:S(2)}, u32[]{:S(2)}) %collective-permute-start.1) | collective-permute-done | bytes 262176 | tf_op jit(solution)/shard_map/ppermute | solution.py:46
  32.6 0.9 shard_map.139
  33.5 0.7 copy-done.6
  34.2 0.8 copy-done.8
  35.0 1.0 shard_map.140
  36.1 0.9 copy-done.9
  36.9 5.7 %all-to-all-start.1 = ((f32[384,4,128]{2,1,0:T(4,128)}), f32[384,4,128]{2,1,0:T(4,128)}, u32[]{:S(2)}, u32[]{:S(2)}) async-start(f32[384,4,128]{2,1,0:T(4,128)} %copy-done.9), calls=%async_computation.1 | async-start | bytes 1572864 | tf_op jit(solution)/shard_map/all_to_all | solution.py:31
  42.6 0.2 shard_map.141
  42.9 0.6 copy-done.20
  43.5 0.8 collective-permute-start.2
  44.2 6.8 %collective-permute-start.3 = (f32[8,256]{1,0:T(8,128)S(1)}, f32[8,256]{1,0:T(8,128)S(1)}, u32[]{:S(2)}, u32[]{:S(2)}) collective-permute-start(f32[8,256]{1,0:T(8,128)S(1)} %get-tuple-element.53), channel_id=1, source_target_pairs={{1,2},{3,4},{5,6},{7,8},{9,10},{11,12},{13,14},{15,16},{17,18},{19... | collective-permute-start | bytes 24584 | tf_op jit(solution)/shard_map/ppermute | solution.py:46
  51.0 6.1 %shard_map.143 = (bf16[2048,256]{1,0:T(8,128)(2,1)}, f32[128,4,128]{2,1,0:T(4,128)}, bf16[128,512]{1,0:T(8,128)(2,1)}) custom-call(f32[128,8,256]{2,1,0:T(8,128)} %bitcast.5, s32[1,128]{1,0:T(1,128)} %bitcast.6, f32[8,64]{1,0:T(8,128)} %copy-done.19), custom_call_target="tpu_custom_call" | custom-call | flops 67108864 | bytes 1048576 | tf_op jit(solution)/shard_map/pallas_call | solution.py:503
  57.1 0.1 collective-permute-done.3.swap_b_ref
  57.2 0.5 copy-done.27
  57.7 0.1 copy-done.28
  57.8 3.6 %shard_map.142 = (f32[2,8,512]{2,1,0:T(8,128)}, f32[2,8,512]{2,1,0:T(8,128)}, f32[8,256]{1,0:T(8,128)}, f32[8,128]{1,0:T(8,128)}) custom-call(s32[1]{0:T(128)} %bitcast.device_ref, f32[2,8,512]{2,1,0:T(8,128)} %copy-done.20, f32[8,256]{1,0:T(8,128)} %copy-done.27, f32[8,256]{1,0:T(8,128)} %copy-done.28, f32[8,64]{1,0:T(8,128)} %copy-done.19, ...), custom_call_target="tpu_custom_call" | custom-call | flops 67108864 | bytes 1048576 | tf_op jit(solution)/shard_map/pallas_call | solution.py:495
  61.4 3.9 %shard_map.144 = (f32[512,4,128]{2,1,0:T(4,128)}, f32[8,64]{1,0:T(8,128)}, f32[8,64]{1,0:T(8,128)}) custom-call(s32[1]{0:T(128)} %bitcast.device_ref, f32[384,4,128]{2,1,0:T(4,128)} %all-to-all-done.1.got_ref, bf16[128,8192]{1,0:T(8,128)(2,1)} %copy-done, f32[64,256]{1,0:T(8,128)} %copy-done.12, f32[8,256]{1,0:T(8,128)} %get-tuple-element.59.local_ref, ...), custom_call_target="tpu_custom_call" | custom-call | flops 16777216 | bytes 1048576 | tf_op jit(solution)/shard_map/pallas_call | solution.py:511
  65.3 4.9 %all-to-all-start.2 = ((f32[512,4,128]{2,1,0:T(4,128)}), f32[512,4,128]{2,1,0:T(4,128)S(1)}, u32[]{:S(2)}, u32[]{:S(2)}) async-start(f32[512,4,128]{2,1,0:T(4,128)} %get-tuple-element.67), calls=%async_computation.2 | async-start | bytes 2097152 | tf_op jit(solution)/shard_map/all_to_all | solution.py:31
  70.3 0.2 shard_map.145
  70.5 0.6 copy-done.21
  71.2 0.9 collective-permute-start.4
  72.0 6.7 %collective-permute-start.5 = (f32[8,256]{1,0:T(8,128)S(1)}, f32[8,256]{1,0:T(8,128)S(1)}, u32[]{:S(2)}, u32[]{:S(2)}) collective-permute-start(f32[8,256]{1,0:T(8,128)S(1)} %get-tuple-element.64), channel_id=1, source_target_pairs={{1,2},{3,4},{5,6},{7,8},{9,10},{11,12},{13,14},{15,16},{17,18},{19... | collective-permute-start | bytes 24584 | tf_op jit(solution)/shard_map/ppermute | solution.py:46
  78.7 0.2 shard_map.147.early_ref
  79.0 0.6 copy-done.11
  79.6 3.3 %collective-permute-done.4.swap_a_ref = f32[8,256]{1,0:T(8,128)S(1)} collective-permute-done((f32[8,256]{1,0:T(8,128)S(1)}, f32[8,256]{1,0:T(8,128)S(1)}, u32[]{:S(2)}, u32[]{:S(2)}) %collective-permute-start.4) | collective-permute-done | bytes 8224 | tf_op jit(solution)/shard_map/ppermute | solution.py:46
  82.9 5.1 %collective-permute-done.5.swap_b_ref = f32[8,256]{1,0:T(8,128)S(1)} collective-permute-done((f32[8,256]{1,0:T(8,128)S(1)}, f32[8,256]{1,0:T(8,128)S(1)}, u32[]{:S(2)}, u32[]{:S(2)}) %collective-permute-start.5) | collective-permute-done | bytes 8224 | tf_op jit(solution)/shard_map/ppermute | solution.py:46
  88.0 0.6 copy-done.30
  88.6 3.6 %shard_map.146 = (f32[2,8,512]{2,1,0:T(8,128)}, f32[2,8,512]{2,1,0:T(8,128)}, f32[8,256]{1,0:T(8,128)}, f32[8,128]{1,0:T(8,128)}) custom-call(s32[1]{0:T(128)} %bitcast.device_ref, f32[2,8,512]{2,1,0:T(8,128)} %copy-done.21, f32[8,256]{1,0:T(8,128)} %copy-done.29, f32[8,256]{1,0:T(8,128)} %copy-done.30, f32[8,64]{1,0:T(8,128)} %get-tuple-element.61.z_ref, ...), custom_call_target="tpu_custom_call" | custom-call | flops 67108864 | bytes 1048576 | tf_op jit(solution)/shard_map/pallas_call | solution.py:495
  92.2 1.0 copy-done.26
  93.1 4.9 %shard_map.148 = (f32[128,3,2,128]{3,2,1,0:T(2,128)}, f32[8,64]{1,0:T(8,128)}) custom-call(s32[1]{0:T(128)} %bitcast.device_ref, f32[512,4,128]{2,1,0:T(4,128)} %copy-done.26, bf16[128,8192]{1,0:T(8,128)(2,1)} %copy-done, f32[2,8,512]{2,1,0:T(8,128)} %get-tuple-element.66.local_ref, f32[2,64,512]{2,1,0:T(8,128)} %modes_ref.15, f32[2,64,512]{2,1,0:T(8,128)} %copy-done.6, ...), custom_call_target="tpu_custom_call" | custom-call | flops 16777216 | bytes 1048576 | tf_op jit(solution)/shard_map/pallas_call | solution.py:517
  98.1 16.8 %all_to_all.30.got_ref.square_ref = f32[128,3,2,128]{3,2,1,0:T(2,128)S(1)} all-to-all(f32[128,3,2,128]{3,2,1,0:T(2,128)} %get-tuple-element.73), channel_id=1, replica_groups=mesh['sub_0'=4,'sub_1'=4,'sub_2'=2,'grp'=4] {'sub_0','sub_1','sub_2','grp'}, dimensions={0} | all-to-all | bytes 786432 | tf_op jit(solution)/shard_map/all_to_all | solution.py:31
  114.9 0.8 shard_map.150
  115.7 8.2 %all_to_all.31 = f32[8,8,384]{2,1,0:T(8,128)S(1)} all-to-all(f32[8,8,384]{2,1,0:T(8,128)S(1)} %get-tuple-element.78), channel_id=1, replica_groups=mesh['sub_0'=4,'sub_1'=4,'sub_2'=2,'grp'=4] {'sub_2','grp'}, dimensions={0} | all-to-all | bytes 196608 | tf_op jit(solution)/shard_map/all_to_all | solution.py:31
  123.8 0.7 broadcast_in_dim.3
  124.5 3.5 %all-to-all-start.5 = ((f32[16,8,384]{2,1,0:T(8,128)}), f32[16,8,384]{2,1,0:T(8,128)S(1)}, u32[]{:S(2)}, u32[]{:S(2)}) async-start(f32[16,8,384]{2,1,0:T(8,128)} %broadcast_in_dim.3), calls=%async_computation.5 | async-start | bytes 393216 | tf_op jit(solution)/shard_map/all_to_all | solution.py:31
  128.1 0.9 collective-permute-start.6
  129.0 7.6 %collective-permute-done.6.ghost_ref = f32[8,64]{1,0:T(8,128)S(1)} collective-permute-done((f32[8,64]{1,0:T(8,128)S(1)}, f32[8,64]{1,0:T(8,128)S(1)}, u32[]{:S(2)}, u32[]{:S(2)}) %collective-permute-start.6) | collective-permute-done | bytes 2080 | tf_op jit(solution)/shard_map/ppermute | solution.py:40
  136.6 0.3 shard_map.149.late_ref
  136.9 0.0 copy-done.16
  136.9 0.7 shard_map.151
  137.7 2.6 %shard_map.152 = (f32[8,1024]{1,0:T(8,128)}, f32[8,256]{1,0:T(8,128)}, f32[8,128]{1,0:T(8,128)}) custom-call(f32[16,8,384]{2,1,0:T(8,128)S(1)} %all-to-all-done.5.got_ref, f32[128,3,2,128]{3,2,1,0:T(2,128)S(1)} %all_to_all.30.got_ref.square_ref, bf16[2048,256]{1,0:T(8,128)(2,1)S(1)} %copy-done.5, f32[8,1024]{1,0:T(8,128)S(1)} %get-tuple-element.79.rows_ref), custom_call_target="tpu_custom_call" | custom-call | flops 16777216 | bytes 1048576 | tf_op jit(solution)/shard_map/pallas_call | solution.py:540
  (56 shorter events, 0.1 us)
Async XLA Ops:
  3.0 32.0 %all-to-all-start = ((f32[128,8,128]{2,1,0:T(8,128)}), f32[128,8,128]{2,1,0:T(8,128)S(1)}, u32[]{:S(2)}, u32[]{:S(2)}) async-start(f32[128,8,128]{2,1,0:T(8,128)} %get-tuple-element.46), calls=%async_computation | async-start | bytes 1048576 | tf_op jit(solution)/shard_map/all_to_all | solution.py:31
  14.2 18.4 %collective-permute-start.1 = (f32[2,64,512]{2,1,0:T(8,128)}, f32[2,64,512]{2,1,0:T(8,128)S(1)}, u32[]{:S(2)}, u32[]{:S(2)}) collective-permute-start(f32[2,64,512]{2,1,0:T(8,128)} %modes_ref.15), channel_id=1, source_target_pairs={{1,2},{3,4},{5,6},{7,8},{9,10},{11,12},{13,14},{15,16},{17,18},{19... | collective-permute-start | bytes 786440 | tf_op jit(solution)/shard_map/ppermute | solution.py:46
  21.3 11.3 %collective-permute-start = (f32[2,64,512]{2,1,0:T(8,128)}, f32[2,64,512]{2,1,0:T(8,128)S(1)}, u32[]{:S(2)}, u32[]{:S(2)}) collective-permute-start(f32[2,64,512]{2,1,0:T(8,128)} %modes_ref.15), channel_id=1, source_target_pairs={{0,1},{2,3},{4,5},{6,7},{8,9},{10,11},{12,13},{14,15},{16,17},{18,... | collective-permute-start | bytes 786440 | tf_op jit(solution)/shard_map/ppermute | solution.py:46
  21.3 1.6 %copy-start.1 = (f32[2,512,512]{2,1,0:T(8,128)S(1)}, f32[2,512,512]{2,1,0:T(8,128)}, u32[]{:S(2)}) copy-start(f32[2,512,512]{2,1,0:T(8,128)} %rr_ref.5) | copy-start | bytes 6291460
  22.9 1.6 %copy-start.7 = (f32[64,8192]{1,0:T(8,128)S(1)}, f32[64,8192]{1,0:T(8,128)}, u32[]{:S(2)}) copy-start(f32[64,8192]{1,0:T(8,128)} %matrix_ref.1) | copy-start | bytes 6291460
  24.5 0.8 copy-start.22
  25.3 7.3 %copy-start.2 = (f32[2,64,512]{2,1,0:T(8,128)S(1)}, f32[2,64,512]{2,1,0:T(8,128)}, u32[]{:S(2)}) copy-start(f32[2,64,512]{2,1,0:T(8,128)} %modes_ref.15) | copy-start | bytes 786436
  26.9 10.1 %copy-start = (bf16[128,8192]{1,0:T(8,128)(2,1)}, bf16[128,8192]{1,0:T(8,128)(2,1)S(1)}, u32[]{:S(2)}) copy-start(bf16[128,8192]{1,0:T(8,128)(2,1)S(1)} %get-tuple-element.47.parts_ref) | copy-start | bytes 6291460
  33.5 0.7 copy-start.6
  34.2 0.8 copy-start.8
  35.0 1.9 %copy-start.12 = (f32[64,256]{1,0:T(8,128)}, f32[64,256]{1,0:T(8,128)S(1)}, u32[]{:S(2)}) copy-start(f32[64,256]{1,0:T(8,128)S(1)} %get-tuple-element.48.coupling_ref) | copy-start | bytes 196612
  36.0 0.9 copy-start.9
  36.9 14.1 %copy-start.19 = (f32[8,64]{1,0:T(8,128)}, f32[8,64]{1,0:T(8,128)S(1)}, u32[]{:S(2)}) copy-start(f32[8,64]{1,0:T(8,128)S(1)} %get-tuple-element.50.z_ref.after_ref) | copy-start | bytes 6148
  36.9 24.4 %all-to-all-start.1 = ((f32[384,4,128]{2,1,0:T(4,128)}), f32[384,4,128]{2,1,0:T(4,128)}, u32[]{:S(2)}, u32[]{:S(2)}) async-start(f32[384,4,128]{2,1,0:T(4,128)} %copy-done.9), calls=%async_computation.1 | async-start | bytes 1572864 | tf_op jit(solution)/shard_map/all_to_all | solution.py:31
  42.9 0.6 copy-start.20
  43.5 13.6 %collective-permute-start.2 = (f32[8,256]{1,0:T(8,128)S(1)}, f32[8,256]{1,0:T(8,128)S(1)}, u32[]{:S(2)}, u32[]{:S(2)}) collective-permute-start(f32[8,256]{1,0:T(8,128)S(1)} %get-tuple-element.52), channel_id=1, source_target_pairs={{0,1},{2,3},{4,5},{6,7},{8,9},{10,11},{12,13},{14,15},{16,17},{18,... | collective-permute-start | bytes 24584 | tf_op jit(solution)/shard_map/ppermute | solution.py:46
  44.2 12.9 %collective-permute-start.3 = (f32[8,256]{1,0:T(8,128)S(1)}, f32[8,256]{1,0:T(8,128)S(1)}, u32[]{:S(2)}, u32[]{:S(2)}) collective-permute-start(f32[8,256]{1,0:T(8,128)S(1)} %get-tuple-element.53), channel_id=1, source_target_pairs={{1,2},{3,4},{5,6},{7,8},{9,10},{11,12},{13,14},{15,16},{17,18},{19... | collective-permute-start | bytes 24584 | tf_op jit(solution)/shard_map/ppermute | solution.py:46
  57.1 0.6 copy-start.27
  57.2 0.6 copy-start.28
  61.4 8.9 %copy-start.3 = (f32[2,64,512]{2,1,0:T(8,128)S(1)}, f32[2,64,512]{2,1,0:T(8,128)}, u32[]{:S(2)}) copy-start(f32[2,64,512]{2,1,0:T(8,128)} %modes_ref.15) | copy-start | bytes 786436
  61.4 8.9 %copy-start.23 = (f32[2,8,512]{2,1,0:T(8,128)S(1)}, f32[2,8,512]{2,1,0:T(8,128)}, u32[]{:S(2)}) copy-start(f32[2,8,512]{2,1,0:T(8,128)} %get-tuple-element.57.local_ref) | copy-start | bytes 98308
  61.4 17.4 %copy-start.10 = (bf16[128,512]{1,0:T(8,128)(2,1)S(1)}, bf16[128,512]{1,0:T(8,128)(2,1)}, u32[]{:S(2)}) copy-start(bf16[128,512]{1,0:T(8,128)(2,1)} %get-tuple-element.68.select_ref) | copy-start | bytes 393220
  61.4 17.4 %copy-start.18 = (f32[2,8,512]{2,1,0:T(8,128)S(1)}, f32[2,8,512]{2,1,0:T(8,128)}, u32[]{:S(2)}) copy-start(f32[2,8,512]{2,1,0:T(8,128)} %get-tuple-element.56.green_ref) | copy-start | bytes 98308
  65.3 5.0 %copy-start.24 = (f32[8,64]{1,0:T(8,128)S(1)}, f32[8,64]{1,0:T(8,128)}, u32[]{:S(2)}) copy-start(f32[8,64]{1,0:T(8,128)} %get-tuple-element.61.z_ref) | copy-start | bytes 6148
  65.3 26.8 %all-to-all-start.2 = ((f32[512,4,128]{2,1,0:T(4,128)}), f32[512,4,128]{2,1,0:T(4,128)S(1)}, u32[]{:S(2)}, u32[]{:S(2)}) async-start(f32[512,4,128]{2,1,0:T(4,128)} %get-tuple-element.67), calls=%async_computation.2 | async-start | bytes 2097152 | tf_op jit(solution)/shard_map/all_to_all | solution.py:31
  70.5 0.6 copy-start.21
  71.2 11.7 %collective-permute-start.4 = (f32[8,256]{1,0:T(8,128)S(1)}, f32[8,256]{1,0:T(8,128)S(1)}, u32[]{:S(2)}, u32[]{:S(2)}) collective-permute-start(f32[8,256]{1,0:T(8,128)S(1)} %get-tuple-element.63), channel_id=1, source_target_pairs={{0,1},{2,3},{4,5},{6,7},{8,9},{10,11},{12,13},{14,15},{16,17},{18,... | collective-permute-start | bytes 24584 | tf_op jit(solution)/shard_map/ppermute | solution.py:46
  72.0 15.9 %collective-permute-start.5 = (f32[8,256]{1,0:T(8,128)S(1)}, f32[8,256]{1,0:T(8,128)S(1)}, u32[]{:S(2)}, u32[]{:S(2)}) collective-permute-start(f32[8,256]{1,0:T(8,128)S(1)} %get-tuple-element.64), channel_id=1, source_target_pairs={{1,2},{3,4},{5,6},{7,8},{9,10},{11,12},{13,14},{15,16},{17,18},{19... | collective-permute-start | bytes 24584 | tf_op jit(solution)/shard_map/ppermute | solution.py:46
  79.0 0.6 copy-start.11
  82.9 5.1 %copy-start.29 = (f32[8,256]{1,0:T(8,128)}, f32[8,256]{1,0:T(8,128)S(1)}, u32[]{:S(2)}) copy-start(f32[8,256]{1,0:T(8,128)S(1)} %collective-permute-done.4.swap_a_ref) | copy-start | bytes 24580
  88.0 0.6 copy-start.30
  92.2 1.0 copy-start.26
  93.1 21.7 %copy-start.5 = (bf16[2048,256]{1,0:T(8,128)(2,1)S(1)}, bf16[2048,256]{1,0:T(8,128)(2,1)}, u32[]{:S(2)}) copy-start(bf16[2048,256]{1,0:T(8,128)(2,1)} %get-tuple-element.74.basis_ref) | copy-start | bytes 3145732
  98.0 30.1 %copy-start.25 = (f32[8,64]{1,0:T(8,128)S(1)}, f32[8,64]{1,0:T(8,128)}, u32[]{:S(2)}) copy-start(f32[8,64]{1,0:T(8,128)} %get-tuple-element.72.z_ref) | copy-start | bytes 6148
  98.0 38.6 %copy-start.4 = (f32[2,64,512]{2,1,0:T(8,128)S(1)}, f32[2,64,512]{2,1,0:T(8,128)}, u32[]{:S(2)}) copy-start(f32[2,64,512]{2,1,0:T(8,128)} %modes_ref.15) | copy-start | bytes 786436
  98.0 38.6 %copy-start.14 = (f32[2,8,512]{2,1,0:T(8,128)S(1)}, f32[2,8,512]{2,1,0:T(8,128)}, u32[]{:S(2)}) copy-start(f32[2,8,512]{2,1,0:T(8,128)} %get-tuple-element.66.local_ref) | copy-start | bytes 98308
  98.0 38.9 %copy-start.13 = (f32[2,8,512]{2,1,0:T(8,128)S(1)}, f32[2,8,512]{2,1,0:T(8,128)}, u32[]{:S(2)}) copy-start(f32[2,8,512]{2,1,0:T(8,128)} %get-tuple-element.65.image_ref) | copy-start | bytes 98308
  98.0 38.9 %copy-start.15 = (f32[8,2,512]{2,1,0:T(2,128)S(1)}, f32[8,2,512]{2,1,0:T(2,128)}, u32[]{:S(2)}) copy-start(f32[8,2,512]{2,1,0:T(2,128)} %disp_ref.3) | copy-start | bytes 98308
  98.0 38.9 %copy-start.16 = (f32[8,2,512]{2,1,0:T(2,128)S(1)}, f32[8,2,512]{2,1,0:T(2,128)}, u32[]{:S(2)}) copy-start(f32[8,2,512]{2,1,0:T(2,128)} %vel_ref.3) | copy-start | bytes 98308
  98.1 38.9 %copy-start.17 = (f32[8,2,512]{2,1,0:T(2,128)S(1)}, f32[8,2,512]{2,1,0:T(2,128)}, u32[]{:S(2)}) copy-start(f32[8,2,512]{2,1,0:T(2,128)} %acc_ref.3) | copy-start | bytes 98308
  124.5 13.1 %all-to-all-start.5 = ((f32[16,8,384]{2,1,0:T(8,128)}), f32[16,8,384]{2,1,0:T(8,128)S(1)}, u32[]{:S(2)}, u32[]{:S(2)}) async-start(f32[16,8,384]{2,1,0:T(8,128)} %broadcast_in_dim.3), calls=%async_computation.5 | async-start | bytes 393216 | tf_op jit(solution)/shard_map/all_to_all | solution.py:31
  128.1 8.5 %collective-permute-start.6 = (f32[8,64]{1,0:T(8,128)S(1)}, f32[8,64]{1,0:T(8,128)S(1)}, u32[]{:S(2)}, u32[]{:S(2)}) collective-permute-start(f32[8,64]{1,0:T(8,128)S(1)} %copy-done.25), channel_id=1, source_target_pairs={{0,1},{1,2},{2,3},{3,4},{4,5},{5,6},{6,7},{7,8},{8,9},{9,10},{10,1... | collective-permute-start | bytes 6152 | tf_op jit(solution)/shard_map/ppermute | solution.py:40

commit v8 on v6

--- a/solution.py
+++ b/solution.py
@@ -291,6 +291,35 @@
     z_ref[...] = z
     terms_ref[...] = owned_terms(device_ref, assembled_ref, z)
     send_blocks(z, coupling_ref, local_ref, pieces_ref, 4, square_ref)
+
+
+def join_second_body(
+    device_ref, got_ref, parts_ref, coupling_ref, square_ref, mine_ref, from_left_ref, from_right_ref, before_ref,
+    modes_ref, right_ref, rr_ref, to_blocks_ref,
+    pieces_ref, z_ref, terms_ref, field_ref, local_ref, sums_ref, assembled_ref, blocks_ref,
+):
+    join_body(
+        mine_ref, from_left_ref, from_right_ref, before_ref, modes_ref, right_ref, rr_ref, to_blocks_ref,
+        field_ref, local_ref, blocks_ref, sums_ref,
+    )
+    second_body(
+        device_ref, got_ref, parts_ref, coupling_ref, blocks_ref, square_ref, pieces_ref, z_ref, terms_ref, assembled_ref
+    )
+
+
+def join_third_body(
+    device_ref, got_ref, parts_ref, mine_ref, from_left_ref, from_right_ref, before_ref,
+    modes_ref, right_ref, rr_ref, to_blocks_ref, select_ref, sums_2_ref, terms_ref, early_ref,
+    sent_ref, z_ref, field_ref, local_ref, assembled_ref, blocks_ref, sums_3_ref,
+):
+    join_body(
+        mine_ref, from_left_ref, from_right_ref, before_ref, modes_ref, right_ref, rr_ref, to_blocks_ref,
+        field_ref, local_ref, blocks_ref, sums_3_ref,
+    )
+    third_body(
+        device_ref, got_ref, parts_ref, local_ref, modes_ref, right_ref, select_ref, sums_2_ref, sums_3_ref, terms_ref,
+        field_ref, early_ref, sent_ref, z_ref, assembled_ref,
+    )
 
 
 def choose_rows(select_ref, rows):
@@ -476,10 +505,10 @@
         )(local, z, corner_modes)
         from_left = shifted(to_right, 1)
         from_right = shifted(to_left, -1)
-        return call(join_body, [pair, pair, blocks_shape, ((case_count, LANES),)], [VMEM] * 8, flops=1 << 26, grant=60 * 1024)(
-            mine, from_left, from_right, z, corner_modes, right_modes, rr_inverse, to_blocks
-        )
-
+        return mine, from_left, from_right, z, corner_modes, right_modes, rr_inverse, to_blocks
+
+    blocks_scratch = pltpu.VMEM((case_count, 2 * LANES), f32)
+    sums_shape = (case_count, LANES)
     pieces, z_0 = call(first_body, [((3 * devices, 4, LANES),), z_shape], [VMEM] * 4, assembled, flops=1 << 24)(
         got_1, coarse_parts, coupling, blocks_0
     )
@@ -491,16 +520,24 @@
         flops=1 << 26,
         grant=60 * 1024,
     )(basis_rows.reshape(devices, -1, rank), piece_owner.reshape(1, devices), z_0)
-    green, local_1, blocks_1, sums_2 = finish(local_0, z_0)
-    pieces, z_1, terms_1 = call(
-        second_body, [((4 * devices, 4, LANES),), z_shape, z_shape], [SMEM] + [VMEM] * 5, assembled, flops=1 << 24, grant=60 * 1024
-    )(device, got_2, coarse_parts, coupling, blocks_1, square)
+    pieces, z_1, terms_1, green, local_1, sums_2 = call(
+        join_second_body,
+        [((4 * devices, 4, LANES),), z_shape, z_shape, pair, pair, (sums_shape,)],
+        [SMEM] + [VMEM] * 12,
+        assembled + [blocks_scratch],
+        flops=1 << 26,
+        grant=60 * 1024,
+    )(device, got_2, coarse_parts, coupling, square, *finish(local_0, z_0))
     got_3 = exchange(pieces)
-    image_1, local_2, _, sums_3 = finish(local_1, z_1)
     (early,) = call(early_body, [((devices, LANES),)], [VMEM] * 2, flops=1 << 24)(select, green)
-    sent, z_2 = call(third_body, [((devices, 3, 2, LANES),), z_shape], [SMEM] + [VMEM] * 11, assembled, flops=1 << 24, grant=60 * 1024)(
-        device, got_3, coarse_parts, local_2, corner_modes, right_modes, select, sums_2, sums_3, terms_1, image_1, early
-    )
+    sent, z_2, image_1, local_2 = call(
+        join_third_body,
+        [((devices, 3, 2, LANES),), z_shape, pair, pair],
+        [SMEM] + [VMEM] * 14,
+        assembled + [blocks_scratch, pltpu.VMEM(sums_shape, f32)],
+        flops=1 << 26,
+        grant=60 * 1024,
+    )(device, got_3, coarse_parts, *finish(local_1, z_1), select, sums_2, terms_1, early)
     got_4 = exchange(sent)
     ghost = shifted(z_2, 1)
     (late,) = call(late_body, [pair], [VMEM] * 4, flops=1 << 20)(local_2, z_2, ghost, corner_modes)

time: 139 us -> 137 us (0.986)
  Pallas kernels: 33 us -> 29.7 us
  waiting for transfers between devices: 20.1 us -> 22.3 us
    pallas_call x4 -> x2, Pallas kernels: 16 us -> 12.6 us  [the longest x1 6.78 us: shards(): call(join_third_body, [((devices, 3, 2, LANES),), z_shape, pair, pair], [...]
    all_to_all x4, waiting for transfers between devices: 0.01 us -> 2.26 us  [exchange(): return lax.all_to_all(pieces, axes, split_axis=0, concat_axis=0, tiled=True)]
  transfers between devices with their start and end apart: 11 -> 11, of which waited for: 5 -> 7; matrix products, arithmetic and copies ran while one was open for 1% -> 1% of each run, Pallas kernels for 13% -> 8%
where the time goes in v8:
time: 137 us; the launch traced here: 136 us
  starting transfers between devices  48.2 us (35%)
  Pallas kernels  29.7 us (22%)
  blocking collectives  24.9 us (18%)
  waiting for transfers between devices  22.3 us (16%)
  local copies, waits for them, and re-layouts  10 us (7%)
    all_to_all x4, starting transfers between devices, exchange(): return lax.all_to_all(pieces, axes, split_axis=0, concat_axis=0, tiled=True)  25.9 us
    all_to_all x2, blocking collectives, exchange(): return lax.all_to_all(pieces, axes, split_axis=0, concat_axis=0, tiled=True)  24.9 us
    ppermute x7, starting transfers between devices, shifted(): lax.ppermute(array, AXES, [(i, (i + by) % count) for i in range(count)])  22.4 us
    ppermute x7, waiting for transfers between devices, shifted(): lax.ppermute(array, AXES, [(i, (i + by) % count) for i in range(count)])  20.1 us
    unnamed x62, local copies, waits for them, and re-layouts  8.57 us
    pallas_call x1, Pallas kernels, shards(): call(join_third_body, [((devices, 3, 2, LANES),), z_shape, pair, pair], [...  6.78 us
    pallas_call x1, Pallas kernels, shards(): call(prep_body, [((2 * basis_rows.shape[0], rank), bf16), ((devices, 4, L...  6.06 us
    pallas_call x1, Pallas kernels, shards(): call(join_second_body, [((4 * devices, 4, LANES),), z_shape, z_shape, pai...  5.83 us
  transfers between devices with their start and end apart: 11, of which 7 were waited for; matrix products, arithmetic and copies ran while one was open for 1% of the time, Pallas kernels for 8%

profile of v8, /device:TPU:0, one launch (start us, length us, event | category | flops | bytes accessed | tf_op | source)
XLA Modules:
  0.0 136.1 jit_solution(12758474035394554302)
XLA Ops:
  0.6 2.4 %shard_map.137 = (f32[128,8,128]{2,1,0:T(8,128)}, f32[2,8,512]{2,1,0:T(8,128)}) custom-call(s32[1]{0:T(128)} %bitcast.device_ref, f32[8,2,512]{2,1,0:T(2,128)} %load_ref.1, f32[2,512]{1,0:T(2,128)} %inertia_ref.1, f32[8,2,512]{2,1,0:T(2,128)} %disp_ref.3, f32[8,2,512]{2,1,0:T(2,128)} %vel_ref.3, f32[8,2,512]{2,1,0:T(2,128)} %acc_ref.3, f32[2,64,512]{2,1,0:T(8,128)} %modes_ref.13), custom_call_target="tpu_custom_call" | custom-call | bytes 1048576 | tf_op jit(solution)/shard_map/pallas_call | solution.py:489
  3.0 11.2 %all-to-all-start = ((f32[128,8,128]{2,1,0:T(8,128)}), f32[128,8,128]{2,1,0:T(8,128)S(1)}, u32[]{:S(2)}, u32[]{:S(2)}) async-start(f32[128,8,128]{2,1,0:T(8,128)} %get-tuple-element.41), calls=%async_computation | async-start | bytes 1048576 | tf_op jit(solution)/shard_map/all_to_all | solution.py:31
  14.2 7.1 %collective-permute-start = (f32[2,64,512]{2,1,0:T(8,128)}, f32[2,64,512]{2,1,0:T(8,128)S(1)}, u32[]{:S(2)}, u32[]{:S(2)}) collective-permute-start(f32[2,64,512]{2,1,0:T(8,128)} %modes_ref.13), channel_id=1, source_target_pairs={{0,127},{1,0},{2,1},{3,2},{4,3},{5,4},{6,5},{7,6},{8,7},{9,8},{10,... | collective-permute-start | bytes 786440 | tf_op jit(solution)/shard_map/ppermute | solution.py:40
  21.3 0.8 slice_bitcast_fusion
  22.1 1.6 %copy-done = f32[2,512,512]{2,1,0:T(8,128)S(1)} copy-done((f32[2,512,512]{2,1,0:T(8,128)S(1)}, f32[2,512,512]{2,1,0:T(8,128)}, u32[]{:S(2)}) %copy-start) | copy-done | bytes 2097176
  23.7 1.6 %copy-done.7 = f32[64,8192]{1,0:T(8,128)S(1)} copy-done((f32[64,8192]{1,0:T(8,128)S(1)}, f32[64,8192]{1,0:T(8,128)}, u32[]{:S(2)}) %copy-start.7) | copy-done | bytes 2097176
  25.3 0.8 copy-done.19
  26.0 1.6 %shard_map.138 = (bf16[128,8192]{1,0:T(8,128)(2,1)S(1)}, f32[2,8,512]{2,1,0:T(8,128)S(1)}) custom-call(f32[64,8192]{1,0:T(8,128)S(1)} %copy-done.7, f32[2,8,512]{2,1,0:T(8,128)S(1)} %copy-done.19, f32[2,512,512]{2,1,0:T(8,128)S(1)} %copy-done), custom_call_target="tpu_custom_call" | custom-call | flops 67108864 | bytes 1048576 | tf_op jit(solution)/shard_map/pallas_call | solution.py:495
  27.7 3.2 %collective-permute-done.1.left_ref = f32[64,128]{1,0:T(8,128)S(1)} collective-permute-done((f32[64,128]{1,0:T(8,128)S(1)}, f32[64,128]{1,0:T(8,128)S(1)}, u32[]{:S(2)}, u32[]{:S(2)}) %collective-permute-start.1) | collective-permute-done | bytes 32800 | tf_op jit(solution)/shard_map/ppermute | solution.py:40
  30.9 0.9 shard_map.139
  31.8 0.8 copy-done.8
  32.6 1.0 shard_map.140
  33.6 0.9 copy-done.9
  34.5 6.4 %all-to-all-start.1 = ((f32[384,4,128]{2,1,0:T(4,128)}), f32[384,4,128]{2,1,0:T(4,128)}, u32[]{:S(2)}, u32[]{:S(2)}) async-start(f32[384,4,128]{2,1,0:T(4,128)} %copy-done.9), calls=%async_computation.1 | async-start | bytes 1572864 | tf_op jit(solution)/shard_map/all_to_all | solution.py:31
  40.9 0.2 shard_map.142
  41.1 0.6 copy-done.18
  41.8 0.9 collective-permute-start.2
  42.7 6.3 %collective-permute-start.3 = (f32[8,128]{1,0:T(8,128)S(1)}, f32[8,128]{1,0:T(8,128)S(1)}, u32[]{:S(2)}, u32[]{:S(2)}) collective-permute-start(f32[8,128]{1,0:T(8,128)S(1)} %get-tuple-element.52), channel_id=1, source_target_pairs={{0,127},{1,0},{2,1},{3,2},{4,3},{5,4},{6,5},{7,6},{8,7},{9,8},{10,... | collective-permute-start | bytes 12296 | tf_op jit(solution)/shard_map/ppermute | solution.py:40
  48.9 6.1 %shard_map.141 = (bf16[2048,256]{1,0:T(8,128)(2,1)}, f32[128,4,128]{2,1,0:T(4,128)}, bf16[128,512]{1,0:T(8,128)(2,1)}) custom-call(f32[128,8,256]{2,1,0:T(8,128)} %bitcast.7, s32[1,128]{1,0:T(1,128)} %bitcast.8, f32[8,64]{1,0:T(8,128)} %copy-done.17), custom_call_target="tpu_custom_call" | custom-call | flops 67108864 | bytes 1048576 | tf_op jit(solution)/shard_map/pallas_call | solution.py:516
  55.0 0.5 collective-permute-done.2.from_left_ref
  55.5 1.1 all-to-all-done.1.got_ref
  56.6 5.8 %shard_map.143 = (f32[512,4,128]{2,1,0:T(4,128)}, f32[8,64]{1,0:T(8,128)}, f32[8,64]{1,0:T(8,128)}, f32[2,8,512]{2,1,0:T(8,128)}, f32[2,8,512]{2,1,0:T(8,128)}, /*index=5*/f32[8,128]{1,0:T(8,128)}) custom-call(s32[1]{0:T(128)} %bitcast.device_ref, f32[384,4,128]{2,1,0:T(4,128)} %all-to-all-done.1.got_ref, bf16[128,8192]{1,0:T(8,128)(2,1)} %copy-done.1, ...), custom_call_target="tpu_custom_call" | custom-call | flops 67108864 | bytes 1048576 | tf_op jit(solution)/shard_map/pallas_call | solution.py:523
  62.4 0.0 copy-start.3
  62.5 4.8 %all-to-all-start.2 = ((f32[512,4,128]{2,1,0:T(4,128)}), f32[512,4,128]{2,1,0:T(4,128)S(1)}, u32[]{:S(2)}, u32[]{:S(2)}) async-start(f32[512,4,128]{2,1,0:T(4,128)} %get-tuple-element.55), calls=%async_computation.2 | async-start | bytes 2097152 | tf_op jit(solution)/shard_map/all_to_all | solution.py:31
  67.3 0.2 shard_map.144
  67.5 0.6 copy-done.23
  68.1 0.8 collective-permute-start.4
  68.9 6.3 %collective-permute-start.5 = (f32[8,128]{1,0:T(8,128)S(1)}, f32[8,128]{1,0:T(8,128)S(1)}, u32[]{:S(2)}, u32[]{:S(2)}) collective-permute-start(f32[8,128]{1,0:T(8,128)S(1)} %get-tuple-element.60), channel_id=1, source_target_pairs={{0,127},{1,0},{2,1},{3,2},{4,3},{5,4},{6,5},{7,6},{8,7},{9,8},{10,... | collective-permute-start | bytes 12296 | tf_op jit(solution)/shard_map/ppermute | solution.py:40
  75.3 0.2 shard_map.145.early_ref
  75.6 0.6 copy-done.12
  76.2 3.5 %collective-permute-done.5.from_right_ref = f32[8,128]{1,0:T(8,128)S(1)} collective-permute-done((f32[8,128]{1,0:T(8,128)S(1)}, f32[8,128]{1,0:T(8,128)S(1)}, u32[]{:S(2)}, u32[]{:S(2)}) %collective-permute-start.5) | collective-permute-done | bytes 4128 | tf_op jit(solution)/shard_map/ppermute | solution.py:40
  79.7 5.2 %collective-permute-done.4.from_left_ref = f32[8,256]{1,0:T(8,128)S(1)} collective-permute-done((f32[8,256]{1,0:T(8,128)S(1)}, f32[8,256]{1,0:T(8,128)S(1)}, u32[]{:S(2)}, u32[]{:S(2)}) %collective-permute-start.4) | collective-permute-done | bytes 8224 | tf_op jit(solution)/shard_map/ppermute | solution.py:40
  84.9 1.1 all-to-all-done.2.got_ref
  86.1 1.0 copy-done.26
  87.1 6.8 %shard_map.146 = (f32[128,3,2,128]{3,2,1,0:T(2,128)}, f32[8,64]{1,0:T(8,128)}, f32[2,8,512]{2,1,0:T(8,128)}, f32[2,8,512]{2,1,0:T(8,128)}) custom-call(s32[1]{0:T(128)} %bitcast.device_ref, f32[512,4,128]{2,1,0:T(4,128)} %copy-done.26, bf16[128,8192]{1,0:T(8,128)(2,1)} %copy-done.1, f32[2,8,512]{2,1,0:T(8,128)} %copy-done.23, f32[8,256]{1,0:T(8,128)} %copy-done.27, ...), custom_call_target="tpu_custom_call" | custom-call | flops 67108864 | bytes 1048576 | tf_op jit(solution)/shard_map/pallas_call | solution.py:533
  93.9 0.0 copy-start.22
  93.9 0.0 copy-start.13
  93.9 16.8 %all_to_all.30.got_ref.square_ref = f32[128,3,2,128]{3,2,1,0:T(2,128)S(1)} all-to-all(f32[128,3,2,128]{3,2,1,0:T(2,128)} %get-tuple-element.67), channel_id=1, replica_groups=mesh['sub_0'=4,'sub_1'=4,'sub_2'=2,'grp'=4] {'sub_0','sub_1','sub_2','grp'}, dimensions={0} | all-to-all | bytes 786432 | tf_op jit(solution)/shard_map/all_to_all | solution.py:31
  110.7 0.8 shard_map.148
  111.5 8.2 %all_to_all.31 = f32[8,8,384]{2,1,0:T(8,128)S(1)} all-to-all(f32[8,8,384]{2,1,0:T(8,128)S(1)} %get-tuple-element.72), channel_id=1, replica_groups=mesh['sub_0'=4,'sub_1'=4,'sub_2'=2,'grp'=4] {'sub_2','grp'}, dimensions={0} | all-to-all | bytes 196608 | tf_op jit(solution)/shard_map/all_to_all | solution.py:31
  119.7 0.7 broadcast_in_dim.3
  120.4 3.5 %all-to-all-start.5 = ((f32[16,8,384]{2,1,0:T(8,128)}), f32[16,8,384]{2,1,0:T(8,128)S(1)}, u32[]{:S(2)}, u32[]{:S(2)}) async-start(f32[16,8,384]{2,1,0:T(8,128)} %broadcast_in_dim.3), calls=%async_computation.5 | async-start | bytes 393216 | tf_op jit(solution)/shard_map/all_to_all | solution.py:31
  123.9 0.9 collective-permute-start.6
  124.8 7.6 %collective-permute-done.6.ghost_ref = f32[8,64]{1,0:T(8,128)S(1)} collective-permute-done((f32[8,64]{1,0:T(8,128)S(1)}, f32[8,64]{1,0:T(8,128)S(1)}, u32[]{:S(2)}, u32[]{:S(2)}) %collective-permute-start.6) | collective-permute-done | bytes 2080 | tf_op jit(solution)/shard_map/ppermute | solution.py:40
  132.5 0.3 shard_map.147.late_ref
  132.7 0.0 copy-done.15
  132.7 0.7 shard_map.149
  133.5 2.6 %shard_map.150 = (f32[8,1024]{1,0:T(8,128)}, f32[8,256]{1,0:T(8,128)}, f32[8,128]{1,0:T(8,128)}) custom-call(f32[16,8,384]{2,1,0:T(8,128)S(1)} %all-to-all-done.5.got_ref, f32[128,3,2,128]{3,2,1,0:T(2,128)S(1)} %all_to_all.30.got_ref.square_ref, bf16[2048,256]{1,0:T(8,128)(2,1)S(1)} %copy-done.5, f32[8,1024]{1,0:T(8,128)S(1)} %get-tuple-element.73.rows_ref), custom_call_target="tpu_custom_call" | custom-call | flops 16777216 | bytes 1048576 | tf_op jit(solution)/shard_map/pallas_call | solution.py:561
  (55 shorter events, 0.1 us)
Async XLA Ops:
  3.0 29.6 %all-to-all-start = ((f32[128,8,128]{2,1,0:T(8,128)}), f32[128,8,128]{2,1,0:T(8,128)S(1)}, u32[]{:S(2)}, u32[]{:S(2)}) async-start(f32[128,8,128]{2,1,0:T(8,128)} %get-tuple-element.41), calls=%async_computation | async-start | bytes 1048576 | tf_op jit(solution)/shard_map/all_to_all | solution.py:31
  14.2 16.7 %collective-permute-start = (f32[2,64,512]{2,1,0:T(8,128)}, f32[2,64,512]{2,1,0:T(8,128)S(1)}, u32[]{:S(2)}, u32[]{:S(2)}) collective-permute-start(f32[2,64,512]{2,1,0:T(8,128)} %modes_ref.13), channel_id=1, source_target_pairs={{0,127},{1,0},{2,1},{3,2},{4,3},{5,4},{6,5},{7,6},{8,7},{9,8},{10,... | collective-permute-start | bytes 786440 | tf_op jit(solution)/shard_map/ppermute | solution.py:40
  22.1 8.8 %collective-permute-start.1 = (f32[64,128]{1,0:T(8,128)S(1)}, f32[64,128]{1,0:T(8,128)S(1)}, u32[]{:S(2)}, u32[]{:S(2)}) collective-permute-start(f32[64,128]{1,0:T(8,128)S(1)} %slice_bitcast_fusion), channel_id=1, source_target_pairs={{0,1},{1,2},{2,3},{3,4},{4,5},{5,6},{6,7},{7,8},{8,9},{9,10},{10,1... | collective-permute-start | bytes 98312 | tf_op jit(solution)/shard_map/ppermute | solution.py:40
  22.1 1.6 %copy-start = (f32[2,512,512]{2,1,0:T(8,128)S(1)}, f32[2,512,512]{2,1,0:T(8,128)}, u32[]{:S(2)}) copy-start(f32[2,512,512]{2,1,0:T(8,128)} %rr_ref.5) | copy-start | bytes 6291460
  23.7 1.6 %copy-start.7 = (f32[64,8192]{1,0:T(8,128)S(1)}, f32[64,8192]{1,0:T(8,128)}, u32[]{:S(2)}) copy-start(f32[64,8192]{1,0:T(8,128)} %matrix_ref.1) | copy-start | bytes 6291460
  25.3 0.8 copy-start.19
  26.0 4.8 %copy-start.2 = (f32[2,64,512]{2,1,0:T(8,128)S(1)}, f32[2,64,512]{2,1,0:T(8,128)}, u32[]{:S(2)}) copy-start(f32[2,64,512]{2,1,0:T(8,128)} %modes_ref.13) | copy-start | bytes 786436
  27.7 6.9 %copy-start.1 = (bf16[128,8192]{1,0:T(8,128)(2,1)}, bf16[128,8192]{1,0:T(8,128)(2,1)S(1)}, u32[]{:S(2)}) copy-start(bf16[128,8192]{1,0:T(8,128)(2,1)S(1)} %get-tuple-element.43.parts_ref) | copy-start | bytes 6291460
  30.9 3.7 %copy-start.6 = (f32[2,64,512]{2,1,0:T(8,128)}, f32[2,64,512]{2,1,0:T(8,128)S(1)}, u32[]{:S(2)}) copy-start(f32[2,64,512]{2,1,0:T(8,128)S(1)} %collective-permute-done.right_ref) | copy-start | bytes 786436
  31.8 0.8 copy-start.8
  32.6 1.9 %copy-start.11 = (f32[64,256]{1,0:T(8,128)}, f32[64,256]{1,0:T(8,128)S(1)}, u32[]{:S(2)}) copy-start(f32[64,256]{1,0:T(8,128)S(1)} %get-tuple-element.45.coupling_ref) | copy-start | bytes 196612
  33.6 0.9 copy-start.9
  34.5 14.4 %copy-start.17 = (f32[8,64]{1,0:T(8,128)}, f32[8,64]{1,0:T(8,128)S(1)}, u32[]{:S(2)}) copy-start(f32[8,64]{1,0:T(8,128)S(1)} %get-tuple-element.48.after_ref.z_ref.before_ref) | copy-start | bytes 6148
  34.5 22.0 %all-to-all-start.1 = ((f32[384,4,128]{2,1,0:T(4,128)}), f32[384,4,128]{2,1,0:T(4,128)}, u32[]{:S(2)}, u32[]{:S(2)}) async-start(f32[384,4,128]{2,1,0:T(4,128)} %copy-done.9), calls=%async_computation.1 | async-start | bytes 1572864 | tf_op jit(solution)/shard_map/all_to_all | solution.py:31
  41.1 0.6 copy-start.18
  41.8 13.7 %collective-permute-start.2 = (f32[8,256]{1,0:T(8,128)S(1)}, f32[8,256]{1,0:T(8,128)S(1)}, u32[]{:S(2)}, u32[]{:S(2)}) collective-permute-start(f32[8,256]{1,0:T(8,128)S(1)} %get-tuple-element.51), channel_id=1, source_target_pairs={{0,1},{1,2},{2,3},{3,4},{4,5},{5,6},{6,7},{7,8},{8,9},{9,10},{10,1... | collective-permute-start | bytes 24584 | tf_op jit(solution)/shard_map/ppermute | solution.py:40
  42.7 12.3 %collective-permute-start.3 = (f32[8,128]{1,0:T(8,128)S(1)}, f32[8,128]{1,0:T(8,128)S(1)}, u32[]{:S(2)}, u32[]{:S(2)}) collective-permute-start(f32[8,128]{1,0:T(8,128)S(1)} %get-tuple-element.52), channel_id=1, source_target_pairs={{0,127},{1,0},{2,1},{3,2},{4,3},{5,4},{6,5},{7,6},{8,7},{9,8},{10,... | collective-permute-start | bytes 12296 | tf_op jit(solution)/shard_map/ppermute | solution.py:40
  55.0 1.6 %copy-start.29 = (f32[8,128]{1,0:T(8,128)}, f32[8,128]{1,0:T(8,128)S(1)}, u32[]{:S(2)}) copy-start(f32[8,128]{1,0:T(8,128)S(1)} %collective-permute-done.3.from_right_ref) | copy-start | bytes 12292
  55.5 1.1 copy-start.28
  62.4 4.8 %copy-start.3 = (f32[2,64,512]{2,1,0:T(8,128)S(1)}, f32[2,64,512]{2,1,0:T(8,128)}, u32[]{:S(2)}) copy-start(f32[2,64,512]{2,1,0:T(8,128)} %modes_ref.13) | copy-start | bytes 786436
  62.4 4.8 %copy-start.21 = (f32[2,8,512]{2,1,0:T(8,128)S(1)}, f32[2,8,512]{2,1,0:T(8,128)}, u32[]{:S(2)}) copy-start(f32[2,8,512]{2,1,0:T(8,128)} %get-tuple-element.56.local_ref) | copy-start | bytes 98308
  62.4 4.8 %copy-start.24 = (f32[8,64]{1,0:T(8,128)S(1)}, f32[8,64]{1,0:T(8,128)}, u32[]{:S(2)}) copy-start(f32[8,64]{1,0:T(8,128)} %get-tuple-element.57.z_ref.before_ref) | copy-start | bytes 6148
  62.4 12.8 %copy-start.10 = (bf16[128,512]{1,0:T(8,128)(2,1)S(1)}, bf16[128,512]{1,0:T(8,128)(2,1)}, u32[]{:S(2)}) copy-start(bf16[128,512]{1,0:T(8,128)(2,1)} %get-tuple-element.61.select_ref) | copy-start | bytes 393220
  62.5 12.8 %copy-start.16 = (f32[2,8,512]{2,1,0:T(8,128)S(1)}, f32[2,8,512]{2,1,0:T(8,128)}, u32[]{:S(2)}) copy-start(f32[2,8,512]{2,1,0:T(8,128)} %get-tuple-element.54.green_ref) | copy-start | bytes 98308
  62.5 23.6 %all-to-all-start.2 = ((f32[512,4,128]{2,1,0:T(4,128)}), f32[512,4,128]{2,1,0:T(4,128)S(1)}, u32[]{:S(2)}, u32[]{:S(2)}) async-start(f32[512,4,128]{2,1,0:T(4,128)} %get-tuple-element.55), calls=%async_computation.2 | async-start | bytes 2097152 | tf_op jit(solution)/shard_map/all_to_all | solution.py:31
  67.5 0.6 copy-start.23
  68.1 16.8 %collective-permute-start.4 = (f32[8,256]{1,0:T(8,128)S(1)}, f32[8,256]{1,0:T(8,128)S(1)}, u32[]{:S(2)}, u32[]{:S(2)}) collective-permute-start(f32[8,256]{1,0:T(8,128)S(1)} %get-tuple-element.59), channel_id=1, source_target_pairs={{0,1},{1,2},{2,3},{3,4},{4,5},{5,6},{6,7},{7,8},{8,9},{9,10},{10,1... | collective-permute-start | bytes 24584 | tf_op jit(solution)/shard_map/ppermute | solution.py:40
  68.9 10.8 %collective-permute-start.5 = (f32[8,128]{1,0:T(8,128)S(1)}, f32[8,128]{1,0:T(8,128)S(1)}, u32[]{:S(2)}, u32[]{:S(2)}) collective-permute-start(f32[8,128]{1,0:T(8,128)S(1)} %get-tuple-element.60), channel_id=1, source_target_pairs={{0,127},{1,0},{2,1},{3,2},{4,3},{5,4},{6,5},{7,6},{8,7},{9,8},{10,... | collective-permute-start | bytes 12296 | tf_op jit(solution)/shard_map/ppermute | solution.py:40
  75.5 0.6 copy-start.12
  79.7 6.4 %copy-start.30 = (f32[8,128]{1,0:T(8,128)}, f32[8,128]{1,0:T(8,128)S(1)}, u32[]{:S(2)}) copy-start(f32[8,128]{1,0:T(8,128)S(1)} %collective-permute-done.5.from_right_ref) | copy-start | bytes 12292
  84.9 1.1 copy-start.27
  86.1 1.0 copy-start.26
  87.1 23.6 %copy-start.5 = (bf16[2048,256]{1,0:T(8,128)(2,1)S(1)}, bf16[2048,256]{1,0:T(8,128)(2,1)}, u32[]{:S(2)}) copy-start(bf16[2048,256]{1,0:T(8,128)(2,1)} %get-tuple-element.68.basis_ref) | copy-start | bytes 3145732
  93.9 30.1 %copy-start.25 = (f32[8,64]{1,0:T(8,128)S(1)}, f32[8,64]{1,0:T(8,128)}, u32[]{:S(2)}) copy-start(f32[8,64]{1,0:T(8,128)} %get-tuple-element.66.z_ref) | copy-start | bytes 6148
  93.9 38.6 %copy-start.4 = (f32[2,64,512]{2,1,0:T(8,128)S(1)}, f32[2,64,512]{2,1,0:T(8,128)}, u32[]{:S(2)}) copy-start(f32[2,64,512]{2,1,0:T(8,128)} %modes_ref.13) | copy-start | bytes 786436
  93.9 38.6 %copy-start.22 = (f32[2,8,512]{2,1,0:T(8,128)S(1)}, f32[2,8,512]{2,1,0:T(8,128)}, u32[]{:S(2)}) copy-start(f32[2,8,512]{2,1,0:T(8,128)} %get-tuple-element.65.local_ref) | copy-start | bytes 98308
  93.9 38.8 %copy-start.13 = (f32[8,2,512]{2,1,0:T(2,128)S(1)}, f32[8,2,512]{2,1,0:T(2,128)}, u32[]{:S(2)}) copy-start(f32[8,2,512]{2,1,0:T(2,128)} %disp_ref.3) | copy-start | bytes 98308
  93.9 38.8 %copy-start.14 = (f32[8,2,512]{2,1,0:T(2,128)S(1)}, f32[8,2,512]{2,1,0:T(2,128)}, u32[]{:S(2)}) copy-start(f32[8,2,512]{2,1,0:T(2,128)} %vel_ref.3) | copy-start | bytes 98308
  93.9 38.8 %copy-start.15 = (f32[8,2,512]{2,1,0:T(2,128)S(1)}, f32[8,2,512]{2,1,0:T(2,128)}, u32[]{:S(2)}) copy-start(f32[8,2,512]{2,1,0:T(2,128)} %acc_ref.3) | copy-start | bytes 98308
  93.9 38.8 %copy-start.20 = (f32[2,8,512]{2,1,0:T(8,128)S(1)}, f32[2,8,512]{2,1,0:T(8,128)}, u32[]{:S(2)}) copy-start(f32[2,8,512]{2,1,0:T(8,128)} %get-tuple-element.64.image_ref) | copy-start | bytes 98308
  120.4 13.1 %all-to-all-start.5 = ((f32[16,8,384]{2,1,0:T(8,128)}), f32[16,8,384]{2,1,0:T(8,128)S(1)}, u32[]{:S(2)}, u32[]{:S(2)}) async-start(f32[16,8,384]{2,1,0:T(8,128)} %broadcast_in_dim.3), calls=%async_computation.5 | async-start | bytes 393216 | tf_op jit(solution)/shard_map/all_to_all | solution.py:31
  123.9 8.5 %collective-permute-start.6 = (f32[8,64]{1,0:T(8,128)S(1)}, f32[8,64]{1,0:T(8,128)S(1)}, u32[]{:S(2)}, u32[]{:S(2)}) collective-permute-start(f32[8,64]{1,0:T(8,128)S(1)} %copy-done.25), channel_id=1, source_target_pairs={{0,1},{1,2},{2,3},{3,4},{4,5},{5,6},{6,7},{7,8},{8,9},{9,10},{10,1... | collective-permute-start | bytes 6152 | tf_op jit(solution)/shard_map/ppermute | solution.py:40

commit v9 on v8

--- a/solution.py
+++ b/solution.py
@@ -72,7 +72,7 @@
     return high, middle, (rest - middle.astype(f32)).astype(bf16)
 
 
-def start_body(device_ref, load_ref, inertia_ref, disp_ref, vel_ref, acc_ref, modes_ref, start_ref, right_ref):
+def start_body(device_ref, load_ref, inertia_ref, disp_ref, vel_ref, acc_ref, modes_ref, start_ref, right_ref, to_left_ref, to_right_ref):
     blank = jnp.zeros((NC, modes_ref.shape[2]), f32)
     fields = []
     for s in range(2):
@@ -87,6 +87,10 @@
     blocks = jnp.where(even, blocks, pltpu.roll(blocks, HALF, 1))
     for d in range(start_ref.shape[0]):
         start_ref[d] = blocks
+    unknowns = modes_ref.shape[2]
+    to_left_ref[:, :unknowns] = modes_ref[0]
+    to_left_ref[:, unknowns:] = modes_ref[1, :, :NI]
+    to_right_ref[...] = modes_ref[1, :, unknowns - NI :]
 
 
 def pre_body(matrix_ref, right_ref, rr_ref, parts_ref, local_ref):
@@ -102,7 +106,8 @@
     last = modes_ref.shape[2] - NI
     even = jnp.where(lax.rem(device_ref[0], 2) == 0, 1, 0)
     first, final = [modes_ref[s, :, :NI] for s in range(2)], [modes_ref[s, :, last:] for s in range(2)]
-    right_first, right_final = [right_ref[s, :, :NI] for s in range(2)], right_ref[0, :, last:]
+    unknowns = modes_ref.shape[2]
+    right_first, right_final = [right_ref[:, :NI], right_ref[:, unknowns:]], right_ref[:, last:unknowns]
     left = left_ref[...]
     rows = [
         {0: left[:NC]},
@@ -120,7 +125,7 @@
     blank = jnp.zeros((NC, modes_ref.shape[2]), f32)
     unit_0 = jnp.concatenate([modes_ref[0, NC:], blank], axis=0)
     unit_1 = modes_ref[1]
-    unit_2 = jnp.concatenate([blank, right_ref[0, :NC]], axis=0)
+    unit_2 = jnp.concatenate([blank, right_ref[:NC, :unknowns]], axis=0)
     jumps = jnp.concatenate(
         [-unit_0[:, :NI], unit_0[:, last:] - unit_1[:, :NI], unit_1[:, last:] - unit_2[:, :NI], unit_2[:, last:]], axis=1
     )
@@ -156,7 +161,7 @@
     field_ref[0], field_ref[1] = mine_0, mine_1
     jump_a = from_left_ref[:, :NI] - mine_0[:, :NI]
     jump_b = mine_0[:, last:] - mine_1[:, :NI]
-    jump_c = mine_1[:, last:] - (from_right_ref[...] + dot(z_ref[:, NC:], right_ref[0, :NC, :NI], NN))
+    jump_c = mine_1[:, last:] - (from_right_ref[...] + dot(z_ref[:, NC:], right_ref[:NC, :NI], NN))
     inner = jnp.zeros((mine_1.shape[0], 1), f32)
     outs = []
     for s, (first, final) in enumerate([(-jump_a, jump_b), (-jump_b, jump_c)]):
@@ -352,7 +357,7 @@
         square = square + got_ref[4 * d + 3]
     y_0 = local_ref[0] + dot(z[:, :NC], modes_ref[0, NC:], NN)
     y_1 = local_ref[1] + dot(z, modes_ref[1], NN)
-    y_2 = dot(z[:, NC:], right_ref[0, :NC], NN)
+    y_2 = dot(z[:, NC:], right_ref[:NC, : modes_ref.shape[2]], NN)
     rows = by_offset(y_0) + by_offset(y_1) + by_offset(y_2)
     rows.append(jnp.zeros((32, y_0.shape[1]), f32))
     late = choose_rows(select_ref, jnp.concatenate(rows, axis=0))
@@ -479,19 +484,22 @@
     devices = lax.axis_size(AXES)
     coarse_total = coarse_inverse.shape[1]
     rank = basis_rows.shape[1]
-    last = unknowns - NI
     device = lax.axis_index(AXES).reshape(1).astype(jnp.int32)
     pair = ((2, case_count, unknowns),)
     z_shape = ((case_count, 2 * NC),)
     blocks_shape = ((case_count, 2 * LANES),)
     assembled = [pltpu.VMEM((case_count, coarse_total), f32)]
 
-    start, right_side = call(start_body, [((devices, case_count, LANES),), pair], [SMEM] + [VMEM] * 6, grant=60 * 1024)(
-        device, load_next, inertia, disp_now, vel_now, acc_now, corner_modes
-    )
+    modes_rows = corner_modes.shape[1]
+    start, right_side, to_left, to_right = call(
+        start_body,
+        [((devices, case_count, LANES),), pair, ((modes_rows, unknowns + NI),), ((modes_rows, NI),)],
+        [SMEM] + [VMEM] * 6,
+        grant=60 * 1024,
+    )(device, load_next, inertia, disp_now, vel_now, acc_now, corner_modes)
     got_1 = exchange(start)
-    left_edge = shifted(corner_modes[1, :, last:], 1)
-    right_modes = shifted(corner_modes, -1)
+    left_edge = shifted(to_right, 1)
+    right_modes = shifted(to_left, -1)
     coarse_parts, local_0 = call(pre_body, [((4 * NC, coarse_total), bf16), pair], [VMEM] * 3, flops=1 << 26)(
         coarse_inverse, right_side, rr_inverse
     )

time: 137 us -> 137 us (level)
  transfers between devices with their start and end apart: 11 -> 11, of which waited for: 7 -> 7; matrix products, arithmetic and copies ran while one was open for 1% -> 0% of each run, Pallas kernels for 8% -> 8%
where the time goes in v9:
time: 137 us; the launch traced here: 136 us
  starting transfers between devices  48 us (35%)
  Pallas kernels  29.6 us (22%)
  blocking collectives  24.9 us (18%)
  waiting for transfers between devices  22.5 us (16%)
  local copies, waits for them, and re-layouts  9.91 us (7%)
    all_to_all x4, starting transfers between devices, exchange(): return lax.all_to_all(pieces, axes, split_axis=0, concat_axis=0, tiled=True)  25.6 us
    all_to_all x2, blocking collectives, exchange(): return lax.all_to_all(pieces, axes, split_axis=0, concat_axis=0, tiled=True)  24.9 us
    ppermute x7, starting transfers between devices, shifted(): lax.ppermute(array, AXES, [(i, (i + by) % count) for i in range(count)])  22.4 us
    ppermute x7, waiting for transfers between devices, shifted(): lax.ppermute(array, AXES, [(i, (i + by) % count) for i in range(count)])  20.3 us
    unnamed x62, local copies, waits for them, and re-layouts  9.22 us
    pallas_call x1, Pallas kernels, shards(): call(join_third_body, [((devices, 3, 2, LANES),), z_shape, pair, pair], [...  6.75 us
    pallas_call x1, Pallas kernels, shards(): call(prep_body, [((2 * basis_rows.shape[0], rank), bf16), ((devices, 4, L...  6.08 us
    pallas_call x1, Pallas kernels, shards(): call(join_second_body, [((4 * devices, 4, LANES),), z_shape, z_shape, pai...  5.8 us
  transfers between devices with their start and end apart: 11, of which 7 were waited for; matrix products, arithmetic and copies ran while one was open for 0% of the time, Pallas kernels for 8%

profile of v9, /device:TPU:0, one launch (start us, length us, event | category | flops | bytes accessed | tf_op | source)
XLA Modules:
  0.0 135.9 jit_solution(13005441487040196873)
XLA Ops:
  0.6 2.4 %shard_map.137 = (f32[128,8,128]{2,1,0:T(8,128)}, f32[2,8,512]{2,1,0:T(8,128)}, f32[64,640]{1,0:T(8,128)}, f32[64,128]{1,0:T(8,128)}) custom-call(s32[1]{0:T(128)} %bitcast.device_ref, f32[8,2,512]{2,1,0:T(2,128)} %load_ref.1, f32[2,512]{1,0:T(2,128)} %inertia_ref.1, f32[8,2,512]{2,1,0:T(2,128)} %disp_ref.3, f32[8,2,512]{2,1,0:T(2,128)} %vel_ref.3, ...), custom_call_target="tpu_custom_call" | custom-call | bytes 1048576 | tf_op jit(solution)/shard_map/pallas_call | solution.py:494
  3.0 11.2 %all-to-all-start = ((f32[128,8,128]{2,1,0:T(8,128)}), f32[128,8,128]{2,1,0:T(8,128)S(1)}, u32[]{:S(2)}, u32[]{:S(2)}) async-start(f32[128,8,128]{2,1,0:T(8,128)} %get-tuple-element.43), calls=%async_computation | async-start | bytes 1048576 | tf_op jit(solution)/shard_map/all_to_all | solution.py:31
  14.2 7.1 %collective-permute-start = (f32[64,640]{1,0:T(8,128)}, f32[64,640]{1,0:T(8,128)S(1)}, u32[]{:S(2)}, u32[]{:S(2)}) collective-permute-start(f32[64,640]{1,0:T(8,128)} %get-tuple-element.46), channel_id=1, source_target_pairs={{0,127},{1,0},{2,1},{3,2},{4,3},{5,4},{6,5},{7,6},{8,7},{9,8},{10,... | collective-permute-start | bytes 491528 | tf_op jit(solution)/shard_map/ppermute | solution.py:40
  21.3 1.6 %copy-done = f32[2,512,512]{2,1,0:T(8,128)S(1)} copy-done((f32[2,512,512]{2,1,0:T(8,128)S(1)}, f32[2,512,512]{2,1,0:T(8,128)}, u32[]{:S(2)}) %copy-start) | copy-done | bytes 2097176
  22.9 1.6 %copy-done.7 = f32[64,8192]{1,0:T(8,128)S(1)} copy-done((f32[64,8192]{1,0:T(8,128)S(1)}, f32[64,8192]{1,0:T(8,128)}, u32[]{:S(2)}) %copy-start.7) | copy-done | bytes 2097176
  24.5 0.8 copy-done.20
  25.3 1.6 %shard_map.138 = (bf16[128,8192]{1,0:T(8,128)(2,1)S(1)}, f32[2,8,512]{2,1,0:T(8,128)S(1)}) custom-call(f32[64,8192]{1,0:T(8,128)S(1)} %copy-done.7, f32[2,8,512]{2,1,0:T(8,128)S(1)} %copy-done.20, f32[2,512,512]{2,1,0:T(8,128)S(1)} %copy-done), custom_call_target="tpu_custom_call" | custom-call | flops 67108864 | bytes 1048576 | tf_op jit(solution)/shard_map/pallas_call | solution.py:503
  26.9 3.4 %collective-permute-done.1.left_ref = f32[64,128]{1,0:T(8,128)S(1)} collective-permute-done((f32[64,128]{1,0:T(8,128)}, f32[64,128]{1,0:T(8,128)S(1)}, u32[]{:S(2)}, u32[]{:S(2)}) %collective-permute-start.1) | collective-permute-done | bytes 32800 | tf_op jit(solution)/shard_map/ppermute | solution.py:40
  30.3 0.9 shard_map.139
  31.2 0.8 copy-done.6
  32.0 0.7 copy-done.8
  32.7 1.0 shard_map.140
  33.7 0.9 copy-done.9
  34.6 6.2 %all-to-all-start.1 = ((f32[384,4,128]{2,1,0:T(4,128)}), f32[384,4,128]{2,1,0:T(4,128)}, u32[]{:S(2)}, u32[]{:S(2)}) async-start(f32[384,4,128]{2,1,0:T(4,128)} %copy-done.9), calls=%async_computation.1 | async-start | bytes 1572864 | tf_op jit(solution)/shard_map/all_to_all | solution.py:31
  40.8 0.2 shard_map.142
  41.0 0.6 copy-done.19
  41.6 0.9 collective-permute-start.2
  42.5 6.3 %collective-permute-start.3 = (f32[8,128]{1,0:T(8,128)S(1)}, f32[8,128]{1,0:T(8,128)S(1)}, u32[]{:S(2)}, u32[]{:S(2)}) collective-permute-start(f32[8,128]{1,0:T(8,128)S(1)} %get-tuple-element.56), channel_id=1, source_target_pairs={{0,127},{1,0},{2,1},{3,2},{4,3},{5,4},{6,5},{7,6},{8,7},{9,8},{10,... | collective-permute-start | bytes 12296 | tf_op jit(solution)/shard_map/ppermute | solution.py:40
  48.8 6.1 %shard_map.141 = (bf16[2048,256]{1,0:T(8,128)(2,1)}, f32[128,4,128]{2,1,0:T(4,128)}, bf16[128,512]{1,0:T(8,128)(2,1)}) custom-call(f32[128,8,256]{2,1,0:T(8,128)} %bitcast.5, s32[1,128]{1,0:T(1,128)} %bitcast.6, f32[8,64]{1,0:T(8,128)} %copy-done.17), custom_call_target="tpu_custom_call" | custom-call | flops 67108864 | bytes 1048576 | tf_op jit(solution)/shard_map/pallas_call | solution.py:524
  54.9 0.4 collective-permute-done.2.from_left_ref
  55.3 1.1 all-to-all-done.1.got_ref
  56.4 5.8 %shard_map.143 = (f32[512,4,128]{2,1,0:T(4,128)}, f32[8,64]{1,0:T(8,128)}, f32[8,64]{1,0:T(8,128)}, f32[2,8,512]{2,1,0:T(8,128)}, f32[2,8,512]{2,1,0:T(8,128)}, /*index=5*/f32[8,128]{1,0:T(8,128)}) custom-call(s32[1]{0:T(128)} %bitcast.device_ref, f32[384,4,128]{2,1,0:T(4,128)} %all-to-all-done.1.got_ref, bf16[128,8192]{1,0:T(8,128)(2,1)} %copy-done.1, ...), custom_call_target="tpu_custom_call" | custom-call | flops 67108864 | bytes 1048576 | tf_op jit(solution)/shard_map/pallas_call | solution.py:531
  62.2 0.0 copy-start.3
  62.2 0.0 copy-start.22
  62.3 4.8 %all-to-all-start.2 = ((f32[512,4,128]{2,1,0:T(4,128)}), f32[512,4,128]{2,1,0:T(4,128)S(1)}, u32[]{:S(2)}, u32[]{:S(2)}) async-start(f32[512,4,128]{2,1,0:T(4,128)} %get-tuple-element.59), calls=%async_computation.2 | async-start | bytes 2097152 | tf_op jit(solution)/shard_map/all_to_all | solution.py:31
  67.1 0.2 shard_map.144
  67.3 0.6 copy-done.18
  67.9 0.8 collective-permute-start.4
  68.8 6.3 %collective-permute-start.5 = (f32[8,128]{1,0:T(8,128)S(1)}, f32[8,128]{1,0:T(8,128)S(1)}, u32[]{:S(2)}, u32[]{:S(2)}) collective-permute-start(f32[8,128]{1,0:T(8,128)S(1)} %get-tuple-element.64), channel_id=1, source_target_pairs={{0,127},{1,0},{2,1},{3,2},{4,3},{5,4},{6,5},{7,6},{8,7},{9,8},{10,... | collective-permute-start | bytes 12296 | tf_op jit(solution)/shard_map/ppermute | solution.py:40
  75.1 0.2 shard_map.145.early_ref
  75.4 0.6 copy-done.11
  76.0 3.5 %collective-permute-done.5.from_right_ref = f32[8,128]{1,0:T(8,128)S(1)} collective-permute-done((f32[8,128]{1,0:T(8,128)S(1)}, f32[8,128]{1,0:T(8,128)S(1)}, u32[]{:S(2)}, u32[]{:S(2)}) %collective-permute-start.5) | collective-permute-done | bytes 4128 | tf_op jit(solution)/shard_map/ppermute | solution.py:40
  79.5 5.2 %collective-permute-done.4.from_left_ref = f32[8,256]{1,0:T(8,128)S(1)} collective-permute-done((f32[8,256]{1,0:T(8,128)S(1)}, f32[8,256]{1,0:T(8,128)S(1)}, u32[]{:S(2)}, u32[]{:S(2)}) %collective-permute-start.4) | collective-permute-done | bytes 8224 | tf_op jit(solution)/shard_map/ppermute | solution.py:40
  84.8 1.1 all-to-all-done.2.got_ref
  85.9 1.0 copy-done.26
  86.9 6.7 %shard_map.146 = (f32[128,3,2,128]{3,2,1,0:T(2,128)}, f32[8,64]{1,0:T(8,128)}, f32[2,8,512]{2,1,0:T(8,128)}, f32[2,8,512]{2,1,0:T(8,128)}) custom-call(s32[1]{0:T(128)} %bitcast.device_ref, f32[512,4,128]{2,1,0:T(4,128)} %copy-done.26, bf16[128,8192]{1,0:T(8,128)(2,1)} %copy-done.1, f32[2,8,512]{2,1,0:T(8,128)} %copy-done.18, f32[8,256]{1,0:T(8,128)} %copy-done.27, ...), custom_call_target="tpu_custom_call" | custom-call | flops 67108864 | bytes 1048576 | tf_op jit(solution)/shard_map/pallas_call | solution.py:541
  93.7 0.0 copy-start.23
  93.7 16.8 %all_to_all.30.got_ref.square_ref = f32[128,3,2,128]{3,2,1,0:T(2,128)S(1)} all-to-all(f32[128,3,2,128]{3,2,1,0:T(2,128)} %get-tuple-element.71), channel_id=1, replica_groups=mesh['sub_0'=4,'sub_1'=4,'sub_2'=2,'grp'=4] {'sub_0','sub_1','sub_2','grp'}, dimensions={0} | all-to-all | bytes 786432 | tf_op jit(solution)/shard_map/all_to_all | solution.py:31
  110.5 0.8 shard_map.148
  111.3 8.2 %all_to_all.31 = f32[8,8,384]{2,1,0:T(8,128)S(1)} all-to-all(f32[8,8,384]{2,1,0:T(8,128)S(1)} %get-tuple-element.76), channel_id=1, replica_groups=mesh['sub_0'=4,'sub_1'=4,'sub_2'=2,'grp'=4] {'sub_2','grp'}, dimensions={0} | all-to-all | bytes 196608 | tf_op jit(solution)/shard_map/all_to_all | solution.py:31
  119.5 0.7 broadcast_in_dim.3
  120.2 3.5 %all-to-all-start.5 = ((f32[16,8,384]{2,1,0:T(8,128)}), f32[16,8,384]{2,1,0:T(8,128)S(1)}, u32[]{:S(2)}, u32[]{:S(2)}) async-start(f32[16,8,384]{2,1,0:T(8,128)} %broadcast_in_dim.3), calls=%async_computation.5 | async-start | bytes 393216 | tf_op jit(solution)/shard_map/all_to_all | solution.py:31
  123.7 0.9 collective-permute-start.6
  124.6 7.6 %collective-permute-done.6.ghost_ref = f32[8,64]{1,0:T(8,128)S(1)} collective-permute-done((f32[8,64]{1,0:T(8,128)S(1)}, f32[8,64]{1,0:T(8,128)S(1)}, u32[]{:S(2)}, u32[]{:S(2)}) %collective-permute-start.6) | collective-permute-done | bytes 2080 | tf_op jit(solution)/shard_map/ppermute | solution.py:40
  132.2 0.3 shard_map.147.late_ref
  132.5 0.0 copy-done.15
  132.5 0.7 shard_map.149
  133.3 2.6 %shard_map.150 = (f32[8,1024]{1,0:T(8,128)}, f32[8,256]{1,0:T(8,128)}, f32[8,128]{1,0:T(8,128)}) custom-call(f32[16,8,384]{2,1,0:T(8,128)S(1)} %all-to-all-done.5.got_ref, f32[128,3,2,128]{3,2,1,0:T(2,128)S(1)} %all_to_all.30.got_ref.square_ref, bf16[2048,256]{1,0:T(8,128)(2,1)S(1)} %copy-done.5, f32[8,1024]{1,0:T(8,128)S(1)} %get-tuple-element.77.rows_ref), custom_call_target="tpu_custom_call" | custom-call | flops 16777216 | bytes 1048576 | tf_op jit(solution)/shard_map/pallas_call | solution.py:569
  (54 shorter events, 0.1 us)
Async XLA Ops:
  3.0 29.7 %all-to-all-start = ((f32[128,8,128]{2,1,0:T(8,128)}), f32[128,8,128]{2,1,0:T(8,128)S(1)}, u32[]{:S(2)}, u32[]{:S(2)}) async-start(f32[128,8,128]{2,1,0:T(8,128)} %get-tuple-element.43), calls=%async_computation | async-start | bytes 1048576 | tf_op jit(solution)/shard_map/all_to_all | solution.py:31
  14.2 16.1 %collective-permute-start = (f32[64,640]{1,0:T(8,128)}, f32[64,640]{1,0:T(8,128)S(1)}, u32[]{:S(2)}, u32[]{:S(2)}) collective-permute-start(f32[64,640]{1,0:T(8,128)} %get-tuple-element.46), channel_id=1, source_target_pairs={{0,127},{1,0},{2,1},{3,2},{4,3},{5,4},{6,5},{7,6},{8,7},{9,8},{10,... | collective-permute-start | bytes 491528 | tf_op jit(solution)/shard_map/ppermute | solution.py:40
  21.3 9.0 %collective-permute-start.1 = (f32[64,128]{1,0:T(8,128)}, f32[64,128]{1,0:T(8,128)S(1)}, u32[]{:S(2)}, u32[]{:S(2)}) collective-permute-start(f32[64,128]{1,0:T(8,128)} %get-tuple-element.47), channel_id=1, source_target_pairs={{0,1},{1,2},{2,3},{3,4},{4,5},{5,6},{6,7},{7,8},{8,9},{9,10},{10,1... | collective-permute-start | bytes 98312 | tf_op jit(solution)/shard_map/ppermute | solution.py:40
  21.3 1.6 %copy-start = (f32[2,512,512]{2,1,0:T(8,128)S(1)}, f32[2,512,512]{2,1,0:T(8,128)}, u32[]{:S(2)}) copy-start(f32[2,512,512]{2,1,0:T(8,128)} %rr_ref.5) | copy-start | bytes 6291460
  22.9 1.6 %copy-start.7 = (f32[64,8192]{1,0:T(8,128)S(1)}, f32[64,8192]{1,0:T(8,128)}, u32[]{:S(2)}) copy-start(f32[64,8192]{1,0:T(8,128)} %matrix_ref.1) | copy-start | bytes 6291460
  24.5 0.8 copy-start.20
  25.3 5.0 %copy-start.2 = (f32[2,64,512]{2,1,0:T(8,128)S(1)}, f32[2,64,512]{2,1,0:T(8,128)}, u32[]{:S(2)}) copy-start(f32[2,64,512]{2,1,0:T(8,128)} %modes_ref.13) | copy-start | bytes 786436
  26.9 7.7 %copy-start.1 = (bf16[128,8192]{1,0:T(8,128)(2,1)}, bf16[128,8192]{1,0:T(8,128)(2,1)S(1)}, u32[]{:S(2)}) copy-start(bf16[128,8192]{1,0:T(8,128)(2,1)S(1)} %get-tuple-element.45.parts_ref) | copy-start | bytes 6291460
  31.2 0.8 copy-start.6
  32.0 0.7 copy-start.8
  32.7 1.9 %copy-start.12 = (f32[64,256]{1,0:T(8,128)}, f32[64,256]{1,0:T(8,128)S(1)}, u32[]{:S(2)}) copy-start(f32[64,256]{1,0:T(8,128)S(1)} %get-tuple-element.49.coupling_ref) | copy-start | bytes 196612
  33.7 0.9 copy-start.9
  34.6 14.2 %copy-start.17 = (f32[8,64]{1,0:T(8,128)}, f32[8,64]{1,0:T(8,128)S(1)}, u32[]{:S(2)}) copy-start(f32[8,64]{1,0:T(8,128)S(1)} %get-tuple-element.52.after_ref.z_ref.before_ref) | copy-start | bytes 6148
  34.6 21.8 %all-to-all-start.1 = ((f32[384,4,128]{2,1,0:T(4,128)}), f32[384,4,128]{2,1,0:T(4,128)}, u32[]{:S(2)}, u32[]{:S(2)}) async-start(f32[384,4,128]{2,1,0:T(4,128)} %copy-done.9), calls=%async_computation.1 | async-start | bytes 1572864 | tf_op jit(solution)/shard_map/all_to_all | solution.py:31
  41.0 0.6 copy-start.19
  41.6 13.7 %collective-permute-start.2 = (f32[8,256]{1,0:T(8,128)S(1)}, f32[8,256]{1,0:T(8,128)S(1)}, u32[]{:S(2)}, u32[]{:S(2)}) collective-permute-start(f32[8,256]{1,0:T(8,128)S(1)} %get-tuple-element.55), channel_id=1, source_target_pairs={{0,1},{1,2},{2,3},{3,4},{4,5},{5,6},{6,7},{7,8},{8,9},{9,10},{10,1... | collective-permute-start | bytes 24584 | tf_op jit(solution)/shard_map/ppermute | solution.py:40
  42.5 12.4 %collective-permute-start.3 = (f32[8,128]{1,0:T(8,128)S(1)}, f32[8,128]{1,0:T(8,128)S(1)}, u32[]{:S(2)}, u32[]{:S(2)}) collective-permute-start(f32[8,128]{1,0:T(8,128)S(1)} %get-tuple-element.56), channel_id=1, source_target_pairs={{0,127},{1,0},{2,1},{3,2},{4,3},{5,4},{6,5},{7,6},{8,7},{9,8},{10,... | collective-permute-start | bytes 12296 | tf_op jit(solution)/shard_map/ppermute | solution.py:40
  54.9 1.5 %copy-start.30 = (f32[8,128]{1,0:T(8,128)}, f32[8,128]{1,0:T(8,128)S(1)}, u32[]{:S(2)}) copy-start(f32[8,128]{1,0:T(8,128)S(1)} %collective-permute-done.3.from_right_ref) | copy-start | bytes 12292
  55.3 1.1 copy-start.28
  62.2 4.8 %copy-start.3 = (f32[2,64,512]{2,1,0:T(8,128)S(1)}, f32[2,64,512]{2,1,0:T(8,128)}, u32[]{:S(2)}) copy-start(f32[2,64,512]{2,1,0:T(8,128)} %modes_ref.13) | copy-start | bytes 786436
  62.2 4.8 %copy-start.22 = (f32[2,8,512]{2,1,0:T(8,128)S(1)}, f32[2,8,512]{2,1,0:T(8,128)}, u32[]{:S(2)}) copy-start(f32[2,8,512]{2,1,0:T(8,128)} %get-tuple-element.60.local_ref) | copy-start | bytes 98308
  62.3 4.8 %copy-start.24 = (f32[8,64]{1,0:T(8,128)S(1)}, f32[8,64]{1,0:T(8,128)}, u32[]{:S(2)}) copy-start(f32[8,64]{1,0:T(8,128)} %get-tuple-element.61.z_ref.before_ref) | copy-start | bytes 6148
  62.3 12.8 %copy-start.10 = (bf16[128,512]{1,0:T(8,128)(2,1)S(1)}, bf16[128,512]{1,0:T(8,128)(2,1)}, u32[]{:S(2)}) copy-start(bf16[128,512]{1,0:T(8,128)(2,1)} %get-tuple-element.65.select_ref) | copy-start | bytes 393220
  62.3 12.8 %copy-start.16 = (f32[2,8,512]{2,1,0:T(8,128)S(1)}, f32[2,8,512]{2,1,0:T(8,128)}, u32[]{:S(2)}) copy-start(f32[2,8,512]{2,1,0:T(8,128)} %get-tuple-element.58.green_ref) | copy-start | bytes 98308
  62.3 23.6 %all-to-all-start.2 = ((f32[512,4,128]{2,1,0:T(4,128)}), f32[512,4,128]{2,1,0:T(4,128)S(1)}, u32[]{:S(2)}, u32[]{:S(2)}) async-start(f32[512,4,128]{2,1,0:T(4,128)} %get-tuple-element.59), calls=%async_computation.2 | async-start | bytes 2097152 | tf_op jit(solution)/shard_map/all_to_all | solution.py:31
  67.3 0.6 copy-start.18
  67.9 16.8 %collective-permute-start.4 = (f32[8,256]{1,0:T(8,128)S(1)}, f32[8,256]{1,0:T(8,128)S(1)}, u32[]{:S(2)}, u32[]{:S(2)}) collective-permute-start(f32[8,256]{1,0:T(8,128)S(1)} %get-tuple-element.63), channel_id=1, source_target_pairs={{0,1},{1,2},{2,3},{3,4},{4,5},{5,6},{6,7},{7,8},{8,9},{9,10},{10,1... | collective-permute-start | bytes 24584 | tf_op jit(solution)/shard_map/ppermute | solution.py:40
  68.8 10.8 %collective-permute-start.5 = (f32[8,128]{1,0:T(8,128)S(1)}, f32[8,128]{1,0:T(8,128)S(1)}, u32[]{:S(2)}, u32[]{:S(2)}) collective-permute-start(f32[8,128]{1,0:T(8,128)S(1)} %get-tuple-element.64), channel_id=1, source_target_pairs={{0,127},{1,0},{2,1},{3,2},{4,3},{5,4},{6,5},{7,6},{8,7},{9,8},{10,... | collective-permute-start | bytes 12296 | tf_op jit(solution)/shard_map/ppermute | solution.py:40
  75.4 0.6 copy-start.11
  79.5 6.4 %copy-start.29 = (f32[8,128]{1,0:T(8,128)}, f32[8,128]{1,0:T(8,128)S(1)}, u32[]{:S(2)}) copy-start(f32[8,128]{1,0:T(8,128)S(1)} %collective-permute-done.5.from_right_ref) | copy-start | bytes 12292
  84.8 1.1 copy-start.27
  85.9 1.0 copy-start.26
  86.9 23.6 %copy-start.5 = (bf16[2048,256]{1,0:T(8,128)(2,1)S(1)}, bf16[2048,256]{1,0:T(8,128)(2,1)}, u32[]{:S(2)}) copy-start(bf16[2048,256]{1,0:T(8,128)(2,1)} %get-tuple-element.72.basis_ref) | copy-start | bytes 3145732
  93.6 30.1 %copy-start.25 = (f32[8,64]{1,0:T(8,128)S(1)}, f32[8,64]{1,0:T(8,128)}, u32[]{:S(2)}) copy-start(f32[8,64]{1,0:T(8,128)} %get-tuple-element.70.z_ref) | copy-start | bytes 6148
  93.7 38.6 %copy-start.4 = (f32[2,64,512]{2,1,0:T(8,128)S(1)}, f32[2,64,512]{2,1,0:T(8,128)}, u32[]{:S(2)}) copy-start(f32[2,64,512]{2,1,0:T(8,128)} %modes_ref.13) | copy-start | bytes 786436
  93.7 38.6 %copy-start.23 = (f32[2,8,512]{2,1,0:T(8,128)S(1)}, f32[2,8,512]{2,1,0:T(8,128)}, u32[]{:S(2)}) copy-start(f32[2,8,512]{2,1,0:T(8,128)} %get-tuple-element.69.local_ref) | copy-start | bytes 98308
  93.7 38.8 %copy-start.13 = (f32[8,2,512]{2,1,0:T(2,128)S(1)}, f32[8,2,512]{2,1,0:T(2,128)}, u32[]{:S(2)}) copy-start(f32[8,2,512]{2,1,0:T(2,128)} %disp_ref.3) | copy-start | bytes 98308
  93.7 38.8 %copy-start.14 = (f32[8,2,512]{2,1,0:T(2,128)S(1)}, f32[8,2,512]{2,1,0:T(2,128)}, u32[]{:S(2)}) copy-start(f32[8,2,512]{2,1,0:T(2,128)} %vel_ref.3) | copy-start | bytes 98308
  93.7 38.8 %copy-start.15 = (f32[8,2,512]{2,1,0:T(2,128)S(1)}, f32[8,2,512]{2,1,0:T(2,128)}, u32[]{:S(2)}) copy-start(f32[8,2,512]{2,1,0:T(2,128)} %acc_ref.3) | copy-start | bytes 98308
  93.7 38.8 %copy-start.21 = (f32[2,8,512]{2,1,0:T(8,128)S(1)}, f32[2,8,512]{2,1,0:T(8,128)}, u32[]{:S(2)}) copy-start(f32[2,8,512]{2,1,0:T(8,128)} %get-tuple-element.68.image_ref) | copy-start | bytes 98308
  120.2 13.1 %all-to-all-start.5 = ((f32[16,8,384]{2,1,0:T(8,128)}), f32[16,8,384]{2,1,0:T(8,128)S(1)}, u32[]{:S(2)}, u32[]{:S(2)}) async-start(f32[16,8,384]{2,1,0:T(8,128)} %broadcast_in_dim.3), calls=%async_computation.5 | async-start | bytes 393216 | tf_op jit(solution)/shard_map/all_to_all | solution.py:31
  123.7 8.5 %collective-permute-start.6 = (f32[8,64]{1,0:T(8,128)S(1)}, f32[8,64]{1,0:T(8,128)S(1)}, u32[]{:S(2)}, u32[]{:S(2)}) collective-permute-start(f32[8,64]{1,0:T(8,128)S(1)} %copy-done.25), channel_id=1, source_target_pairs={{0,1},{1,2},{2,3},{3,4},{4,5},{5,6},{6,7},{7,8},{8,9},{9,10},{10,1... | collective-permute-start | bytes 6152 | tf_op jit(solution)/shard_map/ppermute | solution.py:40

commit v10 on v9

--- a/solution.py
+++ b/solution.py
@@ -199,23 +199,24 @@
     select_ref[...] = jnp.where(owner == rows.astype(f32), 1.0, 0.0).astype(bf16)
 
 
-def late_body(local_ref, z_ref, ghost_ref, modes_ref, late_ref):
+def late_body(local_ref, z_ref, modes_ref, late_ref):
     z = z_ref[...]
-    ghost = ghost_ref[...][:, NC:]
-    late_ref[0] = local_ref[0] + dot(z[:, :NC], modes_ref[0, NC:], NN) + dot(ghost, modes_ref[0, :NC], NN)
+    late_ref[0] = local_ref[0] + dot(z[:, :NC], modes_ref[0, NC:], NN)
     late_ref[1] = local_ref[1] + dot(z, modes_ref[1], NN)
 
 
 def out_body(
-    green_ref, image_ref, late_ref, gains_ref, disp_ref, vel_ref, acc_ref, disp_out_ref, vel_out_ref
+    green_ref, image_ref, late_ref, ghost_ref, modes_ref, gains_ref, disp_ref, vel_ref, acc_ref, disp_out_ref, vel_out_ref
 ):
     kappa_1, kappa_2 = gains_ref[0], gains_ref[1]
     case = lax.broadcasted_iota(jnp.int32, kappa_1.shape, 0)
     lane = lax.broadcasted_iota(jnp.int32, kappa_1.shape, 1)
     kappa_1 = jnp.sum(jnp.where(case == lane, kappa_1, 0.0), axis=1, keepdims=True)
     kappa_2 = jnp.sum(jnp.where(case == lane, kappa_2, 0.0), axis=1, keepdims=True)
+    ghost = ghost_ref[...][:, NC:]
+    late = [late_ref[0] + dot(ghost, modes_ref[0, :NC], NN), late_ref[1]]
     for s in range(2):
-        disp = green_ref[s] - kappa_1 * image_ref[s] + kappa_2 * late_ref[s]
+        disp = green_ref[s] - kappa_1 * image_ref[s] + kappa_2 * late[s]
         vel, acc = vel_ref[:, s, :], acc_ref[:, s, :]
         accel = (
             (disp - disp_ref[:, s, :]) * (1.0 / (newmark_beta * time_step * time_step))
@@ -548,7 +549,7 @@
     )(device, got_3, coarse_parts, *finish(local_1, z_1), select, sums_2, terms_1, early)
     got_4 = exchange(sent)
     ghost = shifted(z_2, 1)
-    (late,) = call(late_body, [pair], [VMEM] * 4, flops=1 << 20)(local_2, z_2, ghost, corner_modes)
+    (late,) = call(late_body, [pair], [VMEM] * 3, flops=1 << 20)(local_2, z_2, corner_modes)
     part, snapshots, gains = call(
         project_body,
         [
@@ -559,12 +560,13 @@
         [VMEM] * 2,
         flops=1 << 24,
     )(got_4, basis_parts)
+    part, ghost = lax.optimization_barrier((part, ghost))
     near = exchange(part, NEAR)
     near = near.sum(axis=0)
     got_5 = to_everyone(near, FAR)
     disp_new, vel_new = call(
-        out_body, [(disp_now.shape,), (disp_now.shape,)], [VMEM] * 7, flops=1 << 22
-    )(green, image_1, late, gains, disp_now, vel_now, acc_now)
+        out_body, [(disp_now.shape,), (disp_now.shape,)], [VMEM] * 9, flops=1 << 22
+    )(green, image_1, late, ghost, corner_modes, gains, disp_now, vel_now, acc_now)
     scale = math.sqrt(basis_rows.shape[0] * devices)
     new_columns, projection, factor = call(
         functools.partial(finish_body, scale=scale),

time: 137 us -> 135 us (0.985)
  blocking collectives: 24.9 us -> 8.16 us
  waiting for transfers between devices: 22.5 us -> 33 us
  starting transfers between devices: 48 us -> 52.8 us
    all_to_all x4 -> x5, waiting for transfers between devices: 2.26 us -> 20.4 us  [exchange(): return lax.all_to_all(pieces, axes, split_axis=0, concat_axis=0, tiled=True)]
    all_to_all x2 -> x1, blocking collectives: 24.9 us -> 8.16 us  [exchange(): return lax.all_to_all(pieces, axes, split_axis=0, concat_axis=0, tiled=True)]
    ppermute x7, waiting for transfers between devices: 20.3 us -> 12.6 us  [shifted(): lax.ppermute(array, AXES, [(i, (i + by) % count) for i in range(count)])]
    all_to_all x4 -> x5, starting transfers between devices: 25.6 us -> 30.4 us  [exchange(): return lax.all_to_all(pieces, axes, split_axis=0, concat_axis=0, tiled=True)]
  transfers between devices with their start and end apart: 11 -> 12, of which waited for: 7 -> 8; matrix products, arithmetic and copies ran while one was open for 0% -> 0% of each run, Pallas kernels for 8% -> 8%
where the time goes in v10:
time: 135 us; the launch traced here: 134 us
  starting transfers between devices  52.8 us (39%)
  waiting for transfers between devices  33 us (24%)
  Pallas kernels  29.7 us (22%)
  local copies, waits for them, and re-layouts  9.89 us (7%)
  blocking collectives  8.16 us (6%)
    all_to_all x5, starting transfers between devices, exchange(): return lax.all_to_all(pieces, axes, split_axis=0, concat_axis=0, tiled=True)  30.4 us
    ppermute x7, starting transfers between devices, shifted(): lax.ppermute(array, AXES, [(i, (i + by) % count) for i in range(count)])  22.4 us
    all_to_all x5, waiting for transfers between devices, exchange(): return lax.all_to_all(pieces, axes, split_axis=0, concat_axis=0, tiled=True)  20.4 us
    ppermute x7, waiting for transfers between devices, shifted(): lax.ppermute(array, AXES, [(i, (i + by) % count) for i in range(count)])  12.6 us
    unnamed x62, local copies, waits for them, and re-layouts  9.19 us
    all_to_all x1, blocking collectives, exchange(): return lax.all_to_all(pieces, axes, split_axis=0, concat_axis=0, tiled=True)  8.16 us
    pallas_call x1, Pallas kernels, shards(): call(join_third_body, [((devices, 3, 2, LANES),), z_shape, pair, pair], [...  6.75 us
    pallas_call x1, Pallas kernels, shards(): call(prep_body, [((2 * basis_rows.shape[0], rank), bf16), ((devices, 4, L...  6.09 us
  transfers between devices with their start and end apart: 12, of which 8 were waited for; matrix products, arithmetic and copies ran while one was open for 0% of the time, Pallas kernels for 8%

profile of v10, /device:TPU:0, one launch (start us, length us, event | category | flops | bytes accessed | tf_op | source)
XLA Modules:
  0.0 134.4 jit_solution(3718814155167387235)
XLA Ops:
  0.6 2.4 %shard_map.137 = (f32[128,8,128]{2,1,0:T(8,128)}, f32[2,8,512]{2,1,0:T(8,128)}, f32[64,640]{1,0:T(8,128)}, f32[64,128]{1,0:T(8,128)}) custom-call(s32[1]{0:T(128)} %bitcast.device_ref, f32[8,2,512]{2,1,0:T(2,128)} %load_ref.1, f32[2,512]{1,0:T(2,128)} %inertia_ref.1, f32[8,2,512]{2,1,0:T(2,128)} %disp_ref.3, f32[8,2,512]{2,1,0:T(2,128)} %vel_ref.3, ...), custom_call_target="tpu_custom_call" | custom-call | bytes 1048576 | tf_op jit(solution)/shard_map/pallas_call | solution.py:495
  3.0 11.2 %all-to-all-start = ((f32[128,8,128]{2,1,0:T(8,128)}), f32[128,8,128]{2,1,0:T(8,128)S(1)}, u32[]{:S(2)}, u32[]{:S(2)}) async-start(f32[128,8,128]{2,1,0:T(8,128)} %get-tuple-element.45), calls=%async_computation | async-start | bytes 1048576 | tf_op jit(solution)/shard_map/all_to_all | solution.py:31
  14.2 7.1 %collective-permute-start = (f32[64,640]{1,0:T(8,128)}, f32[64,640]{1,0:T(8,128)S(1)}, u32[]{:S(2)}, u32[]{:S(2)}) collective-permute-start(f32[64,640]{1,0:T(8,128)} %get-tuple-element.48), channel_id=1, source_target_pairs={{0,127},{1,0},{2,1},{3,2},{4,3},{5,4},{6,5},{7,6},{8,7},{9,8},{10,... | collective-permute-start | bytes 491528 | tf_op jit(solution)/shard_map/ppermute | solution.py:40
  21.3 1.6 %copy-done = f32[2,512,512]{2,1,0:T(8,128)S(1)} copy-done((f32[2,512,512]{2,1,0:T(8,128)S(1)}, f32[2,512,512]{2,1,0:T(8,128)}, u32[]{:S(2)}) %copy-start) | copy-done | bytes 2097176
  22.9 1.6 %copy-done.7 = f32[64,8192]{1,0:T(8,128)S(1)} copy-done((f32[64,8192]{1,0:T(8,128)S(1)}, f32[64,8192]{1,0:T(8,128)}, u32[]{:S(2)}) %copy-start.7) | copy-done | bytes 2097176
  24.5 0.8 copy-done.20
  25.3 1.6 %shard_map.138 = (bf16[128,8192]{1,0:T(8,128)(2,1)S(1)}, f32[2,8,512]{2,1,0:T(8,128)S(1)}) custom-call(f32[64,8192]{1,0:T(8,128)S(1)} %copy-done.7, f32[2,8,512]{2,1,0:T(8,128)S(1)} %copy-done.20, f32[2,512,512]{2,1,0:T(8,128)S(1)} %copy-done), custom_call_target="tpu_custom_call" | custom-call | flops 67108864 | bytes 1048576 | tf_op jit(solution)/shard_map/pallas_call | solution.py:504
  26.9 3.4 %collective-permute-done.1.left_ref = f32[64,128]{1,0:T(8,128)S(1)} collective-permute-done((f32[64,128]{1,0:T(8,128)}, f32[64,128]{1,0:T(8,128)S(1)}, u32[]{:S(2)}, u32[]{:S(2)}) %collective-permute-start.1) | collective-permute-done | bytes 32800 | tf_op jit(solution)/shard_map/ppermute | solution.py:40
  30.3 0.9 shard_map.139
  31.2 0.8 copy-done.6
  32.0 0.7 copy-done.8
  32.7 1.0 shard_map.140
  33.7 0.9 copy-done.9
  34.6 6.2 %all-to-all-start.1 = ((f32[384,4,128]{2,1,0:T(4,128)}), f32[384,4,128]{2,1,0:T(4,128)}, u32[]{:S(2)}, u32[]{:S(2)}) async-start(f32[384,4,128]{2,1,0:T(4,128)} %copy-done.9), calls=%async_computation.1 | async-start | bytes 1572864 | tf_op jit(solution)/shard_map/all_to_all | solution.py:31
  40.8 0.2 shard_map.142
  41.0 0.6 copy-done.19
  41.6 0.9 collective-permute-start.2
  42.5 6.3 %collective-permute-start.3 = (f32[8,128]{1,0:T(8,128)S(1)}, f32[8,128]{1,0:T(8,128)S(1)}, u32[]{:S(2)}, u32[]{:S(2)}) collective-permute-start(f32[8,128]{1,0:T(8,128)S(1)} %get-tuple-element.58), channel_id=1, source_target_pairs={{0,127},{1,0},{2,1},{3,2},{4,3},{5,4},{6,5},{7,6},{8,7},{9,8},{10,... | collective-permute-start | bytes 12296 | tf_op jit(solution)/shard_map/ppermute | solution.py:40
  48.8 6.1 %shard_map.141 = (bf16[2048,256]{1,0:T(8,128)(2,1)}, f32[128,4,128]{2,1,0:T(4,128)}, bf16[128,512]{1,0:T(8,128)(2,1)}) custom-call(f32[128,8,256]{2,1,0:T(8,128)} %bitcast.5, s32[1,128]{1,0:T(1,128)} %bitcast.6, f32[8,64]{1,0:T(8,128)} %copy-done.17), custom_call_target="tpu_custom_call" | custom-call | flops 67108864 | bytes 1048576 | tf_op jit(solution)/shard_map/pallas_call | solution.py:525
  54.9 0.4 collective-permute-done.2.from_left_ref
  55.3 1.1 all-to-all-done.1.got_ref
  56.4 5.8 %shard_map.143 = (f32[512,4,128]{2,1,0:T(4,128)}, f32[8,64]{1,0:T(8,128)}, f32[8,64]{1,0:T(8,128)}, f32[2,8,512]{2,1,0:T(8,128)}, f32[2,8,512]{2,1,0:T(8,128)}, /*index=5*/f32[8,128]{1,0:T(8,128)}) custom-call(s32[1]{0:T(128)} %bitcast.device_ref, f32[384,4,128]{2,1,0:T(4,128)} %all-to-all-done.1.got_ref, bf16[128,8192]{1,0:T(8,128)(2,1)} %copy-done.1, ...), custom_call_target="tpu_custom_call" | custom-call | flops 67108864 | bytes 1048576 | tf_op jit(solution)/shard_map/pallas_call | solution.py:532
  62.2 0.0 copy-start.3
  62.2 0.0 copy-start.22
  62.3 4.8 %all-to-all-start.2 = ((f32[512,4,128]{2,1,0:T(4,128)}), f32[512,4,128]{2,1,0:T(4,128)S(1)}, u32[]{:S(2)}, u32[]{:S(2)}) async-start(f32[512,4,128]{2,1,0:T(4,128)} %get-tuple-element.61), calls=%async_computation.2 | async-start | bytes 2097152 | tf_op jit(solution)/shard_map/all_to_all | solution.py:31
  67.1 0.2 shard_map.144
  67.3 0.6 copy-done.18
  67.9 0.8 collective-permute-start.4
  68.7 6.3 %collective-permute-start.5 = (f32[8,128]{1,0:T(8,128)S(1)}, f32[8,128]{1,0:T(8,128)S(1)}, u32[]{:S(2)}, u32[]{:S(2)}) collective-permute-start(f32[8,128]{1,0:T(8,128)S(1)} %get-tuple-element.66), channel_id=1, source_target_pairs={{0,127},{1,0},{2,1},{3,2},{4,3},{5,4},{6,5},{7,6},{8,7},{9,8},{10,... | collective-permute-start | bytes 12296 | tf_op jit(solution)/shard_map/ppermute | solution.py:40
  75.1 0.2 shard_map.145.early_ref
  75.4 0.6 copy-done.11
  76.0 3.5 %collective-permute-done.5.from_right_ref = f32[8,128]{1,0:T(8,128)S(1)} collective-permute-done((f32[8,128]{1,0:T(8,128)S(1)}, f32[8,128]{1,0:T(8,128)S(1)}, u32[]{:S(2)}, u32[]{:S(2)}) %collective-permute-start.5) | collective-permute-done | bytes 4128 | tf_op jit(solution)/shard_map/ppermute | solution.py:40
  79.5 5.2 %collective-permute-done.4.from_left_ref = f32[8,256]{1,0:T(8,128)S(1)} collective-permute-done((f32[8,256]{1,0:T(8,128)S(1)}, f32[8,256]{1,0:T(8,128)S(1)}, u32[]{:S(2)}, u32[]{:S(2)}) %collective-permute-start.4) | collective-permute-done | bytes 8224 | tf_op jit(solution)/shard_map/ppermute | solution.py:40
  84.8 1.1 all-to-all-done.2.got_ref
  85.9 1.0 copy-done.26
  86.9 6.8 %shard_map.146 = (f32[128,3,2,128]{3,2,1,0:T(2,128)}, f32[8,64]{1,0:T(8,128)}, f32[2,8,512]{2,1,0:T(8,128)}, f32[2,8,512]{2,1,0:T(8,128)}) custom-call(s32[1]{0:T(128)} %bitcast.device_ref, f32[512,4,128]{2,1,0:T(4,128)} %copy-done.26, bf16[128,8192]{1,0:T(8,128)(2,1)} %copy-done.1, f32[2,8,512]{2,1,0:T(8,128)} %copy-done.18, f32[8,256]{1,0:T(8,128)} %copy-done.27, ...), custom_call_target="tpu_custom_call" | custom-call | flops 67108864 | bytes 1048576 | tf_op jit(solution)/shard_map/pallas_call | solution.py:542
  93.6 0.0 copy-start.13
  93.7 4.8 %all-to-all-start.3 = ((f32[128,3,2,128]{3,2,1,0:T(2,128)}), f32[128,3,2,128]{3,2,1,0:T(2,128)S(1)}, u32[]{:S(2)}, u32[]{:S(2)}) async-start(f32[128,3,2,128]{3,2,1,0:T(2,128)} %get-tuple-element.73), calls=%async_computation.3 | async-start | bytes 786432 | tf_op jit(solution)/shard_map/all_to_all | solution.py:31
  98.5 0.9 collective-permute-start.6
  99.4 10.9 %all-to-all-done.3.got_ref.square_ref = f32[128,3,2,128]{3,2,1,0:T(2,128)S(1)} async-done(((f32[128,3,2,128]{3,2,1,0:T(2,128)}), f32[128,3,2,128]{3,2,1,0:T(2,128)S(1)}, u32[]{:S(2)}, u32[]{:S(2)}) %all-to-all-start.3) | async-done | bytes 393248 | tf_op jit(solution)/shard_map/all_to_all | solution.py:31
  110.3 0.8 shard_map.148
  111.1 8.2 %all_to_all.30 = f32[8,8,384]{2,1,0:T(8,128)S(1)} all-to-all(f32[8,8,384]{2,1,0:T(8,128)S(1)} %get-tuple-element.80), channel_id=1, replica_groups=mesh['sub_0'=4,'sub_1'=4,'sub_2'=2,'grp'=4] {'sub_2','grp'}, dimensions={0} | all-to-all | bytes 196608 | tf_op jit(solution)/shard_map/all_to_all | solution.py:31
  119.2 0.7 broadcast_in_dim.3
  119.9 3.5 %all-to-all-start.5 = ((f32[16,8,384]{2,1,0:T(8,128)}), f32[16,8,384]{2,1,0:T(8,128)S(1)}, u32[]{:S(2)}, u32[]{:S(2)}) async-start(f32[16,8,384]{2,1,0:T(8,128)} %broadcast_in_dim.3), calls=%async_computation.5 | async-start | bytes 393216 | tf_op jit(solution)/shard_map/all_to_all | solution.py:31
  123.5 0.2 shard_map.147.late_ref
  123.7 0.9 shard_map.149
  124.6 7.2 %all-to-all-done.5.got_ref = f32[16,8,384]{2,1,0:T(8,128)S(1)} async-done(((f32[16,8,384]{2,1,0:T(8,128)}), f32[16,8,384]{2,1,0:T(8,128)S(1)}, u32[]{:S(2)}, u32[]{:S(2)}) %all-to-all-start.5) | async-done | bytes 196640 | tf_op jit(solution)/shard_map/all_to_all | solution.py:31
  131.8 2.6 %shard_map.150 = (f32[8,1024]{1,0:T(8,128)}, f32[8,256]{1,0:T(8,128)}, f32[8,128]{1,0:T(8,128)}) custom-call(f32[16,8,384]{2,1,0:T(8,128)S(1)} %all-to-all-done.5.got_ref, f32[128,3,2,128]{3,2,1,0:T(2,128)S(1)} %all-to-all-done.3.got_ref.square_ref, bf16[2048,256]{1,0:T(8,128)(2,1)S(1)} %copy-done.5, f32[8,1024]{1,0:T(8,128)S(1)} %get-tuple-element.81.rows_ref), custom_call_target="tpu_custom_call" | custom-call | flops 16777216 | bytes 1048576 | tf_op jit(solution)/shard_map/pallas_call | solution.py:571
  (55 shorter events, 0.1 us)
Async XLA Ops:
  3.0 29.6 %all-to-all-start = ((f32[128,8,128]{2,1,0:T(8,128)}), f32[128,8,128]{2,1,0:T(8,128)S(1)}, u32[]{:S(2)}, u32[]{:S(2)}) async-start(f32[128,8,128]{2,1,0:T(8,128)} %get-tuple-element.45), calls=%async_computation | async-start | bytes 1048576 | tf_op jit(solution)/shard_map/all_to_all | solution.py:31
  14.2 16.1 %collective-permute-start = (f32[64,640]{1,0:T(8,128)}, f32[64,640]{1,0:T(8,128)S(1)}, u32[]{:S(2)}, u32[]{:S(2)}) collective-permute-start(f32[64,640]{1,0:T(8,128)} %get-tuple-element.48), channel_id=1, source_target_pairs={{0,127},{1,0},{2,1},{3,2},{4,3},{5,4},{6,5},{7,6},{8,7},{9,8},{10,... | collective-permute-start | bytes 491528 | tf_op jit(solution)/shard_map/ppermute | solution.py:40
  21.3 9.0 %collective-permute-start.1 = (f32[64,128]{1,0:T(8,128)}, f32[64,128]{1,0:T(8,128)S(1)}, u32[]{:S(2)}, u32[]{:S(2)}) collective-permute-start(f32[64,128]{1,0:T(8,128)} %get-tuple-element.49), channel_id=1, source_target_pairs={{0,1},{1,2},{2,3},{3,4},{4,5},{5,6},{6,7},{7,8},{8,9},{9,10},{10,1... | collective-permute-start | bytes 98312 | tf_op jit(solution)/shard_map/ppermute | solution.py:40
  21.3 1.6 %copy-start = (f32[2,512,512]{2,1,0:T(8,128)S(1)}, f32[2,512,512]{2,1,0:T(8,128)}, u32[]{:S(2)}) copy-start(f32[2,512,512]{2,1,0:T(8,128)} %rr_ref.5) | copy-start | bytes 6291460
  22.9 1.6 %copy-start.7 = (f32[64,8192]{1,0:T(8,128)S(1)}, f32[64,8192]{1,0:T(8,128)}, u32[]{:S(2)}) copy-start(f32[64,8192]{1,0:T(8,128)} %matrix_ref.1) | copy-start | bytes 6291460
  24.5 0.8 copy-start.20
  25.3 5.0 %copy-start.2 = (f32[2,64,512]{2,1,0:T(8,128)S(1)}, f32[2,64,512]{2,1,0:T(8,128)}, u32[]{:S(2)}) copy-start(f32[2,64,512]{2,1,0:T(8,128)} %modes_ref.15) | copy-start | bytes 786436
  26.9 7.7 %copy-start.1 = (bf16[128,8192]{1,0:T(8,128)(2,1)}, bf16[128,8192]{1,0:T(8,128)(2,1)S(1)}, u32[]{:S(2)}) copy-start(bf16[128,8192]{1,0:T(8,128)(2,1)S(1)} %get-tuple-element.47.parts_ref) | copy-start | bytes 6291460
  31.2 0.8 copy-start.6
  32.0 0.7 copy-start.8
  32.7 1.9 %copy-start.12 = (f32[64,256]{1,0:T(8,128)}, f32[64,256]{1,0:T(8,128)S(1)}, u32[]{:S(2)}) copy-start(f32[64,256]{1,0:T(8,128)S(1)} %get-tuple-element.51.coupling_ref) | copy-start | bytes 196612
  33.7 0.9 copy-start.9
  34.6 14.2 %copy-start.17 = (f32[8,64]{1,0:T(8,128)}, f32[8,64]{1,0:T(8,128)S(1)}, u32[]{:S(2)}) copy-start(f32[8,64]{1,0:T(8,128)S(1)} %get-tuple-element.54.after_ref.z_ref.before_ref) | copy-start | bytes 6148
  34.6 21.8 %all-to-all-start.1 = ((f32[384,4,128]{2,1,0:T(4,128)}), f32[384,4,128]{2,1,0:T(4,128)}, u32[]{:S(2)}, u32[]{:S(2)}) async-start(f32[384,4,128]{2,1,0:T(4,128)} %copy-done.9), calls=%async_computation.1 | async-start | bytes 1572864 | tf_op jit(solution)/shard_map/all_to_all | solution.py:31
  41.0 0.6 copy-start.19
  41.6 13.7 %collective-permute-start.2 = (f32[8,256]{1,0:T(8,128)S(1)}, f32[8,256]{1,0:T(8,128)S(1)}, u32[]{:S(2)}, u32[]{:S(2)}) collective-permute-start(f32[8,256]{1,0:T(8,128)S(1)} %get-tuple-element.57), channel_id=1, source_target_pairs={{0,1},{1,2},{2,3},{3,4},{4,5},{5,6},{6,7},{7,8},{8,9},{9,10},{10,1... | collective-permute-start | bytes 24584 | tf_op jit(solution)/shard_map/ppermute | solution.py:40
  42.5 12.4 %collective-permute-start.3 = (f32[8,128]{1,0:T(8,128)S(1)}, f32[8,128]{1,0:T(8,128)S(1)}, u32[]{:S(2)}, u32[]{:S(2)}) collective-permute-start(f32[8,128]{1,0:T(8,128)S(1)} %get-tuple-element.58), channel_id=1, source_target_pairs={{0,127},{1,0},{2,1},{3,2},{4,3},{5,4},{6,5},{7,6},{8,7},{9,8},{10,... | collective-permute-start | bytes 12296 | tf_op jit(solution)/shard_map/ppermute | solution.py:40
  54.9 1.5 %copy-start.30 = (f32[8,128]{1,0:T(8,128)}, f32[8,128]{1,0:T(8,128)S(1)}, u32[]{:S(2)}) copy-start(f32[8,128]{1,0:T(8,128)S(1)} %collective-permute-done.3.from_right_ref) | copy-start | bytes 12292
  55.3 1.1 copy-start.28
  62.2 4.8 %copy-start.3 = (f32[2,64,512]{2,1,0:T(8,128)S(1)}, f32[2,64,512]{2,1,0:T(8,128)}, u32[]{:S(2)}) copy-start(f32[2,64,512]{2,1,0:T(8,128)} %modes_ref.15) | copy-start | bytes 786436
  62.2 4.8 %copy-start.22 = (f32[2,8,512]{2,1,0:T(8,128)S(1)}, f32[2,8,512]{2,1,0:T(8,128)}, u32[]{:S(2)}) copy-start(f32[2,8,512]{2,1,0:T(8,128)} %get-tuple-element.62.local_ref) | copy-start | bytes 98308
  62.2 4.8 %copy-start.24 = (f32[8,64]{1,0:T(8,128)S(1)}, f32[8,64]{1,0:T(8,128)}, u32[]{:S(2)}) copy-start(f32[8,64]{1,0:T(8,128)} %get-tuple-element.63.z_ref.before_ref) | copy-start | bytes 6148
  62.2 12.8 %copy-start.10 = (bf16[128,512]{1,0:T(8,128)(2,1)S(1)}, bf16[128,512]{1,0:T(8,128)(2,1)}, u32[]{:S(2)}) copy-start(bf16[128,512]{1,0:T(8,128)(2,1)} %get-tuple-element.67.select_ref) | copy-start | bytes 393220
  62.3 12.8 %copy-start.16 = (f32[2,8,512]{2,1,0:T(8,128)S(1)}, f32[2,8,512]{2,1,0:T(8,128)}, u32[]{:S(2)}) copy-start(f32[2,8,512]{2,1,0:T(8,128)} %get-tuple-element.60.green_ref) | copy-start | bytes 98308
  62.3 23.6 %all-to-all-start.2 = ((f32[512,4,128]{2,1,0:T(4,128)}), f32[512,4,128]{2,1,0:T(4,128)S(1)}, u32[]{:S(2)}, u32[]{:S(2)}) async-start(f32[512,4,128]{2,1,0:T(4,128)} %get-tuple-element.61), calls=%async_computation.2 | async-start | bytes 2097152 | tf_op jit(solution)/shard_map/all_to_all | solution.py:31
  67.3 0.6 copy-start.18
  67.9 16.8 %collective-permute-start.4 = (f32[8,256]{1,0:T(8,128)S(1)}, f32[8,256]{1,0:T(8,128)S(1)}, u32[]{:S(2)}, u32[]{:S(2)}) collective-permute-start(f32[8,256]{1,0:T(8,128)S(1)} %get-tuple-element.65), channel_id=1, source_target_pairs={{0,1},{1,2},{2,3},{3,4},{4,5},{5,6},{6,7},{7,8},{8,9},{9,10},{10,1... | collective-permute-start | bytes 24584 | tf_op jit(solution)/shard_map/ppermute | solution.py:40
  68.7 10.8 %collective-permute-start.5 = (f32[8,128]{1,0:T(8,128)S(1)}, f32[8,128]{1,0:T(8,128)S(1)}, u32[]{:S(2)}, u32[]{:S(2)}) collective-permute-start(f32[8,128]{1,0:T(8,128)S(1)} %get-tuple-element.66), channel_id=1, source_target_pairs={{0,127},{1,0},{2,1},{3,2},{4,3},{5,4},{6,5},{7,6},{8,7},{9,8},{10,... | collective-permute-start | bytes 12296 | tf_op jit(solution)/shard_map/ppermute | solution.py:40
  75.3 0.6 copy-start.11
  79.5 6.4 %copy-start.29 = (f32[8,128]{1,0:T(8,128)}, f32[8,128]{1,0:T(8,128)S(1)}, u32[]{:S(2)}) copy-start(f32[8,128]{1,0:T(8,128)S(1)} %collective-permute-done.5.from_right_ref) | copy-start | bytes 12292
  84.7 1.1 copy-start.27
  85.9 1.0 copy-start.26
  86.9 23.4 %copy-start.5 = (bf16[2048,256]{1,0:T(8,128)(2,1)S(1)}, bf16[2048,256]{1,0:T(8,128)(2,1)}, u32[]{:S(2)}) copy-start(bf16[2048,256]{1,0:T(8,128)(2,1)} %get-tuple-element.74.basis_ref) | copy-start | bytes 3145732
  93.6 29.8 %copy-start.4 = (f32[2,64,512]{2,1,0:T(8,128)S(1)}, f32[2,64,512]{2,1,0:T(8,128)}, u32[]{:S(2)}) copy-start(f32[2,64,512]{2,1,0:T(8,128)} %modes_ref.15) | copy-start | bytes 786436
  93.6 29.9 %copy-start.23 = (f32[2,8,512]{2,1,0:T(8,128)S(1)}, f32[2,8,512]{2,1,0:T(8,128)}, u32[]{:S(2)}) copy-start(f32[2,8,512]{2,1,0:T(8,128)} %get-tuple-element.71.local_ref) | copy-start | bytes 98308
  93.6 29.8 %copy-start.25 = (f32[8,64]{1,0:T(8,128)S(1)}, f32[8,64]{1,0:T(8,128)}, u32[]{:S(2)}) copy-start(f32[8,64]{1,0:T(8,128)} %get-tuple-element.72.z_ref) | copy-start | bytes 6148
  93.6 30.1 %copy-start.13 = (f32[8,2,512]{2,1,0:T(2,128)S(1)}, f32[8,2,512]{2,1,0:T(2,128)}, u32[]{:S(2)}) copy-start(f32[8,2,512]{2,1,0:T(2,128)} %disp_ref.3) | copy-start | bytes 98308
  93.7 30.0 %copy-start.14 = (f32[8,2,512]{2,1,0:T(2,128)S(1)}, f32[8,2,512]{2,1,0:T(2,128)}, u32[]{:S(2)}) copy-start(f32[8,2,512]{2,1,0:T(2,128)} %vel_ref.3) | copy-start | bytes 98308
  93.7 30.0 %copy-start.15 = (f32[8,2,512]{2,1,0:T(2,128)S(1)}, f32[8,2,512]{2,1,0:T(2,128)}, u32[]{:S(2)}) copy-start(f32[8,2,512]{2,1,0:T(2,128)} %acc_ref.3) | copy-start | bytes 98308
  93.7 30.0 %copy-start.21 = (f32[2,8,512]{2,1,0:T(8,128)S(1)}, f32[2,8,512]{2,1,0:T(8,128)}, u32[]{:S(2)}) copy-start(f32[2,8,512]{2,1,0:T(8,128)} %get-tuple-element.70.image_ref) | copy-start | bytes 98308
  93.7 16.6 %all-to-all-start.3 = ((f32[128,3,2,128]{3,2,1,0:T(2,128)}), f32[128,3,2,128]{3,2,1,0:T(2,128)S(1)}, u32[]{:S(2)}, u32[]{:S(2)}) async-start(f32[128,3,2,128]{3,2,1,0:T(2,128)} %get-tuple-element.73), calls=%async_computation.3 | async-start | bytes 786432 | tf_op jit(solution)/shard_map/all_to_all | solution.py:31
  98.5 12.6 %collective-permute-start.6 = (f32[8,64]{1,0:T(8,128)}, f32[8,64]{1,0:T(8,128)S(1)}, u32[]{:S(2)}, u32[]{:S(2)}) collective-permute-start(f32[8,64]{1,0:T(8,128)} %get-tuple-element.72.z_ref), channel_id=1, source_target_pairs={{0,1},{1,2},{2,3},{3,4},{4,5},{5,6},{6,7},{7,8},{8,9},{9,10},{10,1... | collective-permute-start | bytes 6152 | tf_op jit(solution)/shard_map/ppermute | solution.py:40
  119.9 11.9 %all-to-all-start.5 = ((f32[16,8,384]{2,1,0:T(8,128)}), f32[16,8,384]{2,1,0:T(8,128)S(1)}, u32[]{:S(2)}, u32[]{:S(2)}) async-start(f32[16,8,384]{2,1,0:T(8,128)} %broadcast_in_dim.3), calls=%async_computation.5 | async-start | bytes 393216 | tf_op jit(solution)/shard_map/all_to_all | solution.py:31
